TPU v7x, 32 devices: a whole 2x2x4 slice. The times are simulated.
32 devices in a mesh: vp: 4 (over z), dp: 8 (over y, x, core).
Axes of the slice: x: 2, y: 2, z: 4, core: 2. Of those that a mesh axis runs over, the one named last changes fastest.
Arguments:
- hidden: bfloat16 [128, 512, 1024], P('dp')
- mask_pos: int32 [128, 77], P('dp')
- labels: int32 [128, 77], P('dp')
- w_trans: bfloat16 [1024, 1024], replicated
- b_trans: float32 [1024], replicated
- ln_gain: float32 [1024], replicated
- ln_bias: float32 [1024], replicated
- emb_table: bfloat16 [50304, 1024], P('vp')
- b_vocab: float32 [50304], P('vp')
Outputs:
- output 1: float32 [], replicated
- output 2: bfloat16 [128, 512, 1024], P('dp')
- output 3: float32 [1024, 1024], replicated
- output 4: float32 [1024], replicated
- output 5: float32 [1024], replicated
- output 6: float32 [1024], replicated
- output 7: float32 [50304, 1024], P('vp')
- output 8: float32 [50304], P('vp')
All inputs are finite; a program needn't handle non-finite values.
Results may differ from a plain program's by a relative error of at most 0.0106996.
Values sent between devices are 32-bit elements.
A program may use at most 1 GiB of HBM per device.

v0:
```python
import functools

import jax
import jax.numpy as jnp
from jax import lax
from jax.experimental import pallas as pl
from jax.experimental.pallas import tpu as pltpu
from jax.sharding import PartitionSpec as P


F32, BF16, I32 = jnp.float32, jnp.bfloat16, jnp.int32
NT = (((1,), (1,)), ((), ()))
NN = (((1,), (0,)), ((), ()))
VB = 1024
VMEM_LIMIT = 60 << 20
COVER = 100
CH = 16


def row_cuts(rows, parts=4):
    cuts = [16 * (rows // 16 * k // parts) for k in range(parts)] + [rows]
    return list(zip(cuts[:-1], cuts[1:]))


def dot(a, b, dims):
    return lax.dot_general(a, b, dims, preferred_element_type=F32)


def stats_kernel(n_vocab, u_ref, emb_ref, b_ref, lab_ref, logits_ref, stat_ref, m_sc, s_sc, l_sc):
    i, n_blocks = pl.program_id(0), pl.num_programs(0)
    lane = lax.broadcasted_iota(I32, (1, 128), 1)

    @pl.when(i == 0)
    def _():
        m_sc[...] = jnp.full_like(m_sc, -jnp.inf)
        s_sc[...] = jnp.zeros_like(s_sc)
        l_sc[...] = jnp.zeros_like(l_sc)

    def run(width):
        wide = -(-width // 128) * 128
        for r0, r1 in row_cuts(u_ref.shape[0]):
            tile = dot(u_ref[r0:r1, :], emb_ref[:wide, :], NT) + b_ref[:, :wide]
            if wide > width:
                tile = jnp.where(lax.broadcasted_iota(I32, (1, wide), 1) < width, tile, -jnp.inf)
            logits_ref[r0:r1, :wide] = tile
            for q in range(r0, r1, CH):
                rs = slice(q, min(q + CH, r1))
                parts = [logits_ref[rs, k:k + 128] for k in range(0, wide, 128)]
                m_old = m_sc[rs, :]
                m_new = functools.reduce(jnp.maximum, parts, m_old)
                s_new = s_sc[rs, :] * jnp.exp(m_old - m_new)
                l_new = l_sc[rs, :]
                lab = lab_ref[rs, :] - i * VB
                for k, part in enumerate(parts):
                    s_new += jnp.exp(part - m_new)
                    l_new = jnp.where(lab == lane + k * 128, part, l_new)
                m_sc[rs, :], s_sc[rs, :], l_sc[rs, :] = m_new, s_new, l_new

    tail = n_vocab % VB
    if tail:
        pl.when(i < n_blocks - 1)(functools.partial(run, VB))
        pl.when(i == n_blocks - 1)(functools.partial(run, tail))
    else:
        run(VB)

    @pl.when(i == n_blocks - 1)
    def _():
        m_t, s_t, l_t = m_sc[...].T, s_sc[...].T, l_sc[...].T
        m_all = jnp.max(m_t, axis=0, keepdims=True)
        stat_ref[0:1, :] = m_all
        stat_ref[1:2, :] = jnp.sum(s_t * jnp.exp(m_t - m_all), axis=0, keepdims=True)
        stat_ref[2:3, :] = jnp.sum(l_t, axis=0, keepdims=True)
        stat_ref[3:8, :] = jnp.zeros_like(stat_ref[3:8, :])


def stats(u, emb, bias, lab):
    t, e = u.shape
    v = emb.shape[0]
    n = pl.cdiv(v, VB)
    whole = lambda *s: pl.BlockSpec(s, lambda i: (0,) * len(s))
    return pl.pallas_call(
        functools.partial(stats_kernel, v),
        grid=(n,),
        in_specs=[whole(t, e), pl.BlockSpec((VB, e), lambda i: (i, 0)), pl.BlockSpec((1, VB), lambda i: (0, i)), whole(t, 128)],
        out_specs=[pl.BlockSpec((t, VB), lambda i: (0, i)), whole(8, t)],
        out_shape=[jax.ShapeDtypeStruct((t, v), F32), jax.ShapeDtypeStruct((8, t), F32)],
        scratch_shapes=[pltpu.VMEM((t, 128), F32)] * 3,
        compiler_params=pltpu.CompilerParams(dimension_semantics=("arbitrary",), vmem_limit_bytes=VMEM_LIMIT),
        cost_estimate=pl.CostEstimate(flops=(2 * t * v * e) // COVER, bytes_accessed=t * v * 4 + v * e * 2, transcendentals=t * v),
        name="stats",
    )(u, emb, bias, lab)


def du_kernel(n_vocab, scale, logits_ref, emb_ref, lse_ref, lab_ref, du_ref, db_ref, g_sc, db_sc):
    i, n_blocks = pl.program_id(0), pl.num_programs(0)
    t = logits_ref.shape[0]
    lane = lax.broadcasted_iota(I32, (1, 128), 1)

    @pl.when(i == 0)
    def _():
        du_ref[...] = jnp.zeros_like(du_ref)

    def run(width):
        wide = -(-width // 128) * 128
        emb = emb_ref[:wide, :]
        if wide > width:
            emb = jnp.where(lax.broadcasted_iota(I32, (wide, 1), 0) < width, emb, jnp.zeros_like(emb))
        for r0, r1 in row_cuts(t):
            sums = [None] * (wide // 128)
            for q in range(r0, r1, 16):
                rs = slice(q, q + 16)
                lse = lse_ref[rs, :]
                lab = lab_ref[rs, :] - i * VB
                for k in range(wide // 128):
                    c = k * 128
                    g = jnp.exp(logits_ref[rs, c:c + 128] - lse)
                    g -= jnp.where(lab == lane + c, scale, 0.0)
                    if c + 128 > width:
                        g = jnp.where(lane < width - c, g, 0.0)
                    part = g[:8] + g[8:]
                    sums[k] = part if sums[k] is None else sums[k] + part
                    g_sc[rs, c:c + 128] = g.astype(BF16)
            for k in range(wide // 128):
                cs = slice(k * 128, (k + 1) * 128)
                db_sc[:, cs] = sums[k] if r0 == 0 else db_sc[:, cs] + sums[k]
            du_ref[r0:r1, :] += dot(g_sc[r0:r1, :wide], emb, NN)
        db_ref[:, :wide] = jnp.sum(db_sc[:, :wide], axis=0, keepdims=True)

    tail = n_vocab % VB
    if tail:
        pl.when(i < n_blocks - 1)(functools.partial(run, VB))
        pl.when(i == n_blocks - 1)(functools.partial(run, tail))
    else:
        run(VB)

    @pl.when(i == n_blocks - 1)
    def _():
        du_ref[...] = du_ref[...].astype(BF16).astype(F32)


def du_pass(scale, padded, logits, emb, lse, lab):
    t, v = logits.shape
    e = emb.shape[1]
    n = pl.cdiv(v, VB)
    whole = lambda *s: pl.BlockSpec(s, lambda i: (0,) * len(s))
    return pl.pallas_call(
        functools.partial(du_kernel, v, scale),
        grid=(n,),
        in_specs=[pl.BlockSpec((t, VB), lambda i: (0, i)), pl.BlockSpec((VB, e), lambda i: (i, 0)), whole(t, 128), whole(t, 128)],
        out_specs=[whole(padded, e), pl.BlockSpec((1, VB), lambda i: (0, i))],
        out_shape=[jax.ShapeDtypeStruct((padded, e), F32), jax.ShapeDtypeStruct((1, v), F32)],
        scratch_shapes=[pltpu.VMEM((t, VB), BF16), pltpu.VMEM((8, VB), F32)],
        compiler_params=pltpu.CompilerParams(dimension_semantics=("arbitrary",), vmem_limit_bytes=VMEM_LIMIT),
        cost_estimate=pl.CostEstimate(flops=(2 * t * v * e) // COVER, bytes_accessed=t * v * 4 + v * e * 2, transcendentals=t * v),
        name="du_pass",
    )(logits, emb, lse, lab)


LN_EPS = 1e-5
CORE, X, Y = 1, 2, 4
CHIPS = (0, X, Y, X | Y)
ANY = pl.BlockSpec(memory_space=pl.ANY)
VMEM = pl.BlockSpec(memory_space=pltpu.VMEM)
SMEM = pl.BlockSpec(memory_space=pltpu.SMEM)
DMA = pltpu.SemaphoreType.DMA


def gelu_norm(a):
    cdf = 0.5 * (1.0 + lax.erf(a * (0.5 ** 0.5)))
    g = a * cdf
    centered = g - jnp.mean(g, axis=1, keepdims=True)
    rstd = lax.rsqrt(jnp.mean(centered * centered, axis=1, keepdims=True) + LN_EPS)
    return cdf, centered * rstd, rstd


def head_kernel(n_masks, cut, hid, pos_ref, w_ref, b_ref, gain_ref, bias_ref, z_out, pre_out, u_out, lo_out, hi_out,
                hbuf, zf, zb, pre_v, ub, uf, in_sem, out_sem):
    n_seq, seq_len = hid.shape[0], hid.shape[1]
    n_loc, padded = n_seq * n_masks, zb.shape[0]
    loads = [pltpu.make_async_copy(hid.at[b], hbuf.at[b], in_sem.at[b]) for b in range(n_seq)]
    for c in loads:
        c.start()
    lane = lax.broadcasted_iota(I32, (1, 128), 1)
    zb[n_loc:, :] = jnp.zeros((padded - n_loc, zb.shape[1]), BF16)
    pre_v[n_loc:, :] = jnp.zeros((padded - n_loc, zb.shape[1]), F32)
    cuts = [0, cut // 32 * 16, cut, cut + (n_loc - cut) // 32 * 16, n_loc]
    done, stores = 0, []

    def send(src, dst, r0, r1, base):
        c = pltpu.make_async_copy(src.at[r0:r1, :], dst.at[r0 - base:r1 - base, :], out_sem.at[len(stores)])
        c.start()
        stores.append(c)

    for b in range(n_seq):
        loads[b].wait()
        hot = jnp.concatenate([jnp.where(pos_ref[b] == lane + j, 1.0, 0.0).astype(BF16) for j in range(0, seq_len, 128)], axis=1)
        zf[b * n_masks:(b + 1) * n_masks, :] = dot(hot, hbuf[b], NN)[:n_masks, :]
        while done < 4 and cuts[done + 1] <= (b + 1) * n_masks:
            r0, r1 = cuts[done], cuts[done + 1]
            z = zf[r0:r1, :].astype(BF16)
            zb[r0:r1, :] = z
            a = dot(z, w_ref[...], NN) + b_ref[...]
            pre_v[r0:r1, :] = a
            _, normed, _ = gelu_norm(a)
            u = (normed * gain_ref[...] + bias_ref[...]).astype(BF16)
            ub[r0:r1, :] = u
            uf[r0:r1, :] = u.astype(F32)
            done += 1
            end = padded if done == 4 else r1
            send(uf, hi_out if r0 >= cut else lo_out, r0, r1, cut if r0 >= cut else 0)
            send(ub, u_out, r0, r1, 0)
            send(zb, z_out, r0, end, 0)
            send(pre_v, pre_out, r0, end, 0)
    for c in stores:
        c.wait()


def head_pass(n_masks, padded, cut, hidden, pos, w, b, gain, bias):
    n_seq, seq_len, e = hidden.shape
    n_loc = n_seq * n_masks
    sds = jax.ShapeDtypeStruct
    return pl.pallas_call(
        functools.partial(head_kernel, n_masks, cut),
        in_specs=[ANY] + [VMEM] * 5,
        out_specs=[ANY] * 5,
        out_shape=[sds((padded, e), BF16), sds((padded, e), F32), sds((n_loc, e), BF16), sds((cut, e), F32), sds((n_loc - cut, e), F32)],
        scratch_shapes=[
            pltpu.VMEM((n_seq, seq_len, e), BF16), pltpu.VMEM((n_loc, e), F32), pltpu.VMEM((padded, e), BF16), pltpu.VMEM((padded, e), F32),
            pltpu.VMEM((n_loc, e), BF16), pltpu.VMEM((n_loc, e), F32), DMA((n_seq,)), DMA((16,)),
        ],
        compiler_params=pltpu.CompilerParams(vmem_limit_bytes=VMEM_LIMIT),
        cost_estimate=pl.CostEstimate(flops=(4 * n_loc * e * e) // COVER, bytes_accessed=hidden.size * 2 + n_loc * e * 16, transcendentals=n_loc * e),
        name="head",
    )(hidden, pos, w, b, gain, bias)


def rows_kernel(mode, scale, m, cut, n_loc, chips, n_put, first, pos, emb_hbm, bias_ref, lse_ref, lab_ref, *rest):
    rest = list(rest)
    take = lambda n: [rest.pop(0) for _ in range(n)]
    src = [[take(2), take(2)] for _ in chips]
    if not first and mode != "first":
        take(1)
    puts = take(n_put)
    parts = take(2) if mode == "last" else []
    if mode == "first":
        own_ref, side_ref = take(2)
    else:
        out_ref, big_ref = take(2)
    buf, ub, emb_sc, g_sc, acc, hold, sem, tok_sem, in_sem, out_sem = rest
    i, n_blocks = pl.program_id(0), pl.num_programs(0)
    row = lambda j: pl.multiple_of(pos[j], 8)
    core = pos[2]

    def fetch(step, slot):
        for g, chip in enumerate(src):
            for rel, (lo, hi) in enumerate(chip):
                @pl.when(step == 2 * g + (core ^ rel))
                def _():
                    pltpu.make_async_copy(lo, buf.at[slot, :cut, :], tok_sem.at[slot, 0]).start()
                    pltpu.make_async_copy(hi, buf.at[slot, cut:n_loc, :], tok_sem.at[slot, 1]).start()

    loads = [pltpu.make_async_copy(p, hold.at[j, :p.shape[0], :], in_sem.at[j]) for j, p in enumerate(puts)]
    stores = [pltpu.make_async_copy(hold.at[j, :p.shape[0], :], big_ref.at[pl.ds(row(3 + j), p.shape[0]), :], out_sem.at[j])
              for j, p in enumerate(puts)]

    @pl.when(i == 0)
    def _():
        fetch(0, 0)
        cp = pltpu.make_async_copy(emb_hbm.at[pl.ds(row(0), m), :], emb_sc, sem)
        cp.start()
        acc[...] = jnp.zeros_like(acc)
        ub[n_loc:, :] = jnp.zeros((ub.shape[0] - n_loc, ub.shape[1]), BF16)
        cp.wait()

    slot = lax.rem(i, 2)
    lo, hi = src[0][0]
    pltpu.make_async_copy(lo, buf.at[slot, :cut, :], tok_sem.at[slot, 0]).wait()
    pltpu.make_async_copy(hi, buf.at[slot, cut:n_loc, :], tok_sem.at[slot, 1]).wait()
    fetch(i + 1, 1 - slot)

    @pl.when(i == 1)
    def _():
        for c in loads:
            c.start()

    @pl.when(i == 4)
    def _():
        for a, b in zip(loads, stores):
            a.wait()
            b.start()

    ub[:n_loc, :] = buf[slot].astype(BF16)
    u = ub[...]
    g_id = lax.div(i, 2)
    rel = chips[0] + 2 * g_id + (lax.rem(i, 2) ^ core)
    lse, lab = lse_ref[rel], lab_ref[rel]
    mid = -(-m // 32) * 16
    for r0, r1 in ((0, mid), (mid, m)):
        part = dot(emb_sc[r0:r1, :], u, NT)
        hit = lab == lax.broadcasted_iota(I32, (r1 - r0, 1), 0) + (pos[1] + r0)
        g = jnp.exp(part + bias_ref[r0:r1, :] - lse) - jnp.where(hit, scale, 0.0)
        g_sc[r0:r1, :] = g.astype(BF16)
        acc[g_id, r0:r1, :] += dot(g_sc[r0:r1, :], u, NN)

    @pl.when(i == n_blocks - 1)
    def _():
        if mode == "first":
            own_ref[...] = acc[0]
            side_ref[...] = acc[1] + acc[2]
        else:
            if mode == "whole":
                out_ref[...] = (acc[0] + acc[3]) + (acc[1] + acc[2])
            else:
                out_ref[...] = (parts[0][...] + acc[0]) + parts[1][...]
            own = pltpu.make_async_copy(out_ref, big_ref.at[pl.ds(row(0), m), :], sem)
            own.start()
            for b in stores:
                b.wait()
            own.wait()


def rows_pass(mode, scale, v_rows, m, cut, pos, emb, bias, lse, lab, tokens, big=None, puts=(), parts=()):
    e = emb.shape[1]
    n_loc = tokens[0][0].shape[0] + tokens[0][1].shape[0]
    padded = lse.shape[-1]
    chips = {"whole": CHIPS, "first": CHIPS[:3], "last": CHIPS[3:]}[mode]
    src = [half for c in chips for rel in (0, CORE) for half in tokens[c | rel]]
    has_big = big is not None and mode != "first"
    extra = src + ([big] if has_big else []) + list(puts)
    n_put = max(1, len(puts))
    sds = jax.ShapeDtypeStruct
    block = lambda *s: pl.BlockSpec(s, lambda i, p: (0,) * len(s))
    if mode == "first":
        out_specs, out_shape = [block(m, e)] * 2, [sds((m, e), F32)] * 2
    else:
        out_specs, out_shape = [block(m, e), ANY], [sds((m, e), F32), sds((v_rows, e), F32)]
    gs = pltpu.PrefetchScalarGridSpec(
        num_scalar_prefetch=1,
        grid=(2 * len(chips),),
        in_specs=[ANY, block(m, 1), block(*lse.shape), block(*lab.shape)] + [ANY] * len(extra) + [block(m, e)] * len(parts),
        out_specs=out_specs,
        scratch_shapes=[
            pltpu.VMEM((2, n_loc, e), F32), pltpu.VMEM((padded, e), BF16), pltpu.VMEM((m, e), BF16), pltpu.VMEM((m, padded), BF16),
            pltpu.VMEM((len(chips), m, e), F32), pltpu.VMEM((n_put, max([p.shape[0] for p in puts] + [8]), e), F32),
            DMA, DMA((2, 2)), DMA((n_put,)), DMA((n_put,)),
        ],
    )
    t = n_loc * 2 * len(chips)
    return pl.pallas_call(
        functools.partial(rows_kernel, mode, scale, m, cut, n_loc, chips, len(puts), not has_big),
        grid_spec=gs,
        out_shape=out_shape,
        input_output_aliases={5 + len(src): 1} if has_big else {},
        compiler_params=pltpu.CompilerParams(dimension_semantics=("arbitrary",), vmem_limit_bytes=VMEM_LIMIT),
        cost_estimate=pl.CostEstimate(flops=(4 * t * m * e) // COVER, bytes_accessed=t * e * 4 + m * e * 6, transcendentals=t * m),
    )(pos, emb, bias, lse, lab, *extra, *parts)


def put_kernel(n, pos, *refs):
    pieces, (out_ref, hold, in_sem, out_sem) = refs[1:1 + n], refs[1 + n:]
    loads, stores = [], []
    for j, p in enumerate(pieces):
        slot = hold.at[j, :p.shape[0], :]
        loads.append(pltpu.make_async_copy(p, slot, in_sem.at[j]))
        stores.append(pltpu.make_async_copy(slot, out_ref.at[pl.ds(pl.multiple_of(pos[j], 8), p.shape[0]), :], out_sem.at[j]))
    for a in loads:
        a.start()
    for a, b in zip(loads, stores):
        a.wait()
        b.start()
    for b in stores:
        b.wait()


def put_rows(pos, big, pieces):
    n, e = len(pieces), big.shape[1]
    return pl.pallas_call(
        functools.partial(put_kernel, n),
        in_specs=[SMEM] + [ANY] * (n + 1),
        out_specs=ANY,
        out_shape=jax.ShapeDtypeStruct(big.shape, big.dtype),
        scratch_shapes=[pltpu.VMEM((n, max(p.shape[0] for p in pieces), e), F32), DMA((n,)), DMA((n,))],
        input_output_aliases={1: 0},
        compiler_params=pltpu.CompilerParams(vmem_limit_bytes=VMEM_LIMIT),
        cost_estimate=pl.CostEstimate(flops=(sum(p.size for p in pieces)) // COVER, bytes_accessed=sum(p.size for p in pieces) * 8, transcendentals=0),
        name="put_rows",
    )(pos, big, *pieces)


def back_kernel(d_rows, db_rows, vp, pre_ref, z_ref, du_ref, w_ref, gain_ref, loss_ref, db_ref, dz_ref, pack_ref):
    a, du = pre_ref[...], du_ref[...]
    cdf, normed, rstd = gelu_norm(a)
    dn = du * gain_ref[...]
    dg = rstd * (dn - jnp.mean(dn, axis=1, keepdims=True) - normed * jnp.mean(dn * normed, axis=1, keepdims=True))
    da = dg * (cdf + a * (jnp.exp(-0.5 * a * a) * 0.3989422804014327))
    dab = da.astype(BF16)
    dz_ref[...] = dot(dab, w_ref[...], NT).astype(BF16).astype(F32)
    pack_ref[:d_rows, :] = lax.dot_general(z_ref[...], dab, (((0,), (0,)), ((), ())), preferred_element_type=F32)
    pack_ref[d_rows:, :] = jnp.zeros((pack_ref.shape[0] - d_rows, pack_ref.shape[1]), F32)
    for j, x in enumerate((da, du * normed, du)):
        pack_ref[d_rows + j:d_rows + j + 1, :] = jnp.sum(x, axis=0, keepdims=True)
    pack_ref[d_rows + 3:d_rows + 4, :] = loss_ref[...]
    pack_ref[pl.ds(pl.multiple_of(d_rows + 8 + db_rows * vp[0], 8), db_rows), :] = db_ref[...]


def back_pass(n_shards, vp, pre, z, du, w, gain, loss, db):
    rows, e = du.shape
    db_rows = db.shape[0]
    n_pack = e + 8 + n_shards * db_rows
    block = lambda *s: pl.BlockSpec(s, lambda i, p: (0,) * len(s))
    share = pl.BlockSpec((rows, e), lambda i, p: (p[0], 0))
    gs = pltpu.PrefetchScalarGridSpec(
        num_scalar_prefetch=1,
        grid=(1,),
        in_specs=[share, share, block(rows, e), block(e, e), block(1, e), block(1, e), block(db_rows, e)],
        out_specs=[block(rows, e), block(n_pack, e)],
    )
    return pl.pallas_call(
        functools.partial(back_kernel, e, db_rows),
        grid_spec=gs,
        out_shape=[jax.ShapeDtypeStruct((rows, e), F32), jax.ShapeDtypeStruct((n_pack, e), F32)],
        compiler_params=pltpu.CompilerParams(dimension_semantics=("arbitrary",), vmem_limit_bytes=VMEM_LIMIT),
        cost_estimate=pl.CostEstimate(flops=(4 * rows * e * e) // COVER, bytes_accessed=rows * e * 16 + e * e * 6, transcendentals=rows * e * 2),
        name="back",
    )(vp, pre, z, du, w, gain, loss, db)


def spread_kernel(n_masks, vp, pos_ref, *refs):
    pieces, (out_ref, dz, obuf, in_sem, out_sem) = refs[:4], refs[4:]
    share = pieces[0].shape[0]
    loads = [pltpu.make_async_copy(p, dz.at[pl.ds(pl.multiple_of((vp[0] ^ k) * share, 8), share), :], in_sem.at[k]) for k, p in enumerate(pieces)]
    for c in loads:
        c.start()
    for c in loads:
        c.wait()
    n_seq, seq_len, _ = out_ref.shape
    place = lax.broadcasted_iota(I32, (seq_len, 1), 0)
    slots = pos_ref.shape[2]
    stores = []
    for b in range(n_seq):
        if b >= 4:
            stores[b - 4].wait()
        hot = jnp.where(place == pos_ref[b], 1.0, 0.0).astype(BF16)
        rows = dz[b * n_masks:b * n_masks + slots, :].astype(BF16)
        obuf[b % 4] = dot(hot, rows, NN).astype(BF16)
        c = pltpu.make_async_copy(obuf.at[b % 4], out_ref.at[b], out_sem.at[b])
        c.start()
        stores.append(c)
    for c in stores[-4:]:
        c.wait()


def spread_pass(n_masks, shape, vp, pos, pieces):
    share, e = pieces[0].shape
    return pl.pallas_call(
        functools.partial(spread_kernel, n_masks),
        in_specs=[SMEM, VMEM] + [ANY] * 4,
        out_specs=ANY,
        out_shape=jax.ShapeDtypeStruct(shape, BF16),
        scratch_shapes=[pltpu.VMEM((4 * share, e), F32), pltpu.VMEM((4,) + shape[1:], BF16), DMA((4,)), DMA((shape[0],))],
        compiler_params=pltpu.CompilerParams(vmem_limit_bytes=VMEM_LIMIT),
        cost_estimate=pl.CostEstimate(flops=(2 * shape[0] * shape[1] * 128 * e) // COVER, bytes_accessed=shape[0] * shape[1] * e * 2, transcendentals=0),
        name="spread",
    )(vp, pos, *pieces)


def after(x, *deps):
    return lax.optimization_barrier((x, deps))[0]


def solution(mesh):
    n_groups, n_shards = mesh.shape["dp"], mesh.shape["vp"]

    def swap(a, bit):
        return lax.ppermute(a, "dp", [(d, d ^ bit) for d in range(n_groups)])

    def swap_vp(a, bit):
        return lax.ppermute(a, "vp", [(d, d ^ bit) for d in range(n_shards)])

    def hop(a):
        return lax.ppermute(a, "dp", [(d, d ^ (Y if d & CORE else X)) for d in range(n_groups)])

    def local_step(hidden, mask_pos, labels, w_trans, b_trans, ln_gain, ln_bias, emb_table, b_vocab):
        n_rows, _, width = hidden.shape
        n_masks = mask_pos.shape[1]
        shard_rows = emb_table.shape[0]
        n_loc = n_rows * n_masks
        n_tokens = n_loc * n_groups
        padded = -(-n_loc // 256) * 256
        slots = -(-n_masks // 16) * 16
        cut = n_loc // 32 * 16
        dp, vp = lax.axis_index("dp"), lax.axis_index("vp")
        row_start = vp * shard_rows
        scale = 1.0 / n_tokens

        pos_pad = jnp.pad(mask_pos, ((0, 0), (0, slots - n_masks)), constant_values=-1)
        z, pre, u, u_lo, u_hi = head_pass(
            n_masks, padded, cut, hidden, jnp.broadcast_to(pos_pad[:, :, None], (n_rows, slots, 128)),
            w_trans, b_trans[None], ln_gain[None], ln_bias[None])

        x_lo, y_hi = swap(u_lo, X), swap(u_hi, Y)
        x_hi, y_lo = swap(u_hi, X), swap(u_lo, Y)
        c_lo, c_hi = swap(u_lo, CORE), swap(u_hi, CORE)

        flat_labels = labels.reshape(n_loc)
        lab_local = flat_labels - row_start
        lab_local = jnp.where((lab_local >= 0) & (lab_local < shard_rows), lab_local, -1)
        lab_local = jnp.broadcast_to(lab_local[:, None], (n_loc, 128))
        logits, stat = stats(u, emb_table, b_vocab[None], lab_local)
        all_stats = [stat] + [swap_vp(stat, b) for b in range(1, n_shards)]
        order = lambda f: f(f(all_stats[0], all_stats[1]), f(all_stats[2], all_stats[3]))
        global_max = order(lambda a, b: jnp.maximum(a, b))[0]
        log_norm = global_max + jnp.log(sum(s[1] * jnp.exp(s[0] - global_max) for s in all_stats))
        loss_part = jnp.where(vp == 0, jnp.sum(log_norm - sum(s[2] for s in all_stats)), 0.0)
        lse = log_norm + jnp.log(jnp.float32(n_tokens))
        x_lo, y_hi = after((x_lo, y_hi), lse)
        d_lo, d_hi = swap(x_lo, Y), swap(y_hi, X)
        info = jnp.stack([lse, flat_labels.astype(F32)])
        info = [info] + [swap(info, b) for b in range(1, n_groups)]

        du_part, db_part = du_pass(scale, padded, logits, emb_table, jnp.broadcast_to(lse[:, None], (n_loc, 128)), lab_local)
        du_share = lax.psum_scatter(du_part, "vp", scatter_dimension=0, tiled=True)

        info = jnp.stack(after(info, du_part))
        fill = ((0, 0), (0, padded - n_loc))
        lse_all = jnp.pad(info[:, 0], fill, constant_values=jnp.inf)[:, None]
        lab_all = jnp.pad(info[:, 1].astype(I32), fill, constant_values=-1)[:, None]
        x_lo, x_hi, y_lo, y_hi = after((x_lo, x_hi, y_lo, y_hi), du_part)
        tokens = {
            0: (u_lo, u_hi), CORE: (c_lo, c_hi), X: (x_lo, x_hi), Y: (y_lo, y_hi),
            X | CORE: (swap(x_lo, CORE), swap(x_hi, CORE)), Y | CORE: (swap(y_lo, CORE), swap(y_hi, CORE)),
        }

        core, mine = dp & 1, (dp >> 1 ^ dp >> 2) & 1
        half, quarter = shard_rows // 2, shard_rows // 4
        my_start = mine * half + core * quarter
        twin_start = mine * half + (1 - core) * quarter
        far_start = (1 - mine) * half + core * quarter
        far_twin_start = (1 - mine) * half + (1 - core) * quarter
        bias_col = lax.dynamic_slice(b_vocab, (my_start,), (quarter,))[:, None]
        weights = (640, 608, 576, 528, 448, 344)
        ends = [0]
        for w in weights[:-1]:
            ends.append(ends[-1] + max(16, quarter * w // sum(weights) // 16 * 16))
        spans = list(zip(ends, ends[1:] + [quarter]))

        def rows(mode, k, **kw):
            s0, s1 = spans[k]
            puts = kw.pop("ready", [])
            pos = jnp.stack([my_start + s0, row_start + my_start + s0, core] + [p for p, _ in puts])
            pos = after(pos, *kw.pop("wait", ()))
            return rows_pass(mode, scale, shard_rows, s1 - s0, cut, pos, emb_table, bias_col[s0:s1], lse_all, lab_all, tokens,
                             puts=[a for _, a in puts], **kw)

        early = 2
        parts = []
        for k in range(early):
            parts.append(rows("first", k))
        d_lo, d_hi = after((d_lo, d_hi), *parts)
        tokens[X | Y] = (d_lo, d_hi)
        tokens[X | Y | CORE] = (swap(d_lo, CORE), swap(d_hi, CORE))

        big, arrived, sent, waits = None, [], [], {}
        lag = 4
        for k, (s0, s1) in enumerate(spans):
            ready = []
            if k >= lag:
                ready = arrived[k - lag]
            if k < early:
                chunk, big = rows("last", k, parts=parts[k], big=big)
            else:
                chunk, big = rows("whole", k, big=big, ready=ready, wait=waits.pop(k, ()))
            twin, far = swap(chunk, CORE), hop(chunk)
            sent.append(far)
            arrived.append([(twin_start + s0, twin)])
            for j in {1: (), 2: (0, 1)}.get(k, (k - 1,) if k else ()):
                prev = after(sent[j], chunk)
                passed = swap(prev, CORE)
                arrived[j] += [(far_start + spans[j][0], prev), (far_twin_start + spans[j][0], passed)]
            if k == 2:
                du_share = after(du_share, chunk)
                loss_row = jnp.pad(loss_part[None, None], ((0, 0), (0, width - 1)))
                db_rows = -(-shard_rows // width // 8) * 8
                db_mat = jnp.pad(db_part[0], (0, db_rows * width - shard_rows)).reshape(db_rows, width)
                dz, pack = back_pass(n_shards, vp[None], pre, z, du_share, w_trans, ln_gain[None], loss_row, db_mat)
                waits[k + 1] = (dz,)
                pack = lax.psum(pack, ("vp", "dp"))
                dz = [dz] + [swap_vp(dz, b) for b in range(1, n_shards)]
        far = sent[-1]
        s0 = spans[-1][0]
        arrived[-1] += [(far_start + s0, far), (far_twin_start + s0, swap(far, CORE))]
        dz = after(dz, chunk)
        d_hidden = spread_pass(n_masks, hidden.shape, vp[None], pos_pad[:, None], dz)
        for ready in (arrived[2] + arrived[3], arrived[4], arrived[5]):
            big = put_rows(jnp.stack([p for p, _ in ready]), big, [a for _, a in ready])

        vec = pack[width:width + 4]
        db = lax.dynamic_slice(pack, (width + 8 + db_rows * vp, 0), (db_rows, width)).reshape(-1)[:shard_rows]
        return vec[3, 0] / n_tokens, d_hidden, pack[:width], vec[0], vec[1], vec[2], big, db

    in_specs = (P("dp", None, None), P("dp", None), P("dp", None), P(None, None), P(None), P(None), P(None), P("vp", None), P("vp"))
    out_specs = (P(), P("dp", None, None), P(None, None), P(None), P(None), P(None), P("vp", None), P("vp"))
    return jax.shard_map(local_step, mesh=mesh, in_specs=in_specs, out_specs=out_specs, check_vma=False)
```

profile of v0, /device:TPU:0, one launch (start us, length us, event | category | flops | bytes accessed | tf_op | source)
XLA Modules:
  0.0 668.1 jit_solution(7109049566723991736)
XLA Ops:
  9.0 15.2 %head.1 = (bf16[1280,1024]{1,0:T(8,128)(2,1)}, f32[1280,1024]{1,0:T(8,128)}, bf16[1232,1024]{1,0:T(8,128)(2,1)}, f32[608,1024]{1,0:T(8,128)}, f32[624,1024]{1,0:T(8,128)}) custom-call(bf16[16,512,1024]{2,1,0:T(8,128)(2,1)} %hid.1, s32[16,80,128]{2,1,0:T(8,128)} %broadcast_in_dim.53.pos_ref, bf16[1024,1024]{1,0:T(8,128)(2,1)} %w_ref.3, f32[1,1024]{1,0:T(1,128)} %bitcast.70, ...), custom_call_target="tpu_custom_call" | custom-call | flops 51673824 | bytes 36962304 | tf_op jit(solution)/shard_map/head/pallas_call | solution.py:222
  24.2 3.0 collective-permute-start.12
  27.3 1.5 collective-permute-start.13
  31.3 54.0 %stats.1 = (f32[1232,12576]{1,0:T(8,128)}, f32[8,1232]{1,0:T(8,128)}) custom-call(bf16[1232,1024]{1,0:T(8,128)(2,1)} %get-tuple-element.64.u_ref, bf16[12576,1024]{1,0:T(8,128)(2,1)} %emb_hbm.15, f32[1,12576]{1,0:T(1,128)} %broadcast_in_dim.57.b_ref, s32[1232,128]{1,0:T(8,128)} %broadcast_in_dim.59.lab_ref), custom_call_target="tpu_custom_call" | custom-call | flops 317309568 | bytes 87730176 | tf_op jit(solution)/shard_map/stats/pallas_call | solution.py:81
  85.3 4.0 collective-permute-start.2
  89.3 2.2 collective-permute-done.2
  92.6 4.1 collective-permute-done.1
  96.7 1.6 collective-permute-start
  98.3 2.6 collective-permute-done
  104.2 46.0 %du_pass.1 = (f32[1280,1024]{1,0:T(8,128)}, f32[1,12576]{1,0:T(1,128)}) custom-call(f32[1232,12576]{1,0:T(8,128)} %get-tuple-element.65.logits_ref, bf16[12576,1024]{1,0:T(8,128)(2,1)} %emb_hbm.15, f32[1232,128]{1,0:T(8,128)} %broadcast_in_dim.60.lse_ref, s32[1232,128]{1,0:T(8,128)} %broadcast_in_dim.59.lab_ref), custom_call_target="tpu_custom_call" | custom-call | flops 317309568 | bytes 87730176 | tf_op jit(solution)/shard_map/du_pass/pallas_call | solution.py:146
  152.4 1.7 collective-permute-start.4
  154.1 1.3 collective-permute-done.3
  155.4 1.5 collective-permute-start.5
  156.9 1.5 collective-permute-start.6
  158.5 1.5 collective-permute-start.7
  160.5 1.9 collective-permute-start.8
  162.4 2.0 collective-permute-start.9
  165.1 1.3 collective-permute-done.9
  166.4 1.5 collective-permute-start.21
  167.9 1.6 collective-permute-start.20
  173.7 3.6 collective-permute-done.18.rest_10_
  177.4 1.4 copy-done.2
  178.8 28.9 %shard_map.153 = (f32[608,1024]{1,0:T(8,128)}, f32[608,1024]{1,0:T(8,128)}) custom-call(s32[3]{0:T(128)} %get-tuple-element.136.pos, bf16[12576,1024]{1,0:T(8,128)(2,1)} %emb_hbm.15, f32[608,1]{1,0:T(8,128)} %slice.141.bias_ref, f32[8,1,1280]{2,1,0:T(1,128)} %copy.56.lse_ref, s32[8,1,1280]{2,1,0:T(1,128)} %broadcast_in_dim.62.lab_ref, ...), custom_call_target="tpu_custom_call" | custom-call | flops 184088000 | bytes 34013184 | tf_op jit(solution)/shard_map/pallas_call | solution.py:349
  207.7 30.2 %shard_map.152 = (f32[640,1024]{1,0:T(8,128)}, f32[640,1024]{1,0:T(8,128)}) custom-call(s32[3]{0:T(128)} %get-tuple-element.135.pos, bf16[12576,1024]{1,0:T(8,128)(2,1)} %emb_hbm.15, f32[640,1]{1,0:T(8,128)} %slice.140.bias_ref, f32[8,1,1280]{2,1,0:T(1,128)} %copy.56.lse_ref, s32[8,1,1280]{2,1,0:T(1,128)} %broadcast_in_dim.62.lab_ref, ...), custom_call_target="tpu_custom_call" | custom-call | flops 193776848 | bytes 34209792 | tf_op jit(solution)/shard_map/pallas_call | solution.py:349
  238.5 8.2 %collective-permute-done.22.rest_2_.rest_14_ = f32[608,1024]{1,0:T(8,128)} collective-permute-done((f32[608,1024]{1,0:T(8,128)}, f32[608,1024]{1,0:T(8,128)}, u32[]{:S(2)}, u32[]{:S(2)}) %collective-permute-start.22) | collective-permute-done | bytes 2490400 | tf_op jit(solution)/shard_map/ppermute | solution.py:475
  246.7 1.5 copy-done.1
  248.2 17.4 %shard_map.154 = (f32[640,1024]{1,0:T(8,128)}, f32[12576,1024]{1,0:T(8,128)}) custom-call(s32[3]{0:T(128)} %get-tuple-element.135.pos, bf16[12576,1024]{1,0:T(8,128)(2,1)} %emb_hbm.15, f32[640,1]{1,0:T(8,128)} %slice.140.bias_ref, f32[8,1,1280]{2,1,0:T(1,128)} %copy.56.lse_ref, s32[8,1,1280]{2,1,0:T(1,128)} %broadcast_in_dim.62.lab_ref, ...), custom_call_target="tpu_custom_call" | custom-call | flops 64592280 | bytes 14024704 | tf_op jit(solution)/shard_map/pallas_call | solution.py:349
  266.7 16.5 %shard_map.155 = (f32[608,1024]{1,0:T(8,128)}, f32[12576,1024]{1,0:T(8,128)}) custom-call(s32[3]{0:T(128)} %get-tuple-element.136.pos, bf16[12576,1024]{1,0:T(8,128)(2,1)} %emb_hbm.15, f32[608,1]{1,0:T(8,128)} %slice.141.bias_ref, f32[8,1,1280]{2,1,0:T(1,128)} %copy.56.lse_ref, ...), custom_call_target="tpu_custom_call", output_to_operand_aliasing={{1}: (9, {})} | custom-call | flops 61362668 | bytes 13828096 | tf_op jit(solution)/shard_map/pallas_call | solution.py:349
  283.2 1.1 collective-permute-start.31
  285.9 35.7 %shard_map.156 = (f32[576,1024]{1,0:T(8,128)}, f32[12576,1024]{1,0:T(8,128)}) custom-call(s32[3]{0:T(128)} %add_add_fusion.1.pos, bf16[12576,1024]{1,0:T(8,128)(2,1)} %emb_hbm.15, f32[576,1]{1,0:T(8,128)} %slice.139.bias_ref, f32[8,1,1280]{2,1,0:T(1,128)} %copy.56.lse_ref, s32[8,1,1280]{2,1,0:T(1,128)} %broadcast_in_dim.62.lab_ref, ...), custom_call_target="tpu_custom_call", output_to_operand_aliasing={{1}: (21, {})} | custom-call | flops 232532208 | bytes 43909120 | tf_op jit(solution)/shard_map/pallas_call | solution.py:349
  324.4 2.2 collective-permute-done.33.refs_1_
  328.7 7.8 %back.1 = (f32[320,1024]{1,0:T(8,128)}, f32[1096,1024]{1,0:T(8,128)}) custom-call(s32[1]{0:T(128)} %bitcast.vp, f32[1280,1024]{1,0:T(8,128)} %get-tuple-element.62.pre_ref, bf16[1280,1024]{1,0:T(8,128)(2,1)} %get-tuple-element.63.z_ref, f32[320,1024]{1,0:T(8,128)} %reduce-scatter.2.cloned.1.call-done.du_ref, bf16[1024,1024]{1,0:T(8,128)(2,1)} %w_ref.3, ...), custom_call_target="tpu_custom_call" | custom-call | flops 13421772 | bytes 11534336 | tf_op jit(solution)/shard_map/back/pallas_call | solution.py:418
  336.5 14.8 %collective-permute-done.34.refs_2_ = f32[576,1024]{1,0:T(8,128)} collective-permute-done((f32[576,1024]{1,0:T(8,128)}, f32[576,1024]{1,0:T(8,128)}, u32[]{:S(2)}, u32[]{:S(2)}) %collective-permute-start.34) | collective-permute-done | bytes 2359328 | tf_op jit(solution)/shard_map/ppermute | solution.py:481
  351.3 1.4 collective-permute-start.24
  353.6 3.0 collective-permute-start.25
  357.3 33.1 %shard_map.157 = (f32[528,1024]{1,0:T(8,128)}, f32[12576,1024]{1,0:T(8,128)}) custom-call(s32[3]{0:T(128)} %add_add_fusion.4.pos, bf16[12576,1024]{1,0:T(8,128)(2,1)} %emb_hbm.15, f32[528,1]{1,0:T(8,128)} %slice.143.bias_ref, f32[8,1,1280]{2,1,0:T(1,128)} %copy.56.lse_ref, s32[8,1,1280]{2,1,0:T(1,128)} %broadcast_in_dim.62.lab_ref, ...), custom_call_target="tpu_custom_call", output_to_operand_aliasing={{1}: (21, {})} | custom-call | flops 213154528 | bytes 43614208 | tf_op jit(solution)/shard_map/pallas_call | solution.py:349
  393.0 34.5 %shard_map.158 = (f32[448,1024]{1,0:T(8,128)}, f32[12576,1024]{1,0:T(8,128)}) custom-call(s32[6]{0:T(128)} %stack.196.pos, bf16[12576,1024]{1,0:T(8,128)(2,1)} %emb_hbm.15, f32[448,1]{1,0:T(8,128)} %copy.59.bias_ref, f32[8,1,1280]{2,1,0:T(1,128)} %copy.56.lse_ref, s32[8,1,1280]{2,1,0:T(1,128)} %broadcast_in_dim.62.lab_ref, ...), custom_call_target="tpu_custom_call", output_to_operand_aliasing={{1}: (21, {})} | custom-call | flops 180858384 | bytes 43122688 | tf_op jit(solution)/shard_map/pallas_call | solution.py:349
  427.5 1.2 collective-permute-start.40
  430.6 33.1 %shard_map.159 = (f32[344,1024]{1,0:T(8,128)}, f32[12576,1024]{1,0:T(8,128)}) custom-call(s32[6]{0:T(128)} %stack.190.pos, bf16[12576,1024]{1,0:T(8,128)(2,1)} %emb_hbm.15, f32[344,1]{1,0:T(8,128)} %slice.142.bias_ref, f32[8,1,1280]{2,1,0:T(1,128)} %copy.56.lse_ref, s32[8,1,1280]{2,1,0:T(1,128)} %broadcast_in_dim.62.lab_ref, ...), custom_call_target="tpu_custom_call", output_to_operand_aliasing={{1}: (21, {})} | custom-call | flops 138873408 | bytes 42483712 | tf_op jit(solution)/shard_map/pallas_call | solution.py:349
  465.9 24.2 %collective-permute-done.43.refs_2_ = f32[344,1024]{1,0:T(8,128)} collective-permute-done((f32[344,1024]{1,0:T(8,128)}, f32[344,1024]{1,0:T(8,128)}, u32[]{:S(2)}, u32[]{:S(2)}) %collective-permute-start.43) | collective-permute-done | bytes 1409056 | tf_op jit(solution)/shard_map/ppermute | solution.py:481
  492.0 127.7 %all-reduce.7.cloned.1.call-done = f32[1096,1024]{1,0:T(8,128)} async-done(((f32[1096,1024]{1,0:T(8,128)}), f32[1096,1024]{1,0:T(8,128)}) %all-reduce.7.cloned.1.call-update) | async-done | bytes 4489232 | tf_op jit(solution)/shard_map/psum | solution.py:587
  621.2 1.2 slice.159
  623.0 4.8 slice.160
  627.8 1.5 fusion.3
  629.3 10.9 %spread.1 = bf16[16,512,1024]{2,1,0:T(8,128)(2,1)} custom-call(s32[1]{0:T(128)} %bitcast.vp, s32[16,1,80]{2,1,0:T(1,128)} %bitcast.59, f32[320,1024]{1,0:T(8,128)} %get-tuple-element.106.refs_0_, f32[320,1024]{1,0:T(8,128)} %collective-permute-done.24.refs_1_, f32[320,1024]{1,0:T(8,128)} %collective-permute-done.25.refs_2_, ...), custom_call_target="tpu_custom_call" | custom-call | flops 21474836 | bytes 16777216 | tf_op jit(solution)/shard_map/spread/pallas_call | solution.py:455
  640.1 10.5 %put_rows.3.refs_0_ = f32[12576,1024]{1,0:T(8,128)} custom-call(s32[6]{0:T(128)} %stack.214.pos, f32[12576,1024]{1,0:T(8,128)} %get-tuple-element.110.refs_0_, f32[576,1024]{1,0:T(8,128)} %collective-permute-done.33.refs_1_, f32[576,1024]{1,0:T(8,128)} %collective-permute-done.34.refs_2_, f32[576,1024]{1,0:T(8,128)} %copy-done.4, ...), custom_call_target="tpu_custom_call", output_to_operand_aliasing={{}: (1, {})} | custom-call | flops 33914 | bytes 27131904 | tf_op jit(solution)/shard_map/put_rows/pallas_call | solution.py:377
  650.6 4.9 put_rows.4.refs_0_
  655.6 4.1 put_rows.5
  (140 shorter events, 35.4 us)
Async XLA Ops:
  7.2 321.6 %reduce-scatter.2.cloned.1.call-start = ((), (), s32[]{:S(2)}) async-start(), calls=%async_computation.1 | async-start | bytes 6553600 | tf_op jit(solution)/shard_map/reduce_scatter | solution.py:522
  24.2 78.4 %collective-permute-start.12 = (f32[608,1024]{1,0:T(8,128)}, f32[608,1024]{1,0:T(8,128)}, u32[]{:S(2)}, u32[]{:S(2)}) collective-permute-start(f32[608,1024]{1,0:T(8,128)} %get-tuple-element.76.rest_0_), channel_id=1, source_target_pairs={{0,2},{1,3},{2,0},{3,1},{4,6},{5,7},{6,4},{7,5},{8,10},{9,11},{10,... | collective-permute-start | bytes 7471112 | tf_op jit(solution)/shard_map/ppermute | solution.py:475
  27.3 123.0 %collective-permute-start.13 = (f32[624,1024]{1,0:T(8,128)}, f32[624,1024]{1,0:T(8,128)}, u32[]{:S(2)}, u32[]{:S(2)}) collective-permute-start(f32[624,1024]{1,0:T(8,128)} %get-tuple-element.77.rest_1_), channel_id=1, source_target_pairs={{0,4},{1,5},{2,6},{3,7},{4,0},{5,1},{6,2},{7,3},{8,12},{9,13},{10,... | collective-permute-start | bytes 7667720 | tf_op jit(solution)/shard_map/ppermute | solution.py:475
  28.8 121.5 %collective-permute-start.14 = (f32[624,1024]{1,0:T(8,128)}, f32[624,1024]{1,0:T(8,128)}, u32[]{:S(2)}, u32[]{:S(2)}) collective-permute-start(f32[624,1024]{1,0:T(8,128)} %get-tuple-element.77.rest_1_), channel_id=1, source_target_pairs={{0,2},{1,3},{2,0},{3,1},{4,6},{5,7},{6,4},{7,5},{8,10},{9,11},{10,... | collective-permute-start | bytes 7667720 | tf_op jit(solution)/shard_map/ppermute | solution.py:475
  29.3 120.9 %collective-permute-start.15 = (f32[608,1024]{1,0:T(8,128)}, f32[608,1024]{1,0:T(8,128)}, u32[]{:S(2)}, u32[]{:S(2)}) collective-permute-start(f32[608,1024]{1,0:T(8,128)} %get-tuple-element.76.rest_0_), channel_id=1, source_target_pairs={{0,4},{1,5},{2,6},{3,7},{4,0},{5,1},{6,2},{7,3},{8,12},{9,13},{10,... | collective-permute-start | bytes 7471112 | tf_op jit(solution)/shard_map/ppermute | solution.py:475
  85.3 6.2 collective-permute-start.2
  91.5 5.2 collective-permute-start.1
  96.7 4.2 collective-permute-start
  100.9 65.5 %collective-permute-start.10 = (f32[608,1024]{1,0:T(8,128)}, f32[608,1024]{1,0:T(8,128)}, u32[]{:S(2)}, u32[]{:S(2)}) collective-permute-start(f32[608,1024]{1,0:T(8,128)} %get-tuple-element.76.rest_0_), channel_id=1, source_target_pairs={{0,1},{1,0},{2,3},{3,2},{4,5},{5,4},{6,7},{7,6},{8,9},{9,8},{10,11... | collective-permute-start | bytes 7471112 | tf_op jit(solution)/shard_map/ppermute | solution.py:475
  102.6 65.3 %collective-permute-start.11 = (f32[624,1024]{1,0:T(8,128)S(1)}, f32[624,1024]{1,0:T(8,128)}, u32[]{:S(2)}, u32[]{:S(2)}) collective-permute-start(f32[624,1024]{1,0:T(8,128)S(1)} %copy-done), channel_id=1, source_target_pairs={{0,1},{1,0},{2,3},{3,2},{4,5},{5,4},{6,7},{7,6},{8,9},{9,8},{10,11... | collective-permute-start | bytes 7667720 | tf_op jit(solution)/shard_map/ppermute | solution.py:475
  150.3 17.7 %collective-permute-start.16 = (f32[608,1024]{1,0:T(8,128)}, f32[608,1024]{1,0:T(8,128)}, u32[]{:S(2)}, u32[]{:S(2)}) collective-permute-start(f32[608,1024]{1,0:T(8,128)} %collective-permute-done.12.rest_4_), channel_id=1, source_target_pairs={{0,1},{1,0},{2,3},{3,2},{4,5},{5,4},{6,7},{7,6},{8,9},{9,8},{10,11... | collective-permute-start | bytes 7471112 | tf_op jit(solution)/shard_map/ppermute | solution.py:475
  150.5 469.2 %all-reduce.7.cloned.1.call-start = ((), (), s32[]{:S(2)}) async-start(), calls=%async_computation.2 | async-start | bytes 8978432 | tf_op jit(solution)/shard_map/psum | solution.py:587
  151.9 3.5 collective-permute-start.3
  152.4 4.4 collective-permute-start.4
  155.4 3.1 collective-permute-start.5
  156.9 3.7 collective-permute-start.6
  158.5 3.9 collective-permute-start.7
  160.5 4.6 collective-permute-start.8
  162.4 4.0 collective-permute-start.9
  165.1 12.2 %collective-permute-start.17 = (f32[624,1024]{1,0:T(8,128)}, f32[624,1024]{1,0:T(8,128)}, u32[]{:S(2)}, u32[]{:S(2)}) collective-permute-start(f32[624,1024]{1,0:T(8,128)} %collective-permute-done.14.rest_5_), channel_id=1, source_target_pairs={{0,1},{1,0},{2,3},{3,2},{4,5},{5,4},{6,7},{7,6},{8,9},{9,8},{10,11... | collective-permute-start | bytes 7667720 | tf_op jit(solution)/shard_map/ppermute | solution.py:475
  166.4 10.9 %collective-permute-start.19 = (f32[624,1024]{1,0:T(8,128)}, f32[624,1024]{1,0:T(8,128)}, u32[]{:S(2)}, u32[]{:S(2)}) collective-permute-start(f32[624,1024]{1,0:T(8,128)} %collective-permute-done.13.rest_9_), channel_id=1, source_target_pairs={{0,1},{1,0},{2,3},{3,2},{4,5},{5,4},{6,7},{7,6},{8,9},{9,8},{10,11... | collective-permute-start | bytes 7667720 | tf_op jit(solution)/shard_map/ppermute | solution.py:475
  166.4 71.5 %collective-permute-start.21 = (f32[624,1024]{1,0:T(8,128)}, f32[624,1024]{1,0:T(8,128)}, u32[]{:S(2)}, u32[]{:S(2)}) collective-permute-start(f32[624,1024]{1,0:T(8,128)} %collective-permute-done.13.rest_9_), channel_id=1, source_target_pairs={{0,2},{1,3},{2,0},{3,1},{4,6},{5,7},{6,4},{7,5},{8,10},{9,11},{10,... | collective-permute-start | bytes 7667720 | tf_op jit(solution)/shard_map/ppermute | solution.py:475
  167.9 9.4 %collective-permute-start.18 = (f32[608,1024]{1,0:T(8,128)}, f32[608,1024]{1,0:T(8,128)S(1)}, u32[]{:S(2)}, u32[]{:S(2)}) collective-permute-start(f32[608,1024]{1,0:T(8,128)} %collective-permute-done.15.rest_8_), channel_id=1, source_target_pairs={{0,1},{1,0},{2,3},{3,2},{4,5},{5,4},{6,7},{7,6},{8,9},{9,8},{10,11... | collective-permute-start | bytes 7471112 | tf_op jit(solution)/shard_map/ppermute | solution.py:475
  167.9 70.0 %collective-permute-start.20 = (f32[608,1024]{1,0:T(8,128)}, f32[608,1024]{1,0:T(8,128)}, u32[]{:S(2)}, u32[]{:S(2)}) collective-permute-start(f32[608,1024]{1,0:T(8,128)} %collective-permute-done.12.rest_4_), channel_id=1, source_target_pairs={{0,4},{1,5},{2,6},{3,7},{4,0},{5,1},{6,2},{7,3},{8,12},{9,13},{10,... | collective-permute-start | bytes 7471112 | tf_op jit(solution)/shard_map/ppermute | solution.py:475
  237.9 8.8 %collective-permute-start.23 = (f32[624,1024]{1,0:T(8,128)}, f32[624,1024]{1,0:T(8,128)S(1)}, u32[]{:S(2)}, u32[]{:S(2)}) collective-permute-start(f32[624,1024]{1,0:T(8,128)} %collective-permute-done.21.rest_1_.rest_13_), channel_id=1, source_target_pairs={{0,1},{1,0},{2,3},{3,2},{4,5},{5,4},{6,7},{7,6},{8,9},{9,8},{10,11... | collective-permute-start | bytes 7667720 | tf_op jit(solution)/shard_map/ppermute | solution.py:475
  238.2 8.5 %collective-permute-start.22 = (f32[608,1024]{1,0:T(8,128)}, f32[608,1024]{1,0:T(8,128)}, u32[]{:S(2)}, u32[]{:S(2)}) collective-permute-start(f32[608,1024]{1,0:T(8,128)} %collective-permute-done.20.rest_0_.rest_12_), channel_id=1, source_target_pairs={{0,1},{1,0},{2,3},{3,2},{4,5},{5,4},{6,7},{7,6},{8,9},{9,8},{10,11... | collective-permute-start | bytes 7471112 | tf_op jit(solution)/shard_map/ppermute | solution.py:475
  265.6 57.5 %collective-permute-start.28 = (f32[640,1024]{1,0:T(8,128)}, f32[640,1024]{1,0:T(8,128)S(1)}, u32[]{:S(2)}, u32[]{:S(2)}) collective-permute-start(f32[640,1024]{1,0:T(8,128)} %get-tuple-element.100), channel_id=1, source_target_pairs={{0,2},{1,5},{2,0},{3,7},{4,6},{5,1},{6,4},{7,3},{8,10},{9,13},{10,... | collective-permute-start | bytes 7864328 | tf_op jit(solution)/shard_map/ppermute | solution.py:481
  283.2 41.2 %collective-permute-start.31 = (f32[608,1024]{1,0:T(8,128)}, f32[608,1024]{1,0:T(8,128)}, u32[]{:S(2)}, u32[]{:S(2)}) collective-permute-start(f32[608,1024]{1,0:T(8,128)} %get-tuple-element.103), channel_id=1, source_target_pairs={{0,2},{1,5},{2,0},{3,7},{4,6},{5,1},{6,4},{7,3},{8,10},{9,13},{10,... | collective-permute-start | bytes 7471112 | tf_op jit(solution)/shard_map/ppermute | solution.py:481
  321.6 4.9 collective-permute-start.33
  321.7 31.9 %collective-permute-start.27 = (f32[640,1024]{1,0:T(8,128)}, f32[640,1024]{1,0:T(8,128)}, u32[]{:S(2)}, u32[]{:S(2)}) collective-permute-start(f32[640,1024]{1,0:T(8,128)} %get-tuple-element.100), channel_id=1, source_target_pairs={{0,1},{1,0},{2,3},{3,2},{4,5},{5,4},{6,7},{7,6},{8,9},{9,8},{10,11... | collective-permute-start | bytes 7864328 | tf_op jit(solution)/shard_map/ppermute | solution.py:475
  322.2 29.2 %collective-permute-start.34 = (f32[576,1024]{1,0:T(8,128)}, f32[576,1024]{1,0:T(8,128)}, u32[]{:S(2)}, u32[]{:S(2)}) collective-permute-start(f32[576,1024]{1,0:T(8,128)} %get-tuple-element.92), channel_id=1, source_target_pairs={{0,2},{1,5},{2,0},{3,7},{4,6},{5,1},{6,4},{7,3},{8,10},{9,13},{10,... | collective-permute-start | bytes 7077896 | tf_op jit(solution)/shard_map/ppermute | solution.py:481
  323.1 67.2 %collective-permute-start.29 = (f32[640,1024]{1,0:T(8,128)S(1)}, f32[640,1024]{1,0:T(8,128)}, u32[]{:S(2)}, u32[]{:S(2)}) collective-permute-start(f32[640,1024]{1,0:T(8,128)S(1)} %collective-permute-done.28.rest_18_), channel_id=1, source_target_pairs={{0,1},{1,0},{2,3},{3,2},{4,5},{5,4},{6,7},{7,6},{8,9},{9,8},{10,11... | collective-permute-start | bytes 7864328 | tf_op jit(solution)/shard_map/ppermute | solution.py:475
  324.4 103.1 %collective-permute-start.30 = (f32[608,1024]{1,0:T(8,128)}, f32[608,1024]{1,0:T(8,128)}, u32[]{:S(2)}, u32[]{:S(2)}) collective-permute-start(f32[608,1024]{1,0:T(8,128)} %get-tuple-element.103), channel_id=1, source_target_pairs={{0,1},{1,0},{2,3},{3,2},{4,5},{5,4},{6,7},{7,6},{8,9},{9,8},{10,11... | collective-permute-start | bytes 7471112 | tf_op jit(solution)/shard_map/ppermute | solution.py:475
  326.5 102.6 %collective-permute-start.32 = (f32[608,1024]{1,0:T(8,128)}, f32[608,1024]{1,0:T(8,128)}, u32[]{:S(2)}, u32[]{:S(2)}) collective-permute-start(f32[608,1024]{1,0:T(8,128)} %collective-permute-done.31.rest_18_), channel_id=1, source_target_pairs={{0,1},{1,0},{2,3},{3,2},{4,5},{5,4},{6,7},{7,6},{8,9},{9,8},{10,11... | collective-permute-start | bytes 7471112 | tf_op jit(solution)/shard_map/ppermute | solution.py:475
  351.3 77.3 %collective-permute-start.24 = (f32[320,1024]{1,0:T(8,128)}, f32[320,1024]{1,0:T(8,128)}, u32[]{:S(2)}, u32[]{:S(2)}) collective-permute-start(f32[320,1024]{1,0:T(8,128)} %get-tuple-element.106.refs_0_), channel_id=1, source_target_pairs={{0,8},{8,0},{16,24},{24,16},{1,9},{9,1},{17,25},{25,17},{2,10},{10... | collective-permute-start | bytes 3932168 | tf_op jit(solution)/shard_map/ppermute | solution.py:478
  353.6 75.0 %collective-permute-start.25 = (f32[320,1024]{1,0:T(8,128)}, f32[320,1024]{1,0:T(8,128)}, u32[]{:S(2)}, u32[]{:S(2)}) collective-permute-start(f32[320,1024]{1,0:T(8,128)} %get-tuple-element.106.refs_0_), channel_id=1, source_target_pairs={{0,16},{8,24},{16,0},{24,8},{1,17},{9,25},{17,1},{25,9},{2,18},{10... | collective-permute-start | bytes 3932168 | tf_op jit(solution)/shard_map/ppermute | solution.py:478
  390.4 73.4 %collective-permute-start.37 = (f32[528,1024]{1,0:T(8,128)}, f32[528,1024]{1,0:T(8,128)}, u32[]{:S(2)}, u32[]{:S(2)}) collective-permute-start(f32[528,1024]{1,0:T(8,128)} %get-tuple-element.111), channel_id=1, source_target_pairs={{0,2},{1,5},{2,0},{3,7},{4,6},{5,1},{6,4},{7,3},{8,10},{9,13},{10,... | collective-permute-start | bytes 6488072 | tf_op jit(solution)/shard_map/ppermute | solution.py:481
  427.5 37.3 %collective-permute-start.40 = (f32[448,1024]{1,0:T(8,128)}, f32[448,1024]{1,0:T(8,128)}, u32[]{:S(2)}, u32[]{:S(2)}) collective-permute-start(f32[448,1024]{1,0:T(8,128)} %get-tuple-element.113), channel_id=1, source_target_pairs={{0,2},{1,5},{2,0},{3,7},{4,6},{5,1},{6,4},{7,3},{8,10},{9,13},{10,... | collective-permute-start | bytes 5505032 | tf_op jit(solution)/shard_map/ppermute | solution.py:481
  428.6 36.8 %collective-permute-start.36 = (f32[528,1024]{1,0:T(8,128)}, f32[528,1024]{1,0:T(8,128)}, u32[]{:S(2)}, u32[]{:S(2)}) collective-permute-start(f32[528,1024]{1,0:T(8,128)} %get-tuple-element.111), channel_id=1, source_target_pairs={{0,1},{1,0},{2,3},{3,2},{4,5},{5,4},{6,7},{7,6},{8,9},{9,8},{10,11... | collective-permute-start | bytes 6488072 | tf_op jit(solution)/shard_map/ppermute | solution.py:475
  428.7 37.2 %collective-permute-start.35 = (f32[576,1024]{1,0:T(8,128)}, f32[576,1024]{1,0:T(8,128)S(1)}, u32[]{:S(2)}, u32[]{:S(2)}) collective-permute-start(f32[576,1024]{1,0:T(8,128)} %collective-permute-done.34.refs_2_), channel_id=1, source_target_pairs={{0,1},{1,0},{2,3},{3,2},{4,5},{5,4},{6,7},{7,6},{8,9},{9,8},{10,11... | collective-permute-start | bytes 7077896 | tf_op jit(solution)/shard_map/ppermute | solution.py:475
  429.2 36.1 %collective-permute-start.26 = (f32[320,1024]{1,0:T(8,128)}, f32[320,1024]{1,0:T(8,128)}, u32[]{:S(2)}, u32[]{:S(2)}) collective-permute-start(f32[320,1024]{1,0:T(8,128)} %get-tuple-element.106.refs_0_), channel_id=1, source_target_pairs={{0,24},{8,16},{16,8},{24,0},{1,25},{9,17},{17,9},{25,1},{2,26},{10... | collective-permute-start | bytes 3932168 | tf_op jit(solution)/shard_map/ppermute | solution.py:478
  463.8 26.3 %collective-permute-start.43 = (f32[344,1024]{1,0:T(8,128)}, f32[344,1024]{1,0:T(8,128)}, u32[]{:S(2)}, u32[]{:S(2)}) collective-permute-start(f32[344,1024]{1,0:T(8,128)} %get-tuple-element.105), channel_id=1, source_target_pairs={{0,2},{1,5},{2,0},{3,7},{4,6},{5,1},{6,4},{7,3},{8,10},{9,13},{10,... | collective-permute-start | bytes 4227080 | tf_op jit(solution)/shard_map/ppermute | solution.py:481
  464.8 175.3 %collective-permute-start.38 = (f32[528,1024]{1,0:T(8,128)}, f32[528,1024]{1,0:T(8,128)}, u32[]{:S(2)}, u32[]{:S(2)}) collective-permute-start(f32[528,1024]{1,0:T(8,128)} %collective-permute-done.37.refs_5_), channel_id=1, source_target_pairs={{0,1},{1,0},{2,3},{3,2},{4,5},{5,4},{6,7},{7,6},{8,9},{9,8},{10,11... | collective-permute-start | bytes 6488072 | tf_op jit(solution)/shard_map/ppermute | solution.py:475
  465.3 185.3 %collective-permute-start.39 = (f32[448,1024]{1,0:T(8,128)}, f32[448,1024]{1,0:T(8,128)}, u32[]{:S(2)}, u32[]{:S(2)}) collective-permute-start(f32[448,1024]{1,0:T(8,128)} %get-tuple-element.113), channel_id=1, source_target_pairs={{0,1},{1,0},{2,3},{3,2},{4,5},{5,4},{6,7},{7,6},{8,9},{9,8},{10,11... | collective-permute-start | bytes 5505032 | tf_op jit(solution)/shard_map/ppermute | solution.py:475
  465.4 185.2 %collective-permute-start.41 = (f32[448,1024]{1,0:T(8,128)}, f32[448,1024]{1,0:T(8,128)}, u32[]{:S(2)}, u32[]{:S(2)}) collective-permute-start(f32[448,1024]{1,0:T(8,128)} %collective-permute-done.40.refs_2_), channel_id=1, source_target_pairs={{0,1},{1,0},{2,3},{3,2},{4,5},{5,4},{6,7},{7,6},{8,9},{9,8},{10,11... | collective-permute-start | bytes 5505032 | tf_op jit(solution)/shard_map/ppermute | solution.py:475
  465.8 161.9 %copy-start.4 = (f32[576,1024]{1,0:T(8,128)}, f32[576,1024]{1,0:T(8,128)S(1)}, u32[]{:S(2)}) copy-start(f32[576,1024]{1,0:T(8,128)S(1)} %collective-permute-done.35.refs_3_) | copy-start | bytes 7077892
  465.8 189.7 %collective-permute-start.42 = (f32[344,1024]{1,0:T(8,128)}, f32[344,1024]{1,0:T(8,128)}, u32[]{:S(2)}, u32[]{:S(2)}) collective-permute-start(f32[344,1024]{1,0:T(8,128)} %get-tuple-element.105), channel_id=1, source_target_pairs={{0,1},{1,0},{2,3},{3,2},{4,5},{5,4},{6,7},{7,6},{8,9},{9,8},{10,11... | collective-permute-start | bytes 4227080 | tf_op jit(solution)/shard_map/ppermute | solution.py:475
  490.1 165.4 %collective-permute-start.44 = (f32[344,1024]{1,0:T(8,128)}, f32[344,1024]{1,0:T(8,128)}, u32[]{:S(2)}, u32[]{:S(2)}) collective-permute-start(f32[344,1024]{1,0:T(8,128)} %collective-permute-done.43.refs_2_), channel_id=1, source_target_pairs={{0,1},{1,0},{2,3},{3,2},{4,5},{5,4},{6,7},{7,6},{8,9},{9,8},{10,11... | collective-permute-start | bytes 4227080 | tf_op jit(solution)/shard_map/ppermute | solution.py:475
  (8 other events, 172.2 us)
Sparse Core Ops, SparseCore 0:
  150.6 95.5 reduce-scatter.1
  464.9 154.6 all-reduce.6
where the time goes:
time: 675 us; the launch traced here: 668 us
  Pallas kernels  383 us (57%)
  waiting for transfers between devices  194 us (29%)
  starting transfers between devices  40.6 us (6%)
  local copies, waits for them, and re-layouts  26.9 us (4%)
  between operations  17.4 us (3%)
    pallas_call x8, Pallas kernels, rows_pass(): pl.pallas_call(functools.partial(rows_kernel, mode, scale, m, cut, n_loc,...  229 us
    psum x1, waiting for transfers between devices, local_step(): pack = lax.psum(pack, ('vp', 'dp'))  128 us
    pallas_call x1, Pallas kernels, stats(): pl.pallas_call(functools.partial(stats_kernel, v), grid=(n,), in_specs=[w...  54 us
    pallas_call x1, Pallas kernels, du_pass(): pl.pallas_call(functools.partial(du_kernel, v, scale), grid=(n,), in_spec...  46 us
    ppermute x6, waiting for transfers between devices, hop(): lax.ppermute(a, 'dp', [(d, d ^ (Y if d & CORE else X)) for d in range(n_g...  39.8 us
    ppermute x33, starting transfers between devices, swap(): return lax.ppermute(a, 'dp', [(d, d ^ bit) for d in range(n_groups)])  22.7 us
    pallas_call x3, Pallas kernels, put_rows(): pl.pallas_call(functools.partial(put_kernel, n), in_specs=[SMEM] + [ANY]...  19.5 us
    ppermute x33, waiting for transfers between devices, swap(): return lax.ppermute(a, 'dp', [(d, d ^ bit) for d in range(n_groups)])  18 us
  transfers between devices with their start and end apart: 47, of which 15 were waited for; matrix products, arithmetic and copies ran while one was open for 4% of the time, Pallas kernels for 54%

commit v1 on v0

v1 whole, which is shorter than its diff:
```python
import functools

import jax
import jax.numpy as jnp
from jax import lax
from jax.experimental import pallas as pl
from jax.experimental.pallas import tpu as pltpu
from jax.sharding import PartitionSpec as P


F32, BF16, I32 = jnp.float32, jnp.bfloat16, jnp.int32
NT = (((1,), (1,)), ((), ()))
NN = (((1,), (0,)), ((), ()))
VB = 1024
VMEM_LIMIT = 60 << 20
COVER = 100
CH = 16


def row_cuts(rows, parts=4):
    cuts = [16 * (rows // 16 * k // parts) for k in range(parts)] + [rows]
    return list(zip(cuts[:-1], cuts[1:]))


def dot(a, b, dims):
    return lax.dot_general(a, b, dims, preferred_element_type=F32)


def stats_kernel(n_vocab, u_ref, emb_ref, b_ref, lab_ref, logits_ref, stat_ref, m_sc, s_sc, l_sc):
    i, n_blocks = pl.program_id(0), pl.num_programs(0)
    lane = lax.broadcasted_iota(I32, (1, 128), 1)

    @pl.when(i == 0)
    def _():
        m_sc[...] = jnp.full_like(m_sc, -jnp.inf)
        s_sc[...] = jnp.zeros_like(s_sc)
        l_sc[...] = jnp.zeros_like(l_sc)

    def run(width):
        wide = -(-width // 128) * 128
        for r0, r1 in row_cuts(u_ref.shape[0]):
            tile = dot(u_ref[r0:r1, :], emb_ref[:wide, :], NT) + b_ref[:, :wide]
            if wide > width:
                tile = jnp.where(lax.broadcasted_iota(I32, (1, wide), 1) < width, tile, -jnp.inf)
            logits_ref[r0:r1, :wide] = tile
            for q in range(r0, r1, CH):
                rs = slice(q, min(q + CH, r1))
                parts = [logits_ref[rs, k:k + 128] for k in range(0, wide, 128)]
                m_old = m_sc[rs, :]
                m_new = functools.reduce(jnp.maximum, parts, m_old)
                s_new = s_sc[rs, :] * jnp.exp(m_old - m_new)
                l_new = l_sc[rs, :]
                lab = lab_ref[rs, :] - i * VB
                for k, part in enumerate(parts):
                    s_new += jnp.exp(part - m_new)
                    l_new = jnp.where(lab == lane + k * 128, part, l_new)
                m_sc[rs, :], s_sc[rs, :], l_sc[rs, :] = m_new, s_new, l_new

    tail = n_vocab % VB
    if tail:
        pl.when(i < n_blocks - 1)(functools.partial(run, VB))
        pl.when(i == n_blocks - 1)(functools.partial(run, tail))
    else:
        run(VB)

    @pl.when(i == n_blocks - 1)
    def _():
        m_t, s_t, l_t = m_sc[...].T, s_sc[...].T, l_sc[...].T
        m_all = jnp.max(m_t, axis=0, keepdims=True)
        stat_ref[0:1, :] = m_all
        stat_ref[1:2, :] = jnp.sum(s_t * jnp.exp(m_t - m_all), axis=0, keepdims=True)
        stat_ref[2:3, :] = jnp.sum(l_t, axis=0, keepdims=True)
        stat_ref[3:8, :] = jnp.zeros_like(stat_ref[3:8, :])


def stats(u, emb, bias, lab):
    t, e = u.shape
    v = emb.shape[0]
    n = pl.cdiv(v, VB)
    whole = lambda *s: pl.BlockSpec(s, lambda i: (0,) * len(s))
    return pl.pallas_call(
        functools.partial(stats_kernel, v),
        grid=(n,),
        in_specs=[whole(t, e), pl.BlockSpec((VB, e), lambda i: (i, 0)), pl.BlockSpec((1, VB), lambda i: (0, i)), whole(t, 128)],
        out_specs=[pl.BlockSpec((t, VB), lambda i: (0, i)), whole(8, t)],
        out_shape=[jax.ShapeDtypeStruct((t, v), F32), jax.ShapeDtypeStruct((8, t), F32)],
        scratch_shapes=[pltpu.VMEM((t, 128), F32)] * 3,
        compiler_params=pltpu.CompilerParams(dimension_semantics=("arbitrary",), vmem_limit_bytes=VMEM_LIMIT),
        cost_estimate=pl.CostEstimate(flops=(2 * t * v * e) // COVER, bytes_accessed=t * v * 4 + v * e * 2, transcendentals=t * v),
        name="stats",
    )(u, emb, bias, lab)


def du_kernel(n_vocab, scale, logits_ref, emb_ref, lse_ref, lab_ref, out_ref, db_ref, du_ref, g_sc, db_sc):
    i, n_blocks = pl.program_id(0), pl.num_programs(0)
    t = logits_ref.shape[0]
    lane = lax.broadcasted_iota(I32, (1, 128), 1)

    @pl.when(i == 0)
    def _():
        du_ref[...] = jnp.zeros_like(du_ref)

    def run(width):
        wide = -(-width // 128) * 128
        emb = emb_ref[:wide, :]
        if wide > width:
            emb = jnp.where(lax.broadcasted_iota(I32, (wide, 1), 0) < width, emb, jnp.zeros_like(emb))
        for r0, r1 in row_cuts(t):
            sums = [None] * (wide // 128)
            for q in range(r0, r1, 16):
                rs = slice(q, q + 16)
                lse = lse_ref[rs, :]
                lab = lab_ref[rs, :] - i * VB
                for k in range(wide // 128):
                    c = k * 128
                    g = jnp.exp(logits_ref[rs, c:c + 128] - lse)
                    g -= jnp.where(lab == lane + c, scale, 0.0)
                    if c + 128 > width:
                        g = jnp.where(lane < width - c, g, 0.0)
                    part = g[:8] + g[8:]
                    sums[k] = part if sums[k] is None else sums[k] + part
                    g_sc[rs, c:c + 128] = g.astype(BF16)
            for k in range(wide // 128):
                cs = slice(k * 128, (k + 1) * 128)
                db_sc[:, cs] = sums[k] if r0 == 0 else db_sc[:, cs] + sums[k]
            du_ref[r0:r1, :] += dot(g_sc[r0:r1, :wide], emb, NN)
        db_ref[:, :wide] = jnp.sum(db_sc[:, :wide], axis=0, keepdims=True)

    tail = n_vocab % VB
    if tail:
        pl.when(i < n_blocks - 1)(functools.partial(run, VB))
        pl.when(i == n_blocks - 1)(functools.partial(run, tail))
    else:
        run(VB)

    @pl.when(i == n_blocks - 1)
    def _():
        parts, _, cols = out_ref.shape
        for q in range(parts):
            out_ref[q] = du_ref[:, q * cols:(q + 1) * cols].astype(BF16).astype(F32)


def du_pass(scale, parts, logits, emb, lse, lab):
    t, v = logits.shape
    e = emb.shape[1]
    n = pl.cdiv(v, VB)
    whole = lambda *s: pl.BlockSpec(s, lambda i: (0,) * len(s))
    return pl.pallas_call(
        functools.partial(du_kernel, v, scale),
        grid=(n,),
        in_specs=[pl.BlockSpec((t, VB), lambda i: (0, i)), pl.BlockSpec((VB, e), lambda i: (i, 0)), whole(t, 128), whole(t, 128)],
        out_specs=[whole(parts, t, e // parts), pl.BlockSpec((1, VB), lambda i: (0, i))],
        out_shape=[jax.ShapeDtypeStruct((parts, t, e // parts), F32), jax.ShapeDtypeStruct((1, v), F32)],
        scratch_shapes=[pltpu.VMEM((t, e), F32), pltpu.VMEM((t, VB), BF16), pltpu.VMEM((8, VB), F32)],
        compiler_params=pltpu.CompilerParams(dimension_semantics=("arbitrary",), vmem_limit_bytes=VMEM_LIMIT),
        cost_estimate=pl.CostEstimate(flops=(2 * t * v * e) // COVER, bytes_accessed=t * v * 4 + v * e * 2, transcendentals=t * v),
        name="du_pass",
    )(logits, emb, lse, lab)


LN_EPS = 1e-5
CORE, X, Y = 1, 2, 4
ANY = pl.BlockSpec(memory_space=pl.ANY)
VMEM = pl.BlockSpec(memory_space=pltpu.VMEM)
SMEM = pl.BlockSpec(memory_space=pltpu.SMEM)
DMA = pltpu.SemaphoreType.DMA


def gelu_norm(a):
    cdf = 0.5 * (1.0 + lax.erf(a * (0.5 ** 0.5)))
    g = a * cdf
    centered = g - jnp.mean(g, axis=1, keepdims=True)
    rstd = lax.rsqrt(jnp.mean(centered * centered, axis=1, keepdims=True) + LN_EPS)
    return cdf, centered * rstd, rstd


def head_kernel(n_masks, cut, hid, pos_ref, w_ref, b_ref, gain_ref, bias_ref, z_out, pre_out, norm_out, rstd_out, u_out, lo_out, hi_out,
                hbuf, zf, zb, pre_v, norm_v, rstd_v, ub, uf, in_sem, out_sem):
    n_seq, seq_len = hid.shape[0], hid.shape[1]
    n_loc = n_seq * n_masks
    loads = [pltpu.make_async_copy(hid.at[b], hbuf.at[b], in_sem.at[b]) for b in range(n_seq)]
    for c in loads:
        c.start()
    lane = lax.broadcasted_iota(I32, (1, 128), 1)
    cuts = [0, cut // 32 * 16, cut, cut + (n_loc - cut) // 32 * 16, n_loc]
    done, stores = 0, []

    def send(src, dst, r0, r1, base=0):
        c = pltpu.make_async_copy(src.at[r0:r1, :], dst.at[r0 - base:r1 - base, :], out_sem.at[len(stores)])
        c.start()
        stores.append(c)

    for b in range(n_seq):
        loads[b].wait()
        hot = jnp.concatenate([jnp.where(pos_ref[b] == lane + j, 1.0, 0.0).astype(BF16) for j in range(0, seq_len, 128)], axis=1)
        zf[b * n_masks:(b + 1) * n_masks, :] = dot(hot, hbuf[b], NN)[:n_masks, :]
        while done < 4 and cuts[done + 1] <= (b + 1) * n_masks:
            r0, r1 = cuts[done], cuts[done + 1]
            z = zf[r0:r1, :].astype(BF16)
            zb[r0:r1, :] = z
            a = dot(z, w_ref[...], NN) + b_ref[...]
            pre_v[r0:r1, :] = a
            _, normed, rstd = gelu_norm(a)
            norm_v[r0:r1, :] = normed
            rstd_v[r0:r1, :] = jnp.broadcast_to(rstd, (r1 - r0, 128))
            u = (normed * gain_ref[...] + bias_ref[...]).astype(BF16)
            ub[r0:r1, :] = u
            uf[r0:r1, :] = u.astype(F32)
            done += 1
            send(uf, hi_out if r0 >= cut else lo_out, r0, r1, cut if r0 >= cut else 0)
            for src, dst in ((ub, u_out), (zb, z_out), (pre_v, pre_out), (norm_v, norm_out), (rstd_v, rstd_out)):
                send(src, dst, r0, r1)
    for c in stores:
        c.wait()


def head_pass(n_masks, cut, hidden, pos, w, b, gain, bias):
    n_seq, seq_len, e = hidden.shape
    n = n_seq * n_masks
    kinds = [((n, e), BF16), ((n, e), F32), ((n, e), F32), ((n, 128), F32), ((n, e), BF16), ((cut, e), F32), ((n - cut, e), F32)]
    return pl.pallas_call(
        functools.partial(head_kernel, n_masks, cut),
        in_specs=[ANY] + [VMEM] * 5,
        out_specs=[ANY] * len(kinds),
        out_shape=[jax.ShapeDtypeStruct(*k) for k in kinds],
        scratch_shapes=[pltpu.VMEM((n_seq, seq_len, e), BF16), pltpu.VMEM((n, e), F32)]
        + [pltpu.VMEM(*k) for k in kinds[:5]] + [pltpu.VMEM((n, e), F32), DMA((n_seq,)), DMA((24,))],
        compiler_params=pltpu.CompilerParams(vmem_limit_bytes=VMEM_LIMIT),
        cost_estimate=pl.CostEstimate(flops=(4 * n * e * e) // COVER, bytes_accessed=hidden.size * 2 + n * e * 20, transcendentals=n * e),
        name="head",
    )(hidden, pos, w, b, gain, bias)


def narrow_kernel(first, offs, pos, *refs):
    refs = list(refs)
    n = len(offs)
    if not first:
        refs.pop(0)
    pieces, (out_ref, wide, thin, pad, in_sem, out_sem, sem) = refs[:n], refs[n:]
    loads, stores = [], []
    for j, p in enumerate(pieces):
        m = p.shape[0]
        loads.append(pltpu.make_async_copy(p, wide.at[j, :m, :], in_sem.at[j]))
        row = pl.multiple_of(pos[j], 16)
        stores.append(pltpu.make_async_copy(thin.at[j, :m, :], out_ref.at[pl.ds(row, m), :], out_sem.at[j]))
    for c in loads:
        c.start()
    if first:
        pad[...] = jnp.zeros_like(pad)
        c = pltpu.make_async_copy(pad, out_ref.at[out_ref.shape[0] - pad.shape[0]:, :], sem)
        c.start()
        c.wait()
    for j, p in enumerate(pieces):
        m = p.shape[0]
        loads[j].wait()
        thin[j, :m, :] = wide[j, :m, :].astype(BF16)
        stores[j].start()
    for c in stores:
        c.wait()


def narrow_into(big, n_tok, rows, pieces):
    first = big is None
    n, e = len(pieces), pieces[0].shape[1]
    m = max(p.shape[0] for p in pieces)
    padded = -(-n_tok // TB) * TB
    size = sum(p.size for p in pieces)
    return pl.pallas_call(
        functools.partial(narrow_kernel, first, [p.shape[0] for p in pieces]),
        in_specs=[SMEM] + [ANY] * (n + (not first)),
        out_specs=ANY,
        out_shape=jax.ShapeDtypeStruct((padded, e), BF16),
        scratch_shapes=[pltpu.VMEM((n, m, e), F32), pltpu.VMEM((n, m, e), BF16), pltpu.VMEM((padded - n_tok, e), BF16), DMA((n,)), DMA((n,)), DMA],
        input_output_aliases={} if first else {1: 0},
        compiler_params=pltpu.CompilerParams(vmem_limit_bytes=VMEM_LIMIT),
        cost_estimate=pl.CostEstimate(flops=(size) // COVER, bytes_accessed=size * 6, transcendentals=0),
        name="narrow",
    )(jnp.stack(rows), *([] if first else [big]), *pieces)


TB = 768


def rows_kernel(scale, m, n_put, has_big, pos, emb_hbm, u_hbm, bias_ref, lse_ref, lab_ref, *refs):
    refs = list(refs)
    if has_big:
        refs.pop(0)
    puts, (out_hbm, big_ref, u_all, emb_sc, g_sc, acc, hold, sem, tok_sem, in_sem, out_sem) = refs[:n_put], refs[n_put:]
    n_blocks = lse_ref.shape[0]
    row = lambda j: pl.multiple_of(pos[j], 8)
    blocks = [pltpu.make_async_copy(u_hbm.at[j * TB:(j + 1) * TB, :], u_all.at[j * TB:(j + 1) * TB, :], tok_sem.at[j]) for j in range(n_blocks)]
    loads = [pltpu.make_async_copy(p, hold.at[j, :p.shape[0], :], in_sem.at[j]) for j, p in enumerate(puts)]
    stores = [pltpu.make_async_copy(hold.at[j, :p.shape[0], :], big_ref.at[pl.ds(row(2 + j), p.shape[0]), :], out_sem.at[j])
              for j, p in enumerate(puts)]
    emb_copy = pltpu.make_async_copy(emb_hbm.at[pl.ds(row(0), m), :], emb_sc, sem)
    emb_copy.start()
    for c in blocks + loads:
        c.start()
    acc[...] = jnp.zeros_like(acc)
    emb_copy.wait()
    parts = max(1, round(m / 256))
    cuts = [-(-m * k // (parts * 16)) * 16 for k in range(parts)] + [m]
    cuts = list(zip(cuts[:-1], cuts[1:]))

    @pl.loop(0, n_blocks)
    def _(i):
        at = pl.ds(pl.multiple_of(i * TB, TB), TB)
        pltpu.make_async_copy(u_hbm.at[at, :], u_all.at[at, :], tok_sem.at[i]).wait()
        for j, (a, b) in enumerate(zip(loads, stores)):
            @pl.when(i == 3 + j)
            def _():
                a.wait()
                b.start()

        def weights(r0, r1):
            part = dot(emb_sc[r0:r1, :], u_all[at, :], NT)
            hit = lab_ref[i] == lax.broadcasted_iota(I32, (r1 - r0, 1), 0) + (pos[1] + r0)
            g = jnp.exp(part + bias_ref[r0:r1, :] - lse_ref[i]) - jnp.where(hit, scale, 0.0)
            g_sc[r0:r1, :] = g.astype(BF16)

        weights(*cuts[0])
        for k, (r0, r1) in enumerate(cuts):
            if k + 1 < len(cuts):
                weights(*cuts[k + 1])
            acc[r0:r1, :] += dot(g_sc[r0:r1, :], u_all[at, :], NN)

    own = pltpu.make_async_copy(acc, out_hbm, sem)
    own.start()
    for b in stores:
        b.wait()
    own.wait()


def rows_pass(scale, v_rows, m, pos, emb, u, bias, lse, lab, big, puts):
    t, e = u.shape
    n, n_put = t // TB, max(1, len(puts))
    sds = jax.ShapeDtypeStruct
    has_big = big is not None
    extra = ([big] if has_big else []) + list(puts)
    return pl.pallas_call(
        functools.partial(rows_kernel, scale, m, len(puts), has_big),
        in_specs=[SMEM, ANY, ANY, VMEM, VMEM, VMEM] + [ANY] * len(extra),
        out_specs=[ANY, ANY],
        out_shape=[sds((m, e), F32), sds((v_rows, e), F32)],
        scratch_shapes=[
            pltpu.VMEM((t, e), BF16), pltpu.VMEM((m, e), BF16), pltpu.VMEM((m, TB), BF16), pltpu.VMEM((m, e), F32),
            pltpu.VMEM((n_put, max([p.shape[0] for p in puts] + [8]), e), F32), DMA, DMA((n,)), DMA((n_put,)), DMA((n_put,)),
        ],
        input_output_aliases={6: 1} if has_big else {},
        compiler_params=pltpu.CompilerParams(vmem_limit_bytes=VMEM_LIMIT),
        cost_estimate=pl.CostEstimate(flops=(4 * t * m * e) // COVER, bytes_accessed=t * e * 2 + m * e * 6, transcendentals=t * m),
        name="rows",
    )(pos, emb, u, bias, lse, lab, *extra)


def put_kernel(n, pos, *refs):
    pieces, (out_ref, hold, in_sem, out_sem) = refs[1:1 + n], refs[1 + n:]
    loads, stores = [], []
    for j, p in enumerate(pieces):
        slot = hold.at[j, :p.shape[0], :]
        loads.append(pltpu.make_async_copy(p, slot, in_sem.at[j]))
        stores.append(pltpu.make_async_copy(slot, out_ref.at[pl.ds(pl.multiple_of(pos[j], 8), p.shape[0]), :], out_sem.at[j]))
    for a in loads:
        a.start()
    for a, b in zip(loads, stores):
        a.wait()
        b.start()
    for b in stores:
        b.wait()


def put_rows(pos, big, pieces):
    n, e = len(pieces), big.shape[1]
    return pl.pallas_call(
        functools.partial(put_kernel, n),
        in_specs=[SMEM] + [ANY] * (n + 1),
        out_specs=ANY,
        out_shape=jax.ShapeDtypeStruct(big.shape, big.dtype),
        scratch_shapes=[pltpu.VMEM((n, max(p.shape[0] for p in pieces), e), F32), DMA((n,)), DMA((n,))],
        input_output_aliases={1: 0},
        compiler_params=pltpu.CompilerParams(vmem_limit_bytes=VMEM_LIMIT),
        cost_estimate=pl.CostEstimate(flops=(sum(p.size for p in pieces)) // COVER, bytes_accessed=sum(p.size for p in pieces) * 8, transcendentals=0),
        name="put_rows",
    )(pos, big, *pieces)


def sums_kernel(du_ref, norm_ref, gain_ref, out_ref):
    cols = du_ref.shape[2]
    total = [jnp.zeros((du_ref.shape[1], 128), F32)] * 2
    for q in range(du_ref.shape[0]):
        for c in range(0, cols, 128):
            at = slice(q * cols + c, q * cols + c + 128)
            dn = du_ref[q, :, c:c + 128] * gain_ref[:, at]
            total = [total[0] + dn, total[1] + dn * norm_ref[:, at]]
    out_ref[2:, :] = jnp.zeros_like(out_ref[2:, :])
    for j, x in enumerate(total):
        out_ref[j:j + 1, :] = jnp.sum(x.T, axis=0, keepdims=True)


def sums_pass(du, normed, gain):
    n, e = normed.shape
    return pl.pallas_call(
        sums_kernel,
        in_specs=[VMEM] * 3,
        out_specs=VMEM,
        out_shape=jax.ShapeDtypeStruct((8, n), F32),
        compiler_params=pltpu.CompilerParams(vmem_limit_bytes=VMEM_LIMIT),
        cost_estimate=pl.CostEstimate(flops=(4 * n * e) // COVER, bytes_accessed=n * e * 8, transcendentals=0),
        name="sums",
    )(du, normed, gain)


def back_kernel(vp, pre_ref, norm_ref, rstd_ref, z_ref, du_ref, m1_ref, m2_ref, gain_ref, loss_ref, db_ref, dab_ref, pack_ref):
    e, cols = z_ref.shape[1], du_ref.shape[1]
    for c in range(0, cols, 128):
        cs = slice(c, c + 128)
        a, du, normed = pre_ref[:, cs], du_ref[:, cs], norm_ref[:, cs]
        cdf = 0.5 * (1.0 + lax.erf(a * (0.5 ** 0.5)))
        dg = rstd_ref[...] * (du * gain_ref[:, cs] - m1_ref[...] - normed * m2_ref[...])
        da = dg * (cdf + a * (jnp.exp(-0.5 * a * a) * 0.3989422804014327))
        dab_ref[:, cs] = da.astype(BF16).astype(F32)
        for j, x in enumerate((da, du * normed, du)):
            pack_ref[e + j:e + j + 1, cs] = jnp.sum(x, axis=0, keepdims=True)
    pack_ref[:e, :] = lax.dot_general(z_ref[...], dab_ref[...].astype(BF16), (((0,), (0,)), ((), ())), preferred_element_type=F32)
    pack_ref[e + 3:e + 4, :] = loss_ref[...]
    pack_ref[e + 4:e + 8, :] = jnp.zeros_like(pack_ref[e + 4:e + 8, :])
    pack_ref[e + 8:, :] = db_ref[...]


def back_pass(vp, pre, normed, rstd, z, du, m1, m2, gain, loss, db):
    n, cols = du.shape
    e = z.shape[1]
    n_pack = e + 8 + db.shape[0]
    block = lambda *s: pl.BlockSpec(s, lambda i, p: (0,) * len(s))
    share = lambda r: pl.BlockSpec((r, cols), lambda i, p: (0, p[0]))
    gs = pltpu.PrefetchScalarGridSpec(
        num_scalar_prefetch=1,
        grid=(1,),
        in_specs=[share(n), share(n), block(n, 128), block(n, e), block(n, cols), block(n, 128), block(n, 128), share(1), block(1, cols), block(*db.shape)],
        out_specs=[block(n, cols), block(n_pack, cols)],
    )
    return pl.pallas_call(
        back_kernel,
        grid_spec=gs,
        out_shape=[jax.ShapeDtypeStruct((n, cols), F32), jax.ShapeDtypeStruct((n_pack, cols), F32)],
        compiler_params=pltpu.CompilerParams(dimension_semantics=("arbitrary",), vmem_limit_bytes=VMEM_LIMIT),
        cost_estimate=pl.CostEstimate(flops=(2 * n * e * cols) // COVER, bytes_accessed=n * (cols * 16 + e * 2 + 1536), transcendentals=n * cols * 2),
        name="back",
    )(vp, pre, normed, rstd, z, du, m1, m2, gain, loss, db)


def spread_kernel(n_masks, vp, pos_ref, w_ref, *refs):
    pieces, (out_ref, dab, dz, obuf, in_sem, out_sem) = refs[:4], refs[4:]
    n, cols = pieces[0].shape
    loads = [pltpu.make_async_copy(p, dab.at[:, pl.ds(pl.multiple_of((vp[0] ^ k) * cols, cols), cols)], in_sem.at[k]) for k, p in enumerate(pieces)]
    for c in loads:
        c.start()
    dz[n:, :] = jnp.zeros((dz.shape[0] - n, dz.shape[1]), F32)
    n_seq, seq_len, _ = out_ref.shape
    place = lax.broadcasted_iota(I32, (seq_len, 1), 0)
    slots = pos_ref.shape[2]
    for c in loads:
        c.wait()
    stores, done = [], 0
    for b in range(n_seq):
        while done < min(n, b * n_masks + slots):
            r1 = min(n, done + 304)
            dz[done:r1, :] = dot(dab[done:r1, :].astype(BF16), w_ref[...], NT).astype(BF16).astype(F32)
            done = r1
        if b >= 4:
            stores[b - 4].wait()
        hot = jnp.where(place == pos_ref[b], 1.0, 0.0).astype(BF16)
        obuf[b % 4] = dot(hot, dz[b * n_masks:b * n_masks + slots, :].astype(BF16), NN).astype(BF16)
        c = pltpu.make_async_copy(obuf.at[b % 4], out_ref.at[b], out_sem.at[b])
        c.start()
        stores.append(c)
    for c in stores[-4:]:
        c.wait()


def spread_pass(n_masks, shape, vp, pos, w, pieces):
    n, cols = pieces[0].shape
    e = w.shape[0]
    return pl.pallas_call(
        functools.partial(spread_kernel, n_masks),
        in_specs=[SMEM, VMEM, VMEM] + [ANY] * 4,
        out_specs=ANY,
        out_shape=jax.ShapeDtypeStruct(shape, BF16),
        scratch_shapes=[pltpu.VMEM((n, 4 * cols), F32), pltpu.VMEM((n + 16, e), F32), pltpu.VMEM((4,) + shape[1:], BF16), DMA((4,)), DMA((shape[0],))],
        compiler_params=pltpu.CompilerParams(vmem_limit_bytes=VMEM_LIMIT),
        cost_estimate=pl.CostEstimate(flops=(2 * shape[0] * shape[1] * 128 * e) // COVER, bytes_accessed=shape[0] * shape[1] * e * 2, transcendentals=0),
        name="spread",
    )(vp, pos, w, *pieces)


def order_sum(xs):
    return (xs[0] + xs[1]) + (xs[2] + xs[3])


def after(x, *deps):
    return lax.optimization_barrier((x, deps))[0]


def solution(mesh):
    n_groups, n_shards = mesh.shape["dp"], mesh.shape["vp"]

    def swap(a, bit):
        return lax.ppermute(a, "dp", [(d, d ^ bit) for d in range(n_groups)])

    def swap_vp(a, bit):
        return lax.ppermute(a, "vp", [(d, d ^ bit) for d in range(n_shards)])

    def hop(a):
        return lax.ppermute(a, "dp", [(d, d ^ (Y if d & CORE else X)) for d in range(n_groups)])

    def local_step(hidden, mask_pos, labels, w_trans, b_trans, ln_gain, ln_bias, emb_table, b_vocab):
        n_rows, _, width = hidden.shape
        n_masks = mask_pos.shape[1]
        shard_rows = emb_table.shape[0]
        n_loc = n_rows * n_masks
        n_tokens = n_loc * n_groups
        padded = -(-n_tokens // TB) * TB
        slots = -(-n_masks // 16) * 16
        cut = n_loc // 32 * 16
        cols = width // n_shards
        dp, vp = lax.axis_index("dp"), lax.axis_index("vp")
        row_start = vp * shard_rows
        scale = 1.0 / n_tokens

        pos_pad = jnp.pad(mask_pos, ((0, 0), (0, slots - n_masks)), constant_values=-1)
        z, pre, normed, rstd, u, u_lo, u_hi = head_pass(
            n_masks, cut, hidden, jnp.broadcast_to(pos_pad[:, :, None], (n_rows, slots, 128)),
            w_trans, b_trans[None], ln_gain[None], ln_bias[None])

        x_lo, y_hi = swap(u_lo, X), swap(u_hi, Y)
        x_hi, y_lo = swap(u_hi, X), swap(u_lo, Y)
        c_lo, c_hi = swap(u_lo, CORE), swap(u_hi, CORE)

        flat_labels = labels.reshape(n_loc)
        lab_local = flat_labels - row_start
        lab_local = jnp.where((lab_local >= 0) & (lab_local < shard_rows), lab_local, -1)
        lab_local = jnp.broadcast_to(lab_local[:, None], (n_loc, 128))
        logits, stat = stats(u, emb_table, b_vocab[None], lab_local)
        all_stats = [stat] + [swap_vp(stat, b) for b in range(1, n_shards)]
        global_max = functools.reduce(jnp.maximum, [s[0] for s in all_stats])
        log_norm = global_max + jnp.log(order_sum([s[1] * jnp.exp(s[0] - global_max) for s in all_stats]))
        loss_part = jnp.sum(log_norm - order_sum([s[2] for s in all_stats]))
        lse = log_norm + jnp.log(jnp.float32(n_tokens))
        x_lo, y_hi = after((x_lo, y_hi), lse)
        d_lo, d_hi = swap(x_lo, Y), swap(y_hi, X)

        du_part, db_part = du_pass(scale, n_shards, logits, emb_table, jnp.broadcast_to(lse[:, None], (n_loc, 128)), lab_local)
        du_share = lax.psum_scatter(du_part.reshape(n_shards * n_loc, cols), "vp", scatter_dimension=0, tiled=True)

        lse, x_hi, y_lo, u_lo, u_hi, c_lo, c_hi = after((lse, x_hi, y_lo, u_lo, u_hi, c_lo, c_hi), du_part)
        info = jnp.stack([lse, flat_labels.astype(F32)])
        info = jnp.stack([info] + [swap(info, b) for b in range(1, n_groups)])
        info = jnp.take(info, jnp.arange(n_groups) ^ dp, axis=0, mode="clip")
        fill = (0, padded - n_tokens)
        lse_all = jnp.pad(info[:, 0].reshape(-1), fill, constant_values=jnp.inf).reshape(-1, 1, TB)
        lab_all = jnp.pad(info[:, 1].reshape(-1).astype(I32), fill, constant_values=-1).reshape(-1, 1, TB)

        sums = sums_pass(du_part, normed, ln_gain[None])
        sums = order_sum([sums] + [swap_vp(sums, b) for b in range(1, n_shards)]) / width
        m1, m2 = (jnp.broadcast_to(sums[j][:, None], (n_loc, 128)) for j in range(2))

        at = lambda bits, off: (dp ^ bits) * n_loc + off
        halves = lambda bits, lo, hi: [(at(bits, 0), lo), (at(bits, cut), hi)]

        def narrow(big, items):
            return narrow_into(big, n_tokens, [r for r, _ in items], [a for _, a in items])

        u_all = narrow(None, halves(0, u_lo, u_hi) + halves(CORE, c_lo, c_hi))
        cx = swap(x_lo, CORE), swap(x_hi, CORE)
        cy = swap(y_lo, CORE), swap(y_hi, CORE)
        u_all = narrow(u_all, halves(X, x_lo, x_hi) + halves(Y, y_lo, y_hi) + halves(X | CORE, *cx) + halves(Y | CORE, *cy))
        d_lo, d_hi = after((d_lo, d_hi), u_all)
        u_all = narrow(u_all, halves(X | Y, d_lo, d_hi) + halves(X | Y | CORE, swap(d_lo, CORE), swap(d_hi, CORE)))

        core, mine = dp & 1, (dp >> 1 ^ dp >> 2) & 1
        half, quarter = shard_rows // 2, shard_rows // 4
        my_start = mine * half + core * quarter
        twin_start = mine * half + (1 - core) * quarter
        far_start = (1 - mine) * half + core * quarter
        far_twin_start = (1 - mine) * half + (1 - core) * quarter
        bias_col = lax.dynamic_slice(b_vocab, (my_start,), (quarter,))[:, None]
        shares = (960, 880, 768, 536)
        ends = [0]
        for w in shares[:-1]:
            ends.append(ends[-1] + max(16, quarter * w // sum(shares) // 16 * 16))
        spans = list(zip(ends, ends[1:] + [quarter]))

        def rows(k, big, puts, *wait):
            s0, s1 = spans[k]
            pos = jnp.stack([my_start + s0, row_start + my_start + s0] + [p for p, _ in puts])
            return rows_pass(scale, shard_rows, s1 - s0, after(pos, *wait), emb_table, u_all, bias_col[s0:s1], lse_all, lab_all,
                             big, [a for _, a in puts])

        def send(k, chunk):
            return (twin_start + spans[k][0], swap(chunk, CORE)), hop(chunk)

        def forward(k, far, *wait):
            far = after(far, *wait)
            return (far_start + spans[k][0], far), (far_twin_start + spans[k][0], swap(far, CORE))

        own = lambda k, chunk: (my_start + spans[k][0], chunk)
        chunk0, big = rows(0, None, [])
        twin0, far0 = send(0, chunk0)

        du_share = after(du_share, chunk0)
        loss_row = jnp.pad(loss_part[None, None], ((0, 0), (0, cols - 1)))
        db_rows = -(-shard_rows // cols // 8) * 8
        db_mat = jnp.pad(db_part[0], (0, db_rows * cols - shard_rows)).reshape(db_rows, cols)
        dab, pack = back_pass(vp[None], pre, normed, rstd, z, du_share, m1, m2, ln_gain[None], loss_row, db_mat)
        wait = dab
        pack = lax.psum(pack, "dp")
        dab = [dab] + [swap_vp(dab, b) for b in range(1, n_shards)]

        chunk1, big = rows(1, big, [own(0, chunk0)], wait)
        twin1, far1 = send(1, chunk1)
        far0, far_twin0 = forward(0, far0, chunk1)
        chunk2, big = rows(2, big, [own(1, chunk1), twin0, far0])
        twin2, far2 = send(2, chunk2)
        far1, far_twin1 = forward(1, far1, chunk2)

        pack = after(pack, chunk2)
        n_gather = width + 8
        part = lax.dynamic_slice(pack, (core * (n_gather // 2), 0), (n_gather // 2, cols))
        parts = [swap_vp(part, b) for b in range(1, n_shards)]

        chunk3, big = rows(3, big, [own(2, chunk2), twin1, far1, far_twin0])
        twin3, far3 = send(3, chunk3)
        far2, far_twin2 = forward(2, far2, chunk3)
        *dab_wait, parts = after((*dab, parts), chunk3)
        d_hidden = spread_pass(n_masks, hidden.shape, vp[None], pos_pad[:, None], w_trans, dab_wait)
        others = [swap(p, CORE) for p in parts]
        items = [own(3, chunk3), twin2, far2, far_twin1, far_twin2, twin3]
        big = put_rows(jnp.stack([p for p, _ in items]), big, [a for _, a in items])
        items = forward(3, far3)
        big = put_rows(jnp.stack([p for p, _ in items]), big, [a for _, a in items])

        gathered = [pack[:n_gather]]
        for p, o in zip(parts, others):
            gathered.append(jnp.concatenate([jnp.where(core == 0, p, o), jnp.where(core == 0, o, p)]))
        gathered = jnp.take(jnp.stack(gathered), jnp.arange(n_shards) ^ vp, axis=0, mode="clip")
        gathered = jnp.transpose(gathered, (1, 0, 2)).reshape(n_gather, width)
        db = pack[n_gather:].reshape(-1)[:shard_rows]
        return (pack[width + 3, 0] / n_tokens, d_hidden, gathered[:width], gathered[width], gathered[width + 1], gathered[width + 2], big, db)

    in_specs = (P("dp", None, None), P("dp", None), P("dp", None), P(None, None), P(None), P(None), P(None), P("vp", None), P("vp"))
    out_specs = (P(), P("dp", None, None), P(None, None), P(None), P(None), P(None), P("vp", None), P("vp"))
    return jax.shard_map(local_step, mesh=mesh, in_specs=in_specs, out_specs=out_specs, check_vma=False)
```

time: 675 us -> 659 us (0.976)
  the two profiles are of different devices: /device:TPU:0 before, /device:TPU:9 now
where the time goes in v1:
time: 659 us; the launch traced here: 652 us
  Pallas kernels  378 us (57%)
  waiting for transfers between devices  154 us (23%)
  local copies, waits for them, and re-layouts  47.5 us (7%)
  starting transfers between devices  44.5 us (7%)
  between operations  16.4 us (2%)
  other arithmetic  11.3 us (2%)
    pallas_call x4, Pallas kernels, rows_pass(): pl.pallas_call(functools.partial(rows_kernel, scale, m, len(puts), has_bi...  194 us
    psum x1, waiting for transfers between devices, local_step(): pack = lax.psum(pack, 'dp')  59.9 us
    pallas_call x1, Pallas kernels, stats(): pl.pallas_call(functools.partial(stats_kernel, v), grid=(n,), in_specs=[w...  53.9 us
    ppermute x12, waiting for transfers between devices, swap_vp(): return lax.ppermute(a, 'vp', [(d, d ^ bit) for d in range(n_shards)])  47.9 us
    pallas_call x1, Pallas kernels, du_pass(): pl.pallas_call(functools.partial(du_kernel, v, scale), grid=(n,), in_spec...  46.1 us
    ppermute x32, waiting for transfers between devices, swap(): return lax.ppermute(a, 'dp', [(d, d ^ bit) for d in range(n_groups)])  46 us
    ppermute x32, starting transfers between devices, swap(): return lax.ppermute(a, 'dp', [(d, d ^ bit) for d in range(n_groups)])  28 us
    pallas_call x3, Pallas kernels, narrow_into(): pl.pallas_call(functools.partial(narrow_kernel, first, [p.shape[0] for p...  25.5 us
  transfers between devices with their start and end apart: 50, of which 16 were waited for; matrix products, arithmetic and copies ran while one was open for 8% of the time, Pallas kernels for 55%

profile of v1, /device:TPU:9, one launch (start us, length us, event | category | flops | bytes accessed | tf_op | source)
XLA Modules:
  0.0 651.8 jit_solution(7792562295366547290)
XLA Ops:
  9.0 15.7 %head.1 = (bf16[1232,1024]{1,0:T(8,128)(2,1)}, f32[1232,1024]{1,0:T(8,128)}, f32[1232,1024]{1,0:T(8,128)}, f32[1232,128]{1,0:T(8,128)}, bf16[1232,1024]{1,0:T(8,...) custom-call(bf16[16,512,1024]{2,1,0:T(8,128)(2,1)} %hid.1, s32[16,80,128]{2,1,0:T(8,128)} %broadcast_in_dim.66.pos_ref, ...), custom_call_target="tpu_custom_call" | custom-call | flops 51673824 | bytes 42008576 | tf_op jit(solution)/shard_map/head/pallas_call | solution.py:221
  29.1 53.9 %stats.1 = (f32[1232,12576]{1,0:T(8,128)}, f32[8,1232]{1,0:T(8,128)}) custom-call(bf16[1232,1024]{1,0:T(8,128)(2,1)} %get-tuple-element.57.u_ref, bf16[12576,1024]{1,0:T(8,128)(2,1)} %emb_hbm.7, f32[1,12576]{1,0:T(1,128)} %broadcast_in_dim.70.b_ref, s32[1232,128]{1,0:T(8,128)} %broadcast_in_dim.72.lab_ref), custom_call_target="tpu_custom_call" | custom-call | flops 317309568 | bytes 87730176 | tf_op jit(solution)/shard_map/stats/pallas_call | solution.py:81
  83.1 2.3 collective-permute-start.1
  86.3 1.3 collective-permute-done.1
  87.6 2.3 collective-permute-start.6
  91.2 2.0 collective-permute-start.5
  93.8 1.3 broadcast_in_dim.73.lse_ref
  95.1 46.1 %du_pass.1 = (f32[4,1232,256]{2,1,0:T(8,128)}, f32[1,12576]{1,0:T(1,128)}) custom-call(f32[1232,12576]{1,0:T(8,128)} %get-tuple-element.58.logits_ref, bf16[12576,1024]{1,0:T(8,128)(2,1)} %emb_hbm.7, f32[1232,128]{1,0:T(8,128)} %broadcast_in_dim.73.lse_ref, s32[1232,128]{1,0:T(8,128)} %broadcast_in_dim.72.lab_ref), custom_call_target="tpu_custom_call" | custom-call | flops 317309568 | bytes 87730176 | tf_op jit(solution)/shard_map/du_pass/pallas_call | solution.py:148
  141.7 2.5 collective-permute-done.4.refs_3_
  144.2 2.6 collective-permute-start.11
  147.5 3.9 collective-permute-done.17
  155.6 7.0 %narrow.3.refs_0_ = bf16[9984,1024]{1,0:T(8,128)(2,1)} custom-call(s32[4]{0:T(128)} %pad_add_fusion.2.pos, f32[608,1024]{1,0:T(8,128)} %get-tuple-element.63.refs_0_, f32[624,1024]{1,0:T(8,128)} %get-tuple-element.64.refs_1_, f32[608,1024]{1,0:T(8,128)} %collective-permute-done.5.refs_2_, f32[624,1024]{1,0:T(8,128)} %collective-permute-done.6.refs_3_), custom_call_target="tpu_custom_call" | custom-call | flops 25231 | bytes 15138816 | tf_op jit(solution)/shard_map/narrow/pallas_call | solution.py:268
  163.9 1.4 collective-permute-start.19
  166.5 11.8 %narrow.4.refs_0_ = bf16[9984,1024]{1,0:T(8,128)(2,1)} custom-call(s32[8]{0:T(128)} %stack.204.pos, bf16[9984,1024]{1,0:T(8,128)(2,1)} %narrow.3.refs_0_, f32[608,1024]{1,0:T(8,128)} %collective-permute-done.7.refs_1_, f32[624,1024]{1,0:T(8,128)} %collective-permute-done.3.refs_2_, ...), custom_call_target="tpu_custom_call", output_to_operand_aliasing={{}: (1, {})} | custom-call | flops 50462 | bytes 30277632 | tf_op jit(solution)/shard_map/narrow/pallas_call | solution.py:268
  178.3 28.7 %collective-permute-done.13.refs_1_ = f32[608,1024]{1,0:T(8,128)} collective-permute-done((f32[608,1024]{1,0:T(8,128)}, f32[608,1024]{1,0:T(8,128)}, u32[]{:S(2)}, u32[]{:S(2)}) %collective-permute-start.13) | collective-permute-done | bytes 2490400 | tf_op jit(solution)/shard_map/ppermute | solution.py:508
  207.0 1.7 collective-permute-start.21
  209.7 1.7 collective-permute-start.22
  213.2 2.3 collective-permute-done.23
  218.0 1.5 copy-done.1
  219.5 6.8 %narrow.5.u_hbm = bf16[9984,1024]{1,0:T(8,128)(2,1)} custom-call(s32[4]{0:T(128)} %pad_add_fusion.1.pos, bf16[9984,1024]{1,0:T(8,128)(2,1)} %narrow.4.refs_0_, f32[608,1024]{1,0:T(8,128)} %collective-permute-done.13.refs_1_, f32[624,1024]{1,0:T(8,128)} %collective-permute-done.14.refs_2_, ...), custom_call_target="tpu_custom_call", output_to_operand_aliasing={{}: (1, {})} | custom-call | flops 25231 | bytes 15138816 | tf_op jit(solution)/shard_map/narrow/pallas_call | solution.py:268
  226.3 54.6 %rows.4 = (f32[960,1024]{1,0:T(8,128)}, f32[12576,1024]{1,0:T(8,128)}) custom-call(s32[2]{0:T(128)} %pad_add_fusion.pos, bf16[12576,1024]{1,0:T(8,128)(2,1)} %emb_hbm.7, bf16[9984,1024]{1,0:T(8,128)(2,1)} %narrow.5.u_hbm, f32[960,1]{1,0:T(8,128)} %copy.24.bias_ref, f32[13,1,768]{2,1,0:T(1,128)} %reshape.155.lse_ref, s32[13,1,768]{2,1,0:T(1,128)} %reshape.156.lab_ref), custom_call_target="tpu_custom_call" | custom-call | flops 392586848 | bytes 26345472 | tf_op jit(solution)/shard_map/rows/pallas_call | solution.py:340
  282.1 5.5 sums.1
  287.5 1.7 collective-permute-start.24
  289.2 1.8 collective-permute-start.25
  297.9 6.2 back.1
  304.1 51.1 %rows.5 = (f32[880,1024]{1,0:T(8,128)}, f32[12576,1024]{1,0:T(8,128)}) custom-call(s32[3]{0:T(128)} %pad_add_fusion.3.pos, bf16[12576,1024]{1,0:T(8,128)(2,1)} %emb_hbm.7, bf16[9984,1024]{1,0:T(8,128)(2,1)} %narrow.5.u_hbm, f32[880,1]{1,0:T(8,128)} %slice.140.bias_ref, f32[13,1,768]{2,1,0:T(1,128)} %reshape.155.lse_ref, ...), custom_call_target="tpu_custom_call", output_to_operand_aliasing={{1}: (6, {})} | custom-call | flops 359871296 | bytes 25853952 | tf_op jit(solution)/shard_map/rows/pallas_call | solution.py:340
  359.6 48.6 %rows.6 = (f32[768,1024]{1,0:T(8,128)}, f32[12576,1024]{1,0:T(8,128)}) custom-call(s32[5]{0:T(128)} %stack.226.pos, bf16[12576,1024]{1,0:T(8,128)(2,1)} %emb_hbm.7, bf16[9984,1024]{1,0:T(8,128)(2,1)} %narrow.5.u_hbm, f32[768,1]{1,0:T(8,128)} %slice.139.bias_ref, f32[13,1,768]{2,1,0:T(1,128)} %reshape.155.lse_ref, ...), custom_call_target="tpu_custom_call", output_to_operand_aliasing={{1}: (6, {})} | custom-call | flops 314069472 | bytes 25165824 | tf_op jit(solution)/shard_map/rows/pallas_call | solution.py:340
  408.9 1.8 collective-permute-start.29
  413.5 39.2 %rows.7 = (f32[536,1024]{1,0:T(8,128)}, f32[12576,1024]{1,0:T(8,128)}) custom-call(s32[6]{0:T(128)} %stack.234.pos, bf16[12576,1024]{1,0:T(8,128)(2,1)} %emb_hbm.7, bf16[9984,1024]{1,0:T(8,128)(2,1)} %narrow.5.u_hbm, f32[536,1]{1,0:T(8,128)} %slice.141.bias_ref, f32[13,1,768]{2,1,0:T(1,128)} %reshape.155.lse_ref, ...), custom_call_target="tpu_custom_call", output_to_operand_aliasing={{1}: (6, {})} | custom-call | flops 219194320 | bytes 23740416 | tf_op jit(solution)/shard_map/rows/pallas_call | solution.py:340
  453.7 59.9 %all-reduce.7.cloned.1.call-done = f32[1088,256]{1,0:T(8,128)} async-done(((f32[1088,256]{1,0:T(8,128)}), f32[1088,256]{1,0:T(8,128)}) %all-reduce.7.cloned.1.call-update) | async-done | bytes 1114128 | tf_op jit(solution)/shard_map/psum | solution.py:616
  515.0 2.1 collective-permute-start.33
  517.2 3.6 collective-permute-done.31.refs_3_
  521.7 11.5 %collective-permute-done.32 = f32[516,256]{1,0:T(8,128)S(1)} collective-permute-done((f32[516,256]{1,0:T(8,128)S(1)}, f32[516,256]{1,0:T(8,128)S(1)}, u32[]{:S(2)}, u32[]{:S(2)}) %collective-permute-start.32) | collective-permute-done | bytes 528416 | tf_op jit(solution)/shard_map/ppermute | solution.py:511
  533.2 2.4 collective-permute-start.43
  535.6 18.0 %collective-permute-done.33 = f32[516,256]{1,0:T(8,128)} collective-permute-done((f32[516,256]{1,0:T(8,128)S(1)}, f32[516,256]{1,0:T(8,128)}, u32[]{:S(2)}, u32[]{:S(2)}) %collective-permute-start.33) | collective-permute-done | bytes 528416 | tf_op jit(solution)/shard_map/ppermute | solution.py:511
  553.7 12.8 %collective-permute-done.34 = f32[516,256]{1,0:T(8,128)} collective-permute-done((f32[516,256]{1,0:T(8,128)S(1)}, f32[516,256]{1,0:T(8,128)}, u32[]{:S(2)}, u32[]{:S(2)}) %collective-permute-start.34) | collective-permute-done | bytes 528416 | tf_op jit(solution)/shard_map/ppermute | solution.py:511
  570.2 1.3 slice_bitcast_fusion
  571.5 7.8 %collective-permute-done.38 = f32[516,256]{1,0:T(8,128)S(1)} collective-permute-done((f32[516,256]{1,0:T(8,128)S(1)}, f32[516,256]{1,0:T(8,128)S(1)}, u32[]{:S(2)}, u32[]{:S(2)}) %collective-permute-start.38) | collective-permute-done | bytes 528416 | tf_op jit(solution)/shard_map/ppermute | solution.py:508
  584.6 14.7 %spread.1 = bf16[16,512,1024]{2,1,0:T(8,128)(2,1)} custom-call(s32[1]{0:T(128)} %bitcast.vp, s32[16,1,80]{2,1,0:T(1,128)} %bitcast.86, bf16[1024,1024]{1,0:T(8,128)(2,1)} %w_ref.3, f32[1232,256]{1,0:T(8,128)} %get-tuple-element.89.refs_0_, f32[1232,256]{1,0:T(8,128)} %collective-permute-done.29.refs_1_, f32[1232,256]{1,0:T(8,128)} %collective-permute-done.30.refs_2_, ...), custom_call_target="tpu_custom_call" | custom-call | flops 21474836 | bytes 16777216 | tf_op jit(solution)/shard_map/spread/pallas_call | solution.py:484
  600.7 1.3 broadcast_select_fusion.3
  602.2 2.5 pad_maximum_fusion
  604.7 5.0 gather_fusion.1
  609.7 4.6 slice.159
  614.2 5.4 copy.28
  619.7 5.3 copy.29
  625.0 1.5 fusion.3
  626.5 12.7 %put_rows.2.refs_0_ = f32[12576,1024]{1,0:T(8,128)} custom-call(s32[6]{0:T(128)} %stack.248.pos, f32[12576,1024]{1,0:T(8,128)} %get-tuple-element.96.refs_0_, f32[536,1024]{1,0:T(8,128)} %get-tuple-element.88.refs_1_, f32[768,1024]{1,0:T(8,128)} %collective-permute-done.41.refs_2_, ...), custom_call_target="tpu_custom_call", output_to_operand_aliasing={{}: (1, {})} | custom-call | flops 43581 | bytes 34865152 | tf_op jit(solution)/shard_map/put_rows/pallas_call | solution.py:374
  639.3 4.4 put_rows.3
  (166 shorter events, 51.3 us)
Async XLA Ops:
  7.2 288.6 %reduce-scatter.2.cloned.1.call-start = ((), (), s32[]{:S(2)}) async-start(), calls=%async_computation.1 | async-start | bytes 6307840 | tf_op jit(solution)/shard_map/reduce_scatter | solution.py:553
  24.7 66.5 %collective-permute-start.7 = (f32[608,1024]{1,0:T(8,128)}, f32[608,1024]{1,0:T(8,128)}, u32[]{:S(2)}, u32[]{:S(2)}) collective-permute-start(f32[608,1024]{1,0:T(8,128)} %get-tuple-element.63.refs_0_), channel_id=1, source_target_pairs={{0,2},{1,3},{2,0},{3,1},{4,6},{5,7},{6,4},{7,5},{8,10},{9,11},{10,... | collective-permute-start | bytes 7471112 | tf_op jit(solution)/shard_map/ppermute | solution.py:508
  26.0 67.8 %collective-permute-start.8 = (f32[624,1024]{1,0:T(8,128)}, f32[624,1024]{1,0:T(8,128)S(1)}, u32[]{:S(2)}, u32[]{:S(2)}) collective-permute-start(f32[624,1024]{1,0:T(8,128)} %get-tuple-element.64.refs_1_), channel_id=1, source_target_pairs={{0,4},{1,5},{2,6},{3,7},{4,0},{5,1},{6,2},{7,3},{8,12},{9,13},{10,... | collective-permute-start | bytes 7667720 | tf_op jit(solution)/shard_map/ppermute | solution.py:508
  83.1 4.4 collective-permute-start.1
  85.4 4.5 collective-permute-start.2
  86.0 58.2 %collective-permute-start.3 = (f32[624,1024]{1,0:T(8,128)}, f32[624,1024]{1,0:T(8,128)}, u32[]{:S(2)}, u32[]{:S(2)}) collective-permute-start(f32[624,1024]{1,0:T(8,128)} %get-tuple-element.64.refs_1_), channel_id=1, source_target_pairs={{0,2},{1,3},{2,0},{3,1},{4,6},{5,7},{6,4},{7,5},{8,10},{9,11},{10,... | collective-permute-start | bytes 7667720 | tf_op jit(solution)/shard_map/ppermute | solution.py:508
  87.6 56.6 %collective-permute-start.6 = (f32[624,1024]{1,0:T(8,128)}, f32[624,1024]{1,0:T(8,128)}, u32[]{:S(2)}, u32[]{:S(2)}) collective-permute-start(f32[624,1024]{1,0:T(8,128)} %get-tuple-element.64.refs_1_), channel_id=1, source_target_pairs={{0,1},{1,0},{2,3},{3,2},{4,5},{5,4},{6,7},{7,6},{8,9},{9,8},{10,11... | collective-permute-start | bytes 7667720 | tf_op jit(solution)/shard_map/ppermute | solution.py:508
  89.9 54.3 %collective-permute-start.4 = (f32[608,1024]{1,0:T(8,128)}, f32[608,1024]{1,0:T(8,128)}, u32[]{:S(2)}, u32[]{:S(2)}) collective-permute-start(f32[608,1024]{1,0:T(8,128)} %get-tuple-element.63.refs_0_), channel_id=1, source_target_pairs={{0,4},{1,5},{2,6},{3,7},{4,0},{5,1},{6,2},{7,3},{8,12},{9,13},{10,... | collective-permute-start | bytes 7471112 | tf_op jit(solution)/shard_map/ppermute | solution.py:508
  91.2 53.0 %collective-permute-start.5 = (f32[608,1024]{1,0:T(8,128)}, f32[608,1024]{1,0:T(8,128)}, u32[]{:S(2)}, u32[]{:S(2)}) collective-permute-start(f32[608,1024]{1,0:T(8,128)} %get-tuple-element.63.refs_0_), channel_id=1, source_target_pairs={{0,1},{1,0},{2,3},{3,2},{4,5},{5,4},{6,7},{7,6},{8,9},{9,8},{10,11... | collective-permute-start | bytes 7471112 | tf_op jit(solution)/shard_map/ppermute | solution.py:508
  93.8 58.0 %collective-permute-start.9 = (f32[608,1024]{1,0:T(8,128)}, f32[608,1024]{1,0:T(8,128)}, u32[]{:S(2)}, u32[]{:S(2)}) collective-permute-start(f32[608,1024]{1,0:T(8,128)} %collective-permute-done.7.refs_1_), channel_id=1, source_target_pairs={{0,1},{1,0},{2,3},{3,2},{4,5},{5,4},{6,7},{7,6},{8,9},{9,8},{10,11... | collective-permute-start | bytes 7471112 | tf_op jit(solution)/shard_map/ppermute | solution.py:508
  141.2 372.4 %all-reduce.7.cloned.1.call-start = ((), (), s32[]{:S(2)}) async-start(), calls=%async_computation.2 | async-start | bytes 2228224 | tf_op jit(solution)/shard_map/psum | solution.py:616
  144.2 18.4 %collective-permute-start.11 = (f32[608,1024]{1,0:T(8,128)}, f32[608,1024]{1,0:T(8,128)}, u32[]{:S(2)}, u32[]{:S(2)}) collective-permute-start(f32[608,1024]{1,0:T(8,128)} %collective-permute-done.4.refs_3_), channel_id=1, source_target_pairs={{0,1},{1,0},{2,3},{3,2},{4,5},{5,4},{6,7},{7,6},{8,9},{9,8},{10,11... | collective-permute-start | bytes 7471112 | tf_op jit(solution)/shard_map/ppermute | solution.py:508
  146.9 4.6 collective-permute-start.17
  147.0 17.0 %collective-permute-start.12 = (f32[624,1024]{1,0:T(8,128)S(1)}, f32[624,1024]{1,0:T(8,128)}, u32[]{:S(2)}, u32[]{:S(2)}) collective-permute-start(f32[624,1024]{1,0:T(8,128)S(1)} %collective-permute-done.8.refs_4_), channel_id=1, source_target_pairs={{0,1},{1,0},{2,3},{3,2},{4,5},{5,4},{6,7},{7,6},{8,9},{9,8},{10,11... | collective-permute-start | bytes 7667720 | tf_op jit(solution)/shard_map/ppermute | solution.py:508
  147.5 17.8 %collective-permute-start.10 = (f32[624,1024]{1,0:T(8,128)}, f32[624,1024]{1,0:T(8,128)}, u32[]{:S(2)}, u32[]{:S(2)}) collective-permute-start(f32[624,1024]{1,0:T(8,128)} %collective-permute-done.3.refs_2_), channel_id=1, source_target_pairs={{0,1},{1,0},{2,3},{3,2},{4,5},{5,4},{6,7},{7,6},{8,9},{9,8},{10,11... | collective-permute-start | bytes 7667720 | tf_op jit(solution)/shard_map/ppermute | solution.py:508
  151.5 57.3 %collective-permute-start.14 = (f32[624,1024]{1,0:T(8,128)S(1)}, f32[624,1024]{1,0:T(8,128)}, u32[]{:S(2)}, u32[]{:S(2)}) collective-permute-start(f32[624,1024]{1,0:T(8,128)S(1)} %collective-permute-done.8.refs_4_), channel_id=1, source_target_pairs={{0,2},{1,3},{2,0},{3,1},{4,6},{5,7},{6,4},{7,5},{8,10},{9,11},{10,... | collective-permute-start | bytes 7667720 | tf_op jit(solution)/shard_map/ppermute | solution.py:508
  151.7 55.3 %collective-permute-start.13 = (f32[608,1024]{1,0:T(8,128)}, f32[608,1024]{1,0:T(8,128)}, u32[]{:S(2)}, u32[]{:S(2)}) collective-permute-start(f32[608,1024]{1,0:T(8,128)} %collective-permute-done.7.refs_1_), channel_id=1, source_target_pairs={{0,4},{1,5},{2,6},{3,7},{4,0},{5,1},{6,2},{7,3},{8,12},{9,13},{10,... | collective-permute-start | bytes 7471112 | tf_op jit(solution)/shard_map/ppermute | solution.py:508
  162.6 47.0 %collective-permute-start.18 = (f32[2,1232]{1,0:T(2,128)S(1)}, f32[2,1232]{1,0:T(2,128)S(1)}, u32[]{:S(2)}, u32[]{:S(2)}) collective-permute-start(f32[2,1232]{1,0:T(2,128)S(1)} %pad_maximum_fusion.1), channel_id=1, source_target_pairs={{0,2},{1,3},{2,0},{3,1},{4,6},{5,7},{6,4},{7,5},{8,10},{9,11},{10,... | collective-permute-start | bytes 29576 | tf_op jit(solution)/shard_map/ppermute | solution.py:508
  163.9 45.7 %collective-permute-start.19 = (f32[2,1232]{1,0:T(2,128)S(1)}, f32[2,1232]{1,0:T(2,128)S(1)}, u32[]{:S(2)}, u32[]{:S(2)}) collective-permute-start(f32[2,1232]{1,0:T(2,128)S(1)} %pad_maximum_fusion.1), channel_id=1, source_target_pairs={{0,3},{1,2},{2,1},{3,0},{4,7},{5,6},{6,5},{7,4},{8,11},{9,10},{10,... | collective-permute-start | bytes 29576 | tf_op jit(solution)/shard_map/ppermute | solution.py:508
  165.3 46.1 %collective-permute-start.20 = (f32[2,1232]{1,0:T(2,128)S(1)}, f32[2,1232]{1,0:T(2,128)S(1)}, u32[]{:S(2)}, u32[]{:S(2)}) collective-permute-start(f32[2,1232]{1,0:T(2,128)S(1)} %pad_maximum_fusion.1), channel_id=1, source_target_pairs={{0,4},{1,5},{2,6},{3,7},{4,0},{5,1},{6,2},{7,3},{8,12},{9,13},{10,... | collective-permute-start | bytes 29576 | tf_op jit(solution)/shard_map/ppermute | solution.py:508
  207.0 5.7 collective-permute-start.21
  208.7 9.3 %collective-permute-start.16 = (f32[624,1024]{1,0:T(8,128)}, f32[624,1024]{1,0:T(8,128)S(1)}, u32[]{:S(2)}, u32[]{:S(2)}) collective-permute-start(f32[624,1024]{1,0:T(8,128)} %collective-permute-done.14.refs_2_), channel_id=1, source_target_pairs={{0,1},{1,0},{2,3},{3,2},{4,5},{5,4},{6,7},{7,6},{8,9},{9,8},{10,11... | collective-permute-start | bytes 7667720 | tf_op jit(solution)/shard_map/ppermute | solution.py:508
  209.7 8.3 %collective-permute-start.15 = (f32[608,1024]{1,0:T(8,128)}, f32[608,1024]{1,0:T(8,128)}, u32[]{:S(2)}, u32[]{:S(2)}) collective-permute-start(f32[608,1024]{1,0:T(8,128)} %collective-permute-done.13.refs_1_), channel_id=1, source_target_pairs={{0,1},{1,0},{2,3},{3,2},{4,5},{5,4},{6,7},{7,6},{8,9},{9,8},{10,11... | collective-permute-start | bytes 7471112 | tf_op jit(solution)/shard_map/ppermute | solution.py:508
  209.7 3.5 collective-permute-start.22
  211.4 4.0 collective-permute-start.23
  281.0 74.3 %collective-permute-start.28 = (f32[960,1024]{1,0:T(8,128)}, f32[960,1024]{1,0:T(8,128)}, u32[]{:S(2)}, u32[]{:S(2)}) collective-permute-start(f32[960,1024]{1,0:T(8,128)} %get-tuple-element.74.refs_1_), channel_id=1, source_target_pairs={{0,2},{1,5},{2,0},{3,7},{4,6},{5,1},{6,4},{7,3},{8,10},{9,13},{10,... | collective-permute-start | bytes 11796488 | tf_op jit(solution)/shard_map/ppermute | solution.py:514
  281.7 77.9 %collective-permute-start.27 = (f32[960,1024]{1,0:T(8,128)}, f32[960,1024]{1,0:T(8,128)}, u32[]{:S(2)}, u32[]{:S(2)}) collective-permute-start(f32[960,1024]{1,0:T(8,128)} %get-tuple-element.74.refs_1_), channel_id=1, source_target_pairs={{0,1},{1,0},{2,3},{3,2},{4,5},{5,4},{6,7},{7,6},{8,9},{9,8},{10,11... | collective-permute-start | bytes 11796488 | tf_op jit(solution)/shard_map/ppermute | solution.py:508
  287.5 7.2 %collective-permute-start.24 = (f32[8,1232]{1,0:T(8,128)}, f32[8,1232]{1,0:T(8,128)S(1)}, u32[]{:S(2)}, u32[]{:S(2)}) collective-permute-start(f32[8,1232]{1,0:T(8,128)} %sums.1), channel_id=1, source_target_pairs={{0,8},{8,0},{16,24},{24,16},{1,9},{9,1},{17,25},{25,17},{2,10},{10... | collective-permute-start | bytes 118280 | tf_op jit(solution)/shard_map/ppermute | solution.py:511
  289.2 5.5 collective-permute-start.25
  291.0 3.9 collective-permute-start.26
  355.3 58.2 %collective-permute-start.37 = (f32[960,1024]{1,0:T(8,128)}, f32[960,1024]{1,0:T(8,128)}, u32[]{:S(2)}, u32[]{:S(2)}) collective-permute-start(f32[960,1024]{1,0:T(8,128)} %collective-permute-done.28.refs_3_), channel_id=1, source_target_pairs={{0,1},{1,0},{2,3},{3,2},{4,5},{5,4},{6,7},{7,6},{8,9},{9,8},{10,11... | collective-permute-start | bytes 11796488 | tf_op jit(solution)/shard_map/ppermute | solution.py:508
  356.6 54.2 %collective-permute-start.36 = (f32[880,1024]{1,0:T(8,128)}, f32[880,1024]{1,0:T(8,128)}, u32[]{:S(2)}, u32[]{:S(2)}) collective-permute-start(f32[880,1024]{1,0:T(8,128)} %get-tuple-element.82.refs_1_), channel_id=1, source_target_pairs={{0,2},{1,5},{2,0},{3,7},{4,6},{5,1},{6,4},{7,3},{8,10},{9,13},{10,... | collective-permute-start | bytes 10813448 | tf_op jit(solution)/shard_map/ppermute | solution.py:514
  357.6 54.0 %collective-permute-start.35 = (f32[880,1024]{1,0:T(8,128)}, f32[880,1024]{1,0:T(8,128)}, u32[]{:S(2)}, u32[]{:S(2)}) collective-permute-start(f32[880,1024]{1,0:T(8,128)} %get-tuple-element.82.refs_1_), channel_id=1, source_target_pairs={{0,1},{1,0},{2,3},{3,2},{4,5},{5,4},{6,7},{7,6},{8,9},{9,8},{10,11... | collective-permute-start | bytes 10813448 | tf_op jit(solution)/shard_map/ppermute | solution.py:508
  408.2 159.5 %collective-permute-start.42 = (f32[768,1024]{1,0:T(8,128)}, f32[768,1024]{1,0:T(8,128)}, u32[]{:S(2)}, u32[]{:S(2)}) collective-permute-start(f32[768,1024]{1,0:T(8,128)} %get-tuple-element.84.refs_1_), channel_id=1, source_target_pairs={{0,2},{1,5},{2,0},{3,7},{4,6},{5,1},{6,4},{7,3},{8,10},{9,13},{10,... | collective-permute-start | bytes 9437192 | tf_op jit(solution)/shard_map/ppermute | solution.py:514
  408.9 105.8 %collective-permute-start.29 = (f32[1232,256]{1,0:T(8,128)}, f32[1232,256]{1,0:T(8,128)}, u32[]{:S(2)}, u32[]{:S(2)}) collective-permute-start(f32[1232,256]{1,0:T(8,128)} %get-tuple-element.89.refs_0_), channel_id=1, source_target_pairs={{0,8},{8,0},{16,24},{24,16},{1,9},{9,1},{17,25},{25,17},{2,10},{10... | collective-permute-start | bytes 3784712 | tf_op jit(solution)/shard_map/ppermute | solution.py:511
  410.7 104.3 %collective-permute-start.30 = (f32[1232,256]{1,0:T(8,128)}, f32[1232,256]{1,0:T(8,128)}, u32[]{:S(2)}, u32[]{:S(2)}) collective-permute-start(f32[1232,256]{1,0:T(8,128)} %get-tuple-element.89.refs_0_), channel_id=1, source_target_pairs={{0,16},{8,24},{16,0},{24,8},{1,17},{9,25},{17,1},{25,9},{2,18},{10... | collective-permute-start | bytes 3784712 | tf_op jit(solution)/shard_map/ppermute | solution.py:511
  411.6 109.2 %collective-permute-start.31 = (f32[1232,256]{1,0:T(8,128)}, f32[1232,256]{1,0:T(8,128)}, u32[]{:S(2)}, u32[]{:S(2)}) collective-permute-start(f32[1232,256]{1,0:T(8,128)} %get-tuple-element.89.refs_0_), channel_id=1, source_target_pairs={{0,24},{8,16},{16,8},{24,0},{1,25},{9,17},{17,9},{25,1},{2,26},{10... | collective-permute-start | bytes 3784712 | tf_op jit(solution)/shard_map/ppermute | solution.py:511
  452.7 117.3 %collective-permute-start.46 = (f32[536,1024]{1,0:T(8,128)}, f32[536,1024]{1,0:T(8,128)}, u32[]{:S(2)}, u32[]{:S(2)}) collective-permute-start(f32[536,1024]{1,0:T(8,128)} %get-tuple-element.88.refs_1_), channel_id=1, source_target_pairs={{0,2},{1,5},{2,0},{3,7},{4,6},{5,1},{6,4},{7,3},{8,10},{9,13},{10,... | collective-permute-start | bytes 6586376 | tf_op jit(solution)/shard_map/ppermute | solution.py:514
  514.7 18.5 %collective-permute-start.32 = (f32[516,256]{1,0:T(8,128)S(1)}, f32[516,256]{1,0:T(8,128)S(1)}, u32[]{:S(2)}, u32[]{:S(2)}) collective-permute-start(f32[516,256]{1,0:T(8,128)S(1)} %constant_dynamic-slice_fusion), channel_id=1, source_target_pairs={{0,8},{8,0},{16,24},{24,16},{1,9},{9,1},{17,25},{25,17},{2,10},{10... | collective-permute-start | bytes 1585160 | tf_op jit(solution)/shard_map/ppermute | solution.py:511
  515.0 38.6 %collective-permute-start.33 = (f32[516,256]{1,0:T(8,128)S(1)}, f32[516,256]{1,0:T(8,128)}, u32[]{:S(2)}, u32[]{:S(2)}) collective-permute-start(f32[516,256]{1,0:T(8,128)S(1)} %constant_dynamic-slice_fusion), channel_id=1, source_target_pairs={{0,16},{8,24},{16,0},{24,8},{1,17},{9,25},{17,1},{25,9},{2,18},{10... | collective-permute-start | bytes 1585160 | tf_op jit(solution)/shard_map/ppermute | solution.py:511
  520.8 45.7 %collective-permute-start.34 = (f32[516,256]{1,0:T(8,128)S(1)}, f32[516,256]{1,0:T(8,128)}, u32[]{:S(2)}, u32[]{:S(2)}) collective-permute-start(f32[516,256]{1,0:T(8,128)S(1)} %constant_dynamic-slice_fusion), channel_id=1, source_target_pairs={{0,24},{8,16},{16,8},{24,0},{1,25},{9,17},{17,9},{25,1},{2,26},{10... | collective-permute-start | bytes 1585160 | tf_op jit(solution)/shard_map/ppermute | solution.py:511
  533.2 93.3 %collective-permute-start.43 = (f32[880,1024]{1,0:T(8,128)}, f32[880,1024]{1,0:T(8,128)}, u32[]{:S(2)}, u32[]{:S(2)}) collective-permute-start(f32[880,1024]{1,0:T(8,128)} %collective-permute-done.36.refs_3_), channel_id=1, source_target_pairs={{0,1},{1,0},{2,3},{3,2},{4,5},{5,4},{6,7},{7,6},{8,9},{9,8},{10,11... | collective-permute-start | bytes 10813448 | tf_op jit(solution)/shard_map/ppermute | solution.py:508
  567.8 58.7 %collective-permute-start.41 = (f32[768,1024]{1,0:T(8,128)}, f32[768,1024]{1,0:T(8,128)}, u32[]{:S(2)}, u32[]{:S(2)}) collective-permute-start(f32[768,1024]{1,0:T(8,128)} %get-tuple-element.84.refs_1_), channel_id=1, source_target_pairs={{0,1},{1,0},{2,3},{3,2},{4,5},{5,4},{6,7},{7,6},{8,9},{9,8},{10,11... | collective-permute-start | bytes 9437192 | tf_op jit(solution)/shard_map/ppermute | solution.py:508
  567.8 58.8 %collective-permute-start.44 = (f32[768,1024]{1,0:T(8,128)}, f32[768,1024]{1,0:T(8,128)}, u32[]{:S(2)}, u32[]{:S(2)}) collective-permute-start(f32[768,1024]{1,0:T(8,128)} %collective-permute-done.42.refs_3_), channel_id=1, source_target_pairs={{0,1},{1,0},{2,3},{3,2},{4,5},{5,4},{6,7},{7,6},{8,9},{9,8},{10,11... | collective-permute-start | bytes 9437192 | tf_op jit(solution)/shard_map/ppermute | solution.py:508
  569.7 9.6 %collective-permute-start.38 = (f32[516,256]{1,0:T(8,128)S(1)}, f32[516,256]{1,0:T(8,128)S(1)}, u32[]{:S(2)}, u32[]{:S(2)}) collective-permute-start(f32[516,256]{1,0:T(8,128)S(1)} %collective-permute-done.32), channel_id=1, source_target_pairs={{0,1},{1,0},{2,3},{3,2},{4,5},{5,4},{6,7},{7,6},{8,9},{9,8},{10,11... | collective-permute-start | bytes 1585160 | tf_op jit(solution)/shard_map/ppermute | solution.py:508
  570.0 10.1 %collective-permute-start.40 = (f32[516,256]{1,0:T(8,128)}, f32[516,256]{1,0:T(8,128)S(1)}, u32[]{:S(2)}, u32[]{:S(2)}) collective-permute-start(f32[516,256]{1,0:T(8,128)} %collective-permute-done.34), channel_id=1, source_target_pairs={{0,1},{1,0},{2,3},{3,2},{4,5},{5,4},{6,7},{7,6},{8,9},{9,8},{10,11... | collective-permute-start | bytes 1585160 | tf_op jit(solution)/shard_map/ppermute | solution.py:508
  579.3 47.2 %collective-permute-start.45 = (f32[536,1024]{1,0:T(8,128)S(1)}, f32[536,1024]{1,0:T(8,128)}, u32[]{:S(2)}, u32[]{:S(2)}) collective-permute-start(f32[536,1024]{1,0:T(8,128)S(1)} %copy-done.2), channel_id=1, source_target_pairs={{0,1},{1,0},{2,3},{3,2},{4,5},{5,4},{6,7},{7,6},{8,9},{9,8},{10,11... | collective-permute-start | bytes 6586376 | tf_op jit(solution)/shard_map/ppermute | solution.py:508
  580.9 58.4 %collective-permute-start.47 = (f32[536,1024]{1,0:T(8,128)}, f32[536,1024]{1,0:T(8,128)}, u32[]{:S(2)}, u32[]{:S(2)}) collective-permute-start(f32[536,1024]{1,0:T(8,128)} %collective-permute-done.46.refs_1_), channel_id=1, source_target_pairs={{0,1},{1,0},{2,3},{3,2},{4,5},{5,4},{6,7},{7,6},{8,9},{9,8},{10,11... | collective-permute-start | bytes 6586376 | tf_op jit(solution)/shard_map/ppermute | solution.py:508
  (12 other events, 243.3 us)
Sparse Core Ops, SparseCore 0:
  141.3 90.2 reduce-scatter.1
  453.9 59.6 all-reduce.6

commit v2 on v1

--- a/solution.py
+++ b/solution.py
@@ -91,14 +91,20 @@
     )(u, emb, bias, lab)
 
 
-def du_kernel(n_vocab, scale, logits_ref, emb_ref, lse_ref, lab_ref, out_ref, db_ref, du_ref, g_sc, db_sc):
+def du_kernel(n_vocab, scale, logits_ref, emb_ref, lse_ref, lab_ref, norm_hbm, gain_ref, out_ref, db_ref, sum_ref, du_ref, g_sc, db_sc, norm_sc, db_sc2, sem):
     i, n_blocks = pl.program_id(0), pl.num_programs(0)
     t = logits_ref.shape[0]
     lane = lax.broadcasted_iota(I32, (1, 128), 1)
 
+    norm_copy = pltpu.make_async_copy(norm_hbm, norm_sc, sem)
+
     @pl.when(i == 0)
     def _():
         du_ref[...] = jnp.zeros_like(du_ref)
+
+    @pl.when(i == 2)
+    def _():
+        norm_copy.start()
 
     def run(width):
         wide = -(-width // 128) * 128
@@ -135,12 +141,24 @@
 
     @pl.when(i == n_blocks - 1)
     def _():
-        parts, _, cols = out_ref.shape
-        for q in range(parts):
-            out_ref[q] = du_ref[:, q * cols:(q + 1) * cols].astype(BF16).astype(F32)
-
-
-def du_pass(scale, parts, logits, emb, lse, lab):
+        norm_copy.wait()
+        parts, rows, cols = out_ref.shape
+        for r in range(0, rows, 112):
+            rs = slice(r, r + 112)
+            total = [jnp.zeros((112, 128), F32)] * 2
+            for c in range(0, parts * cols, 128):
+                x = du_ref[rs, c:c + 128].astype(BF16).astype(F32)
+                out_ref[c // cols, rs, c % cols:c % cols + 128] = x
+                dn = x * gain_ref[:, c:c + 128]
+                total = [total[0] + dn, total[1] + dn * norm_sc[rs, c:c + 128]]
+            for j, x in enumerate(total):
+                db_sc2[j, rs, :] = x
+        for j in range(2):
+            sum_ref[j:j + 1, :] = jnp.sum(db_sc2[j].T, axis=0, keepdims=True)
+        sum_ref[2:, :] = jnp.zeros_like(sum_ref[2:, :])
+
+
+def du_pass(scale, parts, logits, emb, lse, lab, normed, gain):
     t, v = logits.shape
     e = emb.shape[1]
     n = pl.cdiv(v, VB)
@@ -148,14 +166,14 @@
     return pl.pallas_call(
         functools.partial(du_kernel, v, scale),
         grid=(n,),
-        in_specs=[pl.BlockSpec((t, VB), lambda i: (0, i)), pl.BlockSpec((VB, e), lambda i: (i, 0)), whole(t, 128), whole(t, 128)],
-        out_specs=[whole(parts, t, e // parts), pl.BlockSpec((1, VB), lambda i: (0, i))],
-        out_shape=[jax.ShapeDtypeStruct((parts, t, e // parts), F32), jax.ShapeDtypeStruct((1, v), F32)],
-        scratch_shapes=[pltpu.VMEM((t, e), F32), pltpu.VMEM((t, VB), BF16), pltpu.VMEM((8, VB), F32)],
+        in_specs=[pl.BlockSpec((t, VB), lambda i: (0, i)), pl.BlockSpec((VB, e), lambda i: (i, 0)), whole(t, 128), whole(t, 128), pl.BlockSpec(memory_space=pl.ANY), whole(1, e)],
+        out_specs=[whole(parts, t, e // parts), pl.BlockSpec((1, VB), lambda i: (0, i)), whole(8, t)],
+        out_shape=[jax.ShapeDtypeStruct((parts, t, e // parts), F32), jax.ShapeDtypeStruct((1, v), F32), jax.ShapeDtypeStruct((8, t), F32)],
+        scratch_shapes=[pltpu.VMEM((t, e), F32), pltpu.VMEM((t, VB), BF16), pltpu.VMEM((8, VB), F32), pltpu.VMEM((t, e), F32), pltpu.VMEM((2, t, 128), F32), pltpu.SemaphoreType.DMA],
         compiler_params=pltpu.CompilerParams(dimension_semantics=("arbitrary",), vmem_limit_bytes=VMEM_LIMIT),
         cost_estimate=pl.CostEstimate(flops=(2 * t * v * e) // COVER, bytes_accessed=t * v * 4 + v * e * 2, transcendentals=t * v),
         name="du_pass",
-    )(logits, emb, lse, lab)
+    )(logits, emb, lse, lab, normed, gain)
 
 
 LN_EPS = 1e-5
@@ -231,135 +249,205 @@
     )(hidden, pos, w, b, gain, bias)
 
 
-def narrow_kernel(first, offs, pos, *refs):
+BLK = 1280
+ME, MINE, MINE_ID, TWIN, FAR, FAR_TWIN = range(6)
+
+
+def rows_kernel(kind, scale, s0, m, cut, n_loc, sources, spots, has_big, pos, emb_hbm, bias_ref, info_ref, *refs):
     refs = list(refs)
-    n = len(offs)
-    if not first:
-        refs.pop(0)
-    pieces, (out_ref, wide, thin, pad, in_sem, out_sem, sem) = refs[:n], refs[n:]
+    take = lambda n: [refs.pop(0) for _ in range(n)]
+    wide = sources is not None
+    if wide:
+        src = {r: take(2) for r in sources}
+        if kind != "own":
+            take(1)
+    else:
+        u_hbm, = take(1)
+    if has_big:
+        take(1)
+    parts = take({"far": 2, "rest": 1}.get(kind, 0))
+    puts = take(len(spots))
+    out_hbm, = take(1)
+    if wide:
+        u_hbm, = take(1)
+    if kind in ("far", "rest", "whole"):
+        big_ref, = take(1)
+    if wide:
+        buf, = take(1)
+    ring, emb_sc, g_sc, acc, hold, sem, tok_sem, back_sem, in_sem, out_sem = refs
+    me = pos[ME]
+    chip = lax.div(me, 2)
+    n_steps = {"own": 2, "again": 2, "side": 4, "far": 2, "rest": 6, "whole": 8}[kind]
+    along_x, along_y = chip ^ 1, chip ^ 2
+
+    def device(i):
+        side = 2 * jnp.where(i < 2, jnp.minimum(along_x, along_y), jnp.maximum(along_x, along_y)) + lax.rem(i, 2)
+        far = 2 * (chip ^ 3) + lax.rem(i, 2)
+        if kind in ("own", "again"):
+            return 2 * chip + i
+        return {"side": side, "far": far, "rest": jnp.where(i < 4, side, far), "whole": i}[kind]
+
+    depth = ring.shape[0]
+
+    def fetch(i):
+        slot = lax.rem(i, 2 if wide else depth)
+        if not wide:
+            pltpu.make_async_copy(u_hbm.at[device(i)], ring.at[slot], tok_sem.at[slot, 0]).start()
+            return
+        for r, (lo, hi) in src.items():
+            @pl.when(device(i) ^ me == r)
+            def _():
+                pltpu.make_async_copy(lo, buf.at[slot, :cut, :], tok_sem.at[slot, 0]).start()
+                pltpu.make_async_copy(hi, buf.at[slot, cut:, :], tok_sem.at[slot, 1]).start()
+
+    row = lambda j, off: pl.multiple_of(pos[j] + off, 8)
+    emb_copy = pltpu.make_async_copy(emb_hbm.at[pl.ds(row(MINE, s0), m), :], emb_sc, sem)
+    emb_copy.start()
+    fetch(0)
     loads, stores = [], []
-    for j, p in enumerate(pieces):
-        m = p.shape[0]
-        loads.append(pltpu.make_async_copy(p, wide.at[j, :m, :], in_sem.at[j]))
-        row = pl.multiple_of(pos[j], 16)
-        stores.append(pltpu.make_async_copy(thin.at[j, :m, :], out_ref.at[pl.ds(row, m), :], out_sem.at[j]))
-    for c in loads:
-        c.start()
-    if first:
-        pad[...] = jnp.zeros_like(pad)
-        c = pltpu.make_async_copy(pad, out_ref.at[out_ref.shape[0] - pad.shape[0]:, :], sem)
-        c.start()
-        c.wait()
-    for j, p in enumerate(pieces):
-        m = p.shape[0]
-        loads[j].wait()
-        thin[j, :m, :] = wide[j, :m, :].astype(BF16)
-        stores[j].start()
-    for c in stores:
-        c.wait()
-
-
-def narrow_into(big, n_tok, rows, pieces):
-    first = big is None
-    n, e = len(pieces), pieces[0].shape[1]
-    m = max(p.shape[0] for p in pieces)
-    padded = -(-n_tok // TB) * TB
-    size = sum(p.size for p in pieces)
-    return pl.pallas_call(
-        functools.partial(narrow_kernel, first, [p.shape[0] for p in pieces]),
-        in_specs=[SMEM] + [ANY] * (n + (not first)),
-        out_specs=ANY,
-        out_shape=jax.ShapeDtypeStruct((padded, e), BF16),
-        scratch_shapes=[pltpu.VMEM((n, m, e), F32), pltpu.VMEM((n, m, e), BF16), pltpu.VMEM((padded - n_tok, e), BF16), DMA((n,)), DMA((n,)), DMA],
-        input_output_aliases={} if first else {1: 0},
-        compiler_params=pltpu.CompilerParams(vmem_limit_bytes=VMEM_LIMIT),
-        cost_estimate=pl.CostEstimate(flops=(size) // COVER, bytes_accessed=size * 6, transcendentals=0),
-        name="narrow",
-    )(jnp.stack(rows), *([] if first else [big]), *pieces)
-
-
-TB = 768
-
-
-def rows_kernel(scale, m, n_put, has_big, pos, emb_hbm, u_hbm, bias_ref, lse_ref, lab_ref, *refs):
-    refs = list(refs)
-    if has_big:
-        refs.pop(0)
-    puts, (out_hbm, big_ref, u_all, emb_sc, g_sc, acc, hold, sem, tok_sem, in_sem, out_sem) = refs[:n_put], refs[n_put:]
-    n_blocks = lse_ref.shape[0]
-    row = lambda j: pl.multiple_of(pos[j], 8)
-    blocks = [pltpu.make_async_copy(u_hbm.at[j * TB:(j + 1) * TB, :], u_all.at[j * TB:(j + 1) * TB, :], tok_sem.at[j]) for j in range(n_blocks)]
-    loads = [pltpu.make_async_copy(p, hold.at[j, :p.shape[0], :], in_sem.at[j]) for j, p in enumerate(puts)]
-    stores = [pltpu.make_async_copy(hold.at[j, :p.shape[0], :], big_ref.at[pl.ds(row(2 + j), p.shape[0]), :], out_sem.at[j])
-              for j, p in enumerate(puts)]
-    emb_copy = pltpu.make_async_copy(emb_hbm.at[pl.ds(row(0), m), :], emb_sc, sem)
-    emb_copy.start()
-    for c in blocks + loads:
-        c.start()
+    for j, (p, (base, off)) in enumerate(zip(puts, spots)):
+        n = p.shape[0]
+        loads.append(pltpu.make_async_copy(p, hold.at[j, :n, :], in_sem.at[j]))
+        stores.append(pltpu.make_async_copy(hold.at[j, :n, :], big_ref.at[pl.ds(row(base, off), n), :], out_sem.at[j]))
+    for j, p in enumerate(parts):
+        loads.append(pltpu.make_async_copy(p, hold.at[len(puts) + j, :m, :], in_sem.at[len(puts) + j]))
     acc[...] = jnp.zeros_like(acc)
+    if wide:
+        for k in range(2):
+            ring[k, n_loc:, :] = jnp.zeros((BLK - n_loc, ring.shape[2]), BF16)
     emb_copy.wait()
-    parts = max(1, round(m / 256))
-    cuts = [-(-m * k // (parts * 16)) * 16 for k in range(parts)] + [m]
+    n_cuts = max(1, round(m / 320))
+    cuts = [-(-m * k // (n_cuts * 16)) * 16 for k in range(n_cuts)] + [m]
     cuts = list(zip(cuts[:-1], cuts[1:]))
-
-    @pl.loop(0, n_blocks)
+    kept = lambda i: pltpu.make_async_copy(ring.at[lax.rem(i, 2)], u_hbm.at[device(i)], back_sem.at[lax.rem(i, 2)])
+
+    @pl.loop(0, n_steps)
     def _(i):
-        at = pl.ds(pl.multiple_of(i * TB, TB), TB)
-        pltpu.make_async_copy(u_hbm.at[at, :], u_all.at[at, :], tok_sem.at[i]).wait()
+        slot = lax.rem(i, 2 if wide else depth)
+        if wide:
+            any_lo, any_hi = next(iter(src.values()))
+            pltpu.make_async_copy(any_lo, buf.at[slot, :cut, :], tok_sem.at[slot, 0]).wait()
+            pltpu.make_async_copy(any_hi, buf.at[slot, cut:, :], tok_sem.at[slot, 1]).wait()
+
+            @pl.when(i >= 2)
+            def _():
+                kept(i - 2).wait()
+        else:
+            pltpu.make_async_copy(u_hbm.at[device(i)], ring.at[slot], tok_sem.at[slot, 0]).wait()
+
+        @pl.when(i + 1 < n_steps)
+        def _():
+            fetch(i + 1)
+
+        @pl.when(i == 0)
+        def _():
+            for c in loads:
+                c.start()
+
         for j, (a, b) in enumerate(zip(loads, stores)):
-            @pl.when(i == 3 + j)
+            @pl.when(i == min(2 + j, n_steps - 1))
             def _():
                 a.wait()
                 b.start()
 
+        if wide:
+            ring[slot, :n_loc, :] = buf[slot].astype(BF16)
+            kept(i).start()
+        group = (i >= 4).astype(I32) if kind == "rest" else 0
+        rel = device(i) ^ me
+        lse, lab = info_ref[rel, 0:1, :], info_ref[rel, 1:2, :]
+
         def weights(r0, r1):
-            part = dot(emb_sc[r0:r1, :], u_all[at, :], NT)
-            hit = lab_ref[i] == lax.broadcasted_iota(I32, (r1 - r0, 1), 0) + (pos[1] + r0)
-            g = jnp.exp(part + bias_ref[r0:r1, :] - lse_ref[i]) - jnp.where(hit, scale, 0.0)
+            part = dot(emb_sc[r0:r1, :], ring[slot], NT)
+            ids = lax.broadcasted_iota(I32, (r1 - r0, 1), 0) + (pos[MINE_ID] + (s0 + r0))
+            g = jnp.exp(part + bias_ref[s0 + r0:s0 + r1, :] - lse) - jnp.where(lab == ids.astype(F32), scale, 0.0)
             g_sc[r0:r1, :] = g.astype(BF16)
 
         weights(*cuts[0])
         for k, (r0, r1) in enumerate(cuts):
             if k + 1 < len(cuts):
                 weights(*cuts[k + 1])
-            acc[r0:r1, :] += dot(g_sc[r0:r1, :], u_all[at, :], NN)
-
-    own = pltpu.make_async_copy(acc, out_hbm, sem)
-    own.start()
-    for b in stores:
-        b.wait()
-    own.wait()
-
-
-def rows_pass(scale, v_rows, m, pos, emb, u, bias, lse, lab, big, puts):
-    t, e = u.shape
-    n, n_put = t // TB, max(1, len(puts))
+            acc[group, r0:r1, :] += dot(g_sc[r0:r1, :], ring[slot], NN)
+
+    for c in loads[len(puts):]:
+        c.wait()
+    if kind == "far":
+        acc[0] = (hold[0, :m, :] + acc[0]) + hold[1, :m, :]
+    if kind == "rest":
+        acc[0] = (hold[len(puts), :m, :] + acc[1]) + acc[0]
+    done = [pltpu.make_async_copy(acc.at[0], out_hbm, sem)]
+    if kind in ("far", "rest", "whole"):
+        done.append(pltpu.make_async_copy(acc.at[0], big_ref.at[pl.ds(row(MINE, s0), m), :], emb_sem(tok_sem)))
+    for c in done:
+        c.start()
+    if wide:
+        for i in range(n_steps - 2, n_steps):
+            kept(i).wait()
+    for c in stores + done:
+        c.wait()
+
+
+def emb_sem(tok_sem):
+    return tok_sem.at[0, 0]
+
+
+def rows_pass(kind, scale, v_rows, span, cut, pos, emb, bias, info, tokens=None, u_all=None, big=None, parts=(), puts=()):
+    s0, s1 = span
+    m, e = s1 - s0, emb.shape[1]
     sds = jax.ShapeDtypeStruct
-    has_big = big is not None
-    extra = ([big] if has_big else []) + list(puts)
+    wide = kind in ("own", "side", "far")
+    final = kind in ("far", "rest", "whole")
+    n_dev = info.shape[0]
+    args, aliases = [pos, emb, bias, info], {}
+    outs = [sds((m, e), F32)]
+    sources = None
+    if wide:
+        sources = {"own": (0, CORE), "side": (X, X | CORE, Y, Y | CORE), "far": (X | Y, X | Y | CORE)}[kind]
+        args += [h for r in sources for h in tokens[r]]
+        n_loc = tokens[0][0].shape[0] + tokens[0][1].shape[0]
+        outs.append(sds((n_dev, BLK, e), BF16))
+        if kind != "own":
+            aliases[len(args)] = 1
+            args.append(u_all)
+    else:
+        n_loc = BLK
+        args.append(u_all)
+    if final:
+        if big is not None:
+            aliases[len(args)] = len(outs)
+            args.append(big)
+        outs.append(sds((v_rows, e), F32))
+    args += list(parts) + [a for _, a in puts]
+    n_hold = max(1, len(parts) + len(puts))
+    tallest = max([m] * len(parts) + [a.shape[0] for _, a in puts] + [8])
+    steps = {"own": 2, "again": 2, "side": 4, "far": 2, "rest": 6, "whole": 8}[kind]
+    t = steps * BLK
+    scratch = [pltpu.VMEM((2, n_loc, e), F32)] if wide else []
+    scratch += [
+        pltpu.VMEM((2 if wide else 3, BLK, e), BF16), pltpu.VMEM((m, e), BF16), pltpu.VMEM((m, BLK), BF16),
+        pltpu.VMEM((2 if kind == "rest" else 1, m, e), F32), pltpu.VMEM((n_hold, tallest, e), F32),
+        DMA, DMA((3, 2)), DMA((2,)), DMA((n_hold,)), DMA((n_hold,)),
+    ]
     return pl.pallas_call(
-        functools.partial(rows_kernel, scale, m, len(puts), has_big),
-        in_specs=[SMEM, ANY, ANY, VMEM, VMEM, VMEM] + [ANY] * len(extra),
-        out_specs=[ANY, ANY],
-        out_shape=[sds((m, e), F32), sds((v_rows, e), F32)],
-        scratch_shapes=[
-            pltpu.VMEM((t, e), BF16), pltpu.VMEM((m, e), BF16), pltpu.VMEM((m, TB), BF16), pltpu.VMEM((m, e), F32),
-            pltpu.VMEM((n_put, max([p.shape[0] for p in puts] + [8]), e), F32), DMA, DMA((n,)), DMA((n_put,)), DMA((n_put,)),
-        ],
-        input_output_aliases={6: 1} if has_big else {},
+        functools.partial(rows_kernel, kind, scale, s0, m, cut, n_loc, sources, [spot for spot, _ in puts], big is not None),
+        in_specs=[SMEM, ANY, VMEM, VMEM] + [ANY] * (len(args) - 4),
+        out_specs=[ANY] * len(outs),
+        out_shape=outs,
+        scratch_shapes=scratch,
+        input_output_aliases=aliases,
         compiler_params=pltpu.CompilerParams(vmem_limit_bytes=VMEM_LIMIT),
         cost_estimate=pl.CostEstimate(flops=(4 * t * m * e) // COVER, bytes_accessed=t * e * 2 + m * e * 6, transcendentals=t * m),
-        name="rows",
-    )(pos, emb, u, bias, lse, lab, *extra)
-
-
-def put_kernel(n, pos, *refs):
+    )(*args)
+
+
+def put_kernel(spots, pos, *refs):
+    n = len(spots)
     pieces, (out_ref, hold, in_sem, out_sem) = refs[1:1 + n], refs[1 + n:]
     loads, stores = [], []
-    for j, p in enumerate(pieces):
+    for j, (p, (base, off)) in enumerate(zip(pieces, spots)):
         slot = hold.at[j, :p.shape[0], :]
         loads.append(pltpu.make_async_copy(p, slot, in_sem.at[j]))
-        stores.append(pltpu.make_async_copy(slot, out_ref.at[pl.ds(pl.multiple_of(pos[j], 8), p.shape[0]), :], out_sem.at[j]))
+        stores.append(pltpu.make_async_copy(slot, out_ref.at[pl.ds(pl.multiple_of(pos[base] + off, 8), p.shape[0]), :], out_sem.at[j]))
     for a in loads:
         a.start()
     for a, b in zip(loads, stores):
@@ -369,45 +457,58 @@
         b.wait()
 
 
-def put_rows(pos, big, pieces):
+def put_rows(pos, big, puts):
+    spots, pieces = [s for s, _ in puts], [a for _, a in puts]
     n, e = len(pieces), big.shape[1]
+    size = sum(p.size for p in pieces)
     return pl.pallas_call(
-        functools.partial(put_kernel, n),
+        functools.partial(put_kernel, spots),
         in_specs=[SMEM] + [ANY] * (n + 1),
         out_specs=ANY,
         out_shape=jax.ShapeDtypeStruct(big.shape, big.dtype),
         scratch_shapes=[pltpu.VMEM((n, max(p.shape[0] for p in pieces), e), F32), DMA((n,)), DMA((n,))],
         input_output_aliases={1: 0},
         compiler_params=pltpu.CompilerParams(vmem_limit_bytes=VMEM_LIMIT),
-        cost_estimate=pl.CostEstimate(flops=(sum(p.size for p in pieces)) // COVER, bytes_accessed=sum(p.size for p in pieces) * 8, transcendentals=0),
+        cost_estimate=pl.CostEstimate(flops=(size) // COVER, bytes_accessed=size * 8, transcendentals=0),
         name="put_rows",
     )(pos, big, *pieces)
 
 
-def sums_kernel(du_ref, norm_ref, gain_ref, out_ref):
-    cols = du_ref.shape[2]
-    total = [jnp.zeros((du_ref.shape[1], 128), F32)] * 2
-    for q in range(du_ref.shape[0]):
-        for c in range(0, cols, 128):
-            at = slice(q * cols + c, q * cols + c + 128)
-            dn = du_ref[q, :, c:c + 128] * gain_ref[:, at]
-            total = [total[0] + dn, total[1] + dn * norm_ref[:, at]]
-    out_ref[2:, :] = jnp.zeros_like(out_ref[2:, :])
-    for j, x in enumerate(total):
-        out_ref[j:j + 1, :] = jnp.sum(x.T, axis=0, keepdims=True)
-
-
-def sums_pass(du, normed, gain):
-    n, e = normed.shape
+def join_kernel(n_vec, idx, *refs):
+    own, mine, theirs, (dw_ref, vec_ref, full, in_sem, out_sem) = refs[0], refs[1:4], refs[4:7], refs[7:]
+    vp, core = idx[0], idx[1]
+    half, cols = mine[0].shape
+    col = lambda k: pl.ds(pl.multiple_of((vp ^ k) * cols, cols), cols)
+    row = lambda c: pl.ds(pl.multiple_of(c * half, 8), half)
+    loads = [pltpu.make_async_copy(own.at[:2 * half, :], full.at[:, col(0)], in_sem.at[0])]
+    for k in range(3):
+        loads.append(pltpu.make_async_copy(mine[k], full.at[row(core), col(k + 1)], in_sem.at[1 + k]))
+        loads.append(pltpu.make_async_copy(theirs[k], full.at[row(1 - core), col(k + 1)], in_sem.at[4 + k]))
+    for c in loads:
+        c.start()
+    for c in loads:
+        c.wait()
+    e = dw_ref.shape[0]
+    stores = [pltpu.make_async_copy(full.at[:e, :], dw_ref, out_sem.at[0]), pltpu.make_async_copy(full.at[e:e + n_vec, :], vec_ref, out_sem.at[1])]
+    for c in stores:
+        c.start()
+    for c in stores:
+        c.wait()
+
+
+def join_pass(idx, own, mine, theirs):
+    half, cols = mine[0].shape
+    e = 4 * cols
     return pl.pallas_call(
-        sums_kernel,
-        in_specs=[VMEM] * 3,
-        out_specs=VMEM,
-        out_shape=jax.ShapeDtypeStruct((8, n), F32),
+        functools.partial(join_kernel, 8),
+        in_specs=[SMEM] + [ANY] * 7,
+        out_specs=[ANY] * 2,
+        out_shape=[jax.ShapeDtypeStruct((e, e), F32), jax.ShapeDtypeStruct((8, e), F32)],
+        scratch_shapes=[pltpu.VMEM((2 * half, e), F32), DMA((7,)), DMA((2,))],
         compiler_params=pltpu.CompilerParams(vmem_limit_bytes=VMEM_LIMIT),
-        cost_estimate=pl.CostEstimate(flops=(4 * n * e) // COVER, bytes_accessed=n * e * 8, transcendentals=0),
-        name="sums",
-    )(du, normed, gain)
+        cost_estimate=pl.CostEstimate(flops=(e * e) // COVER, bytes_accessed=e * e * 8, transcendentals=0),
+        name="join",
+    )(idx, own, *mine, *theirs)
 
 
 def back_kernel(vp, pre_ref, norm_ref, rstd_ref, z_ref, du_ref, m1_ref, m2_ref, gain_ref, loss_ref, db_ref, dab_ref, pack_ref):
@@ -423,14 +524,14 @@
             pack_ref[e + j:e + j + 1, cs] = jnp.sum(x, axis=0, keepdims=True)
     pack_ref[:e, :] = lax.dot_general(z_ref[...], dab_ref[...].astype(BF16), (((0,), (0,)), ((), ())), preferred_element_type=F32)
     pack_ref[e + 3:e + 4, :] = loss_ref[...]
-    pack_ref[e + 4:e + 8, :] = jnp.zeros_like(pack_ref[e + 4:e + 8, :])
-    pack_ref[e + 8:, :] = db_ref[...]
+    pack_ref[e + 4:e + 16, :] = jnp.zeros_like(pack_ref[e + 4:e + 16, :])
+    pack_ref[e + 16:, :] = db_ref[...]
 
 
 def back_pass(vp, pre, normed, rstd, z, du, m1, m2, gain, loss, db):
     n, cols = du.shape
     e = z.shape[1]
-    n_pack = e + 8 + db.shape[0]
+    n_pack = e + 16 + db.shape[0]
     block = lambda *s: pl.BlockSpec(s, lambda i, p: (0,) * len(s))
     share = lambda r: pl.BlockSpec((r, cols), lambda i, p: (0, p[0]))
     gs = pltpu.PrefetchScalarGridSpec(
@@ -519,13 +620,13 @@
         shard_rows = emb_table.shape[0]
         n_loc = n_rows * n_masks
         n_tokens = n_loc * n_groups
-        padded = -(-n_tokens // TB) * TB
         slots = -(-n_masks // 16) * 16
         cut = n_loc // 32 * 16
         cols = width // n_shards
         dp, vp = lax.axis_index("dp"), lax.axis_index("vp")
         row_start = vp * shard_rows
         scale = 1.0 / n_tokens
+        core, mine = dp & 1, (dp >> 1 ^ dp >> 2) & 1
 
         pos_pad = jnp.pad(mask_pos, ((0, 0), (0, slots - n_masks)), constant_values=-1)
         z, pre, normed, rstd, u, u_lo, u_hi = head_pass(
@@ -541,111 +642,99 @@
         lab_local = jnp.where((lab_local >= 0) & (lab_local < shard_rows), lab_local, -1)
         lab_local = jnp.broadcast_to(lab_local[:, None], (n_loc, 128))
         logits, stat = stats(u, emb_table, b_vocab[None], lab_local)
+        x_lo, y_hi = after((x_lo, y_hi), stat)
+        d_lo, d_hi = swap(x_lo, Y), swap(y_hi, X)
+        cx_lo, cy_hi = swap(x_lo, CORE), swap(y_hi, CORE)
         all_stats = [stat] + [swap_vp(stat, b) for b in range(1, n_shards)]
         global_max = functools.reduce(jnp.maximum, [s[0] for s in all_stats])
         log_norm = global_max + jnp.log(order_sum([s[1] * jnp.exp(s[0] - global_max) for s in all_stats]))
         loss_part = jnp.sum(log_norm - order_sum([s[2] for s in all_stats]))
         lse = log_norm + jnp.log(jnp.float32(n_tokens))
-        x_lo, y_hi = after((x_lo, y_hi), lse)
-        d_lo, d_hi = swap(x_lo, Y), swap(y_hi, X)
-
-        du_part, db_part = du_pass(scale, n_shards, logits, emb_table, jnp.broadcast_to(lse[:, None], (n_loc, 128)), lab_local)
+
+        du_part, db_part, sums = du_pass(
+            scale, n_shards, logits, emb_table, jnp.broadcast_to(lse[:, None], (n_loc, 128)), lab_local, normed, ln_gain[None])
         du_share = lax.psum_scatter(du_part.reshape(n_shards * n_loc, cols), "vp", scatter_dimension=0, tiled=True)
 
-        lse, x_hi, y_lo, u_lo, u_hi, c_lo, c_hi = after((lse, x_hi, y_lo, u_lo, u_hi, c_lo, c_hi), du_part)
-        info = jnp.stack([lse, flat_labels.astype(F32)])
-        info = jnp.stack([info] + [swap(info, b) for b in range(1, n_groups)])
-        info = jnp.take(info, jnp.arange(n_groups) ^ dp, axis=0, mode="clip")
-        fill = (0, padded - n_tokens)
-        lse_all = jnp.pad(info[:, 0].reshape(-1), fill, constant_values=jnp.inf).reshape(-1, 1, TB)
-        lab_all = jnp.pad(info[:, 1].reshape(-1).astype(I32), fill, constant_values=-1).reshape(-1, 1, TB)
-
-        sums = sums_pass(du_part, normed, ln_gain[None])
-        sums = order_sum([sums] + [swap_vp(sums, b) for b in range(1, n_shards)]) / width
-        m1, m2 = (jnp.broadcast_to(sums[j][:, None], (n_loc, 128)) for j in range(2))
-
-        at = lambda bits, off: (dp ^ bits) * n_loc + off
-        halves = lambda bits, lo, hi: [(at(bits, 0), lo), (at(bits, cut), hi)]
-
-        def narrow(big, items):
-            return narrow_into(big, n_tokens, [r for r, _ in items], [a for _, a in items])
-
-        u_all = narrow(None, halves(0, u_lo, u_hi) + halves(CORE, c_lo, c_hi))
-        cx = swap(x_lo, CORE), swap(x_hi, CORE)
-        cy = swap(y_lo, CORE), swap(y_hi, CORE)
-        u_all = narrow(u_all, halves(X, x_lo, x_hi) + halves(Y, y_lo, y_hi) + halves(X | CORE, *cx) + halves(Y | CORE, *cy))
-        d_lo, d_hi = after((d_lo, d_hi), u_all)
-        u_all = narrow(u_all, halves(X | Y, d_lo, d_hi) + halves(X | Y | CORE, swap(d_lo, CORE), swap(d_hi, CORE)))
-
-        core, mine = dp & 1, (dp >> 1 ^ dp >> 2) & 1
+        lse, x_hi, y_lo = after((lse, x_hi, y_lo), du_part)
+        fill = (0, BLK - n_loc)
+        info = jnp.stack([jnp.pad(lse, fill, constant_values=jnp.inf), jnp.pad(flat_labels.astype(F32), fill, constant_values=-1.0)])[None]
+        for bit in (CORE, X, Y):
+            info = jnp.concatenate([info, swap(info, bit)])
+
         half, quarter = shard_rows // 2, shard_rows // 4
-        my_start = mine * half + core * quarter
-        twin_start = mine * half + (1 - core) * quarter
-        far_start = (1 - mine) * half + core * quarter
-        far_twin_start = (1 - mine) * half + (1 - core) * quarter
-        bias_col = lax.dynamic_slice(b_vocab, (my_start,), (quarter,))[:, None]
-        shares = (960, 880, 768, 536)
+        start = lambda h, c: h * half + c * quarter
+        pos = jnp.stack([dp, start(mine, core), row_start + start(mine, core), start(mine, 1 - core), start(1 - mine, core), start(1 - mine, 1 - core)])
+        bias_col = lax.dynamic_slice(b_vocab, (start(mine, core),), (quarter,))[:, None]
+        shares = (640, 896, 896, 712)
         ends = [0]
         for w in shares[:-1]:
             ends.append(ends[-1] + max(16, quarter * w // sum(shares) // 16 * 16))
         spans = list(zip(ends, ends[1:] + [quarter]))
 
-        def rows(k, big, puts, *wait):
-            s0, s1 = spans[k]
-            pos = jnp.stack([my_start + s0, row_start + my_start + s0] + [p for p, _ in puts])
-            return rows_pass(scale, shard_rows, s1 - s0, after(pos, *wait), emb_table, u_all, bias_col[s0:s1], lse_all, lab_all,
-                             big, [a for _, a in puts])
+        def rows(kind, k, *wait, **kw):
+            return rows_pass(kind, scale, shard_rows, spans[k], cut, after(pos, *wait), emb_table, bias_col, info, **kw)
 
         def send(k, chunk):
-            return (twin_start + spans[k][0], swap(chunk, CORE)), hop(chunk)
+            return ((TWIN, spans[k][0]), swap(chunk, CORE)), hop(chunk)
 
         def forward(k, far, *wait):
             far = after(far, *wait)
-            return (far_start + spans[k][0], far), (far_twin_start + spans[k][0], swap(far, CORE))
-
-        own = lambda k, chunk: (my_start + spans[k][0], chunk)
-        chunk0, big = rows(0, None, [])
+            return ((FAR, spans[k][0]), far), ((FAR_TWIN, spans[k][0]), swap(far, CORE))
+
+        tokens = {0: (u_lo, u_hi), CORE: (c_lo, c_hi), X: (x_lo, x_hi), Y: (y_lo, y_hi)}
+        own0, u_all = rows("own", 0, tokens=tokens)
+        own1, = rows("again", 1, own0, u_all=u_all)
+        x_hi, y_lo = after((x_hi, y_lo), own1)
+        tokens[X | CORE] = cx_lo, swap(x_hi, CORE)
+        tokens[Y | CORE] = swap(y_lo, CORE), cy_hi
+        tokens[X], tokens[Y] = (x_lo, x_hi), (y_lo, y_hi)
+        side0, u_all = rows("side", 0, tokens=tokens, u_all=u_all)
+        d_lo, d_hi = after((d_lo, d_hi), side0)
+        tokens[X | Y] = d_lo, d_hi
+        tokens[X | Y | CORE] = swap(d_lo, CORE), swap(d_hi, CORE)
+        chunk0, u_all, big = rows("far", 0, tokens=tokens, u_all=u_all, parts=(own0, side0))
         twin0, far0 = send(0, chunk0)
 
         du_share = after(du_share, chunk0)
+        sums = [sums] + [swap_vp(sums, b) for b in range(1, n_shards)]
+        sums = order_sum(sums) / width
+        m1, m2 = (jnp.broadcast_to(sums[j][:, None], (n_loc, 128)) for j in range(2))
         loss_row = jnp.pad(loss_part[None, None], ((0, 0), (0, cols - 1)))
         db_rows = -(-shard_rows // cols // 8) * 8
         db_mat = jnp.pad(db_part[0], (0, db_rows * cols - shard_rows)).reshape(db_rows, cols)
         dab, pack = back_pass(vp[None], pre, normed, rstd, z, du_share, m1, m2, ln_gain[None], loss_row, db_mat)
-        wait = dab
+        back_done = dab
         pack = lax.psum(pack, "dp")
         dab = [dab] + [swap_vp(dab, b) for b in range(1, n_shards)]
 
-        chunk1, big = rows(1, big, [own(0, chunk0)], wait)
+        chunk1, big = rows("rest", 1, back_done, u_all=u_all, big=big, parts=(own1,))
         twin1, far1 = send(1, chunk1)
         far0, far_twin0 = forward(0, far0, chunk1)
-        chunk2, big = rows(2, big, [own(1, chunk1), twin0, far0])
+
+        chunk2, big = rows("whole", 2, u_all=u_all, big=big, puts=[twin0, far0])
         twin2, far2 = send(2, chunk2)
         far1, far_twin1 = forward(1, far1, chunk2)
-
         pack = after(pack, chunk2)
-        n_gather = width + 8
-        part = lax.dynamic_slice(pack, (core * (n_gather // 2), 0), (n_gather // 2, cols))
+        n_half = (width + 16) // 2
+        part = lax.dynamic_slice(pack, (core * n_half, 0), (n_half, cols))
         parts = [swap_vp(part, b) for b in range(1, n_shards)]
 
-        chunk3, big = rows(3, big, [own(2, chunk2), twin1, far1, far_twin0])
+        chunk3, big = rows("whole", 3, part, u_all=u_all, big=big, puts=[far_twin0, twin1, far1])
         twin3, far3 = send(3, chunk3)
         far2, far_twin2 = forward(2, far2, chunk3)
-        *dab_wait, parts = after((*dab, parts), chunk3)
-        d_hidden = spread_pass(n_masks, hidden.shape, vp[None], pos_pad[:, None], w_trans, dab_wait)
+        d_hidden = spread_pass(n_masks, hidden.shape, vp[None], pos_pad[:, None], w_trans, after(dab, chunk3))
+        parts = after(parts, d_hidden)
         others = [swap(p, CORE) for p in parts]
-        items = [own(3, chunk3), twin2, far2, far_twin1, far_twin2, twin3]
-        big = put_rows(jnp.stack([p for p, _ in items]), big, [a for _, a in items])
-        items = forward(3, far3)
-        big = put_rows(jnp.stack([p for p, _ in items]), big, [a for _, a in items])
-
-        gathered = [pack[:n_gather]]
-        for p, o in zip(parts, others):
-            gathered.append(jnp.concatenate([jnp.where(core == 0, p, o), jnp.where(core == 0, o, p)]))
-        gathered = jnp.take(jnp.stack(gathered), jnp.arange(n_shards) ^ vp, axis=0, mode="clip")
-        gathered = jnp.transpose(gathered, (1, 0, 2)).reshape(n_gather, width)
-        db = pack[n_gather:].reshape(-1)[:shard_rows]
-        return (pack[width + 3, 0] / n_tokens, d_hidden, gathered[:width], gathered[width], gathered[width + 1], gathered[width + 2], big, db)
+        big = put_rows(pos, big, [far_twin1, twin2, far2, far_twin2, twin3])
+        pack, parts, others = after((pack, parts, others), big)
+        d_w, vec = join_pass(jnp.stack([vp, core]), pack, parts, others)
+        far3 = after(far3, big)
+        far3, far_twin3 = forward(3, far3)
+        big = put_rows(pos, big, [far3])
+        big = put_rows(pos, big, [far_twin3])
+
+        db = pack[width + 16:].reshape(-1)[:shard_rows]
+        return pack[width + 3, 0] / n_tokens, d_hidden, d_w, vec[0], vec[1], vec[2], big, db
 
     in_specs = (P("dp", None, None), P("dp", None), P("dp", None), P(None, None), P(None), P(None), P(None), P("vp", None), P("vp"))
     out_specs = (P(), P("dp", None, None), P(None, None), P(None), P(None), P(None), P("vp", None), P("vp"))

time: 659 us -> 719 us (1.091)
  waiting for transfers between devices: 154 us -> 266 us
  Pallas kernels: 378 us -> 356 us
  local copies, waits for them, and re-layouts: 47.5 us -> 27.6 us
  other arithmetic: 11.3 us -> 3.1 us
    ppermute x12, waiting for transfers between devices: 47.9 us -> 144 us  [swap_vp(): return lax.ppermute(a, 'vp', [(d, d ^ bit) for d in range(n_shards)])]
    pallas_call x10 -> x11, Pallas kernels: 242 us -> 218 us  [the longest x7 192 us: rows_pass(): pl.pallas_call(functools.partial(rows_kernel, kind, scale, s0, m, cut, n_...]
    slice x13 -> x2, local copies, waits for them, and re-layouts: 16.3 us -> 2.1 us  [the longest x1 1.48 us: local_step(): vec[2]]
    ppermute x32 -> x28, waiting for transfers between devices: 46 us -> 56 us  [swap(): return lax.ppermute(a, 'dp', [(d, d ^ bit) for d in range(n_groups)])]
    ppermute x4, waiting for transfers between devices: 0.01 us -> 7.39 us  [hop(): lax.ppermute(a, 'dp', [(d, d ^ (Y if d & CORE else X)) for d in range(n_g...]
    ppermute x32 -> x28, starting transfers between devices: 28 us -> 21.9 us  [swap(): return lax.ppermute(a, 'dp', [(d, d ^ bit) for d in range(n_groups)])]
  transfers between devices with their start and end apart: 50 -> 46, of which waited for: 16 -> 19; matrix products, arithmetic and copies ran while one was open for 8% -> 3% of each run, Pallas kernels for 55% -> 47%
where the time goes in v2:
time: 719 us; the launch traced here: 711 us
  Pallas kernels  356 us (50%)
  waiting for transfers between devices  266 us (37%)
  starting transfers between devices  41.8 us (6%)
  local copies, waits for them, and re-layouts  27.6 us (4%)
  between operations  16.6 us (2%)
    pallas_call x7, Pallas kernels, rows_pass(): pl.pallas_call(functools.partial(rows_kernel, kind, scale, s0, m, cut, n_...  192 us
    ppermute x12, waiting for transfers between devices, swap_vp(): return lax.ppermute(a, 'vp', [(d, d ^ bit) for d in range(n_shards)])  144 us
    psum x1, waiting for transfers between devices, local_step(): pack = lax.psum(pack, 'dp')  58.2 us
    ppermute x28, waiting for transfers between devices, swap(): return lax.ppermute(a, 'dp', [(d, d ^ bit) for d in range(n_groups)])  56 us
    pallas_call x1, Pallas kernels, stats(): pl.pallas_call(functools.partial(stats_kernel, v), grid=(n,), in_specs=[w...  54 us
    pallas_call x1, Pallas kernels, du_pass(): pl.pallas_call(functools.partial(du_kernel, v, scale), grid=(n,), in_spec...  47.5 us
    ppermute x28, starting transfers between devices, swap(): return lax.ppermute(a, 'dp', [(d, d ^ bit) for d in range(n_groups)])  21.9 us
    pallas_call x3, Pallas kernels, put_rows(): pl.pallas_call(functools.partial(put_kernel, spots), in_specs=[SMEM] + [A...  21.3 us
  transfers between devices with their start and end apart: 46, of which 19 were waited for; matrix products, arithmetic and copies ran while one was open for 3% of the time, Pallas kernels for 47%

profile of v2, /device:TPU:9, one launch (start us, length us, event | category | flops | bytes accessed | tf_op | source)
XLA Modules:
  0.0 711.2 jit_solution(6290949517389899626)
XLA Ops:
  9.0 15.7 %head.1 = (bf16[1232,1024]{1,0:T(8,128)(2,1)}, f32[1232,1024]{1,0:T(8,128)}, f32[1232,1024]{1,0:T(8,128)}, f32[1232,128]{1,0:T(8,128)}, bf16[1232,1024]{1,0:T(8,...) custom-call(bf16[16,512,1024]{2,1,0:T(8,128)(2,1)} %hid.1, s32[16,80,128]{2,1,0:T(8,128)} %broadcast_in_dim.67.pos_ref, ...), custom_call_target="tpu_custom_call" | custom-call | flops 51673824 | bytes 42008576 | tf_op jit(solution)/shard_map/head/pallas_call | solution.py:239
  29.7 54.0 %stats.1 = (f32[1232,12576]{1,0:T(8,128)}, f32[8,1232]{1,0:T(8,128)}) custom-call(bf16[1232,1024]{1,0:T(8,128)(2,1)} %get-tuple-element.73.u_ref, bf16[12576,1024]{1,0:T(8,128)(2,1)} %emb_hbm.13, f32[1,12576]{1,0:T(1,128)} %broadcast_in_dim.71.b_ref, s32[1232,128]{1,0:T(8,128)} %broadcast_in_dim.73.lab_ref), custom_call_target="tpu_custom_call" | custom-call | flops 317309568 | bytes 87730176 | tf_op jit(solution)/shard_map/stats/pallas_call | solution.py:81
  83.7 3.4 collective-permute-done
  87.2 2.3 collective-permute-start.1
  89.5 1.7 collective-permute-done.1
  91.1 1.3 collective-permute-start.2
  92.5 2.5 collective-permute-done.2
  95.0 4.1 collective-permute-start.13
  102.4 47.5 %du_pass.1 = (f32[4,1232,256]{2,1,0:T(8,128)}, f32[1,12576]{1,0:T(1,128)}, f32[8,1232]{1,0:T(8,128)}) custom-call(f32[1232,12576]{1,0:T(8,128)} %get-tuple-element.74.logits_ref, bf16[12576,1024]{1,0:T(8,128)(2,1)} %emb_hbm.13, f32[1232,128]{1,0:T(8,128)} %broadcast_in_dim.74.lse_ref, s32[1232,128]{1,0:T(8,128)} %broadcast_in_dim.73.lab_ref, ...), custom_call_target="tpu_custom_call" | custom-call | flops 317309568 | bytes 87730176 | tf_op jit(solution)/shard_map/du_pass/pallas_call | solution.py:166
  152.7 1.4 collective-permute-done.6
  156.1 1.7 broadcast_in_dim.83.bias_ref
  157.8 1.6 collective-permute-start.17
  160.1 13.9 %shard_map.152 = (f32[640,1024]{1,0:T(8,128)}, bf16[8,1280,1024]{2,1,0:T(8,128)(2,1)}) custom-call(s32[6]{0:T(128)} %stack.43.pos, bf16[12576,1024]{1,0:T(8,128)(2,1)} %emb_hbm.13, f32[3144,1]{1,0:T(8,128)} %broadcast_in_dim.83.bias_ref, f32[8,2,1280]{2,1,0:T(2,128)} %pad_maximum_fusion.info_ref, f32[608,1024]{1,0:T(8,128)} %get-tuple-element.78.refs_0_, ...), custom_call_target="tpu_custom_call" | custom-call | flops 67108864 | bytes 9175040 | tf_op jit(solution)/shard_map/pallas_call | solution.py:431
  174.0 15.8 %shard_map.153.refs_2_ = f32[896,1024]{1,0:T(8,128)} custom-call(s32[6]{0:T(128)} %stack.43.pos, bf16[12576,1024]{1,0:T(8,128)(2,1)} %emb_hbm.13, f32[3144,1]{1,0:T(8,128)} %broadcast_in_dim.83.bias_ref, f32[8,2,1280]{2,1,0:T(2,128)} %pad_maximum_fusion.info_ref, bf16[8,1280,1024]{2,1,0:T(8,128)(2,1)} %get-tuple-element.86.refs_0_.refs_8_), custom_call_target="tpu_custom_call" | custom-call | flops 93952408 | bytes 10747904 | tf_op jit(solution)/shard_map/pallas_call | solution.py:431
  192.9 5.7 collective-permute-done.16.refs_6_
  198.6 21.7 %shard_map.154 = (f32[640,1024]{1,0:T(8,128)}, bf16[8,1280,1024]{2,1,0:T(8,128)(2,1)}) custom-call(s32[6]{0:T(128)} %stack.43.pos, bf16[12576,1024]{1,0:T(8,128)(2,1)} %emb_hbm.13, f32[3144,1]{1,0:T(8,128)} %broadcast_in_dim.83.bias_ref, f32[8,2,1280]{2,1,0:T(2,128)} %pad_maximum_fusion.info_ref, ...), custom_call_target="tpu_custom_call", output_to_operand_aliasing={{1}: (12, {})} | custom-call | flops 134217728 | bytes 14417920 | tf_op jit(solution)/shard_map/pallas_call | solution.py:431
  220.2 27.5 %collective-permute-done.10.refs_0_ = f32[608,1024]{1,0:T(8,128)} collective-permute-done((f32[608,1024]{1,0:T(8,128)}, f32[608,1024]{1,0:T(8,128)}, u32[]{:S(2)}, u32[]{:S(2)}) %collective-permute-start.10) | collective-permute-done | bytes 2490400 | tf_op jit(solution)/shard_map/ppermute | solution.py:609
  248.7 7.9 %collective-permute-done.18.refs_2_ = f32[608,1024]{1,0:T(8,128)S(1)} collective-permute-done((f32[608,1024]{1,0:T(8,128)}, f32[608,1024]{1,0:T(8,128)S(1)}, u32[]{:S(2)}, u32[]{:S(2)}) %collective-permute-start.18) | collective-permute-done | bytes 2490400 | tf_op jit(solution)/shard_map/ppermute | solution.py:609
  256.6 1.5 copy-done.7
  258.1 1.5 copy-done.6
  259.6 14.9 %shard_map.155 = (f32[640,1024]{1,0:T(8,128)}, bf16[8,1280,1024]{2,1,0:T(8,128)(2,1)}, f32[12576,1024]{1,0:T(8,128)}) custom-call(s32[6]{0:T(128)} %stack.43.pos, bf16[12576,1024]{1,0:T(8,128)(2,1)} %emb_hbm.13, f32[3144,1]{1,0:T(8,128)} %broadcast_in_dim.83.bias_ref, f32[8,2,1280]{2,1,0:T(2,128)} %pad_maximum_fusion.info_ref, ...), custom_call_target="tpu_custom_call", output_to_operand_aliasing={{1}: (8, {})} | custom-call | flops 67108864 | bytes 9175040 | tf_op jit(solution)/shard_map/pallas_call | solution.py:431
  275.9 2.0 collective-permute-start.20
  277.9 2.3 collective-permute-start.21
  286.4 6.2 back.1
  292.6 37.7 %shard_map.156 = (f32[896,1024]{1,0:T(8,128)}, f32[12576,1024]{1,0:T(8,128)}) custom-call(s32[6]{0:T(128)} %stack.43.pos, bf16[12576,1024]{1,0:T(8,128)(2,1)} %emb_hbm.13, f32[3144,1]{1,0:T(8,128)} %broadcast_in_dim.83.bias_ref, f32[8,2,1280]{2,1,0:T(2,128)} %pad_maximum_fusion.info_ref, ...), custom_call_target="tpu_custom_call", output_to_operand_aliasing={{1}: (5, {})} | custom-call | flops 281857216 | bytes 21233664 | tf_op jit(solution)/shard_map/pallas_call | solution.py:431
  330.3 1.4 collective-permute-start.33
  332.2 1.4 copy-done.3
  333.6 47.0 %shard_map.157 = (f32[896,1024]{1,0:T(8,128)}, f32[12576,1024]{1,0:T(8,128)}) custom-call(s32[6]{0:T(128)} %stack.43.pos, bf16[12576,1024]{1,0:T(8,128)(2,1)} %emb_hbm.13, f32[3144,1]{1,0:T(8,128)} %broadcast_in_dim.83.bias_ref, f32[8,2,1280]{2,1,0:T(2,128)} %pad_maximum_fusion.info_ref, ...), custom_call_target="tpu_custom_call", output_to_operand_aliasing={{1}: (5, {})} | custom-call | flops 375809632 | bytes 26476544 | tf_op jit(solution)/shard_map/pallas_call | solution.py:431
  382.2 58.2 %all-reduce.7.cloned.1.call-done.refs_0_ = f32[1096,256]{1,0:T(8,128)} async-done(((f32[1096,256]{1,0:T(8,128)}), f32[1096,256]{1,0:T(8,128)}) %all-reduce.7.cloned.1.call-update) | async-done | bytes 1122320 | tf_op jit(solution)/shard_map/psum | solution.py:707
  440.4 1.9 constant_dynamic-slice_fusion
  442.3 1.3 collective-permute-start.37
  443.6 40.8 %shard_map.158 = (f32[712,1024]{1,0:T(8,128)}, f32[12576,1024]{1,0:T(8,128)}) custom-call(s32[6]{0:T(128)} %stack.43.pos, bf16[12576,1024]{1,0:T(8,128)(2,1)} %emb_hbm.13, f32[3144,1]{1,0:T(8,128)} %broadcast_in_dim.83.bias_ref, f32[8,2,1280]{2,1,0:T(2,128)} %pad_maximum_fusion.info_ref, ...), custom_call_target="tpu_custom_call", output_to_operand_aliasing={{1}: (5, {})} | custom-call | flops 298634432 | bytes 25346048 | tf_op jit(solution)/shard_map/pallas_call | solution.py:431
  485.6 9.8 %collective-permute-done.41.refs_5_ = f32[712,1024]{1,0:T(8,128)S(1)} collective-permute-done((f32[712,1024]{1,0:T(8,128)}, f32[712,1024]{1,0:T(8,128)S(1)}, u32[]{:S(2)}, u32[]{:S(2)}) %collective-permute-start.41) | collective-permute-done | bytes 2916384 | tf_op jit(solution)/shard_map/ppermute | solution.py:609
  495.3 1.6 copy-done.2
  496.9 1.8 copy-done
  498.8 13.2 %put_rows.3.refs_0_ = f32[12576,1024]{1,0:T(8,128)} custom-call(s32[6]{0:T(128)} %stack.43.pos, f32[12576,1024]{1,0:T(8,128)} %get-tuple-element.118.refs_0_, f32[896,1024]{1,0:T(8,128)} %copy-done, f32[896,1024]{1,0:T(8,128)} %collective-permute-done.38.refs_2_, f32[896,1024]{1,0:T(8,128)} %collective-permute-done.39.refs_3_, ...), custom_call_target="tpu_custom_call", output_to_operand_aliasing={{}: (1, {})} | custom-call | flops 43991 | bytes 35192832 | tf_op jit(solution)/shard_map/put_rows/pallas_call | solution.py:464
  511.9 7.4 %collective-permute-done.42.refs_1_ = f32[712,1024]{1,0:T(8,128)} collective-permute-done((f32[712,1024]{1,0:T(8,128)}, f32[712,1024]{1,0:T(8,128)}, u32[]{:S(2)}, u32[]{:S(2)}) %collective-permute-start.42) | collective-permute-done | bytes 2916384 | tf_op jit(solution)/shard_map/ppermute | solution.py:615
  520.7 1.9 collective-permute-start.29
  524.2 50.3 %collective-permute-done.28.refs_1_ = f32[1232,256]{1,0:T(8,128)} collective-permute-done((f32[1232,256]{1,0:T(8,128)}, f32[1232,256]{1,0:T(8,128)}, u32[]{:S(2)}, u32[]{:S(2)}) %collective-permute-start.28) | collective-permute-done | bytes 1261600 | tf_op jit(solution)/shard_map/ppermute | solution.py:612
  574.6 3.4 collective-permute-start.26
  578.1 76.7 %collective-permute-done.30.refs_3_ = f32[1232,256]{1,0:T(8,128)} collective-permute-done((f32[1232,256]{1,0:T(8,128)}, f32[1232,256]{1,0:T(8,128)}, u32[]{:S(2)}, u32[]{:S(2)}) %collective-permute-start.30) | collective-permute-done | bytes 1261600 | tf_op jit(solution)/shard_map/ppermute | solution.py:612
  654.8 14.7 %spread.1 = bf16[16,512,1024]{2,1,0:T(8,128)(2,1)} custom-call(s32[1]{0:T(128)} %bitcast.vp, s32[16,1,80]{2,1,0:T(1,128)} %bitcast.25, bf16[1024,1024]{1,0:T(8,128)(2,1)} %w_ref.3, f32[1232,256]{1,0:T(8,128)} %get-tuple-element.111.refs_0_, f32[1232,256]{1,0:T(8,128)} %collective-permute-done.28.refs_1_, f32[1232,256]{1,0:T(8,128)} %collective-permute-done.29.refs_2_, ...), custom_call_target="tpu_custom_call" | custom-call | flops 21474836 | bytes 16777216 | tf_op jit(solution)/shard_map/spread/pallas_call | solution.py:585
  669.5 8.1 %collective-permute-done.27.refs_3_ = f32[520,256]{1,0:T(8,128)} collective-permute-done((f32[520,256]{1,0:T(8,128)}, f32[520,256]{1,0:T(8,128)}, u32[]{:S(2)}, u32[]{:S(2)}) %collective-permute-start.27) | collective-permute-done | bytes 532512 | tf_op jit(solution)/shard_map/ppermute | solution.py:612
  683.3 4.1 put_rows.4.refs_0_
  687.4 4.9 join.1
  695.7 1.5 fusion.2
  697.2 1.6 copy-done.1
  698.7 4.1 put_rows.5
  (136 shorter events, 41.7 us)
Async XLA Ops:
  7.2 277.0 %reduce-scatter.2.cloned.1.call-start = ((), (), s32[]{:S(2)}) async-start(), calls=%async_computation.1 | async-start | bytes 6307840 | tf_op jit(solution)/shard_map/reduce_scatter | solution.py:656
  24.8 76.0 %collective-permute-start.9 = (f32[624,1024]{1,0:T(8,128)}, f32[624,1024]{1,0:T(8,128)}, u32[]{:S(2)}, u32[]{:S(2)}) collective-permute-start(f32[624,1024]{1,0:T(8,128)} %get-tuple-element.77.refs_1_), channel_id=1, source_target_pairs={{0,4},{1,5},{2,6},{3,7},{4,0},{5,1},{6,2},{7,3},{8,12},{9,13},{10,... | collective-permute-start | bytes 7667720 | tf_op jit(solution)/shard_map/ppermute | solution.py:609
  26.1 74.7 %collective-permute-start.8 = (f32[608,1024]{1,0:T(8,128)}, f32[608,1024]{1,0:T(8,128)}, u32[]{:S(2)}, u32[]{:S(2)}) collective-permute-start(f32[608,1024]{1,0:T(8,128)} %get-tuple-element.78.refs_0_), channel_id=1, source_target_pairs={{0,2},{1,3},{2,0},{3,1},{4,6},{5,7},{6,4},{7,5},{8,10},{9,11},{10,... | collective-permute-start | bytes 7471112 | tf_op jit(solution)/shard_map/ppermute | solution.py:609
  27.3 122.8 %collective-permute-start.3 = (f32[624,1024]{1,0:T(8,128)}, f32[624,1024]{1,0:T(8,128)}, u32[]{:S(2)}, u32[]{:S(2)}) collective-permute-start(f32[624,1024]{1,0:T(8,128)} %get-tuple-element.77.refs_1_), channel_id=1, source_target_pairs={{0,2},{1,3},{2,0},{3,1},{4,6},{5,7},{6,4},{7,5},{8,10},{9,11},{10,... | collective-permute-start | bytes 7667720 | tf_op jit(solution)/shard_map/ppermute | solution.py:609
  27.5 122.6 %collective-permute-start.4 = (f32[608,1024]{1,0:T(8,128)}, f32[608,1024]{1,0:T(8,128)}, u32[]{:S(2)}, u32[]{:S(2)}) collective-permute-start(f32[608,1024]{1,0:T(8,128)} %get-tuple-element.78.refs_0_), channel_id=1, source_target_pairs={{0,4},{1,5},{2,6},{3,7},{4,0},{5,1},{6,2},{7,3},{8,12},{9,13},{10,... | collective-permute-start | bytes 7471112 | tf_op jit(solution)/shard_map/ppermute | solution.py:609
  29.7 65.3 %copy-start.4 = (f32[624,1024]{1,0:T(8,128)S(1)}, f32[624,1024]{1,0:T(8,128)}, u32[]{:S(2)}) copy-start(f32[624,1024]{1,0:T(8,128)} %get-tuple-element.77.refs_1_) | copy-start | bytes 7667716
  83.7 3.5 collective-permute-start
  87.2 4.0 collective-permute-start.1
  91.1 3.8 collective-permute-start.2
  95.0 65.1 %collective-permute-start.13 = (f32[624,1024]{1,0:T(8,128)S(1)}, f32[624,1024]{1,0:T(8,128)}, u32[]{:S(2)}, u32[]{:S(2)}) collective-permute-start(f32[624,1024]{1,0:T(8,128)S(1)} %copy-done.4), channel_id=1, source_target_pairs={{0,1},{1,0},{2,3},{3,2},{4,5},{5,4},{6,7},{7,6},{8,9},{9,8},{10,11... | collective-permute-start | bytes 7667720 | tf_op jit(solution)/shard_map/ppermute | solution.py:609
  100.8 59.3 %collective-permute-start.12 = (f32[608,1024]{1,0:T(8,128)}, f32[608,1024]{1,0:T(8,128)}, u32[]{:S(2)}, u32[]{:S(2)}) collective-permute-start(f32[608,1024]{1,0:T(8,128)} %get-tuple-element.78.refs_0_), channel_id=1, source_target_pairs={{0,1},{1,0},{2,3},{3,2},{4,5},{5,4},{6,7},{7,6},{8,9},{9,8},{10,11... | collective-permute-start | bytes 7471112 | tf_op jit(solution)/shard_map/ppermute | solution.py:609
  100.8 91.0 %collective-permute-start.14 = (f32[608,1024]{1,0:T(8,128)}, f32[608,1024]{1,0:T(8,128)}, u32[]{:S(2)}, u32[]{:S(2)}) collective-permute-start(f32[608,1024]{1,0:T(8,128)} %collective-permute-done.8.refs_0_), channel_id=1, source_target_pairs={{0,1},{1,0},{2,3},{3,2},{4,5},{5,4},{6,7},{7,6},{8,9},{9,8},{10,11... | collective-permute-start | bytes 7471112 | tf_op jit(solution)/shard_map/ppermute | solution.py:609
  149.9 290.5 %all-reduce.7.cloned.1.call-start = ((), (), s32[]{:S(2)}) async-start(), calls=%async_computation.2 | async-start | bytes 2244608 | tf_op jit(solution)/shard_map/psum | solution.py:707
  150.2 1.2 collective-permute-start.5
  151.4 2.7 collective-permute-start.6
  154.1 5.2 collective-permute-start.7
  157.8 35.1 %collective-permute-start.17 = (f32[624,1024]{1,0:T(8,128)}, f32[624,1024]{1,0:T(8,128)}, u32[]{:S(2)}, u32[]{:S(2)}) collective-permute-start(f32[624,1024]{1,0:T(8,128)} %collective-permute-done.9.refs_5_), channel_id=1, source_target_pairs={{0,1},{1,0},{2,3},{3,2},{4,5},{5,4},{6,7},{7,6},{8,9},{9,8},{10,11... | collective-permute-start | bytes 7667720 | tf_op jit(solution)/shard_map/ppermute | solution.py:609
  189.8 8.8 %collective-permute-start.15 = (f32[624,1024]{1,0:T(8,128)}, f32[624,1024]{1,0:T(8,128)}, u32[]{:S(2)}, u32[]{:S(2)}) collective-permute-start(f32[624,1024]{1,0:T(8,128)} %collective-permute-done.3.refs_1_), channel_id=1, source_target_pairs={{0,1},{1,0},{2,3},{3,2},{4,5},{5,4},{6,7},{7,6},{8,9},{9,8},{10,11... | collective-permute-start | bytes 7667720 | tf_op jit(solution)/shard_map/ppermute | solution.py:609
  190.1 57.7 %collective-permute-start.11 = (f32[624,1024]{1,0:T(8,128)}, f32[624,1024]{1,0:T(8,128)S(1)}, u32[]{:S(2)}, u32[]{:S(2)}) collective-permute-start(f32[624,1024]{1,0:T(8,128)} %collective-permute-done.9.refs_5_), channel_id=1, source_target_pairs={{0,2},{1,3},{2,0},{3,1},{4,6},{5,7},{6,4},{7,5},{8,10},{9,11},{10,... | collective-permute-start | bytes 7667720 | tf_op jit(solution)/shard_map/ppermute | solution.py:609
  191.3 7.3 %collective-permute-start.16 = (f32[608,1024]{1,0:T(8,128)}, f32[608,1024]{1,0:T(8,128)}, u32[]{:S(2)}, u32[]{:S(2)}) collective-permute-start(f32[608,1024]{1,0:T(8,128)} %collective-permute-done.4.refs_4_), channel_id=1, source_target_pairs={{0,1},{1,0},{2,3},{3,2},{4,5},{5,4},{6,7},{7,6},{8,9},{9,8},{10,11... | collective-permute-start | bytes 7471112 | tf_op jit(solution)/shard_map/ppermute | solution.py:609
  191.8 55.9 %collective-permute-start.10 = (f32[608,1024]{1,0:T(8,128)}, f32[608,1024]{1,0:T(8,128)}, u32[]{:S(2)}, u32[]{:S(2)}) collective-permute-start(f32[608,1024]{1,0:T(8,128)} %collective-permute-done.8.refs_0_), channel_id=1, source_target_pairs={{0,4},{1,5},{2,6},{3,7},{4,0},{5,1},{6,2},{7,3},{8,12},{9,13},{10,... | collective-permute-start | bytes 7471112 | tf_op jit(solution)/shard_map/ppermute | solution.py:609
  247.8 8.9 %collective-permute-start.19 = (f32[624,1024]{1,0:T(8,128)S(1)}, f32[624,1024]{1,0:T(8,128)S(1)}, u32[]{:S(2)}, u32[]{:S(2)}) collective-permute-start(f32[624,1024]{1,0:T(8,128)S(1)} %collective-permute-done.11.refs_1_), channel_id=1, source_target_pairs={{0,1},{1,0},{2,3},{3,2},{4,5},{5,4},{6,7},{7,6},{8,9},{9,8},{10,11... | collective-permute-start | bytes 7667720 | tf_op jit(solution)/shard_map/ppermute | solution.py:609
  248.6 8.0 %collective-permute-start.18 = (f32[608,1024]{1,0:T(8,128)}, f32[608,1024]{1,0:T(8,128)S(1)}, u32[]{:S(2)}, u32[]{:S(2)}) collective-permute-start(f32[608,1024]{1,0:T(8,128)} %collective-permute-done.10.refs_0_), channel_id=1, source_target_pairs={{0,1},{1,0},{2,3},{3,2},{4,5},{5,4},{6,7},{7,6},{8,9},{9,8},{10,11... | collective-permute-start | bytes 7471112 | tf_op jit(solution)/shard_map/ppermute | solution.py:609
  259.6 21.0 %copy-start.15 = (f32[1,12576]{1,0:T(1,128)S(1)}, f32[1,12576]{1,0:T(1,128)}, u32[]{:S(2)}) copy-start(f32[1,12576]{1,0:T(1,128)} %get-tuple-element.96) | copy-start | bytes 150916
  274.5 57.7 %collective-permute-start.24 = (f32[640,1024]{1,0:T(8,128)}, f32[640,1024]{1,0:T(8,128)S(1)}, u32[]{:S(2)}, u32[]{:S(2)}) collective-permute-start(f32[640,1024]{1,0:T(8,128)} %get-tuple-element.93), channel_id=1, source_target_pairs={{0,2},{1,5},{2,0},{3,7},{4,6},{5,1},{6,4},{7,3},{8,10},{9,13},{10,... | collective-permute-start | bytes 7864328 | tf_op jit(solution)/shard_map/ppermute | solution.py:615
  275.5 56.6 %collective-permute-start.23 = (f32[640,1024]{1,0:T(8,128)}, f32[640,1024]{1,0:T(8,128)}, u32[]{:S(2)}, u32[]{:S(2)}) collective-permute-start(f32[640,1024]{1,0:T(8,128)} %get-tuple-element.93), channel_id=1, source_target_pairs={{0,1},{1,0},{2,3},{3,2},{4,5},{5,4},{6,7},{7,6},{8,9},{9,8},{10,11... | collective-permute-start | bytes 7864328 | tf_op jit(solution)/shard_map/ppermute | solution.py:609
  275.9 6.6 collective-permute-start.20
  277.9 5.0 collective-permute-start.21
  280.3 3.8 collective-permute-start.22
  330.3 112.0 %collective-permute-start.33 = (f32[896,1024]{1,0:T(8,128)}, f32[896,1024]{1,0:T(8,128)}, u32[]{:S(2)}, u32[]{:S(2)}) collective-permute-start(f32[896,1024]{1,0:T(8,128)} %get-tuple-element.103), channel_id=1, source_target_pairs={{0,2},{1,5},{2,0},{3,7},{4,6},{5,1},{6,4},{7,3},{8,10},{9,13},{10,... | collective-permute-start | bytes 11010056 | tf_op jit(solution)/shard_map/ppermute | solution.py:615
  331.6 112.0 %collective-permute-start.32 = (f32[896,1024]{1,0:T(8,128)}, f32[896,1024]{1,0:T(8,128)}, u32[]{:S(2)}, u32[]{:S(2)}) collective-permute-start(f32[896,1024]{1,0:T(8,128)} %get-tuple-element.103), channel_id=1, source_target_pairs={{0,1},{1,0},{2,3},{3,2},{4,5},{5,4},{6,7},{7,6},{8,9},{9,8},{10,11... | collective-permute-start | bytes 11010056 | tf_op jit(solution)/shard_map/ppermute | solution.py:609
  380.6 103.8 %collective-permute-start.39 = (f32[896,1024]{1,0:T(8,128)}, f32[896,1024]{1,0:T(8,128)}, u32[]{:S(2)}, u32[]{:S(2)}) collective-permute-start(f32[896,1024]{1,0:T(8,128)} %get-tuple-element.105), channel_id=1, source_target_pairs={{0,2},{1,5},{2,0},{3,7},{4,6},{5,1},{6,4},{7,3},{8,10},{9,13},{10,... | collective-permute-start | bytes 11010056 | tf_op jit(solution)/shard_map/ppermute | solution.py:615
  381.6 62.0 %collective-permute-start.31 = (f32[640,1024]{1,0:T(8,128)}, f32[640,1024]{1,0:T(8,128)}, u32[]{:S(2)}, u32[]{:S(2)}) collective-permute-start(f32[640,1024]{1,0:T(8,128)} %copy-done.3), channel_id=1, source_target_pairs={{0,1},{1,0},{2,3},{3,2},{4,5},{5,4},{6,7},{7,6},{8,9},{9,8},{10,11... | collective-permute-start | bytes 7864328 | tf_op jit(solution)/shard_map/ppermute | solution.py:609
  381.7 103.9 %collective-permute-start.38 = (f32[896,1024]{1,0:T(8,128)}, f32[896,1024]{1,0:T(8,128)}, u32[]{:S(2)}, u32[]{:S(2)}) collective-permute-start(f32[896,1024]{1,0:T(8,128)} %get-tuple-element.105), channel_id=1, source_target_pairs={{0,1},{1,0},{2,3},{3,2},{4,5},{5,4},{6,7},{7,6},{8,9},{9,8},{10,11... | collective-permute-start | bytes 11010056 | tf_op jit(solution)/shard_map/ppermute | solution.py:609
  442.3 53.0 %collective-permute-start.37 = (f32[896,1024]{1,0:T(8,128)}, f32[896,1024]{1,0:T(8,128)S(1)}, u32[]{:S(2)}, u32[]{:S(2)}) collective-permute-start(f32[896,1024]{1,0:T(8,128)} %collective-permute-done.33.refs_4_), channel_id=1, source_target_pairs={{0,1},{1,0},{2,3},{3,2},{4,5},{5,4},{6,7},{7,6},{8,9},{9,8},{10,11... | collective-permute-start | bytes 11010056 | tf_op jit(solution)/shard_map/ppermute | solution.py:609
  484.5 12.5 %collective-permute-start.40 = (f32[896,1024]{1,0:T(8,128)}, f32[896,1024]{1,0:T(8,128)}, u32[]{:S(2)}, u32[]{:S(2)}) collective-permute-start(f32[896,1024]{1,0:T(8,128)} %collective-permute-done.39.refs_3_), channel_id=1, source_target_pairs={{0,1},{1,0},{2,3},{3,2},{4,5},{5,4},{6,7},{7,6},{8,9},{9,8},{10,11... | collective-permute-start | bytes 11010056 | tf_op jit(solution)/shard_map/ppermute | solution.py:609
  484.6 10.8 %collective-permute-start.41 = (f32[712,1024]{1,0:T(8,128)}, f32[712,1024]{1,0:T(8,128)S(1)}, u32[]{:S(2)}, u32[]{:S(2)}) collective-permute-start(f32[712,1024]{1,0:T(8,128)} %get-tuple-element.110), channel_id=1, source_target_pairs={{0,1},{1,0},{2,3},{3,2},{4,5},{5,4},{6,7},{7,6},{8,9},{9,8},{10,11... | collective-permute-start | bytes 8749064 | tf_op jit(solution)/shard_map/ppermute | solution.py:609
  485.1 34.3 %collective-permute-start.42 = (f32[712,1024]{1,0:T(8,128)}, f32[712,1024]{1,0:T(8,128)}, u32[]{:S(2)}, u32[]{:S(2)}) collective-permute-start(f32[712,1024]{1,0:T(8,128)} %get-tuple-element.110), channel_id=1, source_target_pairs={{0,2},{1,5},{2,0},{3,7},{4,6},{5,1},{6,4},{7,3},{8,10},{9,13},{10,... | collective-permute-start | bytes 8749064 | tf_op jit(solution)/shard_map/ppermute | solution.py:615
  519.3 177.8 %collective-permute-start.43 = (f32[712,1024]{1,0:T(8,128)}, f32[712,1024]{1,0:T(8,128)S(1)}, u32[]{:S(2)}, u32[]{:S(2)}) collective-permute-start(f32[712,1024]{1,0:T(8,128)} %collective-permute-done.42.refs_1_), channel_id=1, source_target_pairs={{0,1},{1,0},{2,3},{3,2},{4,5},{5,4},{6,7},{7,6},{8,9},{9,8},{10,11... | collective-permute-start | bytes 8749064 | tf_op jit(solution)/shard_map/ppermute | solution.py:609
  520.3 54.3 %collective-permute-start.28 = (f32[1232,256]{1,0:T(8,128)}, f32[1232,256]{1,0:T(8,128)}, u32[]{:S(2)}, u32[]{:S(2)}) collective-permute-start(f32[1232,256]{1,0:T(8,128)} %get-tuple-element.111.refs_0_), channel_id=1, source_target_pairs={{0,8},{8,0},{16,24},{24,16},{1,9},{9,1},{17,25},{25,17},{2,10},{10... | collective-permute-start | bytes 3784712 | tf_op jit(solution)/shard_map/ppermute | solution.py:612
  520.7 57.3 %collective-permute-start.29 = (f32[1232,256]{1,0:T(8,128)}, f32[1232,256]{1,0:T(8,128)}, u32[]{:S(2)}, u32[]{:S(2)}) collective-permute-start(f32[1232,256]{1,0:T(8,128)} %get-tuple-element.111.refs_0_), channel_id=1, source_target_pairs={{0,16},{8,24},{16,0},{24,8},{1,17},{9,25},{17,1},{25,9},{2,18},{10... | collective-permute-start | bytes 3784712 | tf_op jit(solution)/shard_map/ppermute | solution.py:612
  522.5 132.2 %collective-permute-start.30 = (f32[1232,256]{1,0:T(8,128)}, f32[1232,256]{1,0:T(8,128)}, u32[]{:S(2)}, u32[]{:S(2)}) collective-permute-start(f32[1232,256]{1,0:T(8,128)} %get-tuple-element.111.refs_0_), channel_id=1, source_target_pairs={{0,24},{8,16},{16,8},{24,0},{1,25},{9,17},{17,9},{25,1},{2,26},{10... | collective-permute-start | bytes 3784712 | tf_op jit(solution)/shard_map/ppermute | solution.py:612
  522.9 146.5 %collective-permute-start.25 = (f32[520,256]{1,0:T(8,128)}, f32[520,256]{1,0:T(8,128)S(1)}, u32[]{:S(2)}, u32[]{:S(2)}) collective-permute-start(f32[520,256]{1,0:T(8,128)} %constant_dynamic-slice_fusion), channel_id=1, source_target_pairs={{0,8},{8,0},{16,24},{24,16},{1,9},{9,1},{17,25},{25,17},{2,10},{10... | collective-permute-start | bytes 1597448 | tf_op jit(solution)/shard_map/ppermute | solution.py:612
  574.6 94.9 %collective-permute-start.26 = (f32[520,256]{1,0:T(8,128)}, f32[520,256]{1,0:T(8,128)S(1)}, u32[]{:S(2)}, u32[]{:S(2)}) collective-permute-start(f32[520,256]{1,0:T(8,128)} %constant_dynamic-slice_fusion), channel_id=1, source_target_pairs={{0,16},{8,24},{16,0},{24,8},{1,17},{9,25},{17,1},{25,9},{2,18},{10... | collective-permute-start | bytes 1597448 | tf_op jit(solution)/shard_map/ppermute | solution.py:612
  578.0 99.6 %collective-permute-start.27 = (f32[520,256]{1,0:T(8,128)}, f32[520,256]{1,0:T(8,128)}, u32[]{:S(2)}, u32[]{:S(2)}) collective-permute-start(f32[520,256]{1,0:T(8,128)} %constant_dynamic-slice_fusion), channel_id=1, source_target_pairs={{0,24},{8,16},{16,8},{24,0},{1,25},{9,17},{17,9},{25,1},{2,26},{10... | collective-permute-start | bytes 1597448 | tf_op jit(solution)/shard_map/ppermute | solution.py:612
  677.6 2.7 collective-permute-start.34
  678.7 2.3 collective-permute-start.35
  678.7 3.1 collective-permute-start.36
  (16 other events, 114.5 us)
Sparse Core Ops, SparseCore 0:
  150.0 93.6 reduce-scatter.1
  381.8 58.5 all-reduce.6

commit v3 on v2

--- a/solution.py
+++ b/solution.py
@@ -250,10 +250,11 @@
 
 
 BLK = 1280
+STEPS = {"own": 2, "again": 2, "side": 4, "far": 2, "last": 2, "whole": 8}
 ME, MINE, MINE_ID, TWIN, FAR, FAR_TWIN = range(6)
 
 
-def rows_kernel(kind, scale, s0, m, cut, n_loc, sources, spots, has_big, pos, emb_hbm, bias_ref, info_ref, *refs):
+def rows_kernel(kind, scale, s0, m, cut, n_loc, sources, skips, spots, has_big, pos, emb_hbm, bias_ref, info_ref, *refs):
     refs = list(refs)
     take = lambda n: [refs.pop(0) for _ in range(n)]
     wide = sources is not None
@@ -265,19 +266,19 @@
         u_hbm, = take(1)
     if has_big:
         take(1)
-    parts = take({"far": 2, "rest": 1}.get(kind, 0))
+    parts = take(len(skips))
     puts = take(len(spots))
     out_hbm, = take(1)
     if wide:
         u_hbm, = take(1)
-    if kind in ("far", "rest", "whole"):
+    if kind in ("far", "last", "whole"):
         big_ref, = take(1)
     if wide:
         buf, = take(1)
     ring, emb_sc, g_sc, acc, hold, sem, tok_sem, back_sem, in_sem, out_sem = refs
     me = pos[ME]
     chip = lax.div(me, 2)
-    n_steps = {"own": 2, "again": 2, "side": 4, "far": 2, "rest": 6, "whole": 8}[kind]
+    n_steps = STEPS[kind]
     along_x, along_y = chip ^ 1, chip ^ 2
 
     def device(i):
@@ -285,7 +286,7 @@
         far = 2 * (chip ^ 3) + lax.rem(i, 2)
         if kind in ("own", "again"):
             return 2 * chip + i
-        return {"side": side, "far": far, "rest": jnp.where(i < 4, side, far), "whole": i}[kind]
+        return {"side": side, "far": far, "last": far, "whole": i}[kind]
 
     depth = ring.shape[0]
 
@@ -309,14 +310,14 @@
         n = p.shape[0]
         loads.append(pltpu.make_async_copy(p, hold.at[j, :n, :], in_sem.at[j]))
         stores.append(pltpu.make_async_copy(hold.at[j, :n, :], big_ref.at[pl.ds(row(base, off), n), :], out_sem.at[j]))
-    for j, p in enumerate(parts):
-        loads.append(pltpu.make_async_copy(p, hold.at[len(puts) + j, :m, :], in_sem.at[len(puts) + j]))
+    for j, (p, skip) in enumerate(zip(parts, skips)):
+        loads.append(pltpu.make_async_copy(p.at[skip:skip + m, :], hold.at[len(puts) + j, :m, :], in_sem.at[len(puts) + j]))
     acc[...] = jnp.zeros_like(acc)
     if wide:
         for k in range(2):
             ring[k, n_loc:, :] = jnp.zeros((BLK - n_loc, ring.shape[2]), BF16)
     emb_copy.wait()
-    n_cuts = max(1, round(m / 320))
+    n_cuts = max(1, round(m / 300))
     cuts = [-(-m * k // (n_cuts * 16)) * 16 for k in range(n_cuts)] + [m]
     cuts = list(zip(cuts[:-1], cuts[1:]))
     kept = lambda i: pltpu.make_async_copy(ring.at[lax.rem(i, 2)], u_hbm.at[device(i)], back_sem.at[lax.rem(i, 2)])
@@ -353,7 +354,6 @@
         if wide:
             ring[slot, :n_loc, :] = buf[slot].astype(BF16)
             kept(i).start()
-        group = (i >= 4).astype(I32) if kind == "rest" else 0
         rel = device(i) ^ me
         lse, lab = info_ref[rel, 0:1, :], info_ref[rel, 1:2, :]
 
@@ -367,17 +367,15 @@
         for k, (r0, r1) in enumerate(cuts):
             if k + 1 < len(cuts):
                 weights(*cuts[k + 1])
-            acc[group, r0:r1, :] += dot(g_sc[r0:r1, :], ring[slot], NN)
+            acc[r0:r1, :] += dot(g_sc[r0:r1, :], ring[slot], NN)
 
     for c in loads[len(puts):]:
         c.wait()
-    if kind == "far":
-        acc[0] = (hold[0, :m, :] + acc[0]) + hold[1, :m, :]
-    if kind == "rest":
-        acc[0] = (hold[len(puts), :m, :] + acc[1]) + acc[0]
-    done = [pltpu.make_async_copy(acc.at[0], out_hbm, sem)]
-    if kind in ("far", "rest", "whole"):
-        done.append(pltpu.make_async_copy(acc.at[0], big_ref.at[pl.ds(row(MINE, s0), m), :], emb_sem(tok_sem)))
+    if parts:
+        acc[...] = (hold[len(puts), :m, :] + acc[...]) + hold[len(puts) + 1, :m, :]
+    done = [pltpu.make_async_copy(acc, out_hbm, sem)]
+    if kind in ("far", "last", "whole"):
+        done.append(pltpu.make_async_copy(acc, big_ref.at[pl.ds(row(MINE, s0), m), :], emb_sem(tok_sem)))
     for c in done:
         c.start()
     if wide:
@@ -396,8 +394,7 @@
     m, e = s1 - s0, emb.shape[1]
     sds = jax.ShapeDtypeStruct
     wide = kind in ("own", "side", "far")
-    final = kind in ("far", "rest", "whole")
-    n_dev = info.shape[0]
+    final = kind in ("far", "last", "whole")
     args, aliases = [pos, emb, bias, info], {}
     outs = [sds((m, e), F32)]
     sources = None
@@ -405,7 +402,7 @@
         sources = {"own": (0, CORE), "side": (X, X | CORE, Y, Y | CORE), "far": (X | Y, X | Y | CORE)}[kind]
         args += [h for r in sources for h in tokens[r]]
         n_loc = tokens[0][0].shape[0] + tokens[0][1].shape[0]
-        outs.append(sds((n_dev, BLK, e), BF16))
+        outs.append(sds((8, BLK, e), BF16))
         if kind != "own":
             aliases[len(args)] = 1
             args.append(u_all)
@@ -417,19 +414,18 @@
             aliases[len(args)] = len(outs)
             args.append(big)
         outs.append(sds((v_rows, e), F32))
-    args += list(parts) + [a for _, a in puts]
+    args += [a for a, _ in parts] + [a for _, a in puts]
     n_hold = max(1, len(parts) + len(puts))
     tallest = max([m] * len(parts) + [a.shape[0] for _, a in puts] + [8])
-    steps = {"own": 2, "again": 2, "side": 4, "far": 2, "rest": 6, "whole": 8}[kind]
-    t = steps * BLK
+    t = STEPS[kind] * BLK
     scratch = [pltpu.VMEM((2, n_loc, e), F32)] if wide else []
     scratch += [
         pltpu.VMEM((2 if wide else 3, BLK, e), BF16), pltpu.VMEM((m, e), BF16), pltpu.VMEM((m, BLK), BF16),
-        pltpu.VMEM((2 if kind == "rest" else 1, m, e), F32), pltpu.VMEM((n_hold, tallest, e), F32),
+        pltpu.VMEM((m, e), F32), pltpu.VMEM((n_hold, tallest, e), F32),
         DMA, DMA((3, 2)), DMA((2,)), DMA((n_hold,)), DMA((n_hold,)),
     ]
     return pl.pallas_call(
-        functools.partial(rows_kernel, kind, scale, s0, m, cut, n_loc, sources, [spot for spot, _ in puts], big is not None),
+        functools.partial(rows_kernel, kind, scale, s0, m, cut, n_loc, sources, [skip for _, skip in parts], [spot for spot, _ in puts], big is not None),
         in_specs=[SMEM, ANY, VMEM, VMEM] + [ANY] * (len(args) - 4),
         out_specs=[ANY] * len(outs),
         out_shape=outs,
@@ -642,37 +638,35 @@
         lab_local = jnp.where((lab_local >= 0) & (lab_local < shard_rows), lab_local, -1)
         lab_local = jnp.broadcast_to(lab_local[:, None], (n_loc, 128))
         logits, stat = stats(u, emb_table, b_vocab[None], lab_local)
-        x_lo, y_hi = after((x_lo, y_hi), stat)
-        d_lo, d_hi = swap(x_lo, Y), swap(y_hi, X)
-        cx_lo, cy_hi = swap(x_lo, CORE), swap(y_hi, CORE)
         all_stats = [stat] + [swap_vp(stat, b) for b in range(1, n_shards)]
         global_max = functools.reduce(jnp.maximum, [s[0] for s in all_stats])
         log_norm = global_max + jnp.log(order_sum([s[1] * jnp.exp(s[0] - global_max) for s in all_stats]))
         loss_part = jnp.sum(log_norm - order_sum([s[2] for s in all_stats]))
         lse = log_norm + jnp.log(jnp.float32(n_tokens))
 
+        fill = (0, BLK - n_loc)
+        info = jnp.stack([jnp.pad(lse, fill, constant_values=jnp.inf), jnp.pad(flat_labels.astype(F32), fill, constant_values=-1.0)])
+        near, *away = [swap(info, b) for b in (CORE, X, Y, X | Y)]
+        x_lo, y_hi = after((x_lo, y_hi), stat)
+        d_lo, d_hi = swap(x_lo, Y), swap(y_hi, X)
+        cx_lo, cy_hi = swap(x_lo, CORE), swap(y_hi, CORE)
+
         du_part, db_part, sums = du_pass(
             scale, n_shards, logits, emb_table, jnp.broadcast_to(lse[:, None], (n_loc, 128)), lab_local, normed, ln_gain[None])
         du_share = lax.psum_scatter(du_part.reshape(n_shards * n_loc, cols), "vp", scatter_dimension=0, tiled=True)
-
-        lse, x_hi, y_lo = after((lse, x_hi, y_lo), du_part)
-        fill = (0, BLK - n_loc)
-        info = jnp.stack([jnp.pad(lse, fill, constant_values=jnp.inf), jnp.pad(flat_labels.astype(F32), fill, constant_values=-1.0)])[None]
-        for bit in (CORE, X, Y):
-            info = jnp.concatenate([info, swap(info, bit)])
 
         half, quarter = shard_rows // 2, shard_rows // 4
         start = lambda h, c: h * half + c * quarter
         pos = jnp.stack([dp, start(mine, core), row_start + start(mine, core), start(mine, 1 - core), start(1 - mine, core), start(1 - mine, 1 - core)])
         bias_col = lax.dynamic_slice(b_vocab, (start(mine, core),), (quarter,))[:, None]
-        shares = (640, 896, 896, 712)
+        shares = (640, 896, 960, 648)
         ends = [0]
         for w in shares[:-1]:
             ends.append(ends[-1] + max(16, quarter * w // sum(shares) // 16 * 16))
         spans = list(zip(ends, ends[1:] + [quarter]))
 
-        def rows(kind, k, *wait, **kw):
-            return rows_pass(kind, scale, shard_rows, spans[k], cut, after(pos, *wait), emb_table, bias_col, info, **kw)
+        def rows(kind, k, *wait, info=None, span=None, **kw):
+            return rows_pass(kind, scale, shard_rows, span or spans[k], cut, after(pos, *wait), emb_table, bias_col, info, **kw)
 
         def send(k, chunk):
             return ((TWIN, spans[k][0]), swap(chunk, CORE)), hop(chunk)
@@ -682,20 +676,27 @@
             return ((FAR, spans[k][0]), far), ((FAR_TWIN, spans[k][0]), swap(far, CORE))
 
         tokens = {0: (u_lo, u_hi), CORE: (c_lo, c_hi), X: (x_lo, x_hi), Y: (y_lo, y_hi)}
-        own0, u_all = rows("own", 0, tokens=tokens)
-        own1, = rows("again", 1, own0, u_all=u_all)
-        x_hi, y_lo = after((x_hi, y_lo), own1)
+        pair = jnp.stack([info, near])
+        own0, u_all = rows("own", 0, du_part, info=pair, tokens=tokens)
+        x_hi, y_lo, away = after((x_hi, y_lo, away), own0)
+        away = jnp.stack(away)
         tokens[X | CORE] = cx_lo, swap(x_hi, CORE)
         tokens[Y | CORE] = swap(y_lo, CORE), cy_hi
+        away_near = swap(away, CORE)
         tokens[X], tokens[Y] = (x_lo, x_hi), (y_lo, y_hi)
-        side0, u_all = rows("side", 0, tokens=tokens, u_all=u_all)
-        d_lo, d_hi = after((d_lo, d_hi), side0)
+        own1, = rows("again", 1, own0, info=pair, u_all=u_all)
+        info = jnp.concatenate([pair, jnp.stack([away, away_near], axis=1).reshape(6, 2, BLK)])
+        first_two = (spans[0][0], spans[1][1])
+        side, u_all = rows("side", 0, own1, info=info, span=first_two, tokens=tokens, u_all=u_all)
+        d_lo, d_hi = after((d_lo, d_hi), side)
         tokens[X | Y] = d_lo, d_hi
         tokens[X | Y | CORE] = swap(d_lo, CORE), swap(d_hi, CORE)
-        chunk0, u_all, big = rows("far", 0, tokens=tokens, u_all=u_all, parts=(own0, side0))
+        chunk0, u_all, big = rows("far", 0, info=info, tokens=tokens, u_all=u_all, parts=((own0, 0), (side, 0)))
         twin0, far0 = send(0, chunk0)
-
-        du_share = after(du_share, chunk0)
+        chunk1, big = rows("last", 1, info=info, u_all=u_all, big=big, parts=((own1, 0), (side, spans[1][0])))
+        twin1, far1 = send(1, chunk1)
+
+        du_share = after(du_share, chunk1)
         sums = [sums] + [swap_vp(sums, b) for b in range(1, n_shards)]
         sums = order_sum(sums) / width
         m1, m2 = (jnp.broadcast_to(sums[j][:, None], (n_loc, 128)) for j in range(2))
@@ -707,25 +708,22 @@
         pack = lax.psum(pack, "dp")
         dab = [dab] + [swap_vp(dab, b) for b in range(1, n_shards)]
 
-        chunk1, big = rows("rest", 1, back_done, u_all=u_all, big=big, parts=(own1,))
-        twin1, far1 = send(1, chunk1)
-        far0, far_twin0 = forward(0, far0, chunk1)
-
-        chunk2, big = rows("whole", 2, u_all=u_all, big=big, puts=[twin0, far0])
+        chunk2, big = rows("whole", 2, back_done, info=info, u_all=u_all, big=big, puts=[twin0])
         twin2, far2 = send(2, chunk2)
+        far0, far_twin0 = forward(0, far0, chunk2)
         far1, far_twin1 = forward(1, far1, chunk2)
         pack = after(pack, chunk2)
         n_half = (width + 16) // 2
         part = lax.dynamic_slice(pack, (core * n_half, 0), (n_half, cols))
         parts = [swap_vp(part, b) for b in range(1, n_shards)]
 
-        chunk3, big = rows("whole", 3, part, u_all=u_all, big=big, puts=[far_twin0, twin1, far1])
+        chunk3, big = rows("whole", 3, part, info=info, u_all=u_all, big=big, puts=[far0, twin1, far1])
         twin3, far3 = send(3, chunk3)
         far2, far_twin2 = forward(2, far2, chunk3)
         d_hidden = spread_pass(n_masks, hidden.shape, vp[None], pos_pad[:, None], w_trans, after(dab, chunk3))
         parts = after(parts, d_hidden)
         others = [swap(p, CORE) for p in parts]
-        big = put_rows(pos, big, [far_twin1, twin2, far2, far_twin2, twin3])
+        big = put_rows(pos, big, [far_twin0, far_twin1, twin2, far2, far_twin2, twin3])
         pack, parts, others = after((pack, parts, others), big)
         d_w, vec = join_pass(jnp.stack([vp, core]), pack, parts, others)
         far3 = after(far3, big)

time: 719 us -> 703 us (0.978)
  waiting for transfers between devices: 266 us -> 241 us
    ppermute x12, waiting for transfers between devices: 144 us -> 114 us  [swap_vp(): return lax.ppermute(a, 'vp', [(d, d ^ bit) for d in range(n_shards)])]
    ppermute x4, waiting for transfers between devices: 7.39 us -> 32.4 us  [hop(): lax.ppermute(a, 'dp', [(d, d ^ (Y if d & CORE else X)) for d in range(n_g...]
    ppermute x28 -> x30, waiting for transfers between devices: 56 us -> 36.8 us  [swap(): return lax.ppermute(a, 'dp', [(d, d ^ bit) for d in range(n_groups)])]
    ppermute x28 -> x30, starting transfers between devices: 21.9 us -> 27 us  [swap(): return lax.ppermute(a, 'dp', [(d, d ^ bit) for d in range(n_groups)])]
  transfers between devices with their start and end apart: 46 -> 48, of which waited for: 19 -> 15; matrix products, arithmetic and copies ran while one was open for 3% -> 3% of each run, Pallas kernels for 47% -> 49%
where the time goes in v3:
time: 703 us; the launch traced here: 695 us
  Pallas kernels  359 us (51%)
  waiting for transfers between devices  241 us (34%)
  starting transfers between devices  45.2 us (6%)
  local copies, waits for them, and re-layouts  29.5 us (4%)
  between operations  16.5 us (2%)
    pallas_call x7, Pallas kernels, rows_pass(): pl.pallas_call(functools.partial(rows_kernel, kind, scale, s0, m, cut, n_...  193 us
    ppermute x12, waiting for transfers between devices, swap_vp(): return lax.ppermute(a, 'vp', [(d, d ^ bit) for d in range(n_shards)])  114 us
    psum x1, waiting for transfers between devices, local_step(): pack = lax.psum(pack, 'dp')  57.8 us
    pallas_call x1, Pallas kernels, stats(): pl.pallas_call(functools.partial(stats_kernel, v), grid=(n,), in_specs=[w...  54.1 us
    pallas_call x1, Pallas kernels, du_pass(): pl.pallas_call(functools.partial(du_kernel, v, scale), grid=(n,), in_spec...  48 us
    ppermute x30, waiting for transfers between devices, swap(): return lax.ppermute(a, 'dp', [(d, d ^ bit) for d in range(n_groups)])  36.8 us
    ppermute x4, waiting for transfers between devices, hop(): lax.ppermute(a, 'dp', [(d, d ^ (Y if d & CORE else X)) for d in range(n_g...  32.4 us
    ppermute x30, starting transfers between devices, swap(): return lax.ppermute(a, 'dp', [(d, d ^ bit) for d in range(n_groups)])  27 us
  transfers between devices with their start and end apart: 48, of which 15 were waited for; matrix products, arithmetic and copies ran while one was open for 3% of the time, Pallas kernels for 49%

profile of v3, /device:TPU:9, one launch (start us, length us, event | category | flops | bytes accessed | tf_op | source)
XLA Modules:
  0.0 695.4 jit_solution(17691860787956162530)
XLA Ops:
  9.0 15.7 %head.1 = (bf16[1232,1024]{1,0:T(8,128)(2,1)}, f32[1232,1024]{1,0:T(8,128)}, f32[1232,1024]{1,0:T(8,128)}, f32[1232,128]{1,0:T(8,128)}, bf16[1232,1024]{1,0:T(8,...) custom-call(bf16[16,512,1024]{2,1,0:T(8,128)(2,1)} %hid.1, s32[16,80,128]{2,1,0:T(8,128)} %broadcast_in_dim.64.pos_ref, ...), custom_call_target="tpu_custom_call" | custom-call | flops 51673824 | bytes 42008576 | tf_op jit(solution)/shard_map/head/pallas_call | solution.py:239
  24.7 1.3 collective-permute-start.12
  26.0 1.2 collective-permute-start.13
  29.1 54.1 %stats.1 = (f32[1232,12576]{1,0:T(8,128)}, f32[8,1232]{1,0:T(8,128)}) custom-call(bf16[1232,1024]{1,0:T(8,128)(2,1)} %get-tuple-element.75.u_ref, bf16[12576,1024]{1,0:T(8,128)(2,1)} %emb_hbm.13, f32[1,12576]{1,0:T(1,128)} %broadcast_in_dim.68.b_ref, s32[1232,128]{1,0:T(8,128)} %broadcast_in_dim.70.lab_ref), custom_call_target="tpu_custom_call" | custom-call | flops 317309568 | bytes 87730176 | tf_op jit(solution)/shard_map/stats/pallas_call | solution.py:81
  83.2 1.3 collective-permute-start.2
  86.8 1.9 collective-permute-start.9
  88.7 2.7 collective-permute-start.10
  93.4 2.3 collective-permute-done.6
  96.2 1.9 collective-permute-start.3
  100.3 48.0 %du_pass.1 = (f32[4,1232,256]{2,1,0:T(8,128)}, f32[1,12576]{1,0:T(1,128)}, f32[8,1232]{1,0:T(8,128)}) custom-call(f32[1232,12576]{1,0:T(8,128)} %get-tuple-element.76.logits_ref, bf16[12576,1024]{1,0:T(8,128)(2,1)} %emb_hbm.13, f32[1232,128]{1,0:T(8,128)} %broadcast_in_dim.71.lse_ref, s32[1232,128]{1,0:T(8,128)} %broadcast_in_dim.70.lab_ref, ...), custom_call_target="tpu_custom_call" | custom-call | flops 317309568 | bytes 87730176 | tf_op jit(solution)/shard_map/du_pass/pallas_call | solution.py:166
  148.5 1.6 broadcast_in_dim.79.bias_ref
  153.8 14.3 %shard_map.152 = (f32[640,1024]{1,0:T(8,128)}, bf16[8,1280,1024]{2,1,0:T(8,128)(2,1)}) custom-call(s32[6]{0:T(128)} %stack.73.pos, bf16[12576,1024]{1,0:T(8,128)(2,1)} %emb_hbm.13, f32[3144,1]{1,0:T(8,128)} %broadcast_in_dim.79.bias_ref, f32[2,2,1280]{2,1,0:T(2,128)} %pad_maximum_fusion.3.info_ref, f32[608,1024]{1,0:T(8,128)} %get-tuple-element.80.refs_0_, ...), custom_call_target="tpu_custom_call" | custom-call | flops 67108864 | bytes 9175040 | tf_op jit(solution)/shard_map/pallas_call | solution.py:427
  170.3 7.8 %collective-permute-done.11 = f32[3,2,1280]{2,1,0:T(2,128)S(1)} collective-permute-done((f32[3,2,1280]{2,1,0:T(2,128)S(1)}, f32[3,2,1280]{2,1,0:T(2,128)S(1)}, u32[]{:S(2)}, u32[]{:S(2)}) %collective-permute-start.11) | collective-permute-done | bytes 30752 | tf_op jit(solution)/shard_map/ppermute | solution.py:605
  179.7 15.7 %shard_map.153.refs_2_ = f32[896,1024]{1,0:T(8,128)} custom-call(s32[6]{0:T(128)} %stack.73.pos, bf16[12576,1024]{1,0:T(8,128)(2,1)} %emb_hbm.13, f32[3144,1]{1,0:T(8,128)} %broadcast_in_dim.79.bias_ref, f32[2,2,1280]{2,1,0:T(2,128)} %pad_maximum_fusion.3.info_ref, bf16[8,1280,1024]{2,1,0:T(8,128)(2,1)} %get-tuple-element.89.refs_0_.refs_8_), custom_call_target="tpu_custom_call" | custom-call | flops 93952408 | bytes 10747904 | tf_op jit(solution)/shard_map/pallas_call | solution.py:427
  196.1 1.5 copy-done.6
  197.6 41.4 %shard_map.154 = (f32[1536,1024]{1,0:T(8,128)}, bf16[8,1280,1024]{2,1,0:T(8,128)(2,1)}) custom-call(s32[6]{0:T(128)} %stack.73.pos, bf16[12576,1024]{1,0:T(8,128)(2,1)} %emb_hbm.13, f32[3144,1]{1,0:T(8,128)} %broadcast_in_dim.79.bias_ref, f32[8,2,1280]{2,1,0:T(2,128)} %pad_maximum_fusion.info_ref, ...), custom_call_target="tpu_custom_call", output_to_operand_aliasing={{1}: (12, {})} | custom-call | flops 322122560 | bytes 19922944 | tf_op jit(solution)/shard_map/pallas_call | solution.py:427
  239.6 8.1 %collective-permute-done.20.refs_2_ = f32[608,1024]{1,0:T(8,128)S(1)} collective-permute-done((f32[608,1024]{1,0:T(8,128)}, f32[608,1024]{1,0:T(8,128)S(1)}, u32[]{:S(2)}, u32[]{:S(2)}) %collective-permute-start.20) | collective-permute-done | bytes 2490400 | tf_op jit(solution)/shard_map/ppermute | solution.py:605
  247.7 1.6 copy-done.8
  249.3 1.4 copy-done.7
  250.8 15.3 %shard_map.155 = (f32[640,1024]{1,0:T(8,128)}, bf16[8,1280,1024]{2,1,0:T(8,128)(2,1)}, f32[12576,1024]{1,0:T(8,128)}) custom-call(s32[6]{0:T(128)} %stack.73.pos, bf16[12576,1024]{1,0:T(8,128)(2,1)} %emb_hbm.13, f32[3144,1]{1,0:T(8,128)} %broadcast_in_dim.79.bias_ref, f32[8,2,1280]{2,1,0:T(2,128)} %pad_maximum_fusion.info_ref, ...), custom_call_target="tpu_custom_call", output_to_operand_aliasing={{1}: (8, {})} | custom-call | flops 67108864 | bytes 9175040 | tf_op jit(solution)/shard_map/pallas_call | solution.py:427
  266.5 1.9 collective-permute-start.23
  273.2 17.4 %shard_map.156 = (f32[896,1024]{1,0:T(8,128)}, f32[12576,1024]{1,0:T(8,128)}) custom-call(s32[6]{0:T(128)} %stack.73.pos, bf16[12576,1024]{1,0:T(8,128)(2,1)} %emb_hbm.13, f32[3144,1]{1,0:T(8,128)} %broadcast_in_dim.79.bias_ref, f32[8,2,1280]{2,1,0:T(2,128)} %pad_maximum_fusion.info_ref, ...), custom_call_target="tpu_custom_call", output_to_operand_aliasing={{1}: (5, {})} | custom-call | flops 93952408 | bytes 10747904 | tf_op jit(solution)/shard_map/pallas_call | solution.py:427
  292.8 6.2 back.1
  299.1 1.5 copy-done.4
  300.6 51.0 %shard_map.157 = (f32[960,1024]{1,0:T(8,128)}, f32[12576,1024]{1,0:T(8,128)}) custom-call(s32[6]{0:T(128)} %stack.73.pos, bf16[12576,1024]{1,0:T(8,128)(2,1)} %emb_hbm.13, f32[3144,1]{1,0:T(8,128)} %broadcast_in_dim.79.bias_ref, f32[8,2,1280]{2,1,0:T(2,128)} %pad_maximum_fusion.info_ref, ...), custom_call_target="tpu_custom_call", output_to_operand_aliasing={{1}: (5, {})} | custom-call | flops 402653184 | bytes 26869760 | tf_op jit(solution)/shard_map/pallas_call | solution.py:427
  353.0 2.8 collective-permute-start.33
  356.5 57.8 %all-reduce.7.cloned.1.call-done.refs_0_ = f32[1096,256]{1,0:T(8,128)} async-done(((f32[1096,256]{1,0:T(8,128)}), f32[1096,256]{1,0:T(8,128)}) %all-reduce.7.cloned.1.call-update) | async-done | bytes 1122320 | tf_op jit(solution)/shard_map/psum | solution.py:708
  414.3 1.9 constant_dynamic-slice_fusion
  416.1 32.4 %collective-permute-done.34.refs_4_ = f32[896,1024]{1,0:T(8,128)} collective-permute-done((f32[896,1024]{1,0:T(8,128)}, f32[896,1024]{1,0:T(8,128)}, u32[]{:S(2)}, u32[]{:S(2)}) %collective-permute-start.34) | collective-permute-done | bytes 3670048 | tf_op jit(solution)/shard_map/ppermute | solution.py:611
  448.5 37.7 %shard_map.158 = (f32[648,1024]{1,0:T(8,128)}, f32[12576,1024]{1,0:T(8,128)}) custom-call(s32[6]{0:T(128)} %stack.73.pos, bf16[12576,1024]{1,0:T(8,128)(2,1)} %emb_hbm.13, f32[3144,1]{1,0:T(8,128)} %broadcast_in_dim.79.bias_ref, f32[8,2,1280]{2,1,0:T(2,128)} %pad_maximum_fusion.info_ref, ...), custom_call_target="tpu_custom_call", output_to_operand_aliasing={{1}: (5, {})} | custom-call | flops 271790912 | bytes 24952832 | tf_op jit(solution)/shard_map/pallas_call | solution.py:427
  486.3 3.2 collective-permute-start.42
  490.2 14.9 %collective-permute-done.43.refs_6_ = f32[648,1024]{1,0:T(8,128)S(1)} collective-permute-done((f32[648,1024]{1,0:T(8,128)}, f32[648,1024]{1,0:T(8,128)S(1)}, u32[]{:S(2)}, u32[]{:S(2)}) %collective-permute-start.43) | collective-permute-done | bytes 2654240 | tf_op jit(solution)/shard_map/ppermute | solution.py:605
  505.1 2.0 collective-permute-start.29
  507.8 1.8 copy-done.1
  509.6 1.9 copy-done
  511.5 14.9 %put_rows.3.refs_0_ = f32[12576,1024]{1,0:T(8,128)} custom-call(s32[6]{0:T(128)} %stack.73.pos, f32[12576,1024]{1,0:T(8,128)} %get-tuple-element.122.refs_0_, f32[640,1024]{1,0:T(8,128)} %collective-permute-done.38.refs_1_, f32[896,1024]{1,0:T(8,128)} %copy-done.1, f32[960,1024]{1,0:T(8,128)} %collective-permute-done.40.refs_3_, ...), custom_call_target="tpu_custom_call", output_to_operand_aliasing={{}: (1, {})} | custom-call | flops 51855 | bytes 41484288 | tf_op jit(solution)/shard_map/put_rows/pallas_call | solution.py:460
  527.7 2.6 collective-permute-start.26
  530.3 30.2 %collective-permute-done.29.refs_1_ = f32[1232,256]{1,0:T(8,128)} collective-permute-done((f32[1232,256]{1,0:T(8,128)}, f32[1232,256]{1,0:T(8,128)}, u32[]{:S(2)}, u32[]{:S(2)}) %collective-permute-start.29) | collective-permute-done | bytes 1261600 | tf_op jit(solution)/shard_map/ppermute | solution.py:608
  560.4 2.4 collective-permute-start.27
  563.8 76.1 %collective-permute-done.31.refs_3_ = f32[1232,256]{1,0:T(8,128)S(1)} collective-permute-done((f32[1232,256]{1,0:T(8,128)}, f32[1232,256]{1,0:T(8,128)S(1)}, u32[]{:S(2)}, u32[]{:S(2)}) %collective-permute-start.31) | collective-permute-done | bytes 1261600 | tf_op jit(solution)/shard_map/ppermute | solution.py:608
  641.0 14.7 %spread.1 = bf16[16,512,1024]{2,1,0:T(8,128)(2,1)} custom-call(s32[1]{0:T(128)} %bitcast.vp, s32[16,1,80]{2,1,0:T(1,128)} %bitcast.34, bf16[1024,1024]{1,0:T(8,128)(2,1)} %w_ref.3, f32[1232,256]{1,0:T(8,128)} %get-tuple-element.115.refs_0_, f32[1232,256]{1,0:T(8,128)} %collective-permute-done.29.refs_1_, f32[1232,256]{1,0:T(8,128)} %collective-permute-done.30.refs_2_, ...), custom_call_target="tpu_custom_call" | custom-call | flops 21474836 | bytes 16777216 | tf_op jit(solution)/shard_map/spread/pallas_call | solution.py:581
  655.7 7.2 %collective-permute-done.28.refs_3_ = f32[520,256]{1,0:T(8,128)} collective-permute-done((f32[520,256]{1,0:T(8,128)}, f32[520,256]{1,0:T(8,128)}, u32[]{:S(2)}, u32[]{:S(2)}) %collective-permute-start.28) | collective-permute-done | bytes 532512 | tf_op jit(solution)/shard_map/ppermute | solution.py:608
  664.6 1.2 collective-permute-done.35.refs_4_
  668.1 3.9 put_rows.4.refs_0_
  672.1 4.9 join.1
  680.3 1.5 fusion.3
  681.8 1.5 copy-done.2
  683.3 3.9 put_rows.5
  (141 shorter events, 40.5 us)
Async XLA Ops:
  7.2 283.5 %reduce-scatter.2.cloned.1.call-start = ((), (), s32[]{:S(2)}) async-start(), calls=%async_computation.1 | async-start | bytes 6307840 | tf_op jit(solution)/shard_map/reduce_scatter | solution.py:656
  24.7 71.2 %collective-permute-start.12 = (f32[608,1024]{1,0:T(8,128)}, f32[608,1024]{1,0:T(8,128)}, u32[]{:S(2)}, u32[]{:S(2)}) collective-permute-start(f32[608,1024]{1,0:T(8,128)} %get-tuple-element.80.refs_0_), channel_id=1, source_target_pairs={{0,2},{1,3},{2,0},{3,1},{4,6},{5,7},{6,4},{7,5},{8,10},{9,11},{10,... | collective-permute-start | bytes 7471112 | tf_op jit(solution)/shard_map/ppermute | solution.py:605
  26.0 70.2 %collective-permute-start.13 = (f32[624,1024]{1,0:T(8,128)}, f32[624,1024]{1,0:T(8,128)}, u32[]{:S(2)}, u32[]{:S(2)}) collective-permute-start(f32[624,1024]{1,0:T(8,128)} %get-tuple-element.79.refs_1_), channel_id=1, source_target_pairs={{0,4},{1,5},{2,6},{3,7},{4,0},{5,1},{6,2},{7,3},{8,12},{9,13},{10,... | collective-permute-start | bytes 7667720 | tf_op jit(solution)/shard_map/ppermute | solution.py:605
  83.2 3.6 collective-permute-start.2
  84.5 4.2 collective-permute-start.1
  85.6 5.8 collective-permute-start
  86.8 64.0 %collective-permute-start.9 = (f32[608,1024]{1,0:T(8,128)}, f32[608,1024]{1,0:T(8,128)}, u32[]{:S(2)}, u32[]{:S(2)}) collective-permute-start(f32[608,1024]{1,0:T(8,128)} %get-tuple-element.80.refs_0_), channel_id=1, source_target_pairs={{0,1},{1,0},{2,3},{3,2},{4,5},{5,4},{6,7},{7,6},{8,9},{9,8},{10,11... | collective-permute-start | bytes 7471112 | tf_op jit(solution)/shard_map/ppermute | solution.py:605
  88.7 63.3 %collective-permute-start.10 = (f32[624,1024]{1,0:T(8,128)S(1)}, f32[624,1024]{1,0:T(8,128)}, u32[]{:S(2)}, u32[]{:S(2)}) collective-permute-start(f32[624,1024]{1,0:T(8,128)S(1)} %copy-done.5), channel_id=1, source_target_pairs={{0,1},{1,0},{2,3},{3,2},{4,5},{5,4},{6,7},{7,6},{8,9},{9,8},{10,11... | collective-permute-start | bytes 7667720 | tf_op jit(solution)/shard_map/ppermute | solution.py:605
  93.1 2.6 collective-permute-start.6
  95.7 74.0 %collective-permute-start.4 = (f32[624,1024]{1,0:T(8,128)S(1)}, f32[624,1024]{1,0:T(8,128)}, u32[]{:S(2)}, u32[]{:S(2)}) collective-permute-start(f32[624,1024]{1,0:T(8,128)S(1)} %copy-done.5), channel_id=1, source_target_pairs={{0,2},{1,3},{2,0},{3,1},{4,6},{5,7},{6,4},{7,5},{8,10},{9,11},{10,... | collective-permute-start | bytes 7667720 | tf_op jit(solution)/shard_map/ppermute | solution.py:605
  95.9 73.8 %collective-permute-start.5 = (f32[608,1024]{1,0:T(8,128)}, f32[608,1024]{1,0:T(8,128)}, u32[]{:S(2)}, u32[]{:S(2)}) collective-permute-start(f32[608,1024]{1,0:T(8,128)} %get-tuple-element.80.refs_0_), channel_id=1, source_target_pairs={{0,4},{1,5},{2,6},{3,7},{4,0},{5,1},{6,2},{7,3},{8,12},{9,13},{10,... | collective-permute-start | bytes 7471112 | tf_op jit(solution)/shard_map/ppermute | solution.py:605
  96.2 2.7 collective-permute-start.3
  98.9 79.5 %collective-permute-start.16 = (f32[608,1024]{1,0:T(8,128)}, f32[608,1024]{1,0:T(8,128)}, u32[]{:S(2)}, u32[]{:S(2)}) collective-permute-start(f32[608,1024]{1,0:T(8,128)} %collective-permute-done.12.refs_0_), channel_id=1, source_target_pairs={{0,1},{1,0},{2,3},{3,2},{4,5},{5,4},{6,7},{7,6},{8,9},{9,8},{10,11... | collective-permute-start | bytes 7471112 | tf_op jit(solution)/shard_map/ppermute | solution.py:605
  148.3 265.9 %all-reduce.7.cloned.1.call-start = ((), (), s32[]{:S(2)}) async-start(), calls=%async_computation.2 | async-start | bytes 2244608 | tf_op jit(solution)/shard_map/psum | solution.py:708
  150.8 17.3 %collective-permute-start.7 = (f32[2,1280]{1,0:T(2,128)S(1)}, f32[2,1280]{1,0:T(2,128)S(1)}, u32[]{:S(2)}, u32[]{:S(2)}) collective-permute-start(f32[2,1280]{1,0:T(2,128)S(1)} %get-tuple-element.151), channel_id=1, source_target_pairs={{0,4},{1,5},{2,6},{3,7},{4,0},{5,1},{6,2},{7,3},{8,12},{9,13},{10,... | collective-permute-start | bytes 30728 | tf_op jit(solution)/shard_map/ppermute | solution.py:605
  152.1 16.6 %collective-permute-start.8 = (f32[2,1280]{1,0:T(2,128)S(1)}, f32[2,1280]{1,0:T(2,128)S(1)}, u32[]{:S(2)}, u32[]{:S(2)}) collective-permute-start(f32[2,1280]{1,0:T(2,128)S(1)} %get-tuple-element.151), channel_id=1, source_target_pairs={{0,6},{1,7},{2,4},{3,5},{4,2},{5,3},{6,0},{7,1},{8,14},{9,15},{10,... | collective-permute-start | bytes 30728 | tf_op jit(solution)/shard_map/ppermute | solution.py:605
  168.1 70.9 %collective-permute-start.15 = (f32[624,1024]{1,0:T(8,128)}, f32[624,1024]{1,0:T(8,128)}, u32[]{:S(2)}, u32[]{:S(2)}) collective-permute-start(f32[624,1024]{1,0:T(8,128)} %collective-permute-done.13.refs_5_), channel_id=1, source_target_pairs={{0,2},{1,3},{2,0},{3,1},{4,6},{5,7},{6,4},{7,5},{8,10},{9,11},{10,... | collective-permute-start | bytes 7667720 | tf_op jit(solution)/shard_map/ppermute | solution.py:605
  168.7 27.4 %collective-permute-start.19 = (f32[624,1024]{1,0:T(8,128)}, f32[624,1024]{1,0:T(8,128)}, u32[]{:S(2)}, u32[]{:S(2)}) collective-permute-start(f32[624,1024]{1,0:T(8,128)} %collective-permute-done.13.refs_5_), channel_id=1, source_target_pairs={{0,1},{1,0},{2,3},{3,2},{4,5},{5,4},{6,7},{7,6},{8,9},{9,8},{10,11... | collective-permute-start | bytes 7667720 | tf_op jit(solution)/shard_map/ppermute | solution.py:605
  169.7 26.4 %collective-permute-start.17 = (f32[624,1024]{1,0:T(8,128)}, f32[624,1024]{1,0:T(8,128)S(1)}, u32[]{:S(2)}, u32[]{:S(2)}) collective-permute-start(f32[624,1024]{1,0:T(8,128)} %collective-permute-done.4.refs_1_), channel_id=1, source_target_pairs={{0,1},{1,0},{2,3},{3,2},{4,5},{5,4},{6,7},{7,6},{8,9},{9,8},{10,11... | collective-permute-start | bytes 7667720 | tf_op jit(solution)/shard_map/ppermute | solution.py:605
  169.8 8.2 %collective-permute-start.11 = (f32[3,2,1280]{2,1,0:T(2,128)S(1)}, f32[3,2,1280]{2,1,0:T(2,128)S(1)}, u32[]{:S(2)}, u32[]{:S(2)}) collective-permute-start(f32[3,2,1280]{2,1,0:T(2,128)S(1)} %pad_maximum_fusion.2), channel_id=1, source_target_pairs={{0,1},{1,0},{2,3},{3,2},{4,5},{5,4},{6,7},{7,6},{8,9},{9,8},{10,11... | collective-permute-start | bytes 92168 | tf_op jit(solution)/shard_map/ppermute | solution.py:605
  178.1 18.0 %collective-permute-start.18 = (f32[608,1024]{1,0:T(8,128)}, f32[608,1024]{1,0:T(8,128)}, u32[]{:S(2)}, u32[]{:S(2)}) collective-permute-start(f32[608,1024]{1,0:T(8,128)} %collective-permute-done.5.refs_4_), channel_id=1, source_target_pairs={{0,1},{1,0},{2,3},{3,2},{4,5},{5,4},{6,7},{7,6},{8,9},{9,8},{10,11... | collective-permute-start | bytes 7471112 | tf_op jit(solution)/shard_map/ppermute | solution.py:605
  178.4 60.6 %collective-permute-start.14 = (f32[608,1024]{1,0:T(8,128)}, f32[608,1024]{1,0:T(8,128)}, u32[]{:S(2)}, u32[]{:S(2)}) collective-permute-start(f32[608,1024]{1,0:T(8,128)} %collective-permute-done.12.refs_0_), channel_id=1, source_target_pairs={{0,4},{1,5},{2,6},{3,7},{4,0},{5,1},{6,2},{7,3},{8,12},{9,13},{10,... | collective-permute-start | bytes 7471112 | tf_op jit(solution)/shard_map/ppermute | solution.py:605
  239.0 8.7 %collective-permute-start.21 = (f32[624,1024]{1,0:T(8,128)}, f32[624,1024]{1,0:T(8,128)S(1)}, u32[]{:S(2)}, u32[]{:S(2)}) collective-permute-start(f32[624,1024]{1,0:T(8,128)} %collective-permute-done.15.refs_1_), channel_id=1, source_target_pairs={{0,1},{1,0},{2,3},{3,2},{4,5},{5,4},{6,7},{7,6},{8,9},{9,8},{10,11... | collective-permute-start | bytes 7667720 | tf_op jit(solution)/shard_map/ppermute | solution.py:605
  239.5 8.2 %collective-permute-start.20 = (f32[608,1024]{1,0:T(8,128)}, f32[608,1024]{1,0:T(8,128)S(1)}, u32[]{:S(2)}, u32[]{:S(2)}) collective-permute-start(f32[608,1024]{1,0:T(8,128)} %collective-permute-done.14.refs_0_), channel_id=1, source_target_pairs={{0,1},{1,0},{2,3},{3,2},{4,5},{5,4},{6,7},{7,6},{8,9},{9,8},{10,11... | collective-permute-start | bytes 7471112 | tf_op jit(solution)/shard_map/ppermute | solution.py:605
  266.1 33.0 %collective-permute-start.25 = (f32[640,1024]{1,0:T(8,128)}, f32[640,1024]{1,0:T(8,128)S(1)}, u32[]{:S(2)}, u32[]{:S(2)}) collective-permute-start(f32[640,1024]{1,0:T(8,128)} %get-tuple-element.107), channel_id=1, source_target_pairs={{0,1},{1,0},{2,3},{3,2},{4,5},{5,4},{6,7},{7,6},{8,9},{9,8},{10,11... | collective-permute-start | bytes 7864328 | tf_op jit(solution)/shard_map/ppermute | solution.py:605
  266.5 5.5 collective-permute-start.23
  268.4 4.2 collective-permute-start.24
  269.0 3.7 collective-permute-start.22
  272.8 83.0 %collective-permute-start.32 = (f32[640,1024]{1,0:T(8,128)}, f32[640,1024]{1,0:T(8,128)}, u32[]{:S(2)}, u32[]{:S(2)}) collective-permute-start(f32[640,1024]{1,0:T(8,128)} %get-tuple-element.107), channel_id=1, source_target_pairs={{0,2},{1,5},{2,0},{3,7},{4,6},{5,1},{6,4},{7,3},{8,10},{9,13},{10,... | collective-permute-start | bytes 7864328 | tf_op jit(solution)/shard_map/ppermute | solution.py:611
  351.5 134.7 %collective-permute-start.41 = (f32[960,1024]{1,0:T(8,128)}, f32[960,1024]{1,0:T(8,128)}, u32[]{:S(2)}, u32[]{:S(2)}) collective-permute-start(f32[960,1024]{1,0:T(8,128)} %get-tuple-element.108), channel_id=1, source_target_pairs={{0,2},{1,5},{2,0},{3,7},{4,6},{5,1},{6,4},{7,3},{8,10},{9,13},{10,... | collective-permute-start | bytes 11796488 | tf_op jit(solution)/shard_map/ppermute | solution.py:611
  352.7 95.9 %collective-permute-start.34 = (f32[896,1024]{1,0:T(8,128)}, f32[896,1024]{1,0:T(8,128)}, u32[]{:S(2)}, u32[]{:S(2)}) collective-permute-start(f32[896,1024]{1,0:T(8,128)} %get-tuple-element.99), channel_id=1, source_target_pairs={{0,2},{1,5},{2,0},{3,7},{4,6},{5,1},{6,4},{7,3},{8,10},{9,13},{10,... | collective-permute-start | bytes 11010056 | tf_op jit(solution)/shard_map/ppermute | solution.py:611
  353.0 95.5 %collective-permute-start.33 = (f32[896,1024]{1,0:T(8,128)}, f32[896,1024]{1,0:T(8,128)}, u32[]{:S(2)}, u32[]{:S(2)}) collective-permute-start(f32[896,1024]{1,0:T(8,128)} %get-tuple-element.99), channel_id=1, source_target_pairs={{0,1},{1,0},{2,3},{3,2},{4,5},{5,4},{6,7},{7,6},{8,9},{9,8},{10,11... | collective-permute-start | bytes 11010056 | tf_op jit(solution)/shard_map/ppermute | solution.py:605
  355.9 134.1 %collective-permute-start.38 = (f32[640,1024]{1,0:T(8,128)}, f32[640,1024]{1,0:T(8,128)}, u32[]{:S(2)}, u32[]{:S(2)}) collective-permute-start(f32[640,1024]{1,0:T(8,128)} %collective-permute-done.32.refs_2_), channel_id=1, source_target_pairs={{0,1},{1,0},{2,3},{3,2},{4,5},{5,4},{6,7},{7,6},{8,9},{9,8},{10,11... | collective-permute-start | bytes 7864328 | tf_op jit(solution)/shard_map/ppermute | solution.py:605
  355.9 151.2 %collective-permute-start.40 = (f32[960,1024]{1,0:T(8,128)}, f32[960,1024]{1,0:T(8,128)}, u32[]{:S(2)}, u32[]{:S(2)}) collective-permute-start(f32[960,1024]{1,0:T(8,128)} %get-tuple-element.108), channel_id=1, source_target_pairs={{0,1},{1,0},{2,3},{3,2},{4,5},{5,4},{6,7},{7,6},{8,9},{9,8},{10,11... | collective-permute-start | bytes 11796488 | tf_op jit(solution)/shard_map/ppermute | solution.py:605
  486.3 21.5 %collective-permute-start.42 = (f32[960,1024]{1,0:T(8,128)}, f32[960,1024]{1,0:T(8,128)S(1)}, u32[]{:S(2)}, u32[]{:S(2)}) collective-permute-start(f32[960,1024]{1,0:T(8,128)} %collective-permute-done.41.refs_4_), channel_id=1, source_target_pairs={{0,1},{1,0},{2,3},{3,2},{4,5},{5,4},{6,7},{7,6},{8,9},{9,8},{10,11... | collective-permute-start | bytes 11796488 | tf_op jit(solution)/shard_map/ppermute | solution.py:605
  489.4 18.3 %collective-permute-start.39 = (f32[896,1024]{1,0:T(8,128)}, f32[896,1024]{1,0:T(8,128)S(1)}, u32[]{:S(2)}, u32[]{:S(2)}) collective-permute-start(f32[896,1024]{1,0:T(8,128)} %collective-permute-done.34.refs_4_), channel_id=1, source_target_pairs={{0,1},{1,0},{2,3},{3,2},{4,5},{5,4},{6,7},{7,6},{8,9},{9,8},{10,11... | collective-permute-start | bytes 11010056 | tf_op jit(solution)/shard_map/ppermute | solution.py:605
  489.5 15.6 %collective-permute-start.43 = (f32[648,1024]{1,0:T(8,128)}, f32[648,1024]{1,0:T(8,128)S(1)}, u32[]{:S(2)}, u32[]{:S(2)}) collective-permute-start(f32[648,1024]{1,0:T(8,128)} %get-tuple-element.114), channel_id=1, source_target_pairs={{0,1},{1,0},{2,3},{3,2},{4,5},{5,4},{6,7},{7,6},{8,9},{9,8},{10,11... | collective-permute-start | bytes 7962632 | tf_op jit(solution)/shard_map/ppermute | solution.py:605
  489.9 36.4 %collective-permute-start.44 = (f32[648,1024]{1,0:T(8,128)}, f32[648,1024]{1,0:T(8,128)}, u32[]{:S(2)}, u32[]{:S(2)}) collective-permute-start(f32[648,1024]{1,0:T(8,128)} %get-tuple-element.114), channel_id=1, source_target_pairs={{0,2},{1,5},{2,0},{3,7},{4,6},{5,1},{6,4},{7,3},{8,10},{9,13},{10,... | collective-permute-start | bytes 7962632 | tf_op jit(solution)/shard_map/ppermute | solution.py:611
  505.1 55.3 %collective-permute-start.29 = (f32[1232,256]{1,0:T(8,128)}, f32[1232,256]{1,0:T(8,128)}, u32[]{:S(2)}, u32[]{:S(2)}) collective-permute-start(f32[1232,256]{1,0:T(8,128)} %get-tuple-element.115.refs_0_), channel_id=1, source_target_pairs={{0,8},{8,0},{16,24},{24,16},{1,9},{9,1},{17,25},{25,17},{2,10},{10... | collective-permute-start | bytes 3784712 | tf_op jit(solution)/shard_map/ppermute | solution.py:608
  507.1 55.8 %collective-permute-start.30 = (f32[1232,256]{1,0:T(8,128)}, f32[1232,256]{1,0:T(8,128)}, u32[]{:S(2)}, u32[]{:S(2)}) collective-permute-start(f32[1232,256]{1,0:T(8,128)} %get-tuple-element.115.refs_0_), channel_id=1, source_target_pairs={{0,16},{8,24},{16,0},{24,8},{1,17},{9,25},{17,1},{25,9},{2,18},{10... | collective-permute-start | bytes 3784712 | tf_op jit(solution)/shard_map/ppermute | solution.py:608
  526.4 155.4 %collective-permute-start.45 = (f32[648,1024]{1,0:T(8,128)}, f32[648,1024]{1,0:T(8,128)S(1)}, u32[]{:S(2)}, u32[]{:S(2)}) collective-permute-start(f32[648,1024]{1,0:T(8,128)} %collective-permute-done.44.refs_1_), channel_id=1, source_target_pairs={{0,1},{1,0},{2,3},{3,2},{4,5},{5,4},{6,7},{7,6},{8,9},{9,8},{10,11... | collective-permute-start | bytes 7962632 | tf_op jit(solution)/shard_map/ppermute | solution.py:605
  527.4 112.6 %collective-permute-start.31 = (f32[1232,256]{1,0:T(8,128)}, f32[1232,256]{1,0:T(8,128)S(1)}, u32[]{:S(2)}, u32[]{:S(2)}) collective-permute-start(f32[1232,256]{1,0:T(8,128)} %get-tuple-element.115.refs_0_), channel_id=1, source_target_pairs={{0,24},{8,16},{16,8},{24,0},{1,25},{9,17},{17,9},{25,1},{2,26},{10... | collective-permute-start | bytes 3784712 | tf_op jit(solution)/shard_map/ppermute | solution.py:608
  527.7 128.0 %collective-permute-start.26 = (f32[520,256]{1,0:T(8,128)}, f32[520,256]{1,0:T(8,128)}, u32[]{:S(2)}, u32[]{:S(2)}) collective-permute-start(f32[520,256]{1,0:T(8,128)} %constant_dynamic-slice_fusion), channel_id=1, source_target_pairs={{0,8},{8,0},{16,24},{24,16},{1,9},{9,1},{17,25},{25,17},{2,10},{10... | collective-permute-start | bytes 1597448 | tf_op jit(solution)/shard_map/ppermute | solution.py:608
  560.4 95.3 %collective-permute-start.27 = (f32[520,256]{1,0:T(8,128)}, f32[520,256]{1,0:T(8,128)}, u32[]{:S(2)}, u32[]{:S(2)}) collective-permute-start(f32[520,256]{1,0:T(8,128)} %constant_dynamic-slice_fusion), channel_id=1, source_target_pairs={{0,16},{8,24},{16,0},{24,8},{1,17},{9,25},{17,1},{25,9},{2,18},{10... | collective-permute-start | bytes 1597448 | tf_op jit(solution)/shard_map/ppermute | solution.py:608
  562.9 100.0 %collective-permute-start.28 = (f32[520,256]{1,0:T(8,128)}, f32[520,256]{1,0:T(8,128)}, u32[]{:S(2)}, u32[]{:S(2)}) collective-permute-start(f32[520,256]{1,0:T(8,128)} %constant_dynamic-slice_fusion), channel_id=1, source_target_pairs={{0,24},{8,16},{16,8},{24,0},{1,25},{9,17},{17,9},{25,1},{2,26},{10... | collective-permute-start | bytes 1597448 | tf_op jit(solution)/shard_map/ppermute | solution.py:608
  662.9 3.0 collective-permute-start.35
  664.1 2.5 collective-permute-start.36
  664.1 3.4 collective-permute-start.37
  (17 other events, 160.7 us)
Sparse Core Ops, SparseCore 0:
  148.5 91.1 reduce-scatter.1
  356.0 58.2 all-reduce.6

commit v4 on v3

--- a/solution.py
+++ b/solution.py
@@ -26,7 +26,7 @@
     return lax.dot_general(a, b, dims, preferred_element_type=F32)
 
 
-def stats_kernel(n_vocab, u_ref, emb_ref, b_ref, lab_ref, logits_ref, stat_ref, m_sc, s_sc, l_sc):
+def stats_kernel(n_vocab, u_ref, emb_ref, b_ref, lab_ref, lo_ref, hi_ref, stat_ref, m_sc, s_sc, l_sc):
     i, n_blocks = pl.program_id(0), pl.num_programs(0)
     lane = lax.broadcasted_iota(I32, (1, 128), 1)
 
@@ -42,10 +42,12 @@
             tile = dot(u_ref[r0:r1, :], emb_ref[:wide, :], NT) + b_ref[:, :wide]
             if wide > width:
                 tile = jnp.where(lax.broadcasted_iota(I32, (1, wide), 1) < width, tile, -jnp.inf)
-            logits_ref[r0:r1, :wide] = tile
+            cut = lo_ref.shape[0]
+            out_ref, base = (lo_ref, 0) if r0 < cut else (hi_ref, cut)
+            out_ref[r0 - base:r1 - base, :wide] = tile
             for q in range(r0, r1, CH):
                 rs = slice(q, min(q + CH, r1))
-                parts = [logits_ref[rs, k:k + 128] for k in range(0, wide, 128)]
+                parts = [out_ref[rs.start - base:rs.stop - base, k:k + 128] for k in range(0, wide, 128)]
                 m_old = m_sc[rs, :]
                 m_new = functools.reduce(jnp.maximum, parts, m_old)
                 s_new = s_sc[rs, :] * jnp.exp(m_old - m_new)
@@ -73,7 +75,7 @@
         stat_ref[3:8, :] = jnp.zeros_like(stat_ref[3:8, :])
 
 
-def stats(u, emb, bias, lab):
+def stats(u, emb, bias, lab, cut):
     t, e = u.shape
     v = emb.shape[0]
     n = pl.cdiv(v, VB)
@@ -82,8 +84,8 @@
         functools.partial(stats_kernel, v),
         grid=(n,),
         in_specs=[whole(t, e), pl.BlockSpec((VB, e), lambda i: (i, 0)), pl.BlockSpec((1, VB), lambda i: (0, i)), whole(t, 128)],
-        out_specs=[pl.BlockSpec((t, VB), lambda i: (0, i)), whole(8, t)],
-        out_shape=[jax.ShapeDtypeStruct((t, v), F32), jax.ShapeDtypeStruct((8, t), F32)],
+        out_specs=[pl.BlockSpec((cut, VB), lambda i: (0, i)), pl.BlockSpec((t - cut, VB), lambda i: (0, i)), whole(8, t)],
+        out_shape=[jax.ShapeDtypeStruct((cut, v), F32), jax.ShapeDtypeStruct((t - cut, v), F32), jax.ShapeDtypeStruct((8, t), F32)],
         scratch_shapes=[pltpu.VMEM((t, 128), F32)] * 3,
         compiler_params=pltpu.CompilerParams(dimension_semantics=("arbitrary",), vmem_limit_bytes=VMEM_LIMIT),
         cost_estimate=pl.CostEstimate(flops=(2 * t * v * e) // COVER, bytes_accessed=t * v * 4 + v * e * 2, transcendentals=t * v),
@@ -91,12 +93,12 @@
     )(u, emb, bias, lab)
 
 
-def du_kernel(n_vocab, scale, logits_ref, emb_ref, lse_ref, lab_ref, norm_hbm, gain_ref, out_ref, db_ref, sum_ref, du_ref, g_sc, db_sc, norm_sc, db_sc2, sem):
+def du_kernel(n_vocab, scale, base, logits_ref, emb_ref, lse_ref, lab_ref, norm_hbm, gain_ref, out_ref, db_ref, sum_ref, du_ref, g_sc, db_sc, norm_sc, db_sc2, sem):
     i, n_blocks = pl.program_id(0), pl.num_programs(0)
     t = logits_ref.shape[0]
     lane = lax.broadcasted_iota(I32, (1, 128), 1)
 
-    norm_copy = pltpu.make_async_copy(norm_hbm, norm_sc, sem)
+    norm_copy = pltpu.make_async_copy(norm_hbm.at[base:base + t, :], norm_sc, sem)
 
     @pl.when(i == 0)
     def _():
@@ -111,7 +113,7 @@
         emb = emb_ref[:wide, :]
         if wide > width:
             emb = jnp.where(lax.broadcasted_iota(I32, (wide, 1), 0) < width, emb, jnp.zeros_like(emb))
-        for r0, r1 in row_cuts(t):
+        for r0, r1 in row_cuts(t, 2):
             sums = [None] * (wide // 128)
             for q in range(r0, r1, 16):
                 rs = slice(q, q + 16)
@@ -143,9 +145,10 @@
     def _():
         norm_copy.wait()
         parts, rows, cols = out_ref.shape
-        for r in range(0, rows, 112):
-            rs = slice(r, r + 112)
-            total = [jnp.zeros((112, 128), F32)] * 2
+        run = rows // 4 if rows % 32 == 0 else rows // 3
+        for r in range(0, rows, run):
+            rs = slice(r, r + run)
+            total = [jnp.zeros((run, 128), F32)] * 2
             for c in range(0, parts * cols, 128):
                 x = du_ref[rs, c:c + 128].astype(BF16).astype(F32)
                 out_ref[c // cols, rs, c % cols:c % cols + 128] = x
@@ -158,13 +161,13 @@
         sum_ref[2:, :] = jnp.zeros_like(sum_ref[2:, :])
 
 
-def du_pass(scale, parts, logits, emb, lse, lab, normed, gain):
+def du_pass(scale, parts, base, logits, emb, lse, lab, normed, gain):
     t, v = logits.shape
     e = emb.shape[1]
     n = pl.cdiv(v, VB)
     whole = lambda *s: pl.BlockSpec(s, lambda i: (0,) * len(s))
     return pl.pallas_call(
-        functools.partial(du_kernel, v, scale),
+        functools.partial(du_kernel, v, scale, base),
         grid=(n,),
         in_specs=[pl.BlockSpec((t, VB), lambda i: (0, i)), pl.BlockSpec((VB, e), lambda i: (i, 0)), whole(t, 128), whole(t, 128), pl.BlockSpec(memory_space=pl.ANY), whole(1, e)],
         out_specs=[whole(parts, t, e // parts), pl.BlockSpec((1, VB), lambda i: (0, i)), whole(8, t)],
@@ -507,49 +510,75 @@
     )(idx, own, *mine, *theirs)
 
 
-def back_kernel(vp, pre_ref, norm_ref, rstd_ref, z_ref, du_ref, m1_ref, m2_ref, gain_ref, loss_ref, db_ref, dab_ref, pack_ref):
-    e, cols = z_ref.shape[1], du_ref.shape[1]
-    for c in range(0, cols, 128):
+def back_kernel(base, vp, *refs):
+    refs = list(refs)
+    srcs = [refs.pop(0) for _ in range(7)]
+    gain_ref, = [refs.pop(0)]
+    extra = refs[:-10]
+    dab_ref, pack_ref, pre, norm, rstd, z, m1, m2, du, sem = refs[-10:]
+    n, cols = du.shape
+    e = z.shape[1]
+    col = pl.ds(pl.multiple_of(vp[0] * cols, cols), cols)
+    rows = slice(base, base + n)
+    pre_h, norm_h, rstd_h, z_h, m1_h, m2_h, du_h = srcs
+    loads = [pltpu.make_async_copy(a, b, sem.at[j]) for j, (a, b) in enumerate((
+        (pre_h.at[rows, col], pre), (norm_h.at[rows, col], norm), (rstd_h.at[rows, :], rstd), (m1_h.at[rows, :], m1), (m2_h.at[rows, :], m2),
+        (du_h, du), (z_h.at[rows, :], z)))]
+    for c in loads:
+        c.start()
+    for c in loads:
+        c.wait()
+    for j, c in enumerate(range(0, cols, 128)):
         cs = slice(c, c + 128)
-        a, du, normed = pre_ref[:, cs], du_ref[:, cs], norm_ref[:, cs]
+        a, d, normed = pre[:, cs], du[:, cs], norm[:, cs]
         cdf = 0.5 * (1.0 + lax.erf(a * (0.5 ** 0.5)))
-        dg = rstd_ref[...] * (du * gain_ref[:, cs] - m1_ref[...] - normed * m2_ref[...])
+        dg = rstd[...] * (d * gain_ref[:, cs] - m1[...] - normed * m2[...])
         da = dg * (cdf + a * (jnp.exp(-0.5 * a * a) * 0.3989422804014327))
         dab_ref[:, cs] = da.astype(BF16).astype(F32)
-        for j, x in enumerate((da, du * normed, du)):
+        for j, x in enumerate((da, d * normed, d)):
             pack_ref[e + j:e + j + 1, cs] = jnp.sum(x, axis=0, keepdims=True)
-    pack_ref[:e, :] = lax.dot_general(z_ref[...], dab_ref[...].astype(BF16), (((0,), (0,)), ((), ())), preferred_element_type=F32)
-    pack_ref[e + 3:e + 4, :] = loss_ref[...]
-    pack_ref[e + 4:e + 16, :] = jnp.zeros_like(pack_ref[e + 4:e + 16, :])
-    pack_ref[e + 16:, :] = db_ref[...]
-
-
-def back_pass(vp, pre, normed, rstd, z, du, m1, m2, gain, loss, db):
+    dw = lax.dot_general(z[...], dab_ref[...].astype(BF16), (((0,), (0,)), ((), ())), preferred_element_type=F32)
+    if not extra:
+        pack_ref[:e, :] = dw
+        pack_ref[e + 3:, :] = jnp.zeros_like(pack_ref[e + 3:, :])
+    else:
+        prev, loss_ref, db_ref = extra
+        pack_ref[:e, :] = prev[:e, :] + dw
+        pack_ref[e:e + 3, :] += prev[e:e + 3, :]
+        pack_ref[e + 3:e + 4, :] = loss_ref[...]
+        pack_ref[e + 4:e + 16, :] = jnp.zeros_like(pack_ref[e + 4:e + 16, :])
+        pack_ref[e + 16:, :] = db_ref[...]
+
+
+def back_pass(base, vp, pre, normed, rstd, z, m1, m2, du, gain, *extra):
     n, cols = du.shape
     e = z.shape[1]
-    n_pack = e + 16 + db.shape[0]
+    n_pack = e + 16 + (extra[2].shape[0] if extra else 0)
     block = lambda *s: pl.BlockSpec(s, lambda i, p: (0,) * len(s))
-    share = lambda r: pl.BlockSpec((r, cols), lambda i, p: (0, p[0]))
     gs = pltpu.PrefetchScalarGridSpec(
         num_scalar_prefetch=1,
         grid=(1,),
-        in_specs=[share(n), share(n), block(n, 128), block(n, e), block(n, cols), block(n, 128), block(n, 128), share(1), block(1, cols), block(*db.shape)],
+        in_specs=[ANY] * 7 + [pl.BlockSpec((1, cols), lambda i, p: (0, p[0]))] + [block(*x.shape) for x in extra],
         out_specs=[block(n, cols), block(n_pack, cols)],
+        scratch_shapes=[pltpu.VMEM((n, cols), F32)] * 2 + [pltpu.VMEM((n, 128), F32), pltpu.VMEM((n, e), BF16)] + [pltpu.VMEM((n, 128), F32)] * 2
+        + [pltpu.VMEM((n, cols), F32), DMA((7,))],
     )
     return pl.pallas_call(
-        back_kernel,
+        functools.partial(back_kernel, base),
         grid_spec=gs,
         out_shape=[jax.ShapeDtypeStruct((n, cols), F32), jax.ShapeDtypeStruct((n_pack, cols), F32)],
         compiler_params=pltpu.CompilerParams(dimension_semantics=("arbitrary",), vmem_limit_bytes=VMEM_LIMIT),
         cost_estimate=pl.CostEstimate(flops=(2 * n * e * cols) // COVER, bytes_accessed=n * (cols * 16 + e * 2 + 1536), transcendentals=n * cols * 2),
         name="back",
-    )(vp, pre, normed, rstd, z, du, m1, m2, gain, loss, db)
+    )(vp, pre, normed, rstd, z, m1, m2, du, gain, *extra)
 
 
 def spread_kernel(n_masks, vp, pos_ref, w_ref, *refs):
-    pieces, (out_ref, dab, dz, obuf, in_sem, out_sem) = refs[:4], refs[4:]
-    n, cols = pieces[0].shape
-    loads = [pltpu.make_async_copy(p, dab.at[:, pl.ds(pl.multiple_of((vp[0] ^ k) * cols, cols), cols)], in_sem.at[k]) for k, p in enumerate(pieces)]
+    pieces, (out_ref, dab, dz, obuf, in_sem, out_sem) = refs[:8], refs[8:]
+    cut, cols = pieces[0].shape
+    n = cut + pieces[4].shape[0]
+    col = lambda k: pl.ds(pl.multiple_of((vp[0] ^ k) * cols, cols), cols)
+    loads = [pltpu.make_async_copy(p, dab.at[slice(0, cut) if j < 4 else slice(cut, n), col(j % 4)], in_sem.at[j]) for j, p in enumerate(pieces)]
     for c in loads:
         c.start()
     dz[n:, :] = jnp.zeros((dz.shape[0] - n, dz.shape[1]), F32)
@@ -558,32 +587,41 @@
     slots = pos_ref.shape[2]
     for c in loads:
         c.wait()
-    stores, done = [], 0
-    for b in range(n_seq):
-        while done < min(n, b * n_masks + slots):
-            r1 = min(n, done + 304)
-            dz[done:r1, :] = dot(dab[done:r1, :].astype(BF16), w_ref[...], NT).astype(BF16).astype(F32)
-            done = r1
-        if b >= 4:
-            stores[b - 4].wait()
-        hot = jnp.where(place == pos_ref[b], 1.0, 0.0).astype(BF16)
-        obuf[b % 4] = dot(hot, dz[b * n_masks:b * n_masks + slots, :].astype(BF16), NN).astype(BF16)
-        c = pltpu.make_async_copy(obuf.at[b % 4], out_ref.at[b], out_sem.at[b])
-        c.start()
-        stores.append(c)
-    for c in stores[-4:]:
-        c.wait()
+    for r0, r1 in row_cuts(n):
+        dz[r0:r1, :] = dot(dab[r0:r1, :].astype(BF16), w_ref[...], NT).astype(BF16).astype(F32)
+    group = 8
+    store = lambda b, j: pltpu.make_async_copy(obuf.at[j % 4], out_ref.at[b], out_sem.at[j % 4])
+
+    @pl.loop(0, n_seq // group)
+    def _(g):
+        for j in range(group):
+            b = g * group + j
+
+            @pl.when(b >= 4)
+            def _():
+                store(b - 4, j).wait()
+
+            hot = jnp.where(place == pos_ref[b], 1.0, 0.0).astype(BF16)
+            base = pl.multiple_of(g * (group * n_masks), 8)
+            low = j * n_masks // 8 * 8
+            rows = dz[pl.ds(base + low, slots + 8), :][j * n_masks - low:j * n_masks - low + slots]
+            obuf[j % 4] = dot(hot, rows.astype(BF16), NN).astype(BF16)
+            store(b, j).start()
+
+    for j in range(group - 4, group):
+        store(n_seq - group + j, j).wait()
 
 
 def spread_pass(n_masks, shape, vp, pos, w, pieces):
-    n, cols = pieces[0].shape
+    cols = pieces[0].shape[1]
+    n = pieces[0].shape[0] + pieces[4].shape[0]
     e = w.shape[0]
     return pl.pallas_call(
         functools.partial(spread_kernel, n_masks),
-        in_specs=[SMEM, VMEM, VMEM] + [ANY] * 4,
+        in_specs=[SMEM, VMEM, VMEM] + [ANY] * 8,
         out_specs=ANY,
         out_shape=jax.ShapeDtypeStruct(shape, BF16),
-        scratch_shapes=[pltpu.VMEM((n, 4 * cols), F32), pltpu.VMEM((n + 16, e), F32), pltpu.VMEM((4,) + shape[1:], BF16), DMA((4,)), DMA((shape[0],))],
+        scratch_shapes=[pltpu.VMEM((n, 4 * cols), F32), pltpu.VMEM((n + 16, e), F32), pltpu.VMEM((4,) + shape[1:], BF16), DMA((8,)), DMA((4,))],
         compiler_params=pltpu.CompilerParams(vmem_limit_bytes=VMEM_LIMIT),
         cost_estimate=pl.CostEstimate(flops=(2 * shape[0] * shape[1] * 128 * e) // COVER, bytes_accessed=shape[0] * shape[1] * e * 2, transcendentals=0),
         name="spread",
@@ -636,8 +674,9 @@
         flat_labels = labels.reshape(n_loc)
         lab_local = flat_labels - row_start
         lab_local = jnp.where((lab_local >= 0) & (lab_local < shard_rows), lab_local, -1)
-        lab_local = jnp.broadcast_to(lab_local[:, None], (n_loc, 128))
-        logits, stat = stats(u, emb_table, b_vocab[None], lab_local)
+        column = lambda x: jnp.broadcast_to(x[:, None], (x.shape[0], 128))
+        lab_cols = column(lab_local[:cut]), column(lab_local[cut:])
+        *logits, stat = stats(u, emb_table, b_vocab[None], column(lab_local), cut)
         all_stats = [stat] + [swap_vp(stat, b) for b in range(1, n_shards)]
         global_max = functools.reduce(jnp.maximum, [s[0] for s in all_stats])
         log_norm = global_max + jnp.log(order_sum([s[1] * jnp.exp(s[0] - global_max) for s in all_stats]))
@@ -651,15 +690,23 @@
         d_lo, d_hi = swap(x_lo, Y), swap(y_hi, X)
         cx_lo, cy_hi = swap(x_lo, CORE), swap(y_hi, CORE)
 
-        du_part, db_part, sums = du_pass(
-            scale, n_shards, logits, emb_table, jnp.broadcast_to(lse[:, None], (n_loc, 128)), lab_local, normed, ln_gain[None])
-        du_share = lax.psum_scatter(du_part.reshape(n_shards * n_loc, cols), "vp", scatter_dimension=0, tiled=True)
+        du_shares, db_parts, sums, before = [], [], [], ()
+        for j, (r0, r1) in enumerate(((0, cut), (cut, n_loc))):
+            lse_col = after(column(lse[r0:r1]), *before)
+            part, db, row_sums = du_pass(scale, n_shards, r0, logits[j], emb_table, lse_col, lab_cols[j], normed, ln_gain[None])
+            du_shares.append(lax.psum_scatter(part.reshape(n_shards * (r1 - r0), cols), "vp", scatter_dimension=0, tiled=True))
+            db_parts.append(db)
+            sums.append(row_sums)
+            before = (part,)
+        du_part = before[0]
+        sums = jnp.concatenate(sums, axis=1)
+        sums = [sums] + [swap_vp(sums, b) for b in range(1, n_shards)]
 
         half, quarter = shard_rows // 2, shard_rows // 4
         start = lambda h, c: h * half + c * quarter
         pos = jnp.stack([dp, start(mine, core), row_start + start(mine, core), start(mine, 1 - core), start(1 - mine, core), start(1 - mine, 1 - core)])
         bias_col = lax.dynamic_slice(b_vocab, (start(mine, core),), (quarter,))[:, None]
-        shares = (640, 896, 960, 648)
+        shares = (1280, 1088, 776)
         ends = [0]
         for w in shares[:-1]:
             ends.append(ends[-1] + max(16, quarter * w // sum(shares) // 16 * 16))
@@ -677,59 +724,57 @@
 
         tokens = {0: (u_lo, u_hi), CORE: (c_lo, c_hi), X: (x_lo, x_hi), Y: (y_lo, y_hi)}
         pair = jnp.stack([info, near])
-        own0, u_all = rows("own", 0, du_part, info=pair, tokens=tokens)
-        x_hi, y_lo, away = after((x_hi, y_lo, away), own0)
+        own, u_all = rows("own", 0, du_part, info=pair, tokens=tokens)
+        x_hi, y_lo, away = after((x_hi, y_lo, away), own)
         away = jnp.stack(away)
         tokens[X | CORE] = cx_lo, swap(x_hi, CORE)
         tokens[Y | CORE] = swap(y_lo, CORE), cy_hi
         away_near = swap(away, CORE)
         tokens[X], tokens[Y] = (x_lo, x_hi), (y_lo, y_hi)
-        own1, = rows("again", 1, own0, info=pair, u_all=u_all)
         info = jnp.concatenate([pair, jnp.stack([away, away_near], axis=1).reshape(6, 2, BLK)])
-        first_two = (spans[0][0], spans[1][1])
-        side, u_all = rows("side", 0, own1, info=info, span=first_two, tokens=tokens, u_all=u_all)
+
+        du_a, sums = after((du_shares[0], sums), own)
+        sums = order_sum(sums) / width
+        m1, m2 = column(sums[0]), column(sums[1])
+        dab_a, pack = back_pass(0, vp[None], pre, normed, rstd, z, m1, m2, du_a, ln_gain[None])
+        dab_a = [dab_a] + [swap_vp(dab_a, b) for b in range(1, n_shards)]
+
+        side, u_all = rows("side", 0, pack, info=info, tokens=tokens, u_all=u_all)
         d_lo, d_hi = after((d_lo, d_hi), side)
-        tokens[X | Y] = d_lo, d_hi
-        tokens[X | Y | CORE] = swap(d_lo, CORE), swap(d_hi, CORE)
-        chunk0, u_all, big = rows("far", 0, info=info, tokens=tokens, u_all=u_all, parts=((own0, 0), (side, 0)))
-        twin0, far0 = send(0, chunk0)
-        chunk1, big = rows("last", 1, info=info, u_all=u_all, big=big, parts=((own1, 0), (side, spans[1][0])))
-        twin1, far1 = send(1, chunk1)
-
-        du_share = after(du_share, chunk1)
-        sums = [sums] + [swap_vp(sums, b) for b in range(1, n_shards)]
-        sums = order_sum(sums) / width
-        m1, m2 = (jnp.broadcast_to(sums[j][:, None], (n_loc, 128)) for j in range(2))
+        tokens[X | Y], tokens[X | Y | CORE] = (d_lo, d_hi), (swap(d_lo, CORE), swap(d_hi, CORE))
+
+        du_b = after(du_shares[1], side)
         loss_row = jnp.pad(loss_part[None, None], ((0, 0), (0, cols - 1)))
         db_rows = -(-shard_rows // cols // 8) * 8
-        db_mat = jnp.pad(db_part[0], (0, db_rows * cols - shard_rows)).reshape(db_rows, cols)
-        dab, pack = back_pass(vp[None], pre, normed, rstd, z, du_share, m1, m2, ln_gain[None], loss_row, db_mat)
-        back_done = dab
+        db_mat = jnp.pad((db_parts[0] + db_parts[1])[0], (0, db_rows * cols - shard_rows)).reshape(db_rows, cols)
+        dab_b, pack = back_pass(cut, vp[None], pre, normed, rstd, z, m1, m2, du_b, ln_gain[None], pack, loss_row, db_mat)
+        back_done = dab_b
         pack = lax.psum(pack, "dp")
-        dab = [dab] + [swap_vp(dab, b) for b in range(1, n_shards)]
-
-        chunk2, big = rows("whole", 2, back_done, info=info, u_all=u_all, big=big, puts=[twin0])
-        twin2, far2 = send(2, chunk2)
-        far0, far_twin0 = forward(0, far0, chunk2)
-        far1, far_twin1 = forward(1, far1, chunk2)
-        pack = after(pack, chunk2)
+        dab_b = [dab_b] + [swap_vp(dab_b, b) for b in range(1, n_shards)]
+
+        chunk0, u_all, big = rows("far", 0, back_done, info=info, tokens=tokens, u_all=u_all, parts=((own, 0), (side, 0)))
+        twin0, far0 = send(0, chunk0)
+        chunk1, big = rows("whole", 1, info=info, u_all=u_all, big=big)
+        twin1, far1 = send(1, chunk1)
+        pack = after(pack, chunk1)
         n_half = (width + 16) // 2
         part = lax.dynamic_slice(pack, (core * n_half, 0), (n_half, cols))
         parts = [swap_vp(part, b) for b in range(1, n_shards)]
 
-        chunk3, big = rows("whole", 3, part, info=info, u_all=u_all, big=big, puts=[far0, twin1, far1])
-        twin3, far3 = send(3, chunk3)
-        far2, far_twin2 = forward(2, far2, chunk3)
-        d_hidden = spread_pass(n_masks, hidden.shape, vp[None], pos_pad[:, None], w_trans, after(dab, chunk3))
+        chunk2, big = rows("whole", 2, part, info=info, u_all=u_all, big=big, puts=[twin0])
+        twin2, far2 = send(2, chunk2)
+        far0, far_twin0 = forward(0, far0, chunk2)
+        d_hidden = spread_pass(n_masks, hidden.shape, vp[None], pos_pad[:, None], w_trans, after(dab_a + dab_b, chunk2))
         parts = after(parts, d_hidden)
         others = [swap(p, CORE) for p in parts]
-        big = put_rows(pos, big, [far_twin0, far_twin1, twin2, far2, far_twin2, twin3])
+        big = put_rows(pos, big, [far0, far_twin0, twin1, twin2])
+        far1, far_twin1 = forward(1, far1, big)
         pack, parts, others = after((pack, parts, others), big)
         d_w, vec = join_pass(jnp.stack([vp, core]), pack, parts, others)
-        far3 = after(far3, big)
-        far3, far_twin3 = forward(3, far3)
-        big = put_rows(pos, big, [far3])
-        big = put_rows(pos, big, [far_twin3])
+        big = put_rows(pos, big, [far1, far_twin1])
+        far2, far_twin2 = forward(2, far2, big)
+        big = put_rows(pos, big, [far2])
+        big = put_rows(pos, big, [far_twin2])
 
         db = pack[width + 16:].reshape(-1)[:shard_rows]
         return pack[width + 3, 0] / n_tokens, d_hidden, d_w, vec[0], vec[1], vec[2], big, db

time: 703 us -> 716 us (1.018)
  starting transfers between devices: 45.2 us -> 65.1 us
  waiting for transfers between devices: 241 us -> 224 us
  Pallas kernels: 359 us -> 373 us
    psum x1, waiting for transfers between devices: 57.8 us -> 0.56 us  [local_step(): pack = lax.psum(pack, 'dp')]
    ppermute x30 -> x28, waiting for transfers between devices: 36.8 us -> 89.2 us  [swap(): return lax.ppermute(a, 'dp', [(d, d ^ bit) for d in range(n_groups)])]
    pallas_call x2 -> x4, Pallas kernels: 54.3 us -> 72.3 us  [the longest x2 61.8 us: du_pass(): pl.pallas_call(functools.partial(du_kernel, v, scale, base), grid=(n,), i...]
    ppermute x12 -> x15, starting transfers between devices: 15.9 us -> 33.7 us  [swap_vp(): return lax.ppermute(a, 'vp', [(d, d ^ bit) for d in range(n_shards)])]
    ppermute x4 -> x3, waiting for transfers between devices: 32.4 us -> 16.7 us  [hop(): lax.ppermute(a, 'dp', [(d, d ^ (Y if d & CORE else X)) for d in range(n_g...]
    pallas_call x7 -> x5, Pallas kernels: 193 us -> 183 us  [rows_pass(): pl.pallas_call(functools.partial(rows_kernel, kind, scale, s0, m, cut, n_...]
    unnamed x36, local copies, waits for them, and re-layouts: 13.2 us -> 4.01 us
    pallas_call x3 -> x4, Pallas kernels: 22.7 us -> 28.9 us  [put_rows(): pl.pallas_call(functools.partial(put_kernel, spots), in_specs=[SMEM] + [A...]
  transfers between devices with their start and end apart: 48 -> 49, of which waited for: 15 -> 21; matrix products, arithmetic and copies ran while one was open for 3% -> 3% of each run, Pallas kernels for 49% -> 39%
where the time goes in v4:
time: 716 us; the launch traced here: 708 us
  Pallas kernels  373 us (52%)
  waiting for transfers between devices  224 us (31%)
  starting transfers between devices  65.1 us (9%)
  local copies, waits for them, and re-layouts  24.5 us (3%)
  between operations  16.5 us (2%)
    pallas_call x5, Pallas kernels, rows_pass(): pl.pallas_call(functools.partial(rows_kernel, kind, scale, s0, m, cut, n_...  183 us
    ppermute x15, waiting for transfers between devices, swap_vp(): return lax.ppermute(a, 'vp', [(d, d ^ bit) for d in range(n_shards)])  118 us
    ppermute x28, waiting for transfers between devices, swap(): return lax.ppermute(a, 'dp', [(d, d ^ bit) for d in range(n_groups)])  89.2 us
    pallas_call x2, Pallas kernels, du_pass(): pl.pallas_call(functools.partial(du_kernel, v, scale, base), grid=(n,), i...  61.8 us
    pallas_call x1, Pallas kernels, stats(): pl.pallas_call(functools.partial(stats_kernel, v), grid=(n,), in_specs=[w...  53.9 us
    ppermute x15, starting transfers between devices, swap_vp(): return lax.ppermute(a, 'vp', [(d, d ^ bit) for d in range(n_shards)])  33.7 us
    pallas_call x4, Pallas kernels, put_rows(): pl.pallas_call(functools.partial(put_kernel, spots), in_specs=[SMEM] + [A...  28.9 us
    ppermute x28, starting transfers between devices, swap(): return lax.ppermute(a, 'dp', [(d, d ^ bit) for d in range(n_groups)])  28.3 us
  transfers between devices with their start and end apart: 49, of which 21 were waited for; matrix products, arithmetic and copies ran while one was open for 3% of the time, Pallas kernels for 39%

profile of v4, /device:TPU:9, one launch (start us, length us, event | category | flops | bytes accessed | tf_op | source)
XLA Modules:
  0.0 708.5 jit_solution(4644502404336936146)
XLA Ops:
  8.1 1.5 broadcast_in_dim.45.b_ref
  11.9 15.7 %head.1 = (bf16[1232,1024]{1,0:T(8,128)(2,1)}, f32[1232,1024]{1,0:T(8,128)}, f32[1232,1024]{1,0:T(8,128)}, f32[1232,128]{1,0:T(8,128)}, bf16[1232,1024]{1,0:T(8,...) custom-call(bf16[16,512,1024]{2,1,0:T(8,128)(2,1)} %hid.1, s32[16,80,128]{2,1,0:T(8,128)} %broadcast_in_dim.41.pos_ref, ...), custom_call_target="tpu_custom_call" | custom-call | flops 51673824 | bytes 42008576 | tf_op jit(solution)/shard_map/head/pallas_call | solution.py:242
  28.7 53.9 %stats.1 = (f32[608,12576]{1,0:T(8,128)}, f32[624,12576]{1,0:T(8,128)}, f32[8,1232]{1,0:T(8,128)}) custom-call(bf16[1232,1024]{1,0:T(8,128)(2,1)} %get-tuple-element.87.u_ref, bf16[12576,1024]{1,0:T(8,128)(2,1)} %emb_hbm.9, f32[1,12576]{1,0:T(1,128)} %broadcast_in_dim.45.b_ref, s32[1232,128]{1,0:T(8,128)} %broadcast_in_dim.91.lab_ref), custom_call_target="tpu_custom_call" | custom-call | flops 317309568 | bytes 87730176 | tf_op jit(solution)/shard_map/stats/pallas_call | solution.py:83
  82.6 2.5 collective-permute-start.1
  85.3 1.5 collective-permute-start.7
  87.2 1.7 collective-permute-done.2
  92.3 30.5 %du_pass.2 = (f32[4,608,256]{2,1,0:T(8,128)}, f32[1,12576]{1,0:T(1,128)}, f32[8,608]{1,0:T(8,128)}) custom-call(f32[608,12576]{1,0:T(8,128)} %get-tuple-element.88.logits_ref, bf16[12576,1024]{1,0:T(8,128)(2,1)} %emb_hbm.9, f32[608,128]{1,0:T(8,128)} %broadcast_in_dim.92.lse_ref, s32[608,128]{1,0:T(8,128)} %broadcast_in_dim.93.lab_ref, ...), custom_call_target="tpu_custom_call" | custom-call | flops 156594336 | bytes 56340480 | tf_op jit(solution)/shard_map/du_pass/pallas_call | solution.py:169
  122.9 2.1 collective-permute-start.8
  130.8 51.5 %collective-permute-done.11 = f32[2,1280]{1,0:T(2,128)S(1)} collective-permute-done((f32[2,1280]{1,0:T(2,128)S(1)}, f32[2,1280]{1,0:T(2,128)S(1)}, u32[]{:S(2)}, u32[]{:S(2)}) %collective-permute-start.11) | collective-permute-done | bytes 10272 | tf_op jit(solution)/shard_map/ppermute | solution.py:643
  188.2 1.6 broadcast_in_dim.103.bias_ref
  192.3 31.3 %du_pass.3 = (f32[4,624,256]{2,1,0:T(8,128)}, f32[1,12576]{1,0:T(1,128)}, f32[8,624]{1,0:T(8,128)}) custom-call(f32[624,12576]{1,0:T(8,128)} %get-tuple-element.92.logits_ref, bf16[12576,1024]{1,0:T(8,128)(2,1)} %emb_hbm.9, f32[624,128]{1,0:T(8,128)} %broadcast_in_dim.94.lse_ref, s32[624,128]{1,0:T(8,128)} %broadcast_in_dim.95.lab_ref, ...), custom_call_target="tpu_custom_call" | custom-call | flops 160715248 | bytes 57145344 | tf_op jit(solution)/shard_map/du_pass/pallas_call | solution.py:169
  224.4 21.8 %shard_map.152 = (f32[1280,1024]{1,0:T(8,128)}, bf16[8,1280,1024]{2,1,0:T(8,128)(2,1)}) custom-call(s32[6]{0:T(128)} %stack.73.pos, bf16[12576,1024]{1,0:T(8,128)(2,1)} %emb_hbm.9, f32[3144,1]{1,0:T(8,128)} %broadcast_in_dim.103.bias_ref, f32[2,2,1280]{2,1,0:T(2,128)} %pad_maximum_fusion.4.info_ref, f32[608,1024]{1,0:T(8,128)} %get-tuple-element.97.refs_0_, ...), custom_call_target="tpu_custom_call" | custom-call | flops 134217728 | bytes 13107200 | tf_op jit(solution)/shard_map/pallas_call | solution.py:430
  246.3 2.9 collective-permute-start.19
  249.2 2.7 collective-permute-start.3
  255.8 1.6 collective-permute-start.18
  258.4 4.2 collective-permute-done.14
  267.1 5.0 back.2
  272.2 36.7 %shard_map.153 = (f32[1280,1024]{1,0:T(8,128)}, bf16[8,1280,1024]{2,1,0:T(8,128)(2,1)}) custom-call(s32[6]{0:T(128)} %stack.73.pos, bf16[12576,1024]{1,0:T(8,128)(2,1)} %emb_hbm.9, f32[3144,1]{1,0:T(8,128)} %broadcast_in_dim.103.bias_ref, f32[8,2,1280]{2,1,0:T(2,128)} %pad_maximum_fusion.info_ref, ...), custom_call_target="tpu_custom_call", output_to_operand_aliasing={{1}: (12, {})} | custom-call | flops 268435456 | bytes 18350080 | tf_op jit(solution)/shard_map/pallas_call | solution.py:430
  308.8 9.9 %collective-permute-done.21.refs_0_ = f32[608,1024]{1,0:T(8,128)} collective-permute-done((f32[608,1024]{1,0:T(8,128)}, f32[608,1024]{1,0:T(8,128)}, u32[]{:S(2)}, u32[]{:S(2)}) %collective-permute-start.21) | collective-permute-done | bytes 2490400 | tf_op jit(solution)/shard_map/ppermute | solution.py:643
  321.8 5.5 back.3
  327.8 24.3 %shard_map.154 = (f32[1280,1024]{1,0:T(8,128)}, bf16[8,1280,1024]{2,1,0:T(8,128)(2,1)}, f32[12576,1024]{1,0:T(8,128)}) custom-call(s32[6]{0:T(128)} %stack.73.pos, bf16[12576,1024]{1,0:T(8,128)(2,1)} %emb_hbm.9, f32[3144,1]{1,0:T(8,128)} %broadcast_in_dim.103.bias_ref, f32[8,2,1280]{2,1,0:T(2,128)} %pad_maximum_fusion.info_ref, ...), custom_call_target="tpu_custom_call", output_to_operand_aliasing={{1}: (8, {})} | custom-call | flops 134217728 | bytes 13107200 | tf_op jit(solution)/shard_map/pallas_call | solution.py:430
  353.9 57.8 %shard_map.155 = (f32[1088,1024]{1,0:T(8,128)}, f32[12576,1024]{1,0:T(8,128)}) custom-call(s32[6]{0:T(128)} %stack.73.pos, bf16[12576,1024]{1,0:T(8,128)(2,1)} %emb_hbm.9, f32[3144,1]{1,0:T(8,128)} %broadcast_in_dim.103.bias_ref, f32[8,2,1280]{2,1,0:T(2,128)} %pad_maximum_fusion.info_ref, ...), custom_call_target="tpu_custom_call", output_to_operand_aliasing={{1}: (5, {})} | custom-call | flops 456340288 | bytes 27656192 | tf_op jit(solution)/shard_map/pallas_call | solution.py:430
  412.2 1.9 constant_dynamic-slice_fusion
  414.1 42.1 %shard_map.156 = (f32[776,1024]{1,0:T(8,128)}, f32[12576,1024]{1,0:T(8,128)}) custom-call(s32[6]{0:T(128)} %stack.73.pos, bf16[12576,1024]{1,0:T(8,128)(2,1)} %emb_hbm.9, f32[3144,1]{1,0:T(8,128)} %broadcast_in_dim.103.bias_ref, f32[8,2,1280]{2,1,0:T(2,128)} %pad_maximum_fusion.info_ref, ...), custom_call_target="tpu_custom_call", output_to_operand_aliasing={{1}: (5, {})} | custom-call | flops 325477984 | bytes 25739264 | tf_op jit(solution)/shard_map/pallas_call | solution.py:430
  456.2 1.7 collective-permute-start.39
  459.4 13.5 %collective-permute-done.40.refs_3_ = f32[1088,1024]{1,0:T(8,128)} collective-permute-done((f32[1088,1024]{1,0:T(8,128)}, f32[1088,1024]{1,0:T(8,128)}, u32[]{:S(2)}, u32[]{:S(2)}) %collective-permute-start.40) | collective-permute-done | bytes 4456480 | tf_op jit(solution)/shard_map/ppermute | solution.py:643
  472.8 4.4 collective-permute-done.41.refs_4_
  477.3 1.6 copy-done.1
  478.9 13.1 %put_rows.4.refs_0_ = f32[12576,1024]{1,0:T(8,128)} custom-call(s32[6]{0:T(128)} %stack.73.pos, f32[12576,1024]{1,0:T(8,128)} %get-tuple-element.145.refs_0_, f32[1280,1024]{1,0:T(8,128)} %collective-permute-done.38.refs_1_, f32[1280,1024]{1,0:T(8,128)} %collective-permute-done.39.refs_2_, ...), custom_call_target="tpu_custom_call", output_to_operand_aliasing={{}: (1, {})} | custom-call | flops 45301 | bytes 36241408 | tf_op jit(solution)/shard_map/put_rows/pallas_call | solution.py:463
  492.0 16.7 %collective-permute-done.42.refs_1_ = f32[1088,1024]{1,0:T(8,128)} collective-permute-done((f32[1088,1024]{1,0:T(8,128)}, f32[1088,1024]{1,0:T(8,128)}, u32[]{:S(2)}, u32[]{:S(2)}) %collective-permute-start.42) | collective-permute-done | bytes 4456480 | tf_op jit(solution)/shard_map/ppermute | solution.py:649
  510.8 1.5 collective-permute-start.28
  513.5 25.3 %collective-permute-done.28.refs_1_ = f32[608,256]{1,0:T(8,128)} collective-permute-done((f32[608,256]{1,0:T(8,128)}, f32[608,256]{1,0:T(8,128)}, u32[]{:S(2)}, u32[]{:S(2)}) %collective-permute-start.28) | collective-permute-done | bytes 622624 | tf_op jit(solution)/shard_map/ppermute | solution.py:646
  538.8 2.2 collective-permute-start.31
  541.0 14.8 %collective-permute-start.32 = (f32[624,256]{1,0:T(8,128)S(1)}, f32[624,256]{1,0:T(8,128)S(1)}, u32[]{:S(2)}, u32[]{:S(2)}) collective-permute-start(f32[624,256]{1,0:T(8,128)S(1)} %copy-done.4), channel_id=1, source_target_pairs={{0,16},{8,24},{16,0},{24,8},{1,17},{9,25},{17,1},{25,9},{2,18},{10... | collective-permute-start | bytes 1916936 | tf_op jit(solution)/shard_map/ppermute | solution.py:646
  555.8 11.7 %collective-permute-done.30.refs_3_ = f32[608,256]{1,0:T(8,128)} collective-permute-done((f32[608,256]{1,0:T(8,128)}, f32[608,256]{1,0:T(8,128)}, u32[]{:S(2)}, u32[]{:S(2)}) %collective-permute-start.30) | collective-permute-done | bytes 622624 | tf_op jit(solution)/shard_map/ppermute | solution.py:646
  567.5 1.7 collective-permute-start.33
  569.2 1.5 collective-permute-start.25
  570.7 36.8 %collective-permute-done.32.refs_6_ = f32[624,256]{1,0:T(8,128)S(1)} collective-permute-done((f32[624,256]{1,0:T(8,128)S(1)}, f32[624,256]{1,0:T(8,128)S(1)}, u32[]{:S(2)}, u32[]{:S(2)}) %collective-permute-start.32) | collective-permute-done | bytes 639008 | tf_op jit(solution)/shard_map/ppermute | solution.py:646
  607.5 3.1 collective-permute-start.26
  610.6 34.5 %collective-permute-done.33.refs_7_ = f32[624,256]{1,0:T(8,128)S(1)} collective-permute-done((f32[624,256]{1,0:T(8,128)S(1)}, f32[624,256]{1,0:T(8,128)S(1)}, u32[]{:S(2)}, u32[]{:S(2)}) %collective-permute-start.33) | collective-permute-done | bytes 639008 | tf_op jit(solution)/shard_map/ppermute | solution.py:646
  646.2 14.7 %spread.1 = bf16[16,512,1024]{2,1,0:T(8,128)(2,1)} custom-call(s32[1]{0:T(128)} %bitcast.vp, s32[16,1,80]{2,1,0:T(1,128)} %bitcast.41, bf16[1024,1024]{1,0:T(8,128)(2,1)} %w_ref.3, f32[608,256]{1,0:T(8,128)} %get-tuple-element.134.refs_0_, f32[608,256]{1,0:T(8,128)} %collective-permute-done.28.refs_1_, f32[608,256]{1,0:T(8,128)} %collective-permute-done.29.refs_2_, ...), custom_call_target="tpu_custom_call" | custom-call | flops 21474836 | bytes 16777216 | tf_op jit(solution)/shard_map/spread/pallas_call | solution.py:619
  661.0 6.9 collective-permute-done.27.refs_3_
  667.9 1.3 collective-permute-start.35
  673.4 7.2 %put_rows.5.refs_0_ = f32[12576,1024]{1,0:T(8,128)} custom-call(s32[6]{0:T(128)} %stack.73.pos, f32[12576,1024]{1,0:T(8,128)} %put_rows.4.refs_0_, f32[1088,1024]{1,0:T(8,128)} %collective-permute-done.42.refs_1_, f32[1088,1024]{1,0:T(8,128)} %collective-permute-done.43.refs_2_), custom_call_target="tpu_custom_call", output_to_operand_aliasing={{}: (1, {})} | custom-call | flops 22282 | bytes 17825792 | tf_op jit(solution)/shard_map/put_rows/pallas_call | solution.py:463
  682.0 4.9 join.1
  690.3 1.5 fusion.3
  691.8 4.3 put_rows.6.refs_0_
  696.0 4.3 put_rows.7
  (153 shorter events, 52.8 us)
Async XLA Ops:
  7.2 257.7 %reduce-scatter.3.cloned.1.call-start = ((), (), s32[]{:S(2)}) async-start(), calls=%async_computation.2 | async-start | bytes 3112960 | tf_op jit(solution)/shard_map/reduce_scatter | solution.py:697
  82.6 4.2 collective-permute-start
  82.6 4.6 collective-permute-start.1
  85.1 3.8 collective-permute-start.2
  85.3 100.8 %collective-permute-start.7 = (f32[608,1024]{1,0:T(8,128)}, f32[608,1024]{1,0:T(8,128)}, u32[]{:S(2)}, u32[]{:S(2)}) collective-permute-start(f32[608,1024]{1,0:T(8,128)} %get-tuple-element.97.refs_0_), channel_id=1, source_target_pairs={{0,1},{1,0},{2,3},{3,2},{4,5},{5,4},{6,7},{7,6},{8,9},{9,8},{10,11... | collective-permute-start | bytes 7471112 | tf_op jit(solution)/shard_map/ppermute | solution.py:643
  122.9 198.9 %reduce-scatter.5.cloned.1.call-start = ((), (), s32[]{:S(2)}) async-start(), calls=%async_computation.3 | async-start | bytes 3194880 | tf_op jit(solution)/shard_map/reduce_scatter | solution.py:697
  122.9 101.3 %collective-permute-start.8 = (f32[624,1024]{1,0:T(8,128)S(1)}, f32[624,1024]{1,0:T(8,128)}, u32[]{:S(2)}, u32[]{:S(2)}) collective-permute-start(f32[624,1024]{1,0:T(8,128)S(1)} %copy-done.2), channel_id=1, source_target_pairs={{0,1},{1,0},{2,3},{3,2},{4,5},{5,4},{6,7},{7,6},{8,9},{9,8},{10,11... | collective-permute-start | bytes 7667720 | tf_op jit(solution)/shard_map/ppermute | solution.py:643
  125.0 121.2 %collective-permute-start.9 = (f32[624,1024]{1,0:T(8,128)S(1)}, f32[624,1024]{1,0:T(8,128)}, u32[]{:S(2)}, u32[]{:S(2)}) collective-permute-start(f32[624,1024]{1,0:T(8,128)S(1)} %copy-done.2), channel_id=1, source_target_pairs={{0,2},{1,3},{2,0},{3,1},{4,6},{5,7},{6,4},{7,5},{8,10},{9,11},{10,... | collective-permute-start | bytes 7667720 | tf_op jit(solution)/shard_map/ppermute | solution.py:643
  126.2 120.0 %collective-permute-start.10 = (f32[608,1024]{1,0:T(8,128)}, f32[608,1024]{1,0:T(8,128)}, u32[]{:S(2)}, u32[]{:S(2)}) collective-permute-start(f32[608,1024]{1,0:T(8,128)} %get-tuple-element.97.refs_0_), channel_id=1, source_target_pairs={{0,4},{1,5},{2,6},{3,7},{4,0},{5,1},{6,2},{7,3},{8,12},{9,13},{10,... | collective-permute-start | bytes 7471112 | tf_op jit(solution)/shard_map/ppermute | solution.py:643
  129.6 52.7 %collective-permute-start.11 = (f32[2,1280]{1,0:T(2,128)S(1)}, f32[2,1280]{1,0:T(2,128)S(1)}, u32[]{:S(2)}, u32[]{:S(2)}) collective-permute-start(f32[2,1280]{1,0:T(2,128)S(1)} %get-tuple-element.175), channel_id=1, source_target_pairs={{0,2},{1,3},{2,0},{3,1},{4,6},{5,7},{6,4},{7,5},{8,10},{9,11},{10,... | collective-permute-start | bytes 30728 | tf_op jit(solution)/shard_map/ppermute | solution.py:643
  182.3 2.5 collective-permute-start.12
  184.8 68.7 %collective-permute-start.16 = (f32[624,1024]{1,0:T(8,128)S(1)}, f32[624,1024]{1,0:T(8,128)}, u32[]{:S(2)}, u32[]{:S(2)}) collective-permute-start(f32[624,1024]{1,0:T(8,128)S(1)} %copy-done.2), channel_id=1, source_target_pairs={{0,4},{1,5},{2,6},{3,7},{4,0},{5,1},{6,2},{7,3},{8,12},{9,13},{10,... | collective-permute-start | bytes 7667720 | tf_op jit(solution)/shard_map/ppermute | solution.py:643
  186.1 66.1 %collective-permute-start.15 = (f32[608,1024]{1,0:T(8,128)}, f32[608,1024]{1,0:T(8,128)}, u32[]{:S(2)}, u32[]{:S(2)}) collective-permute-start(f32[608,1024]{1,0:T(8,128)} %get-tuple-element.97.refs_0_), channel_id=1, source_target_pairs={{0,2},{1,3},{2,0},{3,1},{4,6},{5,7},{6,4},{7,5},{8,10},{9,11},{10,... | collective-permute-start | bytes 7471112 | tf_op jit(solution)/shard_map/ppermute | solution.py:643
  224.2 22.0 %collective-permute-start.13 = (f32[2,1280]{1,0:T(2,128)S(1)}, f32[2,1280]{1,0:T(2,128)S(1)}, u32[]{:S(2)}, u32[]{:S(2)}) collective-permute-start(f32[2,1280]{1,0:T(2,128)S(1)} %get-tuple-element.175), channel_id=1, source_target_pairs={{0,6},{1,7},{2,4},{3,5},{4,2},{5,3},{6,0},{7,1},{8,14},{9,15},{10,... | collective-permute-start | bytes 30728 | tf_op jit(solution)/shard_map/ppermute | solution.py:643
  246.3 16.6 %collective-permute-start.19 = (f32[608,1024]{1,0:T(8,128)}, f32[608,1024]{1,0:T(8,128)}, u32[]{:S(2)}, u32[]{:S(2)}) collective-permute-start(f32[608,1024]{1,0:T(8,128)} %collective-permute-done.10.refs_4_), channel_id=1, source_target_pairs={{0,1},{1,0},{2,3},{3,2},{4,5},{5,4},{6,7},{7,6},{8,9},{9,8},{10,11... | collective-permute-start | bytes 7471112 | tf_op jit(solution)/shard_map/ppermute | solution.py:643
  249.2 4.9 collective-permute-start.3
  251.9 3.9 collective-permute-start.4
  251.9 160.3 %all-reduce.7.cloned.1.call-start = ((), (), s32[]{:S(2)}) async-start(), calls=%async_computation.4 | async-start | bytes 2244608 | tf_op jit(solution)/shard_map/psum | solution.py:752
  252.2 5.2 collective-permute-start.5
  253.5 18.6 %collective-permute-start.20 = (f32[624,1024]{1,0:T(8,128)}, f32[624,1024]{1,0:T(8,128)}, u32[]{:S(2)}, u32[]{:S(2)}) collective-permute-start(f32[624,1024]{1,0:T(8,128)} %collective-permute-done.16.refs_5_), channel_id=1, source_target_pairs={{0,1},{1,0},{2,3},{3,2},{4,5},{5,4},{6,7},{7,6},{8,9},{9,8},{10,11... | collective-permute-start | bytes 7667720 | tf_op jit(solution)/shard_map/ppermute | solution.py:643
  254.1 64.6 %collective-permute-start.22 = (f32[624,1024]{1,0:T(8,128)}, f32[624,1024]{1,0:T(8,128)S(1)}, u32[]{:S(2)}, u32[]{:S(2)}) collective-permute-start(f32[624,1024]{1,0:T(8,128)} %collective-permute-done.16.refs_5_), channel_id=1, source_target_pairs={{0,2},{1,3},{2,0},{3,1},{4,6},{5,7},{6,4},{7,5},{8,10},{9,11},{10,... | collective-permute-start | bytes 7667720 | tf_op jit(solution)/shard_map/ppermute | solution.py:643
  255.8 16.3 %collective-permute-start.18 = (f32[624,1024]{1,0:T(8,128)}, f32[624,1024]{1,0:T(8,128)}, u32[]{:S(2)}, u32[]{:S(2)}) collective-permute-start(f32[624,1024]{1,0:T(8,128)} %collective-permute-done.9.refs_1_), channel_id=1, source_target_pairs={{0,1},{1,0},{2,3},{3,2},{4,5},{5,4},{6,7},{7,6},{8,9},{9,8},{10,11... | collective-permute-start | bytes 7667720 | tf_op jit(solution)/shard_map/ppermute | solution.py:643
  257.4 5.1 collective-permute-start.14
  262.5 9.6 %collective-permute-start.17 = (f32[608,1024]{1,0:T(8,128)}, f32[608,1024]{1,0:T(8,128)}, u32[]{:S(2)}, u32[]{:S(2)}) collective-permute-start(f32[608,1024]{1,0:T(8,128)} %collective-permute-done.15.refs_0_), channel_id=1, source_target_pairs={{0,1},{1,0},{2,3},{3,2},{4,5},{5,4},{6,7},{7,6},{8,9},{9,8},{10,11... | collective-permute-start | bytes 7471112 | tf_op jit(solution)/shard_map/ppermute | solution.py:643
  262.9 55.8 %collective-permute-start.21 = (f32[608,1024]{1,0:T(8,128)}, f32[608,1024]{1,0:T(8,128)}, u32[]{:S(2)}, u32[]{:S(2)}) collective-permute-start(f32[608,1024]{1,0:T(8,128)} %collective-permute-done.15.refs_0_), channel_id=1, source_target_pairs={{0,4},{1,5},{2,6},{3,7},{4,0},{5,1},{6,2},{7,3},{8,12},{9,13},{10,... | collective-permute-start | bytes 7471112 | tf_op jit(solution)/shard_map/ppermute | solution.py:643
  318.7 9.1 %collective-permute-start.24 = (f32[624,1024]{1,0:T(8,128)S(1)}, f32[624,1024]{1,0:T(8,128)}, u32[]{:S(2)}, u32[]{:S(2)}) collective-permute-start(f32[624,1024]{1,0:T(8,128)S(1)} %collective-permute-done.22.refs_1_), channel_id=1, source_target_pairs={{0,1},{1,0},{2,3},{3,2},{4,5},{5,4},{6,7},{7,6},{8,9},{9,8},{10,11... | collective-permute-start | bytes 7667720 | tf_op jit(solution)/shard_map/ppermute | solution.py:643
  319.7 8.1 %collective-permute-start.23 = (f32[608,1024]{1,0:T(8,128)}, f32[608,1024]{1,0:T(8,128)}, u32[]{:S(2)}, u32[]{:S(2)}) collective-permute-start(f32[608,1024]{1,0:T(8,128)} %collective-permute-done.21.refs_0_), channel_id=1, source_target_pairs={{0,1},{1,0},{2,3},{3,2},{4,5},{5,4},{6,7},{7,6},{8,9},{9,8},{10,11... | collective-permute-start | bytes 7471112 | tf_op jit(solution)/shard_map/ppermute | solution.py:643
  352.2 61.9 %collective-permute-start.34 = (f32[1280,1024]{1,0:T(8,128)}, f32[1280,1024]{1,0:T(8,128)}, u32[]{:S(2)}, u32[]{:S(2)}) collective-permute-start(f32[1280,1024]{1,0:T(8,128)} %get-tuple-element.132), channel_id=1, source_target_pairs={{0,1},{1,0},{2,3},{3,2},{4,5},{5,4},{6,7},{7,6},{8,9},{9,8},{10,11... | collective-permute-start | bytes 15728648 | tf_op jit(solution)/shard_map/ppermute | solution.py:643
  352.6 103.6 %collective-permute-start.38 = (f32[1280,1024]{1,0:T(8,128)}, f32[1280,1024]{1,0:T(8,128)}, u32[]{:S(2)}, u32[]{:S(2)}) collective-permute-start(f32[1280,1024]{1,0:T(8,128)} %get-tuple-element.132), channel_id=1, source_target_pairs={{0,2},{1,5},{2,0},{3,7},{4,6},{5,1},{6,4},{7,3},{8,10},{9,13},{10,... | collective-permute-start | bytes 15728648 | tf_op jit(solution)/shard_map/ppermute | solution.py:649
  456.2 21.1 %collective-permute-start.39 = (f32[1280,1024]{1,0:T(8,128)}, f32[1280,1024]{1,0:T(8,128)}, u32[]{:S(2)}, u32[]{:S(2)}) collective-permute-start(f32[1280,1024]{1,0:T(8,128)} %collective-permute-done.38.refs_1_), channel_id=1, source_target_pairs={{0,1},{1,0},{2,3},{3,2},{4,5},{5,4},{6,7},{7,6},{8,9},{9,8},{10,11... | collective-permute-start | bytes 15728648 | tf_op jit(solution)/shard_map/ppermute | solution.py:643
  457.8 15.0 %collective-permute-start.40 = (f32[1088,1024]{1,0:T(8,128)}, f32[1088,1024]{1,0:T(8,128)}, u32[]{:S(2)}, u32[]{:S(2)}) collective-permute-start(f32[1088,1024]{1,0:T(8,128)} %get-tuple-element.127), channel_id=1, source_target_pairs={{0,1},{1,0},{2,3},{3,2},{4,5},{5,4},{6,7},{7,6},{8,9},{9,8},{10,11... | collective-permute-start | bytes 13369352 | tf_op jit(solution)/shard_map/ppermute | solution.py:643
  457.9 50.8 %collective-permute-start.42 = (f32[1088,1024]{1,0:T(8,128)}, f32[1088,1024]{1,0:T(8,128)}, u32[]{:S(2)}, u32[]{:S(2)}) collective-permute-start(f32[1088,1024]{1,0:T(8,128)} %get-tuple-element.127), channel_id=1, source_target_pairs={{0,2},{1,5},{2,0},{3,7},{4,6},{5,1},{6,4},{7,3},{8,10},{9,13},{10,... | collective-permute-start | bytes 13369352 | tf_op jit(solution)/shard_map/ppermute | solution.py:649
  458.7 18.6 %collective-permute-start.41 = (f32[776,1024]{1,0:T(8,128)}, f32[776,1024]{1,0:T(8,128)S(1)}, u32[]{:S(2)}, u32[]{:S(2)}) collective-permute-start(f32[776,1024]{1,0:T(8,128)} %get-tuple-element.133), channel_id=1, source_target_pairs={{0,1},{1,0},{2,3},{3,2},{4,5},{5,4},{6,7},{7,6},{8,9},{9,8},{10,11... | collective-permute-start | bytes 9535496 | tf_op jit(solution)/shard_map/ppermute | solution.py:643
  508.7 164.7 %collective-permute-start.43 = (f32[1088,1024]{1,0:T(8,128)}, f32[1088,1024]{1,0:T(8,128)}, u32[]{:S(2)}, u32[]{:S(2)}) collective-permute-start(f32[1088,1024]{1,0:T(8,128)} %collective-permute-done.42.refs_1_), channel_id=1, source_target_pairs={{0,1},{1,0},{2,3},{3,2},{4,5},{5,4},{6,7},{7,6},{8,9},{9,8},{10,11... | collective-permute-start | bytes 13369352 | tf_op jit(solution)/shard_map/ppermute | solution.py:643
  510.0 170.7 %collective-permute-start.44 = (f32[776,1024]{1,0:T(8,128)}, f32[776,1024]{1,0:T(8,128)S(1)}, u32[]{:S(2)}, u32[]{:S(2)}) collective-permute-start(f32[776,1024]{1,0:T(8,128)} %get-tuple-element.133), channel_id=1, source_target_pairs={{0,2},{1,5},{2,0},{3,7},{4,6},{5,1},{6,4},{7,3},{8,10},{9,13},{10,... | collective-permute-start | bytes 9535496 | tf_op jit(solution)/shard_map/ppermute | solution.py:649
  510.8 28.1 %collective-permute-start.28 = (f32[608,256]{1,0:T(8,128)}, f32[608,256]{1,0:T(8,128)}, u32[]{:S(2)}, u32[]{:S(2)}) collective-permute-start(f32[608,256]{1,0:T(8,128)} %get-tuple-element.134.refs_0_), channel_id=1, source_target_pairs={{0,8},{8,0},{16,24},{24,16},{1,9},{9,1},{17,25},{25,17},{2,10},{10... | collective-permute-start | bytes 1867784 | tf_op jit(solution)/shard_map/ppermute | solution.py:646
  512.3 28.7 %collective-permute-start.29 = (f32[608,256]{1,0:T(8,128)}, f32[608,256]{1,0:T(8,128)}, u32[]{:S(2)}, u32[]{:S(2)}) collective-permute-start(f32[608,256]{1,0:T(8,128)} %get-tuple-element.134.refs_0_), channel_id=1, source_target_pairs={{0,16},{8,24},{16,0},{24,8},{1,17},{9,25},{17,1},{25,9},{2,18},{10... | collective-permute-start | bytes 1867784 | tf_op jit(solution)/shard_map/ppermute | solution.py:646
  513.2 54.4 %collective-permute-start.30 = (f32[608,256]{1,0:T(8,128)}, f32[608,256]{1,0:T(8,128)}, u32[]{:S(2)}, u32[]{:S(2)}) collective-permute-start(f32[608,256]{1,0:T(8,128)} %get-tuple-element.134.refs_0_), channel_id=1, source_target_pairs={{0,24},{8,16},{16,8},{24,0},{1,25},{9,17},{17,9},{25,1},{2,26},{10... | collective-permute-start | bytes 1867784 | tf_op jit(solution)/shard_map/ppermute | solution.py:646
  538.8 30.4 %collective-permute-start.31 = (f32[624,256]{1,0:T(8,128)S(1)}, f32[624,256]{1,0:T(8,128)S(1)}, u32[]{:S(2)}, u32[]{:S(2)}) collective-permute-start(f32[624,256]{1,0:T(8,128)S(1)} %copy-done.4), channel_id=1, source_target_pairs={{0,8},{8,0},{16,24},{24,16},{1,9},{9,1},{17,25},{25,17},{2,10},{10... | collective-permute-start | bytes 1916936 | tf_op jit(solution)/shard_map/ppermute | solution.py:646
  541.0 66.5 %collective-permute-start.32 = (f32[624,256]{1,0:T(8,128)S(1)}, f32[624,256]{1,0:T(8,128)S(1)}, u32[]{:S(2)}, u32[]{:S(2)}) collective-permute-start(f32[624,256]{1,0:T(8,128)S(1)} %copy-done.4), channel_id=1, source_target_pairs={{0,16},{8,24},{16,0},{24,8},{1,17},{9,25},{17,1},{25,9},{2,18},{10... | collective-permute-start | bytes 1916936 | tf_op jit(solution)/shard_map/ppermute | solution.py:646
  567.5 77.5 %collective-permute-start.33 = (f32[624,256]{1,0:T(8,128)S(1)}, f32[624,256]{1,0:T(8,128)S(1)}, u32[]{:S(2)}, u32[]{:S(2)}) collective-permute-start(f32[624,256]{1,0:T(8,128)S(1)} %copy-done.4), channel_id=1, source_target_pairs={{0,24},{8,16},{16,8},{24,0},{1,25},{9,17},{17,9},{25,1},{2,26},{10... | collective-permute-start | bytes 1916936 | tf_op jit(solution)/shard_map/ppermute | solution.py:646
  569.2 91.8 %collective-permute-start.25 = (f32[520,256]{1,0:T(8,128)}, f32[520,256]{1,0:T(8,128)}, u32[]{:S(2)}, u32[]{:S(2)}) collective-permute-start(f32[520,256]{1,0:T(8,128)} %constant_dynamic-slice_fusion), channel_id=1, source_target_pairs={{0,8},{8,0},{16,24},{24,16},{1,9},{9,1},{17,25},{25,17},{2,10},{10... | collective-permute-start | bytes 1597448 | tf_op jit(solution)/shard_map/ppermute | solution.py:646
  607.5 53.5 %collective-permute-start.26 = (f32[520,256]{1,0:T(8,128)}, f32[520,256]{1,0:T(8,128)}, u32[]{:S(2)}, u32[]{:S(2)}) collective-permute-start(f32[520,256]{1,0:T(8,128)} %constant_dynamic-slice_fusion), channel_id=1, source_target_pairs={{0,16},{8,24},{16,0},{24,8},{1,17},{9,25},{17,1},{25,9},{2,18},{10... | collective-permute-start | bytes 1597448 | tf_op jit(solution)/shard_map/ppermute | solution.py:646
  645.1 22.8 %collective-permute-start.27 = (f32[520,256]{1,0:T(8,128)}, f32[520,256]{1,0:T(8,128)S(1)}, u32[]{:S(2)}, u32[]{:S(2)}) collective-permute-start(f32[520,256]{1,0:T(8,128)} %constant_dynamic-slice_fusion), channel_id=1, source_target_pairs={{0,24},{8,16},{16,8},{24,0},{1,25},{9,17},{17,9},{25,1},{2,26},{10... | collective-permute-start | bytes 1597448 | tf_op jit(solution)/shard_map/ppermute | solution.py:646
  667.9 3.1 collective-permute-start.35
  669.2 2.5 collective-permute-start.36
  669.2 3.3 collective-permute-start.37
  680.7 15.4 %collective-permute-start.45 = (f32[776,1024]{1,0:T(8,128)S(1)}, f32[776,1024]{1,0:T(8,128)}, u32[]{:S(2)}, u32[]{:S(2)}) collective-permute-start(f32[776,1024]{1,0:T(8,128)S(1)} %collective-permute-done.44.refs_1_), channel_id=1, source_target_pairs={{0,1},{1,0},{2,3},{3,2},{4,5},{5,4},{6,7},{7,6},{8,9},{9,8},{10,11... | collective-permute-start | bytes 9535496 | tf_op jit(solution)/shard_map/ppermute | solution.py:643
  (18 other events, 391.3 us)
Sparse Core Ops, SparseCore 0:
  123.0 49.7 reduce-scatter.2
  252.1 49.8 reduce-scatter.4
  354.0 58.1 all-reduce.6

commit v5 on v4

--- a/solution.py
+++ b/solution.py
@@ -14,7 +14,9 @@
 VB = 1024
 VMEM_LIMIT = 60 << 20
 COVER = 100
-CH = 16
+PARTS = 4
+LEAST = float(jnp.finfo(jnp.float32).min)
+ELSEWHERE = -(1 << 20)
 
 
 def row_cuts(rows, parts=4):
@@ -26,46 +28,57 @@
     return lax.dot_general(a, b, dims, preferred_element_type=F32)
 
 
-def stats_kernel(n_vocab, u_ref, emb_ref, b_ref, lab_ref, lo_ref, hi_ref, stat_ref, m_sc, s_sc, l_sc):
-    i, n_blocks = pl.program_id(0), pl.num_programs(0)
+def stats_kernel(n_vocab, u_ref, emb_ref, b_ref, lab_ref, logits_ref, stat_ref, prev, m_sc, s_sc, l_sc):
+    i, n_steps = pl.program_id(0), pl.num_programs(0)
     lane = lax.broadcasted_iota(I32, (1, 128), 1)
+    cuts = row_cuts(u_ref.shape[0], PARTS)
 
     @pl.when(i == 0)
     def _():
-        m_sc[...] = jnp.full_like(m_sc, -jnp.inf)
+        m_sc[...] = jnp.full_like(m_sc, LEAST)
         s_sc[...] = jnp.zeros_like(s_sc)
         l_sc[...] = jnp.zeros_like(l_sc)
-
-    def run(width):
+        prev[...] = jnp.full_like(prev, -jnp.inf)
+
+    def logits_of(r0, r1, c0, wide, width):
+        tile = dot(u_ref[r0:r1, :], emb_ref[c0:c0 + wide, :], NT) + b_ref[:, c0:c0 + wide]
+        if wide > width:
+            tile = jnp.where(lax.broadcasted_iota(I32, (1, wide), 1) < width, tile, -jnp.inf)
+        logits_ref[r0:r1, c0:c0 + wide] = tile
+        return tile
+
+    def take(r0, r1, read, first, wide):
+        for q in range(r0, r1, 16):
+            rs = slice(q, q + 16)
+            parts = [read(rs, slice(k, k + 128)) for k in range(0, wide, 128)]
+            m_old = m_sc[rs, :]
+            m_new = functools.reduce(jnp.maximum, parts, m_old)
+            s_new = s_sc[rs, :] * jnp.exp(m_old - m_new)
+            l_new = l_sc[rs, :]
+            lab = lab_ref[rs, :] - first
+            for k, part in enumerate(parts):
+                s_new += jnp.exp(part - m_new)
+                l_new = jnp.where(lab == lane + k * 128, part, l_new)
+            m_sc[rs, :], s_sc[rs, :], l_sc[rs, :] = m_new, s_new, l_new
+
+    from_prev = lambda rs, cs: prev[rs, cs]
+    from_out = lambda rs, cs: logits_ref[rs, cs]
+
+    def step(second):
+        width = VB if second else n_vocab % (2 * VB)
         wide = -(-width // 128) * 128
-        for r0, r1 in row_cuts(u_ref.shape[0]):
-            tile = dot(u_ref[r0:r1, :], emb_ref[:wide, :], NT) + b_ref[:, :wide]
-            if wide > width:
-                tile = jnp.where(lax.broadcasted_iota(I32, (1, wide), 1) < width, tile, -jnp.inf)
-            cut = lo_ref.shape[0]
-            out_ref, base = (lo_ref, 0) if r0 < cut else (hi_ref, cut)
-            out_ref[r0 - base:r1 - base, :wide] = tile
-            for q in range(r0, r1, CH):
-                rs = slice(q, min(q + CH, r1))
-                parts = [out_ref[rs.start - base:rs.stop - base, k:k + 128] for k in range(0, wide, 128)]
-                m_old = m_sc[rs, :]
-                m_new = functools.reduce(jnp.maximum, parts, m_old)
-                s_new = s_sc[rs, :] * jnp.exp(m_old - m_new)
-                l_new = l_sc[rs, :]
-                lab = lab_ref[rs, :] - i * VB
-                for k, part in enumerate(parts):
-                    s_new += jnp.exp(part - m_new)
-                    l_new = jnp.where(lab == lane + k * 128, part, l_new)
-                m_sc[rs, :], s_sc[rs, :], l_sc[rs, :] = m_new, s_new, l_new
-
-    tail = n_vocab % VB
-    if tail:
-        pl.when(i < n_blocks - 1)(functools.partial(run, VB))
-        pl.when(i == n_blocks - 1)(functools.partial(run, tail))
-    else:
-        run(VB)
-
-    @pl.when(i == n_blocks - 1)
+        for r0, r1 in cuts:
+            logits_of(r0, r1, 0, wide, width)
+            take(r0, r1, from_prev, (2 * i - 1) * VB, VB)
+        for r0, r1 in cuts:
+            if second:
+                prev[r0:r1, :] = logits_of(r0, r1, VB, VB, VB)
+            take(r0, r1, from_out, 2 * i * VB, wide)
+
+    pl.when(i < n_steps - 1)(functools.partial(step, True))
+    pl.when(i == n_steps - 1)(functools.partial(step, False))
+
+    @pl.when(i == n_steps - 1)
     def _():
         m_t, s_t, l_t = m_sc[...].T, s_sc[...].T, l_sc[...].T
         m_all = jnp.max(m_t, axis=0, keepdims=True)
@@ -75,18 +88,18 @@
         stat_ref[3:8, :] = jnp.zeros_like(stat_ref[3:8, :])
 
 
-def stats(u, emb, bias, lab, cut):
+def stats(u, emb, bias, lab):
     t, e = u.shape
     v = emb.shape[0]
-    n = pl.cdiv(v, VB)
+    n = pl.cdiv(v, 2 * VB)
     whole = lambda *s: pl.BlockSpec(s, lambda i: (0,) * len(s))
     return pl.pallas_call(
         functools.partial(stats_kernel, v),
         grid=(n,),
-        in_specs=[whole(t, e), pl.BlockSpec((VB, e), lambda i: (i, 0)), pl.BlockSpec((1, VB), lambda i: (0, i)), whole(t, 128)],
-        out_specs=[pl.BlockSpec((cut, VB), lambda i: (0, i)), pl.BlockSpec((t - cut, VB), lambda i: (0, i)), whole(8, t)],
-        out_shape=[jax.ShapeDtypeStruct((cut, v), F32), jax.ShapeDtypeStruct((t - cut, v), F32), jax.ShapeDtypeStruct((8, t), F32)],
-        scratch_shapes=[pltpu.VMEM((t, 128), F32)] * 3,
+        in_specs=[whole(t, e), pl.BlockSpec((2 * VB, e), lambda i: (i, 0)), pl.BlockSpec((1, 2 * VB), lambda i: (0, i)), whole(t, 128)],
+        out_specs=[pl.BlockSpec((t, 2 * VB), lambda i: (0, i)), whole(8, t)],
+        out_shape=[jax.ShapeDtypeStruct((t, v), F32), jax.ShapeDtypeStruct((8, t), F32)],
+        scratch_shapes=[pltpu.VMEM((t, VB), F32)] + [pltpu.VMEM((t, 128), F32)] * 3,
         compiler_params=pltpu.CompilerParams(dimension_semantics=("arbitrary",), vmem_limit_bytes=VMEM_LIMIT),
         cost_estimate=pl.CostEstimate(flops=(2 * t * v * e) // COVER, bytes_accessed=t * v * 4 + v * e * 2, transcendentals=t * v),
         name="stats",
@@ -113,7 +126,7 @@
         emb = emb_ref[:wide, :]
         if wide > width:
             emb = jnp.where(lax.broadcasted_iota(I32, (wide, 1), 0) < width, emb, jnp.zeros_like(emb))
-        for r0, r1 in row_cuts(t, 2):
+        for r0, r1 in row_cuts(t):
             sums = [None] * (wide // 128)
             for q in range(r0, r1, 16):
                 rs = slice(q, q + 16)
@@ -145,7 +158,7 @@
     def _():
         norm_copy.wait()
         parts, rows, cols = out_ref.shape
-        run = rows // 4 if rows % 32 == 0 else rows // 3
+        run = rows // 7
         for r in range(0, rows, run):
             rs = slice(r, r + run)
             total = [jnp.zeros((run, 128), F32)] * 2
@@ -181,7 +194,7 @@
 
 LN_EPS = 1e-5
 CORE, X, Y = 1, 2, 4
-ANY = pl.BlockSpec(memory_space=pl.ANY)
+ANY = pl.BlockSpec(memory_space=pltpu.HBM)
 VMEM = pl.BlockSpec(memory_space=pltpu.VMEM)
 SMEM = pl.BlockSpec(memory_space=pltpu.SMEM)
 DMA = pltpu.SemaphoreType.DMA
@@ -253,6 +266,7 @@
 
 
 BLK = 1280
+LOOPED = ('side',)
 STEPS = {"own": 2, "again": 2, "side": 4, "far": 2, "last": 2, "whole": 8}
 ME, MINE, MINE_ID, TWIN, FAR, FAR_TWIN = range(6)
 
@@ -320,8 +334,10 @@
         for k in range(2):
             ring[k, n_loc:, :] = jnp.zeros((BLK - n_loc, ring.shape[2]), BF16)
     emb_copy.wait()
-    n_cuts = max(1, round(m / 300))
-    cuts = [-(-m * k // (n_cuts * 16)) * 16 for k in range(n_cuts)] + [m]
+    n_groups = 2 if kind in LOOPED and m % 32 == 0 else 1
+    tall = m // n_groups
+    n_cuts = max(1, round(tall / 300))
+    cuts = [-(-tall * k // (n_cuts * 16)) * 16 for k in range(n_cuts)] + [tall]
     cuts = list(zip(cuts[:-1], cuts[1:]))
     kept = lambda i: pltpu.make_async_copy(ring.at[lax.rem(i, 2)], u_hbm.at[device(i)], back_sem.at[lax.rem(i, 2)])
 
@@ -360,17 +376,27 @@
         rel = device(i) ^ me
         lse, lab = info_ref[rel, 0:1, :], info_ref[rel, 1:2, :]
 
-        def weights(r0, r1):
-            part = dot(emb_sc[r0:r1, :], ring[slot], NT)
-            ids = lax.broadcasted_iota(I32, (r1 - r0, 1), 0) + (pos[MINE_ID] + (s0 + r0))
-            g = jnp.exp(part + bias_ref[s0 + r0:s0 + r1, :] - lse) - jnp.where(lab == ids.astype(F32), scale, 0.0)
-            g_sc[r0:r1, :] = g.astype(BF16)
-
-        weights(*cuts[0])
-        for k, (r0, r1) in enumerate(cuts):
-            if k + 1 < len(cuts):
-                weights(*cuts[k + 1])
-            acc[r0:r1, :] += dot(g_sc[r0:r1, :], ring[slot], NN)
+        def group(h):
+            def rows(r0, r1):
+                return slice(r0, r1) if n_groups == 1 else pl.ds(pl.multiple_of(h * tall + r0, 16), r1 - r0)
+
+            def weights(r0, r1):
+                part = dot(emb_sc[rows(r0, r1), :], ring[slot], NT)
+                ids = lax.broadcasted_iota(I32, (r1 - r0, 1), 0) + (pos[MINE_ID] + (s0 + h * tall + r0))
+                bias = bias_ref[slice(s0 + r0, s0 + r1) if n_groups == 1 else pl.ds(pl.multiple_of(s0 + h * tall + r0, 8), r1 - r0), :]
+                g = jnp.exp(part + bias - lse) - jnp.where(lab == ids.astype(F32), scale, 0.0)
+                g_sc[r0:r1, :] = g.astype(BF16)
+
+            weights(*cuts[0])
+            for k, (r0, r1) in enumerate(cuts):
+                if k + 1 < len(cuts):
+                    weights(*cuts[k + 1])
+                acc[rows(r0, r1), :] += dot(g_sc[r0:r1, :], ring[slot], NN)
+
+        if n_groups == 1:
+            group(0)
+        else:
+            pl.loop(0, n_groups)(group)
 
     for c in loads[len(puts):]:
         c.wait()
@@ -537,23 +563,17 @@
         dab_ref[:, cs] = da.astype(BF16).astype(F32)
         for j, x in enumerate((da, d * normed, d)):
             pack_ref[e + j:e + j + 1, cs] = jnp.sum(x, axis=0, keepdims=True)
-    dw = lax.dot_general(z[...], dab_ref[...].astype(BF16), (((0,), (0,)), ((), ())), preferred_element_type=F32)
-    if not extra:
-        pack_ref[:e, :] = dw
-        pack_ref[e + 3:, :] = jnp.zeros_like(pack_ref[e + 3:, :])
-    else:
-        prev, loss_ref, db_ref = extra
-        pack_ref[:e, :] = prev[:e, :] + dw
-        pack_ref[e:e + 3, :] += prev[e:e + 3, :]
-        pack_ref[e + 3:e + 4, :] = loss_ref[...]
-        pack_ref[e + 4:e + 16, :] = jnp.zeros_like(pack_ref[e + 4:e + 16, :])
-        pack_ref[e + 16:, :] = db_ref[...]
+    loss_ref, db_ref = extra
+    pack_ref[:e, :] = lax.dot_general(z[...], dab_ref[...].astype(BF16), (((0,), (0,)), ((), ())), preferred_element_type=F32)
+    pack_ref[e + 3:e + 4, :] = loss_ref[...]
+    pack_ref[e + 4:e + 16, :] = jnp.zeros_like(pack_ref[e + 4:e + 16, :])
+    pack_ref[e + 16:, :] = db_ref[...]
 
 
 def back_pass(base, vp, pre, normed, rstd, z, m1, m2, du, gain, *extra):
     n, cols = du.shape
     e = z.shape[1]
-    n_pack = e + 16 + (extra[2].shape[0] if extra else 0)
+    n_pack = e + 16 + extra[1].shape[0]
     block = lambda *s: pl.BlockSpec(s, lambda i, p: (0,) * len(s))
     gs = pltpu.PrefetchScalarGridSpec(
         num_scalar_prefetch=1,
@@ -574,11 +594,10 @@
 
 
 def spread_kernel(n_masks, vp, pos_ref, w_ref, *refs):
-    pieces, (out_ref, dab, dz, obuf, in_sem, out_sem) = refs[:8], refs[8:]
-    cut, cols = pieces[0].shape
-    n = cut + pieces[4].shape[0]
+    pieces, (out_ref, dab, dz, obuf, in_sem, out_sem) = refs[:4], refs[4:]
+    n, cols = pieces[0].shape
     col = lambda k: pl.ds(pl.multiple_of((vp[0] ^ k) * cols, cols), cols)
-    loads = [pltpu.make_async_copy(p, dab.at[slice(0, cut) if j < 4 else slice(cut, n), col(j % 4)], in_sem.at[j]) for j, p in enumerate(pieces)]
+    loads = [pltpu.make_async_copy(p, dab.at[:, col(j)], in_sem.at[j]) for j, p in enumerate(pieces)]
     for c in loads:
         c.start()
     dz[n:, :] = jnp.zeros((dz.shape[0] - n, dz.shape[1]), F32)
@@ -613,15 +632,14 @@
 
 
 def spread_pass(n_masks, shape, vp, pos, w, pieces):
-    cols = pieces[0].shape[1]
-    n = pieces[0].shape[0] + pieces[4].shape[0]
+    n, cols = pieces[0].shape
     e = w.shape[0]
     return pl.pallas_call(
         functools.partial(spread_kernel, n_masks),
-        in_specs=[SMEM, VMEM, VMEM] + [ANY] * 8,
+        in_specs=[SMEM, VMEM, VMEM] + [ANY] * 4,
         out_specs=ANY,
         out_shape=jax.ShapeDtypeStruct(shape, BF16),
-        scratch_shapes=[pltpu.VMEM((n, 4 * cols), F32), pltpu.VMEM((n + 16, e), F32), pltpu.VMEM((4,) + shape[1:], BF16), DMA((8,)), DMA((4,))],
+        scratch_shapes=[pltpu.VMEM((n, 4 * cols), F32), pltpu.VMEM((n + 16, e), F32), pltpu.VMEM((4,) + shape[1:], BF16), DMA((4,)), DMA((4,))],
         compiler_params=pltpu.CompilerParams(vmem_limit_bytes=VMEM_LIMIT),
         cost_estimate=pl.CostEstimate(flops=(2 * shape[0] * shape[1] * 128 * e) // COVER, bytes_accessed=shape[0] * shape[1] * e * 2, transcendentals=0),
         name="spread",
@@ -673,10 +691,10 @@
 
         flat_labels = labels.reshape(n_loc)
         lab_local = flat_labels - row_start
-        lab_local = jnp.where((lab_local >= 0) & (lab_local < shard_rows), lab_local, -1)
+        lab_local = jnp.where((lab_local >= 0) & (lab_local < shard_rows), lab_local, ELSEWHERE)
         column = lambda x: jnp.broadcast_to(x[:, None], (x.shape[0], 128))
-        lab_cols = column(lab_local[:cut]), column(lab_local[cut:])
-        *logits, stat = stats(u, emb_table, b_vocab[None], column(lab_local), cut)
+        lab_col = column(lab_local)
+        logits, stat = stats(u, emb_table, b_vocab[None], lab_col)
         all_stats = [stat] + [swap_vp(stat, b) for b in range(1, n_shards)]
         global_max = functools.reduce(jnp.maximum, [s[0] for s in all_stats])
         log_norm = global_max + jnp.log(order_sum([s[1] * jnp.exp(s[0] - global_max) for s in all_stats]))
@@ -690,23 +708,15 @@
         d_lo, d_hi = swap(x_lo, Y), swap(y_hi, X)
         cx_lo, cy_hi = swap(x_lo, CORE), swap(y_hi, CORE)
 
-        du_shares, db_parts, sums, before = [], [], [], ()
-        for j, (r0, r1) in enumerate(((0, cut), (cut, n_loc))):
-            lse_col = after(column(lse[r0:r1]), *before)
-            part, db, row_sums = du_pass(scale, n_shards, r0, logits[j], emb_table, lse_col, lab_cols[j], normed, ln_gain[None])
-            du_shares.append(lax.psum_scatter(part.reshape(n_shards * (r1 - r0), cols), "vp", scatter_dimension=0, tiled=True))
-            db_parts.append(db)
-            sums.append(row_sums)
-            before = (part,)
-        du_part = before[0]
-        sums = jnp.concatenate(sums, axis=1)
+        du_part, db_part, sums = du_pass(scale, n_shards, 0, logits, emb_table, column(lse), lab_col, normed, ln_gain[None])
+        du_share = lax.psum_scatter(du_part.reshape(n_shards * n_loc, cols), "vp", scatter_dimension=0, tiled=True)
         sums = [sums] + [swap_vp(sums, b) for b in range(1, n_shards)]
 
         half, quarter = shard_rows // 2, shard_rows // 4
         start = lambda h, c: h * half + c * quarter
         pos = jnp.stack([dp, start(mine, core), row_start + start(mine, core), start(mine, 1 - core), start(1 - mine, core), start(1 - mine, 1 - core)])
         bias_col = lax.dynamic_slice(b_vocab, (start(mine, core),), (quarter,))[:, None]
-        shares = (1280, 1088, 776)
+        shares = (1280, 1216, 648)
         ends = [0]
         for w in shares[:-1]:
             ends.append(ends[-1] + max(16, quarter * w // sum(shares) // 16 * 16))
@@ -733,48 +743,42 @@
         tokens[X], tokens[Y] = (x_lo, x_hi), (y_lo, y_hi)
         info = jnp.concatenate([pair, jnp.stack([away, away_near], axis=1).reshape(6, 2, BLK)])
 
-        du_a, sums = after((du_shares[0], sums), own)
-        sums = order_sum(sums) / width
+        sums = order_sum(after(sums, own)) / width
         m1, m2 = column(sums[0]), column(sums[1])
-        dab_a, pack = back_pass(0, vp[None], pre, normed, rstd, z, m1, m2, du_a, ln_gain[None])
-        dab_a = [dab_a] + [swap_vp(dab_a, b) for b in range(1, n_shards)]
-
-        side, u_all = rows("side", 0, pack, info=info, tokens=tokens, u_all=u_all)
+        side, u_all = rows("side", 0, m2, info=info, tokens=tokens, u_all=u_all)
         d_lo, d_hi = after((d_lo, d_hi), side)
         tokens[X | Y], tokens[X | Y | CORE] = (d_lo, d_hi), (swap(d_lo, CORE), swap(d_hi, CORE))
-
-        du_b = after(du_shares[1], side)
+        chunk0, u_all, big = rows("far", 0, info=info, tokens=tokens, u_all=u_all, parts=((own, 0), (side, 0)))
+        twin0, far0 = send(0, chunk0)
+
+        du_share = after(du_share, chunk0)
         loss_row = jnp.pad(loss_part[None, None], ((0, 0), (0, cols - 1)))
         db_rows = -(-shard_rows // cols // 8) * 8
-        db_mat = jnp.pad((db_parts[0] + db_parts[1])[0], (0, db_rows * cols - shard_rows)).reshape(db_rows, cols)
-        dab_b, pack = back_pass(cut, vp[None], pre, normed, rstd, z, m1, m2, du_b, ln_gain[None], pack, loss_row, db_mat)
-        back_done = dab_b
+        db_mat = jnp.pad(db_part[0], (0, db_rows * cols - shard_rows)).reshape(db_rows, cols)
+        dab, pack = back_pass(0, vp[None], pre, normed, rstd, z, m1, m2, du_share, ln_gain[None], loss_row, db_mat)
+        back_done = dab
         pack = lax.psum(pack, "dp")
-        dab_b = [dab_b] + [swap_vp(dab_b, b) for b in range(1, n_shards)]
-
-        chunk0, u_all, big = rows("far", 0, back_done, info=info, tokens=tokens, u_all=u_all, parts=((own, 0), (side, 0)))
-        twin0, far0 = send(0, chunk0)
-        chunk1, big = rows("whole", 1, info=info, u_all=u_all, big=big)
+        dab = [dab] + [swap_vp(dab, b) for b in range(1, n_shards)]
+
+        chunk1, big = rows("whole", 1, back_done, info=info, u_all=u_all, big=big)
         twin1, far1 = send(1, chunk1)
         pack = after(pack, chunk1)
         n_half = (width + 16) // 2
         part = lax.dynamic_slice(pack, (core * n_half, 0), (n_half, cols))
         parts = [swap_vp(part, b) for b in range(1, n_shards)]
-
-        chunk2, big = rows("whole", 2, part, info=info, u_all=u_all, big=big, puts=[twin0])
+        far0, far_twin0 = forward(0, far0, chunk1)
+
+        chunk2, big = rows("whole", 2, part, info=info, u_all=u_all, big=big, puts=[twin0, far0])
         twin2, far2 = send(2, chunk2)
-        far0, far_twin0 = forward(0, far0, chunk2)
-        d_hidden = spread_pass(n_masks, hidden.shape, vp[None], pos_pad[:, None], w_trans, after(dab_a + dab_b, chunk2))
-        parts = after(parts, d_hidden)
-        others = [swap(p, CORE) for p in parts]
-        big = put_rows(pos, big, [far0, far_twin0, twin1, twin2])
-        far1, far_twin1 = forward(1, far1, big)
-        pack, parts, others = after((pack, parts, others), big)
-        d_w, vec = join_pass(jnp.stack([vp, core]), pack, parts, others)
-        big = put_rows(pos, big, [far1, far_twin1])
+        far1, far_twin1 = forward(1, far1, chunk2)
+        d_hidden = spread_pass(n_masks, hidden.shape, vp[None], pos_pad[:, None], w_trans, after(dab, chunk2))
+        big = put_rows(after(pos, d_hidden), big, [far_twin0, twin1, far1, twin2, far_twin1])
         far2, far_twin2 = forward(2, far2, big)
         big = put_rows(pos, big, [far2])
         big = put_rows(pos, big, [far_twin2])
+        parts = after(parts, far2)
+        others = [swap(p, CORE) for p in parts]
+        d_w, vec = join_pass(jnp.stack([vp, core]), pack, parts, others)
 
         db = pack[width + 16:].reshape(-1)[:shard_rows]
         return pack[width + 3, 0] / n_tokens, d_hidden, d_w, vec[0], vec[1], vec[2], big, db

time: 716 us -> 707 us (0.987)
  the two profiles are of different devices: /device:TPU:9 before, /device:TPU:17 now
where the time goes in v5:
time: 707 us; the launch traced here: 700 us
  Pallas kernels  345 us (49%)
  waiting for transfers between devices  271 us (38%)
  starting transfers between devices  43.4 us (6%)
  local copies, waits for them, and re-layouts  20.4 us (3%)
  between operations  16.4 us (2%)
    pallas_call x5, Pallas kernels, rows_pass(): pl.pallas_call(functools.partial(rows_kernel, kind, scale, s0, m, cut, n_...  186 us
    ppermute x12, waiting for transfers between devices, swap_vp(): return lax.ppermute(a, 'vp', [(d, d ^ bit) for d in range(n_shards)])  159 us
    psum x1, waiting for transfers between devices, local_step(): pack = lax.psum(pack, 'dp')  56.5 us
    ppermute x28, waiting for transfers between devices, swap(): return lax.ppermute(a, 'dp', [(d, d ^ bit) for d in range(n_groups)])  55.6 us
    pallas_call x1, Pallas kernels, du_pass(): pl.pallas_call(functools.partial(du_kernel, v, scale, base), grid=(n,), i...  48 us
    pallas_call x1, Pallas kernels, stats(): pl.pallas_call(functools.partial(stats_kernel, v), grid=(n,), in_specs=[w...  43.8 us
    ppermute x28, starting transfers between devices, swap(): return lax.ppermute(a, 'dp', [(d, d ^ bit) for d in range(n_groups)])  29 us
    pallas_call x3, Pallas kernels, put_rows(): pl.pallas_call(functools.partial(put_kernel, spots), in_specs=[SMEM] + [A...  24.8 us
  transfers between devices with their start and end apart: 45, of which 18 were waited for; matrix products, arithmetic and copies ran while one was open for 3% of the time, Pallas kernels for 46%

profile of v5, /device:TPU:17, one launch (start us, length us, event | category | flops | bytes accessed | tf_op | source)
XLA Modules:
  0.0 699.5 jit_solution(7206786805052392365)
XLA Ops:
  9.0 15.7 %head.1 = (bf16[1232,1024]{1,0:T(8,128)(2,1)}, f32[1232,1024]{1,0:T(8,128)}, f32[1232,1024]{1,0:T(8,128)}, f32[1232,128]{1,0:T(8,128)}, bf16[1232,1024]{1,0:T(8,...) custom-call(bf16[16,512,1024]{2,1,0:T(8,128)(2,1)} %hid.1, s32[16,80,128]{2,1,0:T(8,128)} %broadcast_in_dim.64.pos_ref, ...), custom_call_target="tpu_custom_call" | custom-call | flops 51673824 | bytes 42008576 | tf_op jit(solution)/shard_map/head/pallas_call | solution.py:255
  27.3 43.8 %stats.1 = (f32[1232,12576]{1,0:T(8,128)}, f32[8,1232]{1,0:T(8,128)}) custom-call(bf16[1232,1024]{1,0:T(8,128)(2,1)} %get-tuple-element.69.u_ref, bf16[12576,1024]{1,0:T(8,128)(2,1)} %emb_hbm.9, f32[1,12576]{1,0:T(1,128)} %broadcast_in_dim.68.b_ref, s32[1232,128]{1,0:T(8,128)} %broadcast_in_dim.70.lab_ref), custom_call_target="tpu_custom_call" | custom-call | flops 317309568 | bytes 87730176 | tf_op jit(solution)/shard_map/stats/pallas_call | solution.py:96
  71.1 1.3 collective-permute-start
  72.5 1.3 collective-permute-start.2
  80.5 48.0 %du_pass.1 = (f32[4,1232,256]{2,1,0:T(8,128)}, f32[1,12576]{1,0:T(1,128)}, f32[8,1232]{1,0:T(8,128)}) custom-call(f32[1232,12576]{1,0:T(8,128)} %get-tuple-element.70.logits_ref, bf16[12576,1024]{1,0:T(8,128)(2,1)} %emb_hbm.9, f32[1232,128]{1,0:T(8,128)} %broadcast_in_dim.71.lse_ref, s32[1232,128]{1,0:T(8,128)} %broadcast_in_dim.70.lab_ref, ...), custom_call_target="tpu_custom_call" | custom-call | flops 317309568 | bytes 87730176 | tf_op jit(solution)/shard_map/du_pass/pallas_call | solution.py:182
  128.7 1.9 collective-permute-start.6
  132.7 1.3 collective-permute-done.11
  134.8 1.7 collective-permute-done.12
  138.6 1.7 broadcast_in_dim.79.bias_ref
  142.2 21.9 %shard_map.152 = (f32[1280,1024]{1,0:T(8,128)}, bf16[8,1280,1024]{2,1,0:T(8,128)(2,1)}) custom-call(s32[6]{0:T(128)} %stack.73.pos, bf16[12576,1024]{1,0:T(8,128)(2,1)} %emb_hbm.9, f32[3144,1]{1,0:T(8,128)} %broadcast_in_dim.79.bias_ref, f32[2,2,1280]{2,1,0:T(2,128)} %pad_maximum_fusion.3.info_ref, f32[608,1024]{1,0:T(8,128)} %get-tuple-element.75.refs_0_, ...), custom_call_target="tpu_custom_call" | custom-call | flops 134217728 | bytes 13107200 | tf_op jit(solution)/shard_map/pallas_call | solution.py:456
  164.1 26.5 %collective-permute-done.13 = f32[2,1280]{1,0:T(2,128)S(1)} collective-permute-done((f32[2,1280]{1,0:T(2,128)S(1)}, f32[2,1280]{1,0:T(2,128)S(1)}, u32[]{:S(2)}, u32[]{:S(2)}) %collective-permute-start.13) | collective-permute-done | bytes 10272 | tf_op jit(solution)/shard_map/ppermute | solution.py:661
  190.5 4.1 collective-permute-start.21
  194.6 1.8 collective-permute-start.3
  198.3 1.3 collective-permute-done.3
  199.6 1.3 collective-permute-start.18
  201.7 1.3 collective-permute-start.20
  203.0 1.7 collective-permute-done.5
  204.7 1.4 collective-permute-start.14
  206.1 1.7 collective-permute-done.14
  210.4 2.4 collective-permute-done.19.refs_2_
  212.9 37.9 %shard_map.153 = (f32[1280,1024]{1,0:T(8,128)}, bf16[8,1280,1024]{2,1,0:T(8,128)(2,1)}) custom-call(s32[6]{0:T(128)} %stack.73.pos, bf16[12576,1024]{1,0:T(8,128)(2,1)} %emb_hbm.9, f32[3144,1]{1,0:T(8,128)} %broadcast_in_dim.79.bias_ref, f32[8,2,1280]{2,1,0:T(2,128)} %pad_maximum_fusion.info_ref, ...), custom_call_target="tpu_custom_call", output_to_operand_aliasing={{1}: (12, {})} | custom-call | flops 268435456 | bytes 18350080 | tf_op jit(solution)/shard_map/pallas_call | solution.py:456
  250.8 13.2 %collective-permute-done.17.refs_0_ = f32[608,1024]{1,0:T(8,128)} collective-permute-done((f32[608,1024]{1,0:T(8,128)}, f32[608,1024]{1,0:T(8,128)}, u32[]{:S(2)}, u32[]{:S(2)}) %collective-permute-start.17) | collective-permute-done | bytes 2490400 | tf_op jit(solution)/shard_map/ppermute | solution.py:661
  265.0 7.9 %collective-permute-done.23.refs_2_ = f32[608,1024]{1,0:T(8,128)S(1)} collective-permute-done((f32[608,1024]{1,0:T(8,128)}, f32[608,1024]{1,0:T(8,128)S(1)}, u32[]{:S(2)}, u32[]{:S(2)}) %collective-permute-start.23) | collective-permute-done | bytes 2490400 | tf_op jit(solution)/shard_map/ppermute | solution.py:661
  273.0 1.6 copy-done.4
  274.6 1.4 copy-done.3
  276.0 24.3 %shard_map.154 = (f32[1280,1024]{1,0:T(8,128)}, bf16[8,1280,1024]{2,1,0:T(8,128)(2,1)}, f32[12576,1024]{1,0:T(8,128)}) custom-call(s32[6]{0:T(128)} %stack.73.pos, bf16[12576,1024]{1,0:T(8,128)(2,1)} %emb_hbm.9, f32[3144,1]{1,0:T(8,128)} %broadcast_in_dim.79.bias_ref, f32[8,2,1280]{2,1,0:T(2,128)} %pad_maximum_fusion.info_ref, ...), custom_call_target="tpu_custom_call", output_to_operand_aliasing={{1}: (8, {})} | custom-call | flops 134217728 | bytes 13107200 | tf_op jit(solution)/shard_map/pallas_call | solution.py:456
  300.8 1.5 collective-permute-start.28
  305.3 7.2 %back.1 = (f32[1232,256]{1,0:T(8,128)}, f32[1096,256]{1,0:T(8,128)}) custom-call(s32[1]{0:T(128)} %bitcast.vp, f32[1232,1024]{1,0:T(8,128)} %get-tuple-element.65.refs_0_, f32[1232,1024]{1,0:T(8,128)} %get-tuple-element.66.norm_hbm.refs_1_, f32[1232,128]{1,0:T(8,128)} %get-tuple-element.67.refs_2_, bf16[1232,1024]{1,0:T(8,128)(2,1)} %get-tuple-element.68.refs_3_, ...), custom_call_target="tpu_custom_call" | custom-call | flops 6459228 | bytes 9461760 | tf_op jit(solution)/shard_map/back/pallas_call | solution.py:586
  312.5 63.6 %shard_map.155 = (f32[1216,1024]{1,0:T(8,128)}, f32[12576,1024]{1,0:T(8,128)}) custom-call(s32[6]{0:T(128)} %stack.73.pos, bf16[12576,1024]{1,0:T(8,128)(2,1)} %emb_hbm.9, f32[3144,1]{1,0:T(8,128)} %broadcast_in_dim.79.bias_ref, f32[8,2,1280]{2,1,0:T(2,128)} %pad_maximum_fusion.info_ref, ...), custom_call_target="tpu_custom_call", output_to_operand_aliasing={{1}: (5, {})} | custom-call | flops 510027360 | bytes 28442624 | tf_op jit(solution)/shard_map/pallas_call | solution.py:456
  376.8 1.8 collective-permute-start.25
  379.3 56.5 %all-reduce.7.cloned.1.call-done.refs_0_ = f32[1096,256]{1,0:T(8,128)} async-done(((f32[1096,256]{1,0:T(8,128)}), f32[1096,256]{1,0:T(8,128)}) %all-reduce.7.cloned.1.call-update) | async-done | bytes 1122320 | tf_op jit(solution)/shard_map/psum | solution.py:760
  435.8 1.9 constant_dynamic-slice_fusion
  437.7 38.0 %shard_map.156 = (f32[648,1024]{1,0:T(8,128)}, f32[12576,1024]{1,0:T(8,128)}) custom-call(s32[6]{0:T(128)} %stack.73.pos, bf16[12576,1024]{1,0:T(8,128)(2,1)} %emb_hbm.9, f32[3144,1]{1,0:T(8,128)} %broadcast_in_dim.79.bias_ref, f32[8,2,1280]{2,1,0:T(2,128)} %pad_maximum_fusion.info_ref, ...), custom_call_target="tpu_custom_call", output_to_operand_aliasing={{1}: (5, {})} | custom-call | flops 271790912 | bytes 24952832 | tf_op jit(solution)/shard_map/pallas_call | solution.py:456
  475.6 1.5 collective-permute-start.38
  477.4 2.1 collective-permute-start.27
  479.5 78.9 %collective-permute-done.26.refs_2_ = f32[1232,256]{1,0:T(8,128)S(1)} collective-permute-done((f32[1232,256]{1,0:T(8,128)S(1)}, f32[1232,256]{1,0:T(8,128)S(1)}, u32[]{:S(2)}, u32[]{:S(2)}) %collective-permute-start.26) | collective-permute-done | bytes 1261600 | tf_op jit(solution)/shard_map/ppermute | solution.py:664
  558.4 1.5 collective-permute-start.37
  559.9 28.9 %collective-permute-done.27.refs_3_ = f32[1232,256]{1,0:T(8,128)S(1)} collective-permute-done((f32[1232,256]{1,0:T(8,128)S(1)}, f32[1232,256]{1,0:T(8,128)S(1)}, u32[]{:S(2)}, u32[]{:S(2)}) %collective-permute-start.27) | collective-permute-done | bytes 1261600 | tf_op jit(solution)/shard_map/ppermute | solution.py:664
  589.9 14.7 %spread.1 = bf16[16,512,1024]{2,1,0:T(8,128)(2,1)} custom-call(s32[1]{0:T(128)} %bitcast.vp, s32[16,1,80]{2,1,0:T(1,128)} %bitcast.34, bf16[1024,1024]{1,0:T(8,128)(2,1)} %w_ref.3, f32[1232,256]{1,0:T(8,128)} %get-tuple-element.109.refs_0_, f32[1232,256]{1,0:T(8,128)} %copy-done.6, f32[1232,256]{1,0:T(8,128)} %copy-done.7, f32[1232,256]{1,0:T(8,128)} %copy-done.8), custom_call_target="tpu_custom_call" | custom-call | flops 21474836 | bytes 16777216 | tf_op jit(solution)/shard_map/spread/pallas_call | solution.py:637
  604.7 17.0 %put_rows.3.refs_0_ = f32[12576,1024]{1,0:T(8,128)} custom-call(s32[6]{0:T(128)} %stack.73.pos, f32[12576,1024]{1,0:T(8,128)} %get-tuple-element.114.refs_0_, f32[1280,1024]{1,0:T(8,128)} %collective-permute-done.34.refs_1_, f32[1216,1024]{1,0:T(8,128)} %collective-permute-done.35.refs_2_, ...), custom_call_target="tpu_custom_call", output_to_operand_aliasing={{}: (1, {})} | custom-call | flops 57098 | bytes 45678592 | tf_op jit(solution)/shard_map/put_rows/pallas_call | solution.py:489
  622.8 2.1 collective-permute-start.32
  624.9 18.7 %collective-permute-done.30.refs_1_ = f32[520,256]{1,0:T(8,128)S(1)} collective-permute-done((f32[520,256]{1,0:T(8,128)}, f32[520,256]{1,0:T(8,128)S(1)}, u32[]{:S(2)}, u32[]{:S(2)}) %collective-permute-start.30) | collective-permute-done | bytes 532512 | tf_op jit(solution)/shard_map/ppermute | solution.py:664
  643.6 3.0 collective-permute-done.31.refs_2_
  646.6 24.8 %collective-permute-done.32.refs_3_ = f32[520,256]{1,0:T(8,128)} collective-permute-done((f32[520,256]{1,0:T(8,128)}, f32[520,256]{1,0:T(8,128)}, u32[]{:S(2)}, u32[]{:S(2)}) %collective-permute-start.32) | collective-permute-done | bytes 532512 | tf_op jit(solution)/shard_map/ppermute | solution.py:664
  677.0 3.9 put_rows.4.refs_0_
  681.0 4.9 join.1
  686.0 1.5 fusion.3
  687.4 3.9 put_rows.5
  (131 shorter events, 36.9 us)
Async XLA Ops:
  7.2 297.1 %reduce-scatter.2.cloned.1.call-start = ((), (), s32[]{:S(2)}) async-start(), calls=%async_computation.1 | async-start | bytes 6307840 | tf_op jit(solution)/shard_map/reduce_scatter | solution.py:712
  24.7 112.6 %collective-permute-start.7 = (f32[608,1024]{1,0:T(8,128)}, f32[608,1024]{1,0:T(8,128)}, u32[]{:S(2)}, u32[]{:S(2)}) collective-permute-start(f32[608,1024]{1,0:T(8,128)} %get-tuple-element.75.refs_0_), channel_id=1, source_target_pairs={{0,1},{1,0},{2,3},{3,2},{4,5},{5,4},{6,7},{7,6},{8,9},{9,8},{10,11... | collective-permute-start | bytes 7471112 | tf_op jit(solution)/shard_map/ppermute | solution.py:661
  71.1 3.5 collective-permute-start
  72.4 4.1 collective-permute-start.1
  72.5 5.3 collective-permute-start.2
  73.8 67.8 %collective-permute-start.8 = (f32[624,1024]{1,0:T(8,128)S(1)}, f32[624,1024]{1,0:T(8,128)}, u32[]{:S(2)}, u32[]{:S(2)}) collective-permute-start(f32[624,1024]{1,0:T(8,128)S(1)} %copy-done.1), channel_id=1, source_target_pairs={{0,1},{1,0},{2,3},{3,2},{4,5},{5,4},{6,7},{7,6},{8,9},{9,8},{10,11... | collective-permute-start | bytes 7667720 | tf_op jit(solution)/shard_map/ppermute | solution.py:661
  74.7 115.9 %collective-permute-start.9 = (f32[624,1024]{1,0:T(8,128)S(1)}, f32[624,1024]{1,0:T(8,128)}, u32[]{:S(2)}, u32[]{:S(2)}) collective-permute-start(f32[624,1024]{1,0:T(8,128)S(1)} %copy-done.1), channel_id=1, source_target_pairs={{0,2},{1,3},{2,0},{3,1},{4,6},{5,7},{6,4},{7,5},{8,10},{9,11},{10,... | collective-permute-start | bytes 7667720 | tf_op jit(solution)/shard_map/ppermute | solution.py:661
  76.5 114.1 %collective-permute-start.10 = (f32[608,1024]{1,0:T(8,128)}, f32[608,1024]{1,0:T(8,128)}, u32[]{:S(2)}, u32[]{:S(2)}) collective-permute-start(f32[608,1024]{1,0:T(8,128)} %get-tuple-element.75.refs_0_), channel_id=1, source_target_pairs={{0,4},{1,5},{2,6},{3,7},{4,0},{5,1},{6,2},{7,3},{8,12},{9,13},{10,... | collective-permute-start | bytes 7471112 | tf_op jit(solution)/shard_map/ppermute | solution.py:661
  128.5 307.2 %all-reduce.7.cloned.1.call-start = ((), (), s32[]{:S(2)}) async-start(), calls=%async_computation.2 | async-start | bytes 2244608 | tf_op jit(solution)/shard_map/psum | solution.py:760
  128.7 2.7 collective-permute-start.6
  131.5 2.5 collective-permute-start.11
  134.0 2.5 collective-permute-start.12
  136.5 61.1 %collective-permute-start.16 = (f32[624,1024]{1,0:T(8,128)S(1)}, f32[624,1024]{1,0:T(8,128)}, u32[]{:S(2)}, u32[]{:S(2)}) collective-permute-start(f32[624,1024]{1,0:T(8,128)S(1)} %copy-done.1), channel_id=1, source_target_pairs={{0,4},{1,5},{2,6},{3,7},{4,0},{5,1},{6,2},{7,3},{8,12},{9,13},{10,... | collective-permute-start | bytes 7667720 | tf_op jit(solution)/shard_map/ppermute | solution.py:661
  137.3 59.1 %collective-permute-start.15 = (f32[608,1024]{1,0:T(8,128)}, f32[608,1024]{1,0:T(8,128)}, u32[]{:S(2)}, u32[]{:S(2)}) collective-permute-start(f32[608,1024]{1,0:T(8,128)} %get-tuple-element.75.refs_0_), channel_id=1, source_target_pairs={{0,2},{1,3},{2,0},{3,1},{4,6},{5,7},{6,4},{7,5},{8,10},{9,11},{10,... | collective-permute-start | bytes 7471112 | tf_op jit(solution)/shard_map/ppermute | solution.py:661
  141.6 49.0 %collective-permute-start.13 = (f32[2,1280]{1,0:T(2,128)S(1)}, f32[2,1280]{1,0:T(2,128)S(1)}, u32[]{:S(2)}, u32[]{:S(2)}) collective-permute-start(f32[2,1280]{1,0:T(2,128)S(1)} %get-tuple-element.139), channel_id=1, source_target_pairs={{0,6},{1,7},{2,4},{3,5},{4,2},{5,3},{6,0},{7,1},{8,14},{9,15},{10,... | collective-permute-start | bytes 30728 | tf_op jit(solution)/shard_map/ppermute | solution.py:661
  190.5 17.6 %collective-permute-start.21 = (f32[608,1024]{1,0:T(8,128)}, f32[608,1024]{1,0:T(8,128)}, u32[]{:S(2)}, u32[]{:S(2)}) collective-permute-start(f32[608,1024]{1,0:T(8,128)} %collective-permute-done.10.refs_4_), channel_id=1, source_target_pairs={{0,1},{1,0},{2,3},{3,2},{4,5},{5,4},{6,7},{7,6},{8,9},{9,8},{10,11... | collective-permute-start | bytes 7471112 | tf_op jit(solution)/shard_map/ppermute | solution.py:661
  194.6 5.0 collective-permute-start.3
  196.4 5.3 collective-permute-start.4
  196.4 8.3 %collective-permute-start.5 = (f32[8,1232]{1,0:T(8,128)S(1)}, f32[8,1232]{1,0:T(8,128)S(1)}, u32[]{:S(2)}, u32[]{:S(2)}) collective-permute-start(f32[8,1232]{1,0:T(8,128)S(1)} %copy-done.14), channel_id=1, source_target_pairs={{0,24},{8,16},{16,8},{24,0},{1,25},{9,17},{17,9},{25,1},{2,26},{10... | collective-permute-start | bytes 118280 | tf_op jit(solution)/shard_map/ppermute | solution.py:664
  197.6 15.2 %collective-permute-start.22 = (f32[624,1024]{1,0:T(8,128)}, f32[624,1024]{1,0:T(8,128)}, u32[]{:S(2)}, u32[]{:S(2)}) collective-permute-start(f32[624,1024]{1,0:T(8,128)} %collective-permute-done.16.refs_5_), channel_id=1, source_target_pairs={{0,1},{1,0},{2,3},{3,2},{4,5},{5,4},{6,7},{7,6},{8,9},{9,8},{10,11... | collective-permute-start | bytes 7667720 | tf_op jit(solution)/shard_map/ppermute | solution.py:661
  199.6 64.3 %collective-permute-start.18 = (f32[624,1024]{1,0:T(8,128)}, f32[624,1024]{1,0:T(8,128)S(1)}, u32[]{:S(2)}, u32[]{:S(2)}) collective-permute-start(f32[624,1024]{1,0:T(8,128)} %collective-permute-done.16.refs_5_), channel_id=1, source_target_pairs={{0,2},{1,3},{2,0},{3,1},{4,6},{5,7},{6,4},{7,5},{8,10},{9,11},{10,... | collective-permute-start | bytes 7667720 | tf_op jit(solution)/shard_map/ppermute | solution.py:661
  201.7 11.2 %collective-permute-start.20 = (f32[624,1024]{1,0:T(8,128)}, f32[624,1024]{1,0:T(8,128)}, u32[]{:S(2)}, u32[]{:S(2)}) collective-permute-start(f32[624,1024]{1,0:T(8,128)} %collective-permute-done.9.refs_1_), channel_id=1, source_target_pairs={{0,1},{1,0},{2,3},{3,2},{4,5},{5,4},{6,7},{7,6},{8,9},{9,8},{10,11... | collective-permute-start | bytes 7667720 | tf_op jit(solution)/shard_map/ppermute | solution.py:661
  204.7 3.1 collective-permute-start.14
  207.8 5.1 collective-permute-start.19
  208.2 55.8 %collective-permute-start.17 = (f32[608,1024]{1,0:T(8,128)}, f32[608,1024]{1,0:T(8,128)}, u32[]{:S(2)}, u32[]{:S(2)}) collective-permute-start(f32[608,1024]{1,0:T(8,128)} %collective-permute-done.15.refs_0_), channel_id=1, source_target_pairs={{0,4},{1,5},{2,6},{3,7},{4,0},{5,1},{6,2},{7,3},{8,12},{9,13},{10,... | collective-permute-start | bytes 7471112 | tf_op jit(solution)/shard_map/ppermute | solution.py:661
  264.0 9.0 %collective-permute-start.24 = (f32[624,1024]{1,0:T(8,128)S(1)}, f32[624,1024]{1,0:T(8,128)S(1)}, u32[]{:S(2)}, u32[]{:S(2)}) collective-permute-start(f32[624,1024]{1,0:T(8,128)S(1)} %collective-permute-done.18.refs_1_), channel_id=1, source_target_pairs={{0,1},{1,0},{2,3},{3,2},{4,5},{5,4},{6,7},{7,6},{8,9},{9,8},{10,11... | collective-permute-start | bytes 7667720 | tf_op jit(solution)/shard_map/ppermute | solution.py:661
  265.0 8.0 %collective-permute-start.23 = (f32[608,1024]{1,0:T(8,128)}, f32[608,1024]{1,0:T(8,128)S(1)}, u32[]{:S(2)}, u32[]{:S(2)}) collective-permute-start(f32[608,1024]{1,0:T(8,128)} %collective-permute-done.17.refs_0_), channel_id=1, source_target_pairs={{0,1},{1,0},{2,3},{3,2},{4,5},{5,4},{6,7},{7,6},{8,9},{9,8},{10,11... | collective-permute-start | bytes 7471112 | tf_op jit(solution)/shard_map/ppermute | solution.py:661
  300.4 76.3 %collective-permute-start.29 = (f32[1280,1024]{1,0:T(8,128)}, f32[1280,1024]{1,0:T(8,128)}, u32[]{:S(2)}, u32[]{:S(2)}) collective-permute-start(f32[1280,1024]{1,0:T(8,128)} %get-tuple-element.95), channel_id=1, source_target_pairs={{0,2},{1,5},{2,0},{3,7},{4,6},{5,1},{6,4},{7,3},{8,10},{9,13},{10,... | collective-permute-start | bytes 15728648 | tf_op jit(solution)/shard_map/ppermute | solution.py:667
  300.8 136.8 %collective-permute-start.28 = (f32[1280,1024]{1,0:T(8,128)}, f32[1280,1024]{1,0:T(8,128)}, u32[]{:S(2)}, u32[]{:S(2)}) collective-permute-start(f32[1280,1024]{1,0:T(8,128)} %get-tuple-element.95), channel_id=1, source_target_pairs={{0,1},{1,0},{2,3},{3,2},{4,5},{5,4},{6,7},{7,6},{8,9},{9,8},{10,11... | collective-permute-start | bytes 15728648 | tf_op jit(solution)/shard_map/ppermute | solution.py:661
  312.5 64.3 %copy-start.5 = (f32[1232,256]{1,0:T(8,128)S(1)}, f32[1232,256]{1,0:T(8,128)}, u32[]{:S(2)}) copy-start(f32[1232,256]{1,0:T(8,128)} %get-tuple-element.109.refs_0_) | copy-start | bytes 3784708
  376.1 99.5 %collective-permute-start.36 = (f32[1216,1024]{1,0:T(8,128)}, f32[1216,1024]{1,0:T(8,128)}, u32[]{:S(2)}, u32[]{:S(2)}) collective-permute-start(f32[1216,1024]{1,0:T(8,128)} %get-tuple-element.103), channel_id=1, source_target_pairs={{0,2},{1,5},{2,0},{3,7},{4,6},{5,1},{6,4},{7,3},{8,10},{9,13},{10,... | collective-permute-start | bytes 14942216 | tf_op jit(solution)/shard_map/ppermute | solution.py:667
  376.6 228.0 %collective-permute-start.34 = (f32[1280,1024]{1,0:T(8,128)}, f32[1280,1024]{1,0:T(8,128)}, u32[]{:S(2)}, u32[]{:S(2)}) collective-permute-start(f32[1280,1024]{1,0:T(8,128)} %collective-permute-done.29.refs_3_), channel_id=1, source_target_pairs={{0,1},{1,0},{2,3},{3,2},{4,5},{5,4},{6,7},{7,6},{8,9},{9,8},{10,11... | collective-permute-start | bytes 15728648 | tf_op jit(solution)/shard_map/ppermute | solution.py:661
  376.8 100.5 %collective-permute-start.25 = (f32[1232,256]{1,0:T(8,128)S(1)}, f32[1232,256]{1,0:T(8,128)S(1)}, u32[]{:S(2)}, u32[]{:S(2)}) collective-permute-start(f32[1232,256]{1,0:T(8,128)S(1)} %copy-done.5), channel_id=1, source_target_pairs={{0,8},{8,0},{16,24},{24,16},{1,9},{9,1},{17,25},{25,17},{2,10},{10... | collective-permute-start | bytes 3784712 | tf_op jit(solution)/shard_map/ppermute | solution.py:664
  378.6 226.0 %collective-permute-start.35 = (f32[1216,1024]{1,0:T(8,128)}, f32[1216,1024]{1,0:T(8,128)}, u32[]{:S(2)}, u32[]{:S(2)}) collective-permute-start(f32[1216,1024]{1,0:T(8,128)} %get-tuple-element.103), channel_id=1, source_target_pairs={{0,1},{1,0},{2,3},{3,2},{4,5},{5,4},{6,7},{7,6},{8,9},{9,8},{10,11... | collective-permute-start | bytes 14942216 | tf_op jit(solution)/shard_map/ppermute | solution.py:661
  475.6 129.0 %collective-permute-start.38 = (f32[1216,1024]{1,0:T(8,128)}, f32[1216,1024]{1,0:T(8,128)}, u32[]{:S(2)}, u32[]{:S(2)}) collective-permute-start(f32[1216,1024]{1,0:T(8,128)} %collective-permute-done.36.refs_3_), channel_id=1, source_target_pairs={{0,1},{1,0},{2,3},{3,2},{4,5},{5,4},{6,7},{7,6},{8,9},{9,8},{10,11... | collective-permute-start | bytes 14942216 | tf_op jit(solution)/shard_map/ppermute | solution.py:661
  477.1 81.3 %collective-permute-start.26 = (f32[1232,256]{1,0:T(8,128)S(1)}, f32[1232,256]{1,0:T(8,128)S(1)}, u32[]{:S(2)}, u32[]{:S(2)}) collective-permute-start(f32[1232,256]{1,0:T(8,128)S(1)} %copy-done.5), channel_id=1, source_target_pairs={{0,16},{8,24},{16,0},{24,8},{1,17},{9,25},{17,1},{25,9},{2,18},{10... | collective-permute-start | bytes 3784712 | tf_op jit(solution)/shard_map/ppermute | solution.py:664
  477.4 82.5 %copy-start.6 = (f32[1232,256]{1,0:T(8,128)}, f32[1232,256]{1,0:T(8,128)S(1)}, u32[]{:S(2)}) copy-start(f32[1232,256]{1,0:T(8,128)S(1)} %collective-permute-done.25.refs_1_) | copy-start | bytes 3784708
  477.4 111.5 %collective-permute-start.27 = (f32[1232,256]{1,0:T(8,128)S(1)}, f32[1232,256]{1,0:T(8,128)S(1)}, u32[]{:S(2)}, u32[]{:S(2)}) collective-permute-start(f32[1232,256]{1,0:T(8,128)S(1)} %copy-done.5), channel_id=1, source_target_pairs={{0,24},{8,16},{16,8},{24,0},{1,25},{9,17},{17,9},{25,1},{2,26},{10... | collective-permute-start | bytes 3784712 | tf_op jit(solution)/shard_map/ppermute | solution.py:664
  558.4 46.2 %collective-permute-start.37 = (f32[648,1024]{1,0:T(8,128)}, f32[648,1024]{1,0:T(8,128)}, u32[]{:S(2)}, u32[]{:S(2)}) collective-permute-start(f32[648,1024]{1,0:T(8,128)} %get-tuple-element.108), channel_id=1, source_target_pairs={{0,1},{1,0},{2,3},{3,2},{4,5},{5,4},{6,7},{7,6},{8,9},{9,8},{10,11... | collective-permute-start | bytes 7962632 | tf_op jit(solution)/shard_map/ppermute | solution.py:661
  588.8 32.8 %collective-permute-start.33 = (f32[648,1024]{1,0:T(8,128)}, f32[648,1024]{1,0:T(8,128)S(1)}, u32[]{:S(2)}, u32[]{:S(2)}) collective-permute-start(f32[648,1024]{1,0:T(8,128)} %get-tuple-element.108), channel_id=1, source_target_pairs={{0,2},{1,5},{2,0},{3,7},{4,6},{5,1},{6,4},{7,3},{8,10},{9,13},{10,... | collective-permute-start | bytes 7962632 | tf_op jit(solution)/shard_map/ppermute | solution.py:667
  621.7 55.4 %copy-start = (f32[648,1024]{1,0:T(8,128)}, f32[648,1024]{1,0:T(8,128)S(1)}, u32[]{:S(2)}) copy-start(f32[648,1024]{1,0:T(8,128)S(1)} %collective-permute-done.33.refs_1_) | copy-start | bytes 7962628
  621.7 65.8 %collective-permute-start.42 = (f32[648,1024]{1,0:T(8,128)S(1)}, f32[648,1024]{1,0:T(8,128)}, u32[]{:S(2)}, u32[]{:S(2)}) collective-permute-start(f32[648,1024]{1,0:T(8,128)S(1)} %collective-permute-done.33.refs_1_), channel_id=1, source_target_pairs={{0,1},{1,0},{2,3},{3,2},{4,5},{5,4},{6,7},{7,6},{8,9},{9,8},{10,11... | collective-permute-start | bytes 7962632 | tf_op jit(solution)/shard_map/ppermute | solution.py:661
  622.3 21.3 %collective-permute-start.30 = (f32[520,256]{1,0:T(8,128)}, f32[520,256]{1,0:T(8,128)S(1)}, u32[]{:S(2)}, u32[]{:S(2)}) collective-permute-start(f32[520,256]{1,0:T(8,128)} %constant_dynamic-slice_fusion), channel_id=1, source_target_pairs={{0,8},{8,0},{16,24},{24,16},{1,9},{9,1},{17,25},{25,17},{2,10},{10... | collective-permute-start | bytes 1597448 | tf_op jit(solution)/shard_map/ppermute | solution.py:664
  622.3 24.3 %collective-permute-start.31 = (f32[520,256]{1,0:T(8,128)}, f32[520,256]{1,0:T(8,128)S(1)}, u32[]{:S(2)}, u32[]{:S(2)}) collective-permute-start(f32[520,256]{1,0:T(8,128)} %constant_dynamic-slice_fusion), channel_id=1, source_target_pairs={{0,16},{8,24},{16,0},{24,8},{1,17},{9,25},{17,1},{25,9},{2,18},{10... | collective-permute-start | bytes 1597448 | tf_op jit(solution)/shard_map/ppermute | solution.py:664
  622.8 48.5 %collective-permute-start.32 = (f32[520,256]{1,0:T(8,128)}, f32[520,256]{1,0:T(8,128)}, u32[]{:S(2)}, u32[]{:S(2)}) collective-permute-start(f32[520,256]{1,0:T(8,128)} %constant_dynamic-slice_fusion), channel_id=1, source_target_pairs={{0,24},{8,16},{16,8},{24,0},{1,25},{9,17},{17,9},{25,1},{2,26},{10... | collective-permute-start | bytes 1597448 | tf_op jit(solution)/shard_map/ppermute | solution.py:664
  671.4 9.6 %collective-permute-start.39 = (f32[520,256]{1,0:T(8,128)S(1)}, f32[520,256]{1,0:T(8,128)}, u32[]{:S(2)}, u32[]{:S(2)}) collective-permute-start(f32[520,256]{1,0:T(8,128)S(1)} %collective-permute-done.30.refs_1_), channel_id=1, source_target_pairs={{0,1},{1,0},{2,3},{3,2},{4,5},{5,4},{6,7},{7,6},{8,9},{9,8},{10,11... | collective-permute-start | bytes 1597448 | tf_op jit(solution)/shard_map/ppermute | solution.py:661
  672.6 8.4 %collective-permute-start.40 = (f32[520,256]{1,0:T(8,128)S(1)}, f32[520,256]{1,0:T(8,128)}, u32[]{:S(2)}, u32[]{:S(2)}) collective-permute-start(f32[520,256]{1,0:T(8,128)S(1)} %collective-permute-done.31.refs_2_), channel_id=1, source_target_pairs={{0,1},{1,0},{2,3},{3,2},{4,5},{5,4},{6,7},{7,6},{8,9},{9,8},{10,11... | collective-permute-start | bytes 1597448 | tf_op jit(solution)/shard_map/ppermute | solution.py:661
  672.6 8.4 %collective-permute-start.41 = (f32[520,256]{1,0:T(8,128)}, f32[520,256]{1,0:T(8,128)}, u32[]{:S(2)}, u32[]{:S(2)}) collective-permute-start(f32[520,256]{1,0:T(8,128)} %collective-permute-done.32.refs_3_), channel_id=1, source_target_pairs={{0,1},{1,0},{2,3},{3,2},{4,5},{5,4},{6,7},{7,6},{8,9},{9,8},{10,11... | collective-permute-start | bytes 1597448 | tf_op jit(solution)/shard_map/ppermute | solution.py:661
  (13 other events, 278.3 us)
Sparse Core Ops, SparseCore 0:
  128.6 95.4 reduce-scatter.1
  376.7 58.9 all-reduce.6

commit v6 on v5

--- a/solution.py
+++ b/solution.py
@@ -701,22 +701,23 @@
         loss_part = jnp.sum(log_norm - order_sum([s[2] for s in all_stats]))
         lse = log_norm + jnp.log(jnp.float32(n_tokens))
 
+        du_part, db_part, sums = du_pass(scale, n_shards, 0, logits, emb_table, column(lse), lab_col, normed, ln_gain[None])
+        du_share = lax.psum_scatter(du_part.reshape(n_shards * n_loc, cols), "vp", scatter_dimension=0, tiled=True)
+        lse = after(lse, du_part)
         fill = (0, BLK - n_loc)
         info = jnp.stack([jnp.pad(lse, fill, constant_values=jnp.inf), jnp.pad(flat_labels.astype(F32), fill, constant_values=-1.0)])
         near, *away = [swap(info, b) for b in (CORE, X, Y, X | Y)]
-        x_lo, y_hi = after((x_lo, y_hi), stat)
+        x_lo, y_hi = after((x_lo, y_hi), du_part)
         d_lo, d_hi = swap(x_lo, Y), swap(y_hi, X)
         cx_lo, cy_hi = swap(x_lo, CORE), swap(y_hi, CORE)
 
-        du_part, db_part, sums = du_pass(scale, n_shards, 0, logits, emb_table, column(lse), lab_col, normed, ln_gain[None])
-        du_share = lax.psum_scatter(du_part.reshape(n_shards * n_loc, cols), "vp", scatter_dimension=0, tiled=True)
         sums = [sums] + [swap_vp(sums, b) for b in range(1, n_shards)]
 
         half, quarter = shard_rows // 2, shard_rows // 4
         start = lambda h, c: h * half + c * quarter
         pos = jnp.stack([dp, start(mine, core), row_start + start(mine, core), start(mine, 1 - core), start(1 - mine, core), start(1 - mine, 1 - core)])
         bias_col = lax.dynamic_slice(b_vocab, (start(mine, core),), (quarter,))[:, None]
-        shares = (1280, 1216, 648)
+        shares = (1280, 1088, 776)
         ends = [0]
         for w in shares[:-1]:
             ends.append(ends[-1] + max(16, quarter * w // sum(shares) // 16 * 16))
@@ -748,10 +749,7 @@
         side, u_all = rows("side", 0, m2, info=info, tokens=tokens, u_all=u_all)
         d_lo, d_hi = after((d_lo, d_hi), side)
         tokens[X | Y], tokens[X | Y | CORE] = (d_lo, d_hi), (swap(d_lo, CORE), swap(d_hi, CORE))
-        chunk0, u_all, big = rows("far", 0, info=info, tokens=tokens, u_all=u_all, parts=((own, 0), (side, 0)))
-        twin0, far0 = send(0, chunk0)
-
-        du_share = after(du_share, chunk0)
+        du_share = after(du_share, side)
         loss_row = jnp.pad(loss_part[None, None], ((0, 0), (0, cols - 1)))
         db_rows = -(-shard_rows // cols // 8) * 8
         db_mat = jnp.pad(db_part[0], (0, db_rows * cols - shard_rows)).reshape(db_rows, cols)
@@ -760,7 +758,9 @@
         pack = lax.psum(pack, "dp")
         dab = [dab] + [swap_vp(dab, b) for b in range(1, n_shards)]
 
-        chunk1, big = rows("whole", 1, back_done, info=info, u_all=u_all, big=big)
+        chunk0, u_all, big = rows("far", 0, back_done, info=info, tokens=tokens, u_all=u_all, parts=((own, 0), (side, 0)))
+        twin0, far0 = send(0, chunk0)
+        chunk1, big = rows("whole", 1, info=info, u_all=u_all, big=big)
         twin1, far1 = send(1, chunk1)
         pack = after(pack, chunk1)
         n_half = (width + 16) // 2
@@ -770,18 +770,22 @@
 
         chunk2, big = rows("whole", 2, part, info=info, u_all=u_all, big=big, puts=[twin0, far0])
         twin2, far2 = send(2, chunk2)
-        far1, far_twin1 = forward(1, far1, chunk2)
         d_hidden = spread_pass(n_masks, hidden.shape, vp[None], pos_pad[:, None], w_trans, after(dab, chunk2))
-        big = put_rows(after(pos, d_hidden), big, [far_twin0, twin1, far1, twin2, far_twin1])
-        far2, far_twin2 = forward(2, far2, big)
+        far1, far_twin1 = forward(1, far1, d_hidden)
+        big = put_rows(pos, big, [far_twin0, twin1, far1, twin2])
+        parts = after(parts, big)
+        others = [swap(p, CORE) for p in parts]
+        big = put_rows(pos, big, [far_twin1])
+        pack, parts, others = after((pack, parts, others), big)
+        d_w, vec = join_pass(jnp.stack([vp, core]), pack, parts, others)
+        db = pack[width + 16:].reshape(-1)[:shard_rows]
+        loss = pack[width + 3, 0] / n_tokens
+        grads = vec[0], vec[1], vec[2]
+        far2, far_twin2 = forward(2, far2, big, d_w, db, loss, *grads)
         big = put_rows(pos, big, [far2])
         big = put_rows(pos, big, [far_twin2])
-        parts = after(parts, far2)
-        others = [swap(p, CORE) for p in parts]
-        d_w, vec = join_pass(jnp.stack([vp, core]), pack, parts, others)
-
-        db = pack[width + 16:].reshape(-1)[:shard_rows]
-        return pack[width + 3, 0] / n_tokens, d_hidden, d_w, vec[0], vec[1], vec[2], big, db
+
+        return loss, d_hidden, d_w, *grads, big, db
 
     in_specs = (P("dp", None, None), P("dp", None), P("dp", None), P(None, None), P(None), P(None), P(None), P("vp", None), P("vp"))
     out_specs = (P(), P("dp", None, None), P(None, None), P(None), P(None), P(None), P("vp", None), P("vp"))

time: 707 us -> 674 us (0.953)
  waiting for transfers between devices: 271 us -> 239 us
    ppermute x12, waiting for transfers between devices: 159 us -> 86.1 us  [swap_vp(): return lax.ppermute(a, 'vp', [(d, d ^ bit) for d in range(n_shards)])]
    ppermute x28, waiting for transfers between devices: 55.6 us -> 95.1 us  [swap(): return lax.ppermute(a, 'dp', [(d, d ^ bit) for d in range(n_groups)])]
    pallas_call x3 -> x4, Pallas kernels: 24.8 us -> 25.9 us  [put_rows(): pl.pallas_call(functools.partial(put_kernel, spots), in_specs=[SMEM] + [A...]
  transfers between devices with their start and end apart: 45 -> 45, of which waited for: 18 -> 14; matrix products, arithmetic and copies ran while one was open for 3% -> 3% of each run, Pallas kernels for 46% -> 39%
where the time goes in v6:
time: 674 us; the launch traced here: 667 us
  Pallas kernels  345 us (51%)
  waiting for transfers between devices  239 us (35%)
  starting transfers between devices  40.3 us (6%)
  local copies, waits for them, and re-layouts  21 us (3%)
  between operations  16.4 us (2%)
    pallas_call x5, Pallas kernels, rows_pass(): pl.pallas_call(functools.partial(rows_kernel, kind, scale, s0, m, cut, n_...  185 us
    ppermute x28, waiting for transfers between devices, swap(): return lax.ppermute(a, 'dp', [(d, d ^ bit) for d in range(n_groups)])  95.1 us
    ppermute x12, waiting for transfers between devices, swap_vp(): return lax.ppermute(a, 'vp', [(d, d ^ bit) for d in range(n_shards)])  86.1 us
    psum x1, waiting for transfers between devices, local_step(): pack = lax.psum(pack, 'dp')  58.1 us
    pallas_call x1, Pallas kernels, du_pass(): pl.pallas_call(functools.partial(du_kernel, v, scale, base), grid=(n,), i...  48.1 us
    pallas_call x1, Pallas kernels, stats(): pl.pallas_call(functools.partial(stats_kernel, v), grid=(n,), in_specs=[w...  43.9 us
    pallas_call x4, Pallas kernels, put_rows(): pl.pallas_call(functools.partial(put_kernel, spots), in_specs=[SMEM] + [A...  25.9 us
    ppermute x28, starting transfers between devices, swap(): return lax.ppermute(a, 'dp', [(d, d ^ bit) for d in range(n_groups)])  25.9 us
  transfers between devices with their start and end apart: 45, of which 14 were waited for; matrix products, arithmetic and copies ran while one was open for 3% of the time, Pallas kernels for 39%

profile of v6, /device:TPU:17, one launch (start us, length us, event | category | flops | bytes accessed | tf_op | source)
XLA Modules:
  0.0 666.6 jit_solution(824788230441536374)
XLA Ops:
  8.1 1.5 broadcast_in_dim.68.b_ref
  12.0 15.7 %head.1 = (bf16[1232,1024]{1,0:T(8,128)(2,1)}, f32[1232,1024]{1,0:T(8,128)}, f32[1232,1024]{1,0:T(8,128)}, f32[1232,128]{1,0:T(8,128)}, bf16[1232,1024]{1,0:T(8,...) custom-call(bf16[16,512,1024]{2,1,0:T(8,128)(2,1)} %hid.1, s32[16,80,128]{2,1,0:T(8,128)} %broadcast_in_dim.64.pos_ref, ...), custom_call_target="tpu_custom_call" | custom-call | flops 51673824 | bytes 42008576 | tf_op jit(solution)/shard_map/head/pallas_call | solution.py:255
  28.8 43.9 %stats.1 = (f32[1232,12576]{1,0:T(8,128)}, f32[8,1232]{1,0:T(8,128)}) custom-call(bf16[1232,1024]{1,0:T(8,128)(2,1)} %get-tuple-element.76.u_ref, bf16[12576,1024]{1,0:T(8,128)(2,1)} %emb_hbm.9, f32[1,12576]{1,0:T(1,128)} %broadcast_in_dim.68.b_ref, s32[1232,128]{1,0:T(8,128)} %broadcast_in_dim.70.lab_ref), custom_call_target="tpu_custom_call" | custom-call | flops 317309568 | bytes 87730176 | tf_op jit(solution)/shard_map/stats/pallas_call | solution.py:96
  72.6 1.3 collective-permute-start
  74.0 1.3 collective-permute-start.2
  75.3 1.2 collective-permute-start.16
  80.6 48.1 %du_pass.1 = (f32[4,1232,256]{2,1,0:T(8,128)}, f32[1,12576]{1,0:T(1,128)}, f32[8,1232]{1,0:T(8,128)}) custom-call(f32[1232,12576]{1,0:T(8,128)} %get-tuple-element.77.logits_ref, bf16[12576,1024]{1,0:T(8,128)(2,1)} %emb_hbm.9, f32[1232,128]{1,0:T(8,128)} %broadcast_in_dim.71.lse_ref, s32[1232,128]{1,0:T(8,128)} %broadcast_in_dim.70.lab_ref, ...), custom_call_target="tpu_custom_call" | custom-call | flops 317309568 | bytes 87730176 | tf_op jit(solution)/shard_map/du_pass/pallas_call | solution.py:182
  128.8 2.9 collective-permute-start.8
  132.4 7.4 %collective-permute-done.6 = f32[2,1280]{1,0:T(2,128)S(1)} collective-permute-done((f32[2,1280]{1,0:T(2,128)S(1)}, f32[2,1280]{1,0:T(2,128)S(1)}, u32[]{:S(2)}, u32[]{:S(2)}) %collective-permute-start.6) | collective-permute-done | bytes 10272 | tf_op jit(solution)/shard_map/ppermute | solution.py:661
  139.8 1.2 collective-permute-start.11
  141.0 1.7 collective-permute-done.11
  142.8 1.2 collective-permute-start.12
  144.0 1.7 collective-permute-done.12
  146.9 1.3 collective-permute-start.10
  148.3 53.4 %collective-permute-done.13 = f32[2,1280]{1,0:T(2,128)S(1)} collective-permute-done((f32[2,1280]{1,0:T(2,128)S(1)}, f32[2,1280]{1,0:T(2,128)S(1)}, u32[]{:S(2)}, u32[]{:S(2)}) %collective-permute-start.13) | collective-permute-done | bytes 10272 | tf_op jit(solution)/shard_map/ppermute | solution.py:661
  201.7 3.0 collective-permute-start.17
  205.5 1.6 broadcast_in_dim.79.bias_ref
  208.8 1.9 collective-permute-start.4
  211.3 21.8 %shard_map.152 = (f32[1280,1024]{1,0:T(8,128)}, bf16[8,1280,1024]{2,1,0:T(8,128)(2,1)}) custom-call(s32[6]{0:T(128)} %stack.73.pos, bf16[12576,1024]{1,0:T(8,128)(2,1)} %emb_hbm.9, f32[3144,1]{1,0:T(8,128)} %broadcast_in_dim.79.bias_ref, f32[2,2,1280]{2,1,0:T(2,128)} %pad_maximum_fusion.3.info_ref, f32[608,1024]{1,0:T(8,128)} %get-tuple-element.83.refs_0_, ...), custom_call_target="tpu_custom_call" | custom-call | flops 134217728 | bytes 13107200 | tf_op jit(solution)/shard_map/pallas_call | solution.py:456
  236.1 1.4 collective-permute-start.14
  237.6 4.9 collective-permute-done.14
  245.0 2.5 collective-permute-done.19.refs_6_
  247.6 37.9 %shard_map.153 = (f32[1280,1024]{1,0:T(8,128)}, bf16[8,1280,1024]{2,1,0:T(8,128)(2,1)}) custom-call(s32[6]{0:T(128)} %stack.73.pos, bf16[12576,1024]{1,0:T(8,128)(2,1)} %emb_hbm.9, f32[3144,1]{1,0:T(8,128)} %broadcast_in_dim.79.bias_ref, f32[8,2,1280]{2,1,0:T(2,128)} %pad_maximum_fusion.info_ref, ...), custom_call_target="tpu_custom_call", output_to_operand_aliasing={{1}: (12, {})} | custom-call | flops 268435456 | bytes 18350080 | tf_op jit(solution)/shard_map/pallas_call | solution.py:456
  285.5 13.2 %collective-permute-done.21.refs_0_ = f32[608,1024]{1,0:T(8,128)} collective-permute-done((f32[608,1024]{1,0:T(8,128)}, f32[608,1024]{1,0:T(8,128)}, u32[]{:S(2)}, u32[]{:S(2)}) %collective-permute-start.21) | collective-permute-done | bytes 2490400 | tf_op jit(solution)/shard_map/ppermute | solution.py:661
  302.8 7.2 %back.1 = (f32[1232,256]{1,0:T(8,128)}, f32[1096,256]{1,0:T(8,128)}) custom-call(s32[1]{0:T(128)} %bitcast.vp, f32[1232,1024]{1,0:T(8,128)} %get-tuple-element.72.refs_0_, f32[1232,1024]{1,0:T(8,128)} %get-tuple-element.73.norm_hbm.refs_1_, f32[1232,128]{1,0:T(8,128)} %get-tuple-element.74.refs_2_, bf16[1232,1024]{1,0:T(8,128)(2,1)} %get-tuple-element.75.refs_3_, ...), custom_call_target="tpu_custom_call" | custom-call | flops 6459228 | bytes 9461760 | tf_op jit(solution)/shard_map/back/pallas_call | solution.py:586
  310.1 24.3 %shard_map.154 = (f32[1280,1024]{1,0:T(8,128)}, bf16[8,1280,1024]{2,1,0:T(8,128)(2,1)}, f32[12576,1024]{1,0:T(8,128)}) custom-call(s32[6]{0:T(128)} %stack.73.pos, bf16[12576,1024]{1,0:T(8,128)(2,1)} %emb_hbm.9, f32[3144,1]{1,0:T(8,128)} %broadcast_in_dim.79.bias_ref, f32[8,2,1280]{2,1,0:T(2,128)} %pad_maximum_fusion.info_ref, ...), custom_call_target="tpu_custom_call", output_to_operand_aliasing={{1}: (8, {})} | custom-call | flops 134217728 | bytes 13107200 | tf_op jit(solution)/shard_map/pallas_call | solution.py:456
  334.8 1.8 collective-permute-start.28
  336.6 58.0 %shard_map.155 = (f32[1088,1024]{1,0:T(8,128)}, f32[12576,1024]{1,0:T(8,128)}) custom-call(s32[6]{0:T(128)} %stack.73.pos, bf16[12576,1024]{1,0:T(8,128)(2,1)} %emb_hbm.9, f32[3144,1]{1,0:T(8,128)} %broadcast_in_dim.79.bias_ref, f32[8,2,1280]{2,1,0:T(2,128)} %pad_maximum_fusion.info_ref, ...), custom_call_target="tpu_custom_call", output_to_operand_aliasing={{1}: (5, {})} | custom-call | flops 456340288 | bytes 27656192 | tf_op jit(solution)/shard_map/pallas_call | solution.py:456
  394.9 1.7 collective-permute-start.33
  397.2 1.6 collective-permute-start.34
  398.8 50.7 %collective-permute-done.33.refs_1_ = f32[1232,256]{1,0:T(8,128)S(1)} collective-permute-done((f32[1232,256]{1,0:T(8,128)S(1)}, f32[1232,256]{1,0:T(8,128)S(1)}, u32[]{:S(2)}, u32[]{:S(2)}) %collective-permute-start.33) | collective-permute-done | bytes 1261600 | tf_op jit(solution)/shard_map/ppermute | solution.py:664
  450.0 1.5 collective-permute-start.31
  451.5 58.1 %all-reduce.7.cloned.1.call-done.refs_0_ = f32[1096,256]{1,0:T(8,128)} async-done(((f32[1096,256]{1,0:T(8,128)}), f32[1096,256]{1,0:T(8,128)}) %all-reduce.7.cloned.1.call-update) | async-done | bytes 1122320 | tf_op jit(solution)/shard_map/psum | solution.py:758
  509.7 1.9 constant_dynamic-slice_fusion
  511.5 42.5 %shard_map.156 = (f32[776,1024]{1,0:T(8,128)}, f32[12576,1024]{1,0:T(8,128)}) custom-call(s32[6]{0:T(128)} %stack.73.pos, bf16[12576,1024]{1,0:T(8,128)(2,1)} %emb_hbm.9, f32[3144,1]{1,0:T(8,128)} %broadcast_in_dim.79.bias_ref, f32[8,2,1280]{2,1,0:T(2,128)} %pad_maximum_fusion.info_ref, ...), custom_call_target="tpu_custom_call", output_to_operand_aliasing={{1}: (5, {})} | custom-call | flops 325477984 | bytes 25739264 | tf_op jit(solution)/shard_map/pallas_call | solution.py:456
  554.1 14.8 %spread.1 = bf16[16,512,1024]{2,1,0:T(8,128)(2,1)} custom-call(s32[1]{0:T(128)} %bitcast.vp, s32[16,1,80]{2,1,0:T(1,128)} %bitcast.34, bf16[1024,1024]{1,0:T(8,128)(2,1)} %w_ref.3, f32[1232,256]{1,0:T(8,128)} %get-tuple-element.118.refs_0_, f32[1232,256]{1,0:T(8,128)} %copy-done.4, f32[1232,256]{1,0:T(8,128)} %collective-permute-done.34.refs_2_, ...), custom_call_target="tpu_custom_call" | custom-call | flops 21474836 | bytes 16777216 | tf_op jit(solution)/shard_map/spread/pallas_call | solution.py:637
  568.9 1.4 collective-permute-start.40
  572.1 10.3 %collective-permute-done.36.refs_4_ = f32[776,1024]{1,0:T(8,128)} collective-permute-done((f32[776,1024]{1,0:T(8,128)}, f32[776,1024]{1,0:T(8,128)}, u32[]{:S(2)}, u32[]{:S(2)}) %collective-permute-start.36) | collective-permute-done | bytes 3178528 | tf_op jit(solution)/shard_map/ppermute | solution.py:661
  582.7 2.1 collective-permute-start.27
  584.7 12.3 %put_rows.4.refs_0_ = f32[12576,1024]{1,0:T(8,128)} custom-call(s32[6]{0:T(128)} %stack.73.pos, f32[12576,1024]{1,0:T(8,128)} %get-tuple-element.116.refs_0_, f32[1280,1024]{1,0:T(8,128)} %collective-permute-done.30.refs_1_, f32[1088,1024]{1,0:T(8,128)} %collective-permute-done.31.refs_2_, ...), custom_call_target="tpu_custom_call", output_to_operand_aliasing={{}: (1, {})} | custom-call | flops 43335 | bytes 34668544 | tf_op jit(solution)/shard_map/put_rows/pallas_call | solution.py:489
  597.1 19.8 %collective-permute-done.26.refs_2_ = f32[520,256]{1,0:T(8,128)} collective-permute-done((f32[520,256]{1,0:T(8,128)}, f32[520,256]{1,0:T(8,128)}, u32[]{:S(2)}, u32[]{:S(2)}) %collective-permute-start.26) | collective-permute-done | bytes 532512 | tf_op jit(solution)/shard_map/ppermute | solution.py:664
  616.9 14.9 %collective-permute-done.27.refs_3_ = f32[520,256]{1,0:T(8,128)} collective-permute-done((f32[520,256]{1,0:T(8,128)}, f32[520,256]{1,0:T(8,128)}, u32[]{:S(2)}, u32[]{:S(2)}) %collective-permute-start.27) | collective-permute-done | bytes 532512 | tf_op jit(solution)/shard_map/ppermute | solution.py:664
  633.4 5.0 put_rows.5.refs_0_
  638.5 4.9 join.1
  646.8 1.5 fusion.3
  648.3 1.6 copy-done
  650.0 4.2 put_rows.6.refs_0_
  654.2 4.3 put_rows.7
  (118 shorter events, 31.6 us)
Async XLA Ops:
  7.2 294.6 %reduce-scatter.2.cloned.1.call-start = ((), (), s32[]{:S(2)}) async-start(), calls=%async_computation.1 | async-start | bytes 6307840 | tf_op jit(solution)/shard_map/reduce_scatter | solution.py:705
  72.6 5.1 collective-permute-start
  73.9 4.0 collective-permute-start.1
  74.0 3.9 collective-permute-start.2
  75.3 72.9 %collective-permute-start.16 = (f32[624,1024]{1,0:T(8,128)S(1)}, f32[624,1024]{1,0:T(8,128)}, u32[]{:S(2)}, u32[]{:S(2)}) collective-permute-start(f32[624,1024]{1,0:T(8,128)S(1)} %copy-done.1), channel_id=1, source_target_pairs={{0,4},{1,5},{2,6},{3,7},{4,0},{5,1},{6,2},{7,3},{8,12},{9,13},{10,... | collective-permute-start | bytes 7667720 | tf_op jit(solution)/shard_map/ppermute | solution.py:661
  76.5 70.4 %collective-permute-start.15 = (f32[608,1024]{1,0:T(8,128)}, f32[608,1024]{1,0:T(8,128)}, u32[]{:S(2)}, u32[]{:S(2)}) collective-permute-start(f32[608,1024]{1,0:T(8,128)} %get-tuple-element.83.refs_0_), channel_id=1, source_target_pairs={{0,2},{1,3},{2,0},{3,1},{4,6},{5,7},{6,4},{7,5},{8,10},{9,11},{10,... | collective-permute-start | bytes 7471112 | tf_op jit(solution)/shard_map/ppermute | solution.py:661
  128.7 79.2 %copy-start.8 = (f32[8,1232]{1,0:T(8,128)S(1)}, f32[8,1232]{1,0:T(8,128)}, u32[]{:S(2)}) copy-start(f32[8,1232]{1,0:T(8,128)} %get-tuple-element.86) | copy-start | bytes 118276
  128.7 380.9 %all-reduce.7.cloned.1.call-start = ((), (), s32[]{:S(2)}) async-start(), calls=%async_computation.2 | async-start | bytes 2244608 | tf_op jit(solution)/shard_map/psum | solution.py:758
  128.8 80.1 %collective-permute-start.8 = (f32[624,1024]{1,0:T(8,128)S(1)}, f32[624,1024]{1,0:T(8,128)}, u32[]{:S(2)}, u32[]{:S(2)}) collective-permute-start(f32[624,1024]{1,0:T(8,128)S(1)} %copy-done.1), channel_id=1, source_target_pairs={{0,1},{1,0},{2,3},{3,2},{4,5},{5,4},{6,7},{7,6},{8,9},{9,8},{10,11... | collective-permute-start | bytes 7667720 | tf_op jit(solution)/shard_map/ppermute | solution.py:661
  131.7 76.2 %collective-permute-start.7 = (f32[608,1024]{1,0:T(8,128)}, f32[608,1024]{1,0:T(8,128)}, u32[]{:S(2)}, u32[]{:S(2)}) collective-permute-start(f32[608,1024]{1,0:T(8,128)} %get-tuple-element.83.refs_0_), channel_id=1, source_target_pairs={{0,1},{1,0},{2,3},{3,2},{4,5},{5,4},{6,7},{7,6},{8,9},{9,8},{10,11... | collective-permute-start | bytes 7471112 | tf_op jit(solution)/shard_map/ppermute | solution.py:661
  131.9 7.9 %collective-permute-start.6 = (f32[2,1280]{1,0:T(2,128)S(1)}, f32[2,1280]{1,0:T(2,128)S(1)}, u32[]{:S(2)}, u32[]{:S(2)}) collective-permute-start(f32[2,1280]{1,0:T(2,128)S(1)} %get-tuple-element.153), channel_id=1, source_target_pairs={{0,1},{1,0},{2,3},{3,2},{4,5},{5,4},{6,7},{7,6},{8,9},{9,8},{10,11... | collective-permute-start | bytes 30728 | tf_op jit(solution)/shard_map/ppermute | solution.py:661
  139.8 2.9 collective-permute-start.11
  142.8 2.9 collective-permute-start.12
  145.7 87.8 %collective-permute-start.9 = (f32[624,1024]{1,0:T(8,128)S(1)}, f32[624,1024]{1,0:T(8,128)}, u32[]{:S(2)}, u32[]{:S(2)}) collective-permute-start(f32[624,1024]{1,0:T(8,128)S(1)} %copy-done.1), channel_id=1, source_target_pairs={{0,2},{1,3},{2,0},{3,1},{4,6},{5,7},{6,4},{7,5},{8,10},{9,11},{10,... | collective-permute-start | bytes 7667720 | tf_op jit(solution)/shard_map/ppermute | solution.py:661
  146.9 86.3 %collective-permute-start.10 = (f32[608,1024]{1,0:T(8,128)}, f32[608,1024]{1,0:T(8,128)}, u32[]{:S(2)}, u32[]{:S(2)}) collective-permute-start(f32[608,1024]{1,0:T(8,128)} %get-tuple-element.83.refs_0_), channel_id=1, source_target_pairs={{0,4},{1,5},{2,6},{3,7},{4,0},{5,1},{6,2},{7,3},{8,12},{9,13},{10,... | collective-permute-start | bytes 7471112 | tf_op jit(solution)/shard_map/ppermute | solution.py:661
  148.2 53.5 %collective-permute-start.13 = (f32[2,1280]{1,0:T(2,128)S(1)}, f32[2,1280]{1,0:T(2,128)S(1)}, u32[]{:S(2)}, u32[]{:S(2)}) collective-permute-start(f32[2,1280]{1,0:T(2,128)S(1)} %get-tuple-element.153), channel_id=1, source_target_pairs={{0,6},{1,7},{2,4},{3,5},{4,2},{5,3},{6,0},{7,1},{8,14},{9,15},{10,... | collective-permute-start | bytes 30728 | tf_op jit(solution)/shard_map/ppermute | solution.py:661
  201.7 41.2 %collective-permute-start.17 = (f32[608,1024]{1,0:T(8,128)}, f32[608,1024]{1,0:T(8,128)}, u32[]{:S(2)}, u32[]{:S(2)}) collective-permute-start(f32[608,1024]{1,0:T(8,128)} %collective-permute-done.15.refs_0_), channel_id=1, source_target_pairs={{0,1},{1,0},{2,3},{3,2},{4,5},{5,4},{6,7},{7,6},{8,9},{9,8},{10,11... | collective-permute-start | bytes 7471112 | tf_op jit(solution)/shard_map/ppermute | solution.py:661
  207.9 26.2 %collective-permute-start.3 = (f32[8,1232]{1,0:T(8,128)S(1)}, f32[8,1232]{1,0:T(8,128)S(1)}, u32[]{:S(2)}, u32[]{:S(2)}) collective-permute-start(f32[8,1232]{1,0:T(8,128)S(1)} %copy-done.8), channel_id=1, source_target_pairs={{0,8},{8,0},{16,24},{24,16},{1,9},{9,1},{17,25},{25,17},{2,10},{10... | collective-permute-start | bytes 118280 | tf_op jit(solution)/shard_map/ppermute | solution.py:664
  208.8 26.4 %collective-permute-start.4 = (f32[8,1232]{1,0:T(8,128)S(1)}, f32[8,1232]{1,0:T(8,128)S(1)}, u32[]{:S(2)}, u32[]{:S(2)}) collective-permute-start(f32[8,1232]{1,0:T(8,128)S(1)} %copy-done.8), channel_id=1, source_target_pairs={{0,16},{8,24},{16,0},{24,8},{1,17},{9,25},{17,1},{25,9},{2,18},{10... | collective-permute-start | bytes 118280 | tf_op jit(solution)/shard_map/ppermute | solution.py:664
  233.2 2.9 collective-permute-start.5
  233.5 14.1 %collective-permute-start.20 = (f32[624,1024]{1,0:T(8,128)}, f32[624,1024]{1,0:T(8,128)}, u32[]{:S(2)}, u32[]{:S(2)}) collective-permute-start(f32[624,1024]{1,0:T(8,128)} %collective-permute-done.16.refs_5_), channel_id=1, source_target_pairs={{0,1},{1,0},{2,3},{3,2},{4,5},{5,4},{6,7},{7,6},{8,9},{9,8},{10,11... | collective-permute-start | bytes 7667720 | tf_op jit(solution)/shard_map/ppermute | solution.py:661
  234.1 64.6 %collective-permute-start.22 = (f32[624,1024]{1,0:T(8,128)}, f32[624,1024]{1,0:T(8,128)S(1)}, u32[]{:S(2)}, u32[]{:S(2)}) collective-permute-start(f32[624,1024]{1,0:T(8,128)} %collective-permute-done.16.refs_5_), channel_id=1, source_target_pairs={{0,2},{1,3},{2,0},{3,1},{4,6},{5,7},{6,4},{7,5},{8,10},{9,11},{10,... | collective-permute-start | bytes 7667720 | tf_op jit(solution)/shard_map/ppermute | solution.py:661
  235.3 12.3 %collective-permute-start.18 = (f32[624,1024]{1,0:T(8,128)}, f32[624,1024]{1,0:T(8,128)}, u32[]{:S(2)}, u32[]{:S(2)}) collective-permute-start(f32[624,1024]{1,0:T(8,128)} %collective-permute-done.9.refs_1_), channel_id=1, source_target_pairs={{0,1},{1,0},{2,3},{3,2},{4,5},{5,4},{6,7},{7,6},{8,9},{9,8},{10,11... | collective-permute-start | bytes 7667720 | tf_op jit(solution)/shard_map/ppermute | solution.py:661
  236.1 6.4 collective-permute-start.14
  242.5 5.1 collective-permute-start.19
  242.9 55.8 %collective-permute-start.21 = (f32[608,1024]{1,0:T(8,128)}, f32[608,1024]{1,0:T(8,128)}, u32[]{:S(2)}, u32[]{:S(2)}) collective-permute-start(f32[608,1024]{1,0:T(8,128)} %collective-permute-done.15.refs_0_), channel_id=1, source_target_pairs={{0,4},{1,5},{2,6},{3,7},{4,0},{5,1},{6,2},{7,3},{8,12},{9,13},{10,... | collective-permute-start | bytes 7471112 | tf_op jit(solution)/shard_map/ppermute | solution.py:661
  298.7 11.4 %collective-permute-start.24 = (f32[624,1024]{1,0:T(8,128)S(1)}, f32[624,1024]{1,0:T(8,128)}, u32[]{:S(2)}, u32[]{:S(2)}) collective-permute-start(f32[624,1024]{1,0:T(8,128)S(1)} %collective-permute-done.22.refs_1_), channel_id=1, source_target_pairs={{0,1},{1,0},{2,3},{3,2},{4,5},{5,4},{6,7},{7,6},{8,9},{9,8},{10,11... | collective-permute-start | bytes 7667720 | tf_op jit(solution)/shard_map/ppermute | solution.py:661
  299.7 10.4 %collective-permute-start.23 = (f32[608,1024]{1,0:T(8,128)}, f32[608,1024]{1,0:T(8,128)}, u32[]{:S(2)}, u32[]{:S(2)}) collective-permute-start(f32[608,1024]{1,0:T(8,128)} %collective-permute-done.21.refs_0_), channel_id=1, source_target_pairs={{0,1},{1,0},{2,3},{3,2},{4,5},{5,4},{6,7},{7,6},{8,9},{9,8},{10,11... | collective-permute-start | bytes 7471112 | tf_op jit(solution)/shard_map/ppermute | solution.py:661
  334.4 62.2 %collective-permute-start.29 = (f32[1280,1024]{1,0:T(8,128)}, f32[1280,1024]{1,0:T(8,128)}, u32[]{:S(2)}, u32[]{:S(2)}) collective-permute-start(f32[1280,1024]{1,0:T(8,128)} %get-tuple-element.114), channel_id=1, source_target_pairs={{0,2},{1,5},{2,0},{3,7},{4,6},{5,1},{6,4},{7,3},{8,10},{9,13},{10,... | collective-permute-start | bytes 15728648 | tf_op jit(solution)/shard_map/ppermute | solution.py:667
  334.8 115.3 %collective-permute-start.28 = (f32[1280,1024]{1,0:T(8,128)}, f32[1280,1024]{1,0:T(8,128)}, u32[]{:S(2)}, u32[]{:S(2)}) collective-permute-start(f32[1280,1024]{1,0:T(8,128)} %get-tuple-element.114), channel_id=1, source_target_pairs={{0,1},{1,0},{2,3},{3,2},{4,5},{5,4},{6,7},{7,6},{8,9},{9,8},{10,11... | collective-permute-start | bytes 15728648 | tf_op jit(solution)/shard_map/ppermute | solution.py:661
  336.6 58.3 %copy-start.3 = (f32[1232,256]{1,0:T(8,128)S(1)}, f32[1232,256]{1,0:T(8,128)}, u32[]{:S(2)}) copy-start(f32[1232,256]{1,0:T(8,128)} %get-tuple-element.118.refs_0_) | copy-start | bytes 3784708
  394.6 174.3 %collective-permute-start.32 = (f32[1088,1024]{1,0:T(8,128)}, f32[1088,1024]{1,0:T(8,128)}, u32[]{:S(2)}, u32[]{:S(2)}) collective-permute-start(f32[1088,1024]{1,0:T(8,128)} %get-tuple-element.110), channel_id=1, source_target_pairs={{0,2},{1,5},{2,0},{3,7},{4,6},{5,1},{6,4},{7,3},{8,10},{9,13},{10,... | collective-permute-start | bytes 13369352 | tf_op jit(solution)/shard_map/ppermute | solution.py:667
  394.9 54.7 %collective-permute-start.33 = (f32[1232,256]{1,0:T(8,128)S(1)}, f32[1232,256]{1,0:T(8,128)S(1)}, u32[]{:S(2)}, u32[]{:S(2)}) collective-permute-start(f32[1232,256]{1,0:T(8,128)S(1)} %copy-done.3), channel_id=1, source_target_pairs={{0,8},{8,0},{16,24},{24,16},{1,9},{9,1},{17,25},{25,17},{2,10},{10... | collective-permute-start | bytes 3784712 | tf_op jit(solution)/shard_map/ppermute | solution.py:664
  396.6 186.1 %collective-permute-start.30 = (f32[1280,1024]{1,0:T(8,128)}, f32[1280,1024]{1,0:T(8,128)}, u32[]{:S(2)}, u32[]{:S(2)}) collective-permute-start(f32[1280,1024]{1,0:T(8,128)} %collective-permute-done.29.refs_3_), channel_id=1, source_target_pairs={{0,1},{1,0},{2,3},{3,2},{4,5},{5,4},{6,7},{7,6},{8,9},{9,8},{10,11... | collective-permute-start | bytes 15728648 | tf_op jit(solution)/shard_map/ppermute | solution.py:661
  397.2 156.9 %collective-permute-start.34 = (f32[1232,256]{1,0:T(8,128)S(1)}, f32[1232,256]{1,0:T(8,128)}, u32[]{:S(2)}, u32[]{:S(2)}) collective-permute-start(f32[1232,256]{1,0:T(8,128)S(1)} %copy-done.3), channel_id=1, source_target_pairs={{0,16},{8,24},{16,0},{24,8},{1,17},{9,25},{17,1},{25,9},{2,18},{10... | collective-permute-start | bytes 3784712 | tf_op jit(solution)/shard_map/ppermute | solution.py:664
  449.5 104.6 %copy-start.4 = (f32[1232,256]{1,0:T(8,128)}, f32[1232,256]{1,0:T(8,128)S(1)}, u32[]{:S(2)}) copy-start(f32[1232,256]{1,0:T(8,128)S(1)} %collective-permute-done.33.refs_1_) | copy-start | bytes 3784708
  449.5 104.6 %collective-permute-start.35 = (f32[1232,256]{1,0:T(8,128)S(1)}, f32[1232,256]{1,0:T(8,128)}, u32[]{:S(2)}, u32[]{:S(2)}) collective-permute-start(f32[1232,256]{1,0:T(8,128)S(1)} %copy-done.3), channel_id=1, source_target_pairs={{0,24},{8,16},{16,8},{24,0},{1,25},{9,17},{17,9},{25,1},{2,26},{10... | collective-permute-start | bytes 3784712 | tf_op jit(solution)/shard_map/ppermute | solution.py:664
  450.0 120.9 %collective-permute-start.31 = (f32[1088,1024]{1,0:T(8,128)}, f32[1088,1024]{1,0:T(8,128)}, u32[]{:S(2)}, u32[]{:S(2)}) collective-permute-start(f32[1088,1024]{1,0:T(8,128)} %get-tuple-element.110), channel_id=1, source_target_pairs={{0,1},{1,0},{2,3},{3,2},{4,5},{5,4},{6,7},{7,6},{8,9},{9,8},{10,11... | collective-permute-start | bytes 13369352 | tf_op jit(solution)/shard_map/ppermute | solution.py:661
  568.9 64.5 %collective-permute-start.40 = (f32[1088,1024]{1,0:T(8,128)}, f32[1088,1024]{1,0:T(8,128)}, u32[]{:S(2)}, u32[]{:S(2)}) collective-permute-start(f32[1088,1024]{1,0:T(8,128)} %collective-permute-done.32.refs_3_), channel_id=1, source_target_pairs={{0,1},{1,0},{2,3},{3,2},{4,5},{5,4},{6,7},{7,6},{8,9},{9,8},{10,11... | collective-permute-start | bytes 13369352 | tf_op jit(solution)/shard_map/ppermute | solution.py:661
  570.3 12.0 %collective-permute-start.36 = (f32[776,1024]{1,0:T(8,128)}, f32[776,1024]{1,0:T(8,128)}, u32[]{:S(2)}, u32[]{:S(2)}) collective-permute-start(f32[776,1024]{1,0:T(8,128)} %get-tuple-element.117), channel_id=1, source_target_pairs={{0,1},{1,0},{2,3},{3,2},{4,5},{5,4},{6,7},{7,6},{8,9},{9,8},{10,11... | collective-permute-start | bytes 9535496 | tf_op jit(solution)/shard_map/ppermute | solution.py:661
  570.4 77.9 %collective-permute-start.41 = (f32[776,1024]{1,0:T(8,128)}, f32[776,1024]{1,0:T(8,128)S(1)}, u32[]{:S(2)}, u32[]{:S(2)}) collective-permute-start(f32[776,1024]{1,0:T(8,128)} %get-tuple-element.117), channel_id=1, source_target_pairs={{0,2},{1,5},{2,0},{3,7},{4,6},{5,1},{6,4},{7,3},{8,10},{9,13},{10,... | collective-permute-start | bytes 9535496 | tf_op jit(solution)/shard_map/ppermute | solution.py:667
  571.0 26.1 %collective-permute-start.25 = (f32[520,256]{1,0:T(8,128)}, f32[520,256]{1,0:T(8,128)S(1)}, u32[]{:S(2)}, u32[]{:S(2)}) collective-permute-start(f32[520,256]{1,0:T(8,128)} %constant_dynamic-slice_fusion), channel_id=1, source_target_pairs={{0,8},{8,0},{16,24},{24,16},{1,9},{9,1},{17,25},{25,17},{2,10},{10... | collective-permute-start | bytes 1597448 | tf_op jit(solution)/shard_map/ppermute | solution.py:664
  582.3 34.6 %collective-permute-start.26 = (f32[520,256]{1,0:T(8,128)}, f32[520,256]{1,0:T(8,128)}, u32[]{:S(2)}, u32[]{:S(2)}) collective-permute-start(f32[520,256]{1,0:T(8,128)} %constant_dynamic-slice_fusion), channel_id=1, source_target_pairs={{0,16},{8,24},{16,0},{24,8},{1,17},{9,25},{17,1},{25,9},{2,18},{10... | collective-permute-start | bytes 1597448 | tf_op jit(solution)/shard_map/ppermute | solution.py:664
  582.7 49.1 %collective-permute-start.27 = (f32[520,256]{1,0:T(8,128)}, f32[520,256]{1,0:T(8,128)}, u32[]{:S(2)}, u32[]{:S(2)}) collective-permute-start(f32[520,256]{1,0:T(8,128)} %constant_dynamic-slice_fusion), channel_id=1, source_target_pairs={{0,24},{8,16},{16,8},{24,0},{1,25},{9,17},{17,9},{25,1},{2,26},{10... | collective-permute-start | bytes 1597448 | tf_op jit(solution)/shard_map/ppermute | solution.py:664
  631.8 6.6 collective-permute-start.37
  632.3 6.2 collective-permute-start.38
  632.3 6.1 collective-permute-start.39
  648.2 6.0 collective-permute-start.42
  (6 other events, 153.7 us)
Sparse Core Ops, SparseCore 0:
  128.8 95.7 reduce-scatter.1
  451.6 57.9 all-reduce.6

commit v7 on v6

--- a/solution.py
+++ b/solution.py
@@ -711,13 +711,11 @@
         d_lo, d_hi = swap(x_lo, Y), swap(y_hi, X)
         cx_lo, cy_hi = swap(x_lo, CORE), swap(y_hi, CORE)
 
-        sums = [sums] + [swap_vp(sums, b) for b in range(1, n_shards)]
-
         half, quarter = shard_rows // 2, shard_rows // 4
         start = lambda h, c: h * half + c * quarter
         pos = jnp.stack([dp, start(mine, core), row_start + start(mine, core), start(mine, 1 - core), start(1 - mine, core), start(1 - mine, 1 - core)])
         bias_col = lax.dynamic_slice(b_vocab, (start(mine, core),), (quarter,))[:, None]
-        shares = (1280, 1088, 776)
+        shares = (1088, 1088, 968)
         ends = [0]
         for w in shares[:-1]:
             ends.append(ends[-1] + max(16, quarter * w // sum(shares) // 16 * 16))
@@ -744,12 +742,17 @@
         tokens[X], tokens[Y] = (x_lo, x_hi), (y_lo, y_hi)
         info = jnp.concatenate([pair, jnp.stack([away, away_near], axis=1).reshape(6, 2, BLK)])
 
-        sums = order_sum(after(sums, own)) / width
-        m1, m2 = column(sums[0]), column(sums[1])
-        side, u_all = rows("side", 0, m2, info=info, tokens=tokens, u_all=u_all)
+        sums = after(sums, own)
+        sums = [sums] + [swap_vp(sums, b) for b in range(1, n_shards)]
+        side, u_all = rows("side", 0, info=info, tokens=tokens, u_all=u_all)
         d_lo, d_hi = after((d_lo, d_hi), side)
         tokens[X | Y], tokens[X | Y | CORE] = (d_lo, d_hi), (swap(d_lo, CORE), swap(d_hi, CORE))
-        du_share = after(du_share, side)
+        sums = order_sum(after(sums, side)) / width
+        m1, m2 = column(sums[0]), column(sums[1])
+        chunk0, u_all, big = rows("far", 0, m1, m2, info=info, tokens=tokens, u_all=u_all, parts=((own, 0), (side, 0)))
+        twin0, far0 = send(0, chunk0)
+
+        du_share = after(du_share, chunk0)
         loss_row = jnp.pad(loss_part[None, None], ((0, 0), (0, cols - 1)))
         db_rows = -(-shard_rows // cols // 8) * 8
         db_mat = jnp.pad(db_part[0], (0, db_rows * cols - shard_rows)).reshape(db_rows, cols)
@@ -758,9 +761,7 @@
         pack = lax.psum(pack, "dp")
         dab = [dab] + [swap_vp(dab, b) for b in range(1, n_shards)]
 
-        chunk0, u_all, big = rows("far", 0, back_done, info=info, tokens=tokens, u_all=u_all, parts=((own, 0), (side, 0)))
-        twin0, far0 = send(0, chunk0)
-        chunk1, big = rows("whole", 1, info=info, u_all=u_all, big=big)
+        chunk1, big = rows("whole", 1, back_done, info=info, u_all=u_all, big=big, puts=[twin0])
         twin1, far1 = send(1, chunk1)
         pack = after(pack, chunk1)
         n_half = (width + 16) // 2
@@ -768,14 +769,14 @@
         parts = [swap_vp(part, b) for b in range(1, n_shards)]
         far0, far_twin0 = forward(0, far0, chunk1)
 
-        chunk2, big = rows("whole", 2, part, info=info, u_all=u_all, big=big, puts=[twin0, far0])
+        chunk2, big = rows("whole", 2, part, info=info, u_all=u_all, big=big, puts=[far0, far_twin0])
         twin2, far2 = send(2, chunk2)
-        d_hidden = spread_pass(n_masks, hidden.shape, vp[None], pos_pad[:, None], w_trans, after(dab, chunk2))
-        far1, far_twin1 = forward(1, far1, d_hidden)
-        big = put_rows(pos, big, [far_twin0, twin1, far1, twin2])
-        parts = after(parts, big)
+        big = put_rows(pos, big, [twin1, ((FAR, spans[1][0]), far1)])
+        far1, far_twin1 = forward(1, far1, big)
+        d_hidden = spread_pass(n_masks, hidden.shape, vp[None], pos_pad[:, None], w_trans, after(dab, big))
+        parts = after(parts, d_hidden)
         others = [swap(p, CORE) for p in parts]
-        big = put_rows(pos, big, [far_twin1])
+        big = put_rows(after(pos, d_hidden), big, [far_twin1, twin2])
         pack, parts, others = after((pack, parts, others), big)
         d_w, vec = join_pass(jnp.stack([vp, core]), pack, parts, others)
         db = pack[width + 16:].reshape(-1)[:shard_rows]

time: 674 us -> 688 us (1.021)
  the two profiles are of different devices: /device:TPU:17 before, /device:TPU:9 now
where the time goes in v7:
time: 688 us; the launch traced here: 681 us
  Pallas kernels  342 us (50%)
  waiting for transfers between devices  258 us (38%)
  starting transfers between devices  36.4 us (5%)
  local copies, waits for them, and re-layouts  24.8 us (4%)
  between operations  16.4 us (2%)
    pallas_call x5, Pallas kernels, rows_pass(): pl.pallas_call(functools.partial(rows_kernel, kind, scale, s0, m, cut, n_...  184 us
    ppermute x12, waiting for transfers between devices, swap_vp(): return lax.ppermute(a, 'vp', [(d, d ^ bit) for d in range(n_shards)])  142 us
    psum x1, waiting for transfers between devices, local_step(): pack = lax.psum(pack, 'dp')  59.4 us
    ppermute x28, waiting for transfers between devices, swap(): return lax.ppermute(a, 'dp', [(d, d ^ bit) for d in range(n_groups)])  56.7 us
    pallas_call x1, Pallas kernels, du_pass(): pl.pallas_call(functools.partial(du_kernel, v, scale, base), grid=(n,), i...  48 us
    pallas_call x1, Pallas kernels, stats(): pl.pallas_call(functools.partial(stats_kernel, v), grid=(n,), in_specs=[w...  43.8 us
    pallas_call x4, Pallas kernels, put_rows(): pl.pallas_call(functools.partial(put_kernel, spots), in_specs=[SMEM] + [A...  23.3 us
    ppermute x28, starting transfers between devices, swap(): return lax.ppermute(a, 'dp', [(d, d ^ bit) for d in range(n_groups)])  22.2 us
  transfers between devices with their start and end apart: 45, of which 17 were waited for; matrix products, arithmetic and copies ran while one was open for 3% of the time, Pallas kernels for 47%

profile of v7, /device:TPU:9, one launch (start us, length us, event | category | flops | bytes accessed | tf_op | source)
XLA Modules:
  0.0 680.9 jit_solution(13947655959800086786)
XLA Ops:
  9.0 15.7 %head.1 = (bf16[1232,1024]{1,0:T(8,128)(2,1)}, f32[1232,1024]{1,0:T(8,128)}, f32[1232,1024]{1,0:T(8,128)}, f32[1232,128]{1,0:T(8,128)}, bf16[1232,1024]{1,0:T(8,...) custom-call(bf16[16,512,1024]{2,1,0:T(8,128)(2,1)} %hid.1, s32[16,80,128]{2,1,0:T(8,128)} %broadcast_in_dim.64.pos_ref, ...), custom_call_target="tpu_custom_call" | custom-call | flops 51673824 | bytes 42008576 | tf_op jit(solution)/shard_map/head/pallas_call | solution.py:255
  24.7 1.3 collective-permute-start.15
  26.0 1.2 collective-permute-start.16
  29.1 43.8 %stats.1 = (f32[1232,12576]{1,0:T(8,128)}, f32[8,1232]{1,0:T(8,128)}) custom-call(bf16[1232,1024]{1,0:T(8,128)(2,1)} %get-tuple-element.78.u_ref, bf16[12576,1024]{1,0:T(8,128)(2,1)} %emb_hbm.9, f32[1,12576]{1,0:T(1,128)} %broadcast_in_dim.68.b_ref, s32[1232,128]{1,0:T(8,128)} %broadcast_in_dim.70.lab_ref), custom_call_target="tpu_custom_call" | custom-call | flops 317309568 | bytes 87730176 | tf_op jit(solution)/shard_map/stats/pallas_call | solution.py:96
  73.1 2.3 collective-permute-start.1
  76.4 2.0 collective-permute-start.5
  81.5 48.0 %du_pass.1 = (f32[4,1232,256]{2,1,0:T(8,128)}, f32[1,12576]{1,0:T(1,128)}, f32[8,1232]{1,0:T(8,128)}) custom-call(f32[1232,12576]{1,0:T(8,128)} %get-tuple-element.79.logits_ref, bf16[12576,1024]{1,0:T(8,128)(2,1)} %emb_hbm.9, f32[1232,128]{1,0:T(8,128)} %broadcast_in_dim.71.lse_ref, s32[1232,128]{1,0:T(8,128)} %broadcast_in_dim.70.lab_ref, ...), custom_call_target="tpu_custom_call" | custom-call | flops 317309568 | bytes 87730176 | tf_op jit(solution)/shard_map/du_pass/pallas_call | solution.py:182
  129.6 2.7 collective-permute-start.3
  134.0 2.3 collective-permute-done.11
  136.3 1.6 collective-permute-start.17
  138.1 1.6 broadcast_in_dim.79.bias_ref
  141.0 1.2 collective-permute-start.12
  142.4 20.2 %shard_map.152 = (f32[1088,1024]{1,0:T(8,128)}, bf16[8,1280,1024]{2,1,0:T(8,128)(2,1)}) custom-call(s32[6]{0:T(128)} %stack.73.pos, bf16[12576,1024]{1,0:T(8,128)(2,1)} %emb_hbm.9, f32[3144,1]{1,0:T(8,128)} %broadcast_in_dim.79.bias_ref, f32[2,2,1280]{2,1,0:T(2,128)} %pad_maximum_fusion.3.info_ref, f32[608,1024]{1,0:T(8,128)} %get-tuple-element.85.refs_0_, ...), custom_call_target="tpu_custom_call" | custom-call | flops 114085072 | bytes 11927552 | tf_op jit(solution)/shard_map/pallas_call | solution.py:456
  162.6 27.1 %collective-permute-done.12 = f32[2,1280]{1,0:T(2,128)S(1)} collective-permute-done((f32[2,1280]{1,0:T(2,128)S(1)}, f32[2,1280]{1,0:T(2,128)S(1)}, u32[]{:S(2)}, u32[]{:S(2)}) %collective-permute-start.12) | collective-permute-done | bytes 10272 | tf_op jit(solution)/shard_map/ppermute | solution.py:661
  191.5 7.5 %collective-permute-done.14 = f32[3,2,1280]{2,1,0:T(2,128)S(1)} collective-permute-done((f32[3,2,1280]{2,1,0:T(2,128)S(1)}, f32[3,2,1280]{2,1,0:T(2,128)S(1)}, u32[]{:S(2)}, u32[]{:S(2)}) %collective-permute-start.14) | collective-permute-done | bytes 30752 | tf_op jit(solution)/shard_map/ppermute | solution.py:661
  200.3 3.6 collective-permute-done.19.refs_6_
  203.9 1.4 copy-done.5
  205.4 1.5 copy-done.3
  206.9 33.3 %shard_map.153 = (f32[1088,1024]{1,0:T(8,128)}, bf16[8,1280,1024]{2,1,0:T(8,128)(2,1)}) custom-call(s32[6]{0:T(128)} %stack.73.pos, bf16[12576,1024]{1,0:T(8,128)(2,1)} %emb_hbm.9, f32[3144,1]{1,0:T(8,128)} %broadcast_in_dim.79.bias_ref, f32[8,2,1280]{2,1,0:T(2,128)} %pad_maximum_fusion.info_ref, ...), custom_call_target="tpu_custom_call", output_to_operand_aliasing={{1}: (12, {})} | custom-call | flops 228170144 | bytes 17170432 | tf_op jit(solution)/shard_map/pallas_call | solution.py:456
  240.2 15.0 %collective-permute-done.21.refs_0_ = f32[608,1024]{1,0:T(8,128)} collective-permute-done((f32[608,1024]{1,0:T(8,128)}, f32[608,1024]{1,0:T(8,128)}, u32[]{:S(2)}, u32[]{:S(2)}) %collective-permute-start.21) | collective-permute-done | bytes 2490400 | tf_op jit(solution)/shard_map/ppermute | solution.py:661
  256.2 3.0 collective-permute-start.6
  259.2 1.2 collective-permute-start.8
  260.6 2.5 collective-permute-done.7
  265.3 1.4 copy-done.4
  266.7 1.5 copy-done.2
  268.1 21.7 %shard_map.154 = (f32[1088,1024]{1,0:T(8,128)}, bf16[8,1280,1024]{2,1,0:T(8,128)(2,1)}, f32[12576,1024]{1,0:T(8,128)}) custom-call(s32[6]{0:T(128)} %stack.73.pos, bf16[12576,1024]{1,0:T(8,128)(2,1)} %emb_hbm.9, f32[3144,1]{1,0:T(8,128)} %broadcast_in_dim.79.bias_ref, f32[8,2,1280]{2,1,0:T(2,128)} %pad_maximum_fusion.info_ref, ...), custom_call_target="tpu_custom_call", output_to_operand_aliasing={{1}: (8, {})} | custom-call | flops 114085072 | bytes 11927552 | tf_op jit(solution)/shard_map/pallas_call | solution.py:456
  289.8 2.8 collective-permute-start.25
  294.8 7.2 %back.1 = (f32[1232,256]{1,0:T(8,128)}, f32[1096,256]{1,0:T(8,128)}) custom-call(s32[1]{0:T(128)} %bitcast.vp, f32[1232,1024]{1,0:T(8,128)} %get-tuple-element.74.refs_0_, f32[1232,1024]{1,0:T(8,128)} %get-tuple-element.75.norm_hbm.refs_1_, f32[1232,128]{1,0:T(8,128)} %get-tuple-element.76.refs_2_, bf16[1232,1024]{1,0:T(8,128)(2,1)} %get-tuple-element.77.refs_3_, ...), custom_call_target="tpu_custom_call" | custom-call | flops 6459228 | bytes 9461760 | tf_op jit(solution)/shard_map/back/pallas_call | solution.py:586
  302.0 57.9 %shard_map.155 = (f32[1088,1024]{1,0:T(8,128)}, f32[12576,1024]{1,0:T(8,128)}) custom-call(s32[6]{0:T(128)} %stack.73.pos, bf16[12576,1024]{1,0:T(8,128)(2,1)} %emb_hbm.9, f32[3144,1]{1,0:T(8,128)} %broadcast_in_dim.79.bias_ref, f32[8,2,1280]{2,1,0:T(2,128)} %pad_maximum_fusion.info_ref, ...), custom_call_target="tpu_custom_call", output_to_operand_aliasing={{1}: (5, {})} | custom-call | flops 456340288 | bytes 27656192 | tf_op jit(solution)/shard_map/pallas_call | solution.py:456
  361.8 59.4 %all-reduce.7.cloned.1.call-done.refs_0_ = f32[1096,256]{1,0:T(8,128)} async-done(((f32[1096,256]{1,0:T(8,128)}), f32[1096,256]{1,0:T(8,128)}) %all-reduce.7.cloned.1.call-update) | async-done | bytes 1122320 | tf_op jit(solution)/shard_map/psum | solution.py:761
  421.1 1.9 constant_dynamic-slice_fusion
  423.0 50.8 %shard_map.156 = (f32[968,1024]{1,0:T(8,128)}, f32[12576,1024]{1,0:T(8,128)}) custom-call(s32[6]{0:T(128)} %stack.73.pos, bf16[12576,1024]{1,0:T(8,128)(2,1)} %emb_hbm.9, f32[3144,1]{1,0:T(8,128)} %broadcast_in_dim.79.bias_ref, f32[8,2,1280]{2,1,0:T(2,128)} %pad_maximum_fusion.info_ref, ...), custom_call_target="tpu_custom_call", output_to_operand_aliasing={{1}: (5, {})} | custom-call | flops 406008640 | bytes 26918912 | tf_op jit(solution)/shard_map/pallas_call | solution.py:456
  473.8 1.5 collective-permute-start.40
  475.3 7.2 %put_rows.4.refs_0_ = f32[12576,1024]{1,0:T(8,128)} custom-call(s32[6]{0:T(128)} %stack.73.pos, f32[12576,1024]{1,0:T(8,128)} %get-tuple-element.119.refs_0_, f32[1088,1024]{1,0:T(8,128)} %collective-permute-done.34.refs_1_, f32[1088,1024]{1,0:T(8,128)} %collective-permute-done.35.refs_2_), custom_call_target="tpu_custom_call", output_to_operand_aliasing={{}: (1, {})} | custom-call | flops 22282 | bytes 17825792 | tf_op jit(solution)/shard_map/put_rows/pallas_call | solution.py:489
  483.9 2.1 collective-permute-start.30
  486.0 49.8 %collective-permute-done.29.refs_1_ = f32[1232,256]{1,0:T(8,128)} collective-permute-done((f32[1232,256]{1,0:T(8,128)}, f32[1232,256]{1,0:T(8,128)}, u32[]{:S(2)}, u32[]{:S(2)}) %collective-permute-start.29) | collective-permute-done | bytes 1261600 | tf_op jit(solution)/shard_map/ppermute | solution.py:664
  537.1 2.8 collective-permute-done.30.refs_2_
  540.2 54.8 %collective-permute-done.31.refs_3_ = f32[1232,256]{1,0:T(8,128)} collective-permute-done((f32[1232,256]{1,0:T(8,128)}, f32[1232,256]{1,0:T(8,128)}, u32[]{:S(2)}, u32[]{:S(2)}) %collective-permute-start.31) | collective-permute-done | bytes 1261600 | tf_op jit(solution)/shard_map/ppermute | solution.py:664
  595.9 14.7 %spread.1 = bf16[16,512,1024]{2,1,0:T(8,128)(2,1)} custom-call(s32[1]{0:T(128)} %bitcast.vp, s32[16,1,80]{2,1,0:T(1,128)} %bitcast.34, bf16[1024,1024]{1,0:T(8,128)(2,1)} %w_ref.3, f32[1232,256]{1,0:T(8,128)} %get-tuple-element.120.refs_0_, f32[1232,256]{1,0:T(8,128)} %collective-permute-done.29.refs_1_, f32[1232,256]{1,0:T(8,128)} %collective-permute-done.30.refs_2_, ...), custom_call_target="tpu_custom_call" | custom-call | flops 21474836 | bytes 16777216 | tf_op jit(solution)/shard_map/spread/pallas_call | solution.py:637
  610.7 17.6 %collective-permute-done.27.refs_2_ = f32[520,256]{1,0:T(8,128)} collective-permute-done((f32[520,256]{1,0:T(8,128)}, f32[520,256]{1,0:T(8,128)}, u32[]{:S(2)}, u32[]{:S(2)}) %collective-permute-start.27) | collective-permute-done | bytes 532512 | tf_op jit(solution)/shard_map/ppermute | solution.py:664
  628.3 13.3 %collective-permute-done.28.refs_3_ = f32[520,256]{1,0:T(8,128)} collective-permute-done((f32[520,256]{1,0:T(8,128)}, f32[520,256]{1,0:T(8,128)}, u32[]{:S(2)}, u32[]{:S(2)}) %collective-permute-start.28) | collective-permute-done | bytes 532512 | tf_op jit(solution)/shard_map/ppermute | solution.py:664
  641.6 1.9 collective-permute-start.36
  644.6 6.6 put_rows.5.refs_0_
  651.2 4.9 join.1
  659.5 1.5 fusion.3
  661.1 1.8 copy-done
  662.9 4.7 put_rows.6.refs_0_
  668.0 4.7 put_rows.7
  (122 shorter events, 29.8 us)
Async XLA Ops:
  7.2 287.6 %reduce-scatter.2.cloned.1.call-start = ((), (), s32[]{:S(2)}) async-start(), calls=%async_computation.1 | async-start | bytes 6307840 | tf_op jit(solution)/shard_map/reduce_scatter | solution.py:705
  24.7 108.8 %collective-permute-start.15 = (f32[608,1024]{1,0:T(8,128)}, f32[608,1024]{1,0:T(8,128)}, u32[]{:S(2)}, u32[]{:S(2)}) collective-permute-start(f32[608,1024]{1,0:T(8,128)} %get-tuple-element.85.refs_0_), channel_id=1, source_target_pairs={{0,2},{1,3},{2,0},{3,1},{4,6},{5,7},{6,4},{7,5},{8,10},{9,11},{10,... | collective-permute-start | bytes 7471112 | tf_op jit(solution)/shard_map/ppermute | solution.py:661
  26.0 107.7 %collective-permute-start.16 = (f32[624,1024]{1,0:T(8,128)}, f32[624,1024]{1,0:T(8,128)}, u32[]{:S(2)}, u32[]{:S(2)}) collective-permute-start(f32[624,1024]{1,0:T(8,128)} %get-tuple-element.86.refs_1_), channel_id=1, source_target_pairs={{0,4},{1,5},{2,6},{3,7},{4,0},{5,1},{6,2},{7,3},{8,12},{9,13},{10,... | collective-permute-start | bytes 7667720 | tf_op jit(solution)/shard_map/ppermute | solution.py:661
  29.1 47.3 %copy-start.1 = (f32[624,1024]{1,0:T(8,128)S(1)}, f32[624,1024]{1,0:T(8,128)}, u32[]{:S(2)}) copy-start(f32[624,1024]{1,0:T(8,128)} %get-tuple-element.86.refs_1_) | copy-start | bytes 7667716
  72.9 3.5 collective-permute-start
  73.1 5.3 collective-permute-start.1
  75.4 3.5 collective-permute-start.2
  76.4 65.9 %collective-permute-start.5 = (f32[624,1024]{1,0:T(8,128)S(1)}, f32[624,1024]{1,0:T(8,128)}, u32[]{:S(2)}, u32[]{:S(2)}) collective-permute-start(f32[624,1024]{1,0:T(8,128)S(1)} %copy-done.1), channel_id=1, source_target_pairs={{0,1},{1,0},{2,3},{3,2},{4,5},{5,4},{6,7},{7,6},{8,9},{9,8},{10,11... | collective-permute-start | bytes 7667720 | tf_op jit(solution)/shard_map/ppermute | solution.py:661
  78.4 112.6 %collective-permute-start.9 = (f32[624,1024]{1,0:T(8,128)S(1)}, f32[624,1024]{1,0:T(8,128)}, u32[]{:S(2)}, u32[]{:S(2)}) collective-permute-start(f32[624,1024]{1,0:T(8,128)S(1)} %copy-done.1), channel_id=1, source_target_pairs={{0,2},{1,3},{2,0},{3,1},{4,6},{5,7},{6,4},{7,5},{8,10},{9,11},{10,... | collective-permute-start | bytes 7667720 | tf_op jit(solution)/shard_map/ppermute | solution.py:661
  129.6 3.5 collective-permute-start.3
  133.2 7.8 %collective-permute-start.4 = (f32[608,1024]{1,0:T(8,128)}, f32[608,1024]{1,0:T(8,128)}, u32[]{:S(2)}, u32[]{:S(2)}) collective-permute-start(f32[608,1024]{1,0:T(8,128)} %get-tuple-element.85.refs_0_), channel_id=1, source_target_pairs={{0,1},{1,0},{2,3},{3,2},{4,5},{5,4},{6,7},{7,6},{8,9},{9,8},{10,11... | collective-permute-start | bytes 7471112 | tf_op jit(solution)/shard_map/ppermute | solution.py:661
  133.5 57.4 %collective-permute-start.10 = (f32[608,1024]{1,0:T(8,128)}, f32[608,1024]{1,0:T(8,128)}, u32[]{:S(2)}, u32[]{:S(2)}) collective-permute-start(f32[608,1024]{1,0:T(8,128)} %get-tuple-element.85.refs_0_), channel_id=1, source_target_pairs={{0,4},{1,5},{2,6},{3,7},{4,0},{5,1},{6,2},{7,3},{8,12},{9,13},{10,... | collective-permute-start | bytes 7471112 | tf_op jit(solution)/shard_map/ppermute | solution.py:661
  133.8 2.5 collective-permute-start.11
  136.3 63.1 %collective-permute-start.17 = (f32[608,1024]{1,0:T(8,128)}, f32[608,1024]{1,0:T(8,128)}, u32[]{:S(2)}, u32[]{:S(2)}) collective-permute-start(f32[608,1024]{1,0:T(8,128)} %collective-permute-done.15.refs_0_), channel_id=1, source_target_pairs={{0,1},{1,0},{2,3},{3,2},{4,5},{5,4},{6,7},{7,6},{8,9},{9,8},{10,11... | collective-permute-start | bytes 7471112 | tf_op jit(solution)/shard_map/ppermute | solution.py:661
  137.9 283.2 %all-reduce.7.cloned.1.call-start = ((), (), s32[]{:S(2)}) async-start(), calls=%async_computation.2 | async-start | bytes 2244608 | tf_op jit(solution)/shard_map/psum | solution.py:761
  141.0 48.7 %collective-permute-start.12 = (f32[2,1280]{1,0:T(2,128)S(1)}, f32[2,1280]{1,0:T(2,128)S(1)}, u32[]{:S(2)}, u32[]{:S(2)}) collective-permute-start(f32[2,1280]{1,0:T(2,128)S(1)} %get-tuple-element.157), channel_id=1, source_target_pairs={{0,4},{1,5},{2,6},{3,7},{4,0},{5,1},{6,2},{7,3},{8,12},{9,13},{10,... | collective-permute-start | bytes 30728 | tf_op jit(solution)/shard_map/ppermute | solution.py:661
  142.2 48.4 %collective-permute-start.13 = (f32[2,1280]{1,0:T(2,128)S(1)}, f32[2,1280]{1,0:T(2,128)S(1)}, u32[]{:S(2)}, u32[]{:S(2)}) collective-permute-start(f32[2,1280]{1,0:T(2,128)S(1)} %get-tuple-element.157), channel_id=1, source_target_pairs={{0,6},{1,7},{2,4},{3,5},{4,2},{5,3},{6,0},{7,1},{8,14},{9,15},{10,... | collective-permute-start | bytes 30728 | tf_op jit(solution)/shard_map/ppermute | solution.py:661
  189.7 14.2 %collective-permute-start.20 = (f32[624,1024]{1,0:T(8,128)}, f32[624,1024]{1,0:T(8,128)}, u32[]{:S(2)}, u32[]{:S(2)}) collective-permute-start(f32[624,1024]{1,0:T(8,128)} %collective-permute-done.16.refs_5_), channel_id=1, source_target_pairs={{0,1},{1,0},{2,3},{3,2},{4,5},{5,4},{6,7},{7,6},{8,9},{9,8},{10,11... | collective-permute-start | bytes 7667720 | tf_op jit(solution)/shard_map/ppermute | solution.py:661
  190.7 64.5 %collective-permute-start.22 = (f32[624,1024]{1,0:T(8,128)}, f32[624,1024]{1,0:T(8,128)}, u32[]{:S(2)}, u32[]{:S(2)}) collective-permute-start(f32[624,1024]{1,0:T(8,128)} %collective-permute-done.16.refs_5_), channel_id=1, source_target_pairs={{0,2},{1,3},{2,0},{3,1},{4,6},{5,7},{6,4},{7,5},{8,10},{9,11},{10,... | collective-permute-start | bytes 7667720 | tf_op jit(solution)/shard_map/ppermute | solution.py:661
  190.9 13.0 %collective-permute-start.18 = (f32[624,1024]{1,0:T(8,128)}, f32[624,1024]{1,0:T(8,128)S(1)}, u32[]{:S(2)}, u32[]{:S(2)}) collective-permute-start(f32[624,1024]{1,0:T(8,128)} %collective-permute-done.9.refs_1_), channel_id=1, source_target_pairs={{0,1},{1,0},{2,3},{3,2},{4,5},{5,4},{6,7},{7,6},{8,9},{9,8},{10,11... | collective-permute-start | bytes 7667720 | tf_op jit(solution)/shard_map/ppermute | solution.py:661
  191.2 7.8 %collective-permute-start.14 = (f32[3,2,1280]{2,1,0:T(2,128)S(1)}, f32[3,2,1280]{2,1,0:T(2,128)S(1)}, u32[]{:S(2)}, u32[]{:S(2)}) collective-permute-start(f32[3,2,1280]{2,1,0:T(2,128)S(1)} %pad_maximum_fusion.2), channel_id=1, source_target_pairs={{0,1},{1,0},{2,3},{3,2},{4,5},{5,4},{6,7},{7,6},{8,9},{9,8},{10,11... | collective-permute-start | bytes 92168 | tf_op jit(solution)/shard_map/ppermute | solution.py:661
  199.0 4.9 collective-permute-start.19
  199.4 55.8 %collective-permute-start.21 = (f32[608,1024]{1,0:T(8,128)}, f32[608,1024]{1,0:T(8,128)}, u32[]{:S(2)}, u32[]{:S(2)}) collective-permute-start(f32[608,1024]{1,0:T(8,128)} %collective-permute-done.15.refs_0_), channel_id=1, source_target_pairs={{0,4},{1,5},{2,6},{3,7},{4,0},{5,1},{6,2},{7,3},{8,12},{9,13},{10,... | collective-permute-start | bytes 7471112 | tf_op jit(solution)/shard_map/ppermute | solution.py:661
  206.9 49.3 %copy-start.9 = (f32[8,1232]{1,0:T(8,128)S(1)}, f32[8,1232]{1,0:T(8,128)}, u32[]{:S(2)}) copy-start(f32[8,1232]{1,0:T(8,128)} %get-tuple-element.98) | copy-start | bytes 118276
  255.2 10.1 %collective-permute-start.24 = (f32[624,1024]{1,0:T(8,128)}, f32[624,1024]{1,0:T(8,128)S(1)}, u32[]{:S(2)}, u32[]{:S(2)}) collective-permute-start(f32[624,1024]{1,0:T(8,128)} %collective-permute-done.22.refs_1_), channel_id=1, source_target_pairs={{0,1},{1,0},{2,3},{3,2},{4,5},{5,4},{6,7},{7,6},{8,9},{9,8},{10,11... | collective-permute-start | bytes 7667720 | tf_op jit(solution)/shard_map/ppermute | solution.py:661
  256.2 9.1 %collective-permute-start.23 = (f32[608,1024]{1,0:T(8,128)}, f32[608,1024]{1,0:T(8,128)S(1)}, u32[]{:S(2)}, u32[]{:S(2)}) collective-permute-start(f32[608,1024]{1,0:T(8,128)} %collective-permute-done.21.refs_0_), channel_id=1, source_target_pairs={{0,1},{1,0},{2,3},{3,2},{4,5},{5,4},{6,7},{7,6},{8,9},{9,8},{10,11... | collective-permute-start | bytes 7471112 | tf_op jit(solution)/shard_map/ppermute | solution.py:661
  256.2 4.4 collective-permute-start.6
  259.2 3.9 collective-permute-start.7
  259.2 3.9 collective-permute-start.8
  268.1 24.6 %copy-start.8 = (f32[1,12576]{1,0:T(1,128)S(1)}, f32[1,12576]{1,0:T(1,128)}, u32[]{:S(2)}) copy-start(f32[1,12576]{1,0:T(1,128)} %get-tuple-element.108) | copy-start | bytes 150916
  289.8 12.2 %collective-permute-start.25 = (f32[1088,1024]{1,0:T(8,128)}, f32[1088,1024]{1,0:T(8,128)}, u32[]{:S(2)}, u32[]{:S(2)}) collective-permute-start(f32[1088,1024]{1,0:T(8,128)} %get-tuple-element.106), channel_id=1, source_target_pairs={{0,1},{1,0},{2,3},{3,2},{4,5},{5,4},{6,7},{7,6},{8,9},{9,8},{10,11... | collective-permute-start | bytes 13369352 | tf_op jit(solution)/shard_map/ppermute | solution.py:661
  292.6 67.3 %collective-permute-start.32 = (f32[1088,1024]{1,0:T(8,128)}, f32[1088,1024]{1,0:T(8,128)}, u32[]{:S(2)}, u32[]{:S(2)}) collective-permute-start(f32[1088,1024]{1,0:T(8,128)} %get-tuple-element.106), channel_id=1, source_target_pairs={{0,2},{1,5},{2,0},{3,7},{4,6},{5,1},{6,4},{7,3},{8,10},{9,13},{10,... | collective-permute-start | bytes 13369352 | tf_op jit(solution)/shard_map/ppermute | solution.py:667
  359.9 63.1 %collective-permute-start.33 = (f32[1088,1024]{1,0:T(8,128)}, f32[1088,1024]{1,0:T(8,128)}, u32[]{:S(2)}, u32[]{:S(2)}) collective-permute-start(f32[1088,1024]{1,0:T(8,128)} %collective-permute-done.32.refs_2_), channel_id=1, source_target_pairs={{0,1},{1,0},{2,3},{3,2},{4,5},{5,4},{6,7},{7,6},{8,9},{9,8},{10,11... | collective-permute-start | bytes 13369352 | tf_op jit(solution)/shard_map/ppermute | solution.py:661
  360.4 114.9 %collective-permute-start.34 = (f32[1088,1024]{1,0:T(8,128)}, f32[1088,1024]{1,0:T(8,128)}, u32[]{:S(2)}, u32[]{:S(2)}) collective-permute-start(f32[1088,1024]{1,0:T(8,128)} %get-tuple-element.114), channel_id=1, source_target_pairs={{0,1},{1,0},{2,3},{3,2},{4,5},{5,4},{6,7},{7,6},{8,9},{9,8},{10,11... | collective-permute-start | bytes 13369352 | tf_op jit(solution)/shard_map/ppermute | solution.py:661
  360.5 114.8 %collective-permute-start.35 = (f32[1088,1024]{1,0:T(8,128)}, f32[1088,1024]{1,0:T(8,128)}, u32[]{:S(2)}, u32[]{:S(2)}) collective-permute-start(f32[1088,1024]{1,0:T(8,128)} %get-tuple-element.114), channel_id=1, source_target_pairs={{0,2},{1,5},{2,0},{3,7},{4,6},{5,1},{6,4},{7,3},{8,10},{9,13},{10,... | collective-permute-start | bytes 13369352 | tf_op jit(solution)/shard_map/ppermute | solution.py:667
  473.8 169.7 %collective-permute-start.40 = (f32[968,1024]{1,0:T(8,128)}, f32[968,1024]{1,0:T(8,128)}, u32[]{:S(2)}, u32[]{:S(2)}) collective-permute-start(f32[968,1024]{1,0:T(8,128)} %get-tuple-element.129), channel_id=1, source_target_pairs={{0,1},{1,0},{2,3},{3,2},{4,5},{5,4},{6,7},{7,6},{8,9},{9,8},{10,11... | collective-permute-start | bytes 11894792 | tf_op jit(solution)/shard_map/ppermute | solution.py:661
  482.6 162.0 %collective-permute-start.39 = (f32[1088,1024]{1,0:T(8,128)}, f32[1088,1024]{1,0:T(8,128)}, u32[]{:S(2)}, u32[]{:S(2)}) collective-permute-start(f32[1088,1024]{1,0:T(8,128)} %collective-permute-done.35.refs_2_), channel_id=1, source_target_pairs={{0,1},{1,0},{2,3},{3,2},{4,5},{5,4},{6,7},{7,6},{8,9},{9,8},{10,11... | collective-permute-start | bytes 13369352 | tf_op jit(solution)/shard_map/ppermute | solution.py:661
  482.7 53.2 %collective-permute-start.29 = (f32[1232,256]{1,0:T(8,128)}, f32[1232,256]{1,0:T(8,128)}, u32[]{:S(2)}, u32[]{:S(2)}) collective-permute-start(f32[1232,256]{1,0:T(8,128)} %get-tuple-element.120.refs_0_), channel_id=1, source_target_pairs={{0,8},{8,0},{16,24},{24,16},{1,9},{9,1},{17,25},{25,17},{2,10},{10... | collective-permute-start | bytes 3784712 | tf_op jit(solution)/shard_map/ppermute | solution.py:664
  483.0 178.0 %collective-permute-start.41 = (f32[968,1024]{1,0:T(8,128)}, f32[968,1024]{1,0:T(8,128)S(1)}, u32[]{:S(2)}, u32[]{:S(2)}) collective-permute-start(f32[968,1024]{1,0:T(8,128)} %get-tuple-element.129), channel_id=1, source_target_pairs={{0,2},{1,5},{2,0},{3,7},{4,6},{5,1},{6,4},{7,3},{8,10},{9,13},{10,... | collective-permute-start | bytes 11894792 | tf_op jit(solution)/shard_map/ppermute | solution.py:667
  483.9 56.0 %collective-permute-start.30 = (f32[1232,256]{1,0:T(8,128)}, f32[1232,256]{1,0:T(8,128)}, u32[]{:S(2)}, u32[]{:S(2)}) collective-permute-start(f32[1232,256]{1,0:T(8,128)} %get-tuple-element.120.refs_0_), channel_id=1, source_target_pairs={{0,16},{8,24},{16,0},{24,8},{1,17},{9,25},{17,1},{25,9},{2,18},{10... | collective-permute-start | bytes 3784712 | tf_op jit(solution)/shard_map/ppermute | solution.py:664
  535.9 59.1 %collective-permute-start.31 = (f32[1232,256]{1,0:T(8,128)}, f32[1232,256]{1,0:T(8,128)}, u32[]{:S(2)}, u32[]{:S(2)}) collective-permute-start(f32[1232,256]{1,0:T(8,128)} %get-tuple-element.120.refs_0_), channel_id=1, source_target_pairs={{0,24},{8,16},{16,8},{24,0},{1,25},{9,17},{17,9},{25,1},{2,26},{10... | collective-permute-start | bytes 3784712 | tf_op jit(solution)/shard_map/ppermute | solution.py:664
  539.9 55.1 %collective-permute-start.26 = (f32[520,256]{1,0:T(8,128)}, f32[520,256]{1,0:T(8,128)}, u32[]{:S(2)}, u32[]{:S(2)}) collective-permute-start(f32[520,256]{1,0:T(8,128)} %constant_dynamic-slice_fusion), channel_id=1, source_target_pairs={{0,8},{8,0},{16,24},{24,16},{1,9},{9,1},{17,25},{25,17},{2,10},{10... | collective-permute-start | bytes 1597448 | tf_op jit(solution)/shard_map/ppermute | solution.py:664
  595.0 33.3 %collective-permute-start.27 = (f32[520,256]{1,0:T(8,128)}, f32[520,256]{1,0:T(8,128)}, u32[]{:S(2)}, u32[]{:S(2)}) collective-permute-start(f32[520,256]{1,0:T(8,128)} %constant_dynamic-slice_fusion), channel_id=1, source_target_pairs={{0,16},{8,24},{16,0},{24,8},{1,17},{9,25},{17,1},{25,9},{2,18},{10... | collective-permute-start | bytes 1597448 | tf_op jit(solution)/shard_map/ppermute | solution.py:664
  595.0 46.6 %collective-permute-start.28 = (f32[520,256]{1,0:T(8,128)}, f32[520,256]{1,0:T(8,128)}, u32[]{:S(2)}, u32[]{:S(2)}) collective-permute-start(f32[520,256]{1,0:T(8,128)} %constant_dynamic-slice_fusion), channel_id=1, source_target_pairs={{0,24},{8,16},{16,8},{24,0},{1,25},{9,17},{17,9},{25,1},{2,26},{10... | collective-permute-start | bytes 1597448 | tf_op jit(solution)/shard_map/ppermute | solution.py:664
  641.6 9.6 %collective-permute-start.36 = (f32[520,256]{1,0:T(8,128)}, f32[520,256]{1,0:T(8,128)}, u32[]{:S(2)}, u32[]{:S(2)}) collective-permute-start(f32[520,256]{1,0:T(8,128)} %collective-permute-done.26.refs_1_), channel_id=1, source_target_pairs={{0,1},{1,0},{2,3},{3,2},{4,5},{5,4},{6,7},{7,6},{8,9},{9,8},{10,11... | collective-permute-start | bytes 1597448 | tf_op jit(solution)/shard_map/ppermute | solution.py:661
  643.5 7.7 %collective-permute-start.37 = (f32[520,256]{1,0:T(8,128)}, f32[520,256]{1,0:T(8,128)}, u32[]{:S(2)}, u32[]{:S(2)}) collective-permute-start(f32[520,256]{1,0:T(8,128)} %collective-permute-done.27.refs_2_), channel_id=1, source_target_pairs={{0,1},{1,0},{2,3},{3,2},{4,5},{5,4},{6,7},{7,6},{8,9},{9,8},{10,11... | collective-permute-start | bytes 1597448 | tf_op jit(solution)/shard_map/ppermute | solution.py:661
  643.5 7.7 %collective-permute-start.38 = (f32[520,256]{1,0:T(8,128)}, f32[520,256]{1,0:T(8,128)}, u32[]{:S(2)}, u32[]{:S(2)}) collective-permute-start(f32[520,256]{1,0:T(8,128)} %collective-permute-done.28.refs_3_), channel_id=1, source_target_pairs={{0,1},{1,0},{2,3},{3,2},{4,5},{5,4},{6,7},{7,6},{8,9},{9,8},{10,11... | collective-permute-start | bytes 1597448 | tf_op jit(solution)/shard_map/ppermute | solution.py:661
  661.0 7.0 %collective-permute-start.42 = (f32[968,1024]{1,0:T(8,128)S(1)}, f32[968,1024]{1,0:T(8,128)}, u32[]{:S(2)}, u32[]{:S(2)}) collective-permute-start(f32[968,1024]{1,0:T(8,128)S(1)} %collective-permute-done.41.refs_1_), channel_id=1, source_target_pairs={{0,1},{1,0},{2,3},{3,2},{4,5},{5,4},{6,7},{7,6},{8,9},{9,8},{10,11... | collective-permute-start | bytes 11894792 | tf_op jit(solution)/shard_map/ppermute | solution.py:661
  (8 other events, 45.4 us)
Sparse Core Ops, SparseCore 0:
  138.0 90.0 reduce-scatter.1
  361.9 59.2 all-reduce.6

commit v8 on v7

--- a/solution.py
+++ b/solution.py
@@ -715,7 +715,7 @@
         start = lambda h, c: h * half + c * quarter
         pos = jnp.stack([dp, start(mine, core), row_start + start(mine, core), start(mine, 1 - core), start(1 - mine, core), start(1 - mine, 1 - core)])
         bias_col = lax.dynamic_slice(b_vocab, (start(mine, core),), (quarter,))[:, None]
-        shares = (1088, 1088, 968)
+        shares = (1088, 960, 640, 456)
         ends = [0]
         for w in shares[:-1]:
             ends.append(ends[-1] + max(16, quarter * w // sum(shares) // 16 * 16))
@@ -759,7 +759,7 @@
         dab, pack = back_pass(0, vp[None], pre, normed, rstd, z, m1, m2, du_share, ln_gain[None], loss_row, db_mat)
         back_done = dab
         pack = lax.psum(pack, "dp")
-        dab = [dab] + [swap_vp(dab, b) for b in range(1, n_shards)]
+        dab_1, dab_2 = swap_vp(dab, 1), swap_vp(dab, 2)
 
         chunk1, big = rows("whole", 1, back_done, info=info, u_all=u_all, big=big, puts=[twin0])
         twin1, far1 = send(1, chunk1)
@@ -768,23 +768,27 @@
         part = lax.dynamic_slice(pack, (core * n_half, 0), (n_half, cols))
         parts = [swap_vp(part, b) for b in range(1, n_shards)]
         far0, far_twin0 = forward(0, far0, chunk1)
+        dab_2 = after(dab_2, chunk1)
+        dab_3 = swap_vp(dab_2, 1)
 
         chunk2, big = rows("whole", 2, part, info=info, u_all=u_all, big=big, puts=[far0, far_twin0])
         twin2, far2 = send(2, chunk2)
-        big = put_rows(pos, big, [twin1, ((FAR, spans[1][0]), far1)])
-        far1, far_twin1 = forward(1, far1, big)
-        d_hidden = spread_pass(n_masks, hidden.shape, vp[None], pos_pad[:, None], w_trans, after(dab, big))
+        far1, far_twin1 = forward(1, far1, chunk2)
+        chunk3, big = rows("whole", 3, info=info, u_all=u_all, big=big, puts=[twin1, far1])
+        twin3, far3 = send(3, chunk3)
+        far2, far_twin2 = forward(2, far2, chunk3)
+        d_hidden = spread_pass(n_masks, hidden.shape, vp[None], pos_pad[:, None], w_trans, after([dab, dab_1, dab_2, dab_3], chunk3))
         parts = after(parts, d_hidden)
         others = [swap(p, CORE) for p in parts]
-        big = put_rows(after(pos, d_hidden), big, [far_twin1, twin2])
+        big = put_rows(after(pos, d_hidden), big, [far_twin1, twin2, far2, far_twin2, twin3])
         pack, parts, others = after((pack, parts, others), big)
         d_w, vec = join_pass(jnp.stack([vp, core]), pack, parts, others)
         db = pack[width + 16:].reshape(-1)[:shard_rows]
         loss = pack[width + 3, 0] / n_tokens
         grads = vec[0], vec[1], vec[2]
-        far2, far_twin2 = forward(2, far2, big, d_w, db, loss, *grads)
-        big = put_rows(pos, big, [far2])
-        big = put_rows(pos, big, [far_twin2])
+        far3, far_twin3 = forward(3, far3, big, d_w, db, loss, *grads)
+        big = put_rows(pos, big, [far3])
+        big = put_rows(pos, big, [far_twin3])
 
         return loss, d_hidden, d_w, *grads, big, db
 

time: 688 us -> 643 us (0.935)
  the two profiles are of different devices: /device:TPU:9 before, /device:TPU:0 now
where the time goes in v8:
time: 643 us; the launch traced here: 636 us
  Pallas kernels  344 us (53%)
  waiting for transfers between devices  213 us (33%)
  starting transfers between devices  33.4 us (5%)
  local copies, waits for them, and re-layouts  25.5 us (4%)
  between operations  16.4 us (3%)
    pallas_call x6, Pallas kernels, rows_pass(): pl.pallas_call(functools.partial(rows_kernel, kind, scale, s0, m, cut, n_...  193 us
    ppermute x12, waiting for transfers between devices, swap_vp(): return lax.ppermute(a, 'vp', [(d, d ^ bit) for d in range(n_shards)])  93 us
    ppermute x30, waiting for transfers between devices, swap(): return lax.ppermute(a, 'dp', [(d, d ^ bit) for d in range(n_groups)])  59.8 us
    psum x1, waiting for transfers between devices, local_step(): pack = lax.psum(pack, 'dp')  59.7 us
    pallas_call x1, Pallas kernels, du_pass(): pl.pallas_call(functools.partial(du_kernel, v, scale, base), grid=(n,), i...  48.1 us
    pallas_call x1, Pallas kernels, stats(): pl.pallas_call(functools.partial(stats_kernel, v), grid=(n,), in_specs=[w...  43.8 us
    pallas_call x3, Pallas kernels, put_rows(): pl.pallas_call(functools.partial(put_kernel, spots), in_specs=[SMEM] + [A...  17.3 us
    ppermute x12, starting transfers between devices, swap_vp(): return lax.ppermute(a, 'vp', [(d, d ^ bit) for d in range(n_shards)])  16.5 us
  transfers between devices with their start and end apart: 48, of which 17 were waited for; matrix products, arithmetic and copies ran while one was open for 3% of the time, Pallas kernels for 51%

profile of v8, /device:TPU:0, one launch (start us, length us, event | category | flops | bytes accessed | tf_op | source)
XLA Modules:
  0.0 636.0 jit_solution(17820986802297823143)
XLA Ops:
  9.0 15.7 %head.1 = (bf16[1232,1024]{1,0:T(8,128)(2,1)}, f32[1232,1024]{1,0:T(8,128)}, f32[1232,1024]{1,0:T(8,128)}, f32[1232,128]{1,0:T(8,128)}, bf16[1232,1024]{1,0:T(8,...) custom-call(bf16[16,512,1024]{2,1,0:T(8,128)(2,1)} %hid.1, s32[16,80,128]{2,1,0:T(8,128)} %broadcast_in_dim.64.pos_ref, ...), custom_call_target="tpu_custom_call" | custom-call | flops 51673824 | bytes 42008576 | tf_op jit(solution)/shard_map/head/pallas_call | solution.py:255
  24.8 3.0 collective-permute-start.15
  27.8 1.5 collective-permute-start.16
  31.1 43.8 %stats.1 = (f32[1232,12576]{1,0:T(8,128)}, f32[8,1232]{1,0:T(8,128)}) custom-call(bf16[1232,1024]{1,0:T(8,128)(2,1)} %get-tuple-element.82.u_ref, bf16[12576,1024]{1,0:T(8,128)(2,1)} %emb_hbm.11, f32[1,12576]{1,0:T(1,128)} %broadcast_in_dim.68.b_ref, s32[1232,128]{1,0:T(8,128)} %broadcast_in_dim.70.lab_ref), custom_call_target="tpu_custom_call" | custom-call | flops 317309568 | bytes 87730176 | tf_op jit(solution)/shard_map/stats/pallas_call | solution.py:96
  74.9 1.6 collective-permute-start
  76.5 2.6 collective-permute-start.1
  79.5 2.5 collective-permute-done.1
  82.6 2.5 collective-permute-done.2
  87.8 48.1 %du_pass.1 = (f32[4,1232,256]{2,1,0:T(8,128)}, f32[1,12576]{1,0:T(1,128)}, f32[8,1232]{1,0:T(8,128)}) custom-call(f32[1232,12576]{1,0:T(8,128)} %get-tuple-element.83.logits_ref, bf16[12576,1024]{1,0:T(8,128)(2,1)} %emb_hbm.11, f32[1232,128]{1,0:T(8,128)} %broadcast_in_dim.71.lse_ref, s32[1232,128]{1,0:T(8,128)} %broadcast_in_dim.70.lab_ref, ...), custom_call_target="tpu_custom_call" | custom-call | flops 317309568 | bytes 87730176 | tf_op jit(solution)/shard_map/du_pass/pallas_call | solution.py:182
  138.4 3.1 collective-permute-done.11
  141.7 1.7 broadcast_in_dim.79.bias_ref
  144.7 1.5 collective-permute-start.12
  146.8 19.5 %shard_map.152 = (f32[1088,1024]{1,0:T(8,128)}, bf16[8,1280,1024]{2,1,0:T(8,128)(2,1)}) custom-call(s32[6]{0:T(128)} %stack.73.pos, bf16[12576,1024]{1,0:T(8,128)(2,1)} %emb_hbm.11, f32[3144,1]{1,0:T(8,128)} %broadcast_in_dim.79.bias_ref, f32[2,2,1280]{2,1,0:T(2,128)} %pad_maximum_fusion.3.info_ref, f32[608,1024]{1,0:T(8,128)} %get-tuple-element.89.refs_0_, ...), custom_call_target="tpu_custom_call" | custom-call | flops 114085072 | bytes 11927552 | tf_op jit(solution)/shard_map/pallas_call | solution.py:456
  166.3 28.0 %collective-permute-done.12 = f32[2,1280]{1,0:T(2,128)S(1)} collective-permute-done((f32[2,1280]{1,0:T(2,128)S(1)}, f32[2,1280]{1,0:T(2,128)S(1)}, u32[]{:S(2)}, u32[]{:S(2)}) %collective-permute-start.12) | collective-permute-done | bytes 10272 | tf_op jit(solution)/shard_map/ppermute | solution.py:661
  195.5 7.6 %collective-permute-done.14 = f32[3,2,1280]{2,1,0:T(2,128)S(1)} collective-permute-done((f32[3,2,1280]{2,1,0:T(2,128)S(1)}, f32[3,2,1280]{2,1,0:T(2,128)S(1)}, u32[]{:S(2)}, u32[]{:S(2)}) %collective-permute-start.14) | collective-permute-done | bytes 30752 | tf_op jit(solution)/shard_map/ppermute | solution.py:661
  204.4 3.5 collective-permute-done.19.refs_6_
  208.0 1.4 copy-done.5
  209.4 1.5 copy-done.3
  210.9 33.1 %shard_map.153 = (f32[1088,1024]{1,0:T(8,128)}, bf16[8,1280,1024]{2,1,0:T(8,128)(2,1)}) custom-call(s32[6]{0:T(128)} %stack.73.pos, bf16[12576,1024]{1,0:T(8,128)(2,1)} %emb_hbm.11, f32[3144,1]{1,0:T(8,128)} %broadcast_in_dim.79.bias_ref, f32[8,2,1280]{2,1,0:T(2,128)} %pad_maximum_fusion.info_ref, ...), custom_call_target="tpu_custom_call", output_to_operand_aliasing={{1}: (12, {})} | custom-call | flops 228170144 | bytes 17170432 | tf_op jit(solution)/shard_map/pallas_call | solution.py:456
  244.0 15.8 %collective-permute-done.21.refs_0_ = f32[608,1024]{1,0:T(8,128)} collective-permute-done((f32[608,1024]{1,0:T(8,128)}, f32[608,1024]{1,0:T(8,128)}, u32[]{:S(2)}, u32[]{:S(2)}) %collective-permute-start.21) | collective-permute-done | bytes 2490400 | tf_op jit(solution)/shard_map/ppermute | solution.py:661
  261.4 3.4 collective-permute-start.8
  264.8 1.3 collective-permute-done.7
  269.4 1.5 copy-done.4
  270.8 1.5 copy-done.2
  272.3 21.8 %shard_map.154 = (f32[1088,1024]{1,0:T(8,128)}, bf16[8,1280,1024]{2,1,0:T(8,128)(2,1)}, f32[12576,1024]{1,0:T(8,128)}) custom-call(s32[6]{0:T(128)} %stack.73.pos, bf16[12576,1024]{1,0:T(8,128)(2,1)} %emb_hbm.11, f32[3144,1]{1,0:T(8,128)} %broadcast_in_dim.79.bias_ref, f32[8,2,1280]{2,1,0:T(2,128)} %pad_maximum_fusion.info_ref, ...), custom_call_target="tpu_custom_call", output_to_operand_aliasing={{1}: (8, {})} | custom-call | flops 114085072 | bytes 11927552 | tf_op jit(solution)/shard_map/pallas_call | solution.py:456
  296.9 7.2 %back.1 = (f32[1232,256]{1,0:T(8,128)}, f32[1096,256]{1,0:T(8,128)}) custom-call(s32[1]{0:T(128)} %bitcast.vp, f32[1232,1024]{1,0:T(8,128)} %get-tuple-element.78.refs_0_, f32[1232,1024]{1,0:T(8,128)} %get-tuple-element.79.norm_hbm.refs_1_, f32[1232,128]{1,0:T(8,128)} %get-tuple-element.80.refs_2_, bf16[1232,1024]{1,0:T(8,128)(2,1)} %get-tuple-element.81.refs_3_, ...), custom_call_target="tpu_custom_call" | custom-call | flops 6459228 | bytes 9461760 | tf_op jit(solution)/shard_map/back/pallas_call | solution.py:586
  304.1 51.2 %shard_map.155 = (f32[960,1024]{1,0:T(8,128)}, f32[12576,1024]{1,0:T(8,128)}) custom-call(s32[6]{0:T(128)} %stack.73.pos, bf16[12576,1024]{1,0:T(8,128)(2,1)} %emb_hbm.11, f32[3144,1]{1,0:T(8,128)} %broadcast_in_dim.79.bias_ref, f32[8,2,1280]{2,1,0:T(2,128)} %pad_maximum_fusion.info_ref, ...), custom_call_target="tpu_custom_call", output_to_operand_aliasing={{1}: (5, {})} | custom-call | flops 402653184 | bytes 26869760 | tf_op jit(solution)/shard_map/pallas_call | solution.py:456
  355.4 1.4 collective-permute-start.35
  356.9 59.7 %all-reduce.7.cloned.1.call-done.refs_0_ = f32[1096,256]{1,0:T(8,128)} async-done(((f32[1096,256]{1,0:T(8,128)}), f32[1096,256]{1,0:T(8,128)}) %all-reduce.7.cloned.1.call-update) | async-done | bytes 1122320 | tf_op jit(solution)/shard_map/psum | solution.py:761
  416.6 1.9 constant_dynamic-slice_fusion
  418.5 36.5 %shard_map.156 = (f32[640,1024]{1,0:T(8,128)}, f32[12576,1024]{1,0:T(8,128)}) custom-call(s32[6]{0:T(128)} %stack.73.pos, bf16[12576,1024]{1,0:T(8,128)(2,1)} %emb_hbm.11, f32[3144,1]{1,0:T(8,128)} %broadcast_in_dim.79.bias_ref, f32[8,2,1280]{2,1,0:T(2,128)} %pad_maximum_fusion.info_ref, ...), custom_call_target="tpu_custom_call", output_to_operand_aliasing={{1}: (5, {})} | custom-call | flops 268435456 | bytes 24903680 | tf_op jit(solution)/shard_map/pallas_call | solution.py:456
  456.2 1.9 collective-permute-start.30
  458.1 2.0 collective-permute-start.29
  460.1 52.3 %collective-permute-done.30.refs_2_ = f32[1232,256]{1,0:T(8,128)} collective-permute-done((f32[1232,256]{1,0:T(8,128)}, f32[1232,256]{1,0:T(8,128)}, u32[]{:S(2)}, u32[]{:S(2)}) %collective-permute-start.30) | collective-permute-done | bytes 1261600 | tf_op jit(solution)/shard_map/ppermute | solution.py:664
  512.8 2.1 collective-permute-done.29.refs_1_
  514.9 1.3 collective-permute-start.27
  516.2 19.8 %collective-permute-done.26.refs_1_ = f32[520,256]{1,0:T(8,128)} collective-permute-done((f32[520,256]{1,0:T(8,128)}, f32[520,256]{1,0:T(8,128)}, u32[]{:S(2)}, u32[]{:S(2)}) %collective-permute-start.26) | collective-permute-done | bytes 532512 | tf_op jit(solution)/shard_map/ppermute | solution.py:664
  536.0 2.1 collective-permute-start.28
  538.1 30.3 %shard_map.157 = (f32[456,1024]{1,0:T(8,128)}, f32[12576,1024]{1,0:T(8,128)}) custom-call(s32[6]{0:T(128)} %stack.73.pos, bf16[12576,1024]{1,0:T(8,128)(2,1)} %emb_hbm.11, f32[3144,1]{1,0:T(8,128)} %broadcast_in_dim.79.bias_ref, f32[8,2,1280]{2,1,0:T(2,128)} %pad_maximum_fusion.info_ref, ...), custom_call_target="tpu_custom_call", output_to_operand_aliasing={{1}: (5, {})} | custom-call | flops 191260256 | bytes 23773184 | tf_op jit(solution)/shard_map/pallas_call | solution.py:456
  569.0 11.3 %collective-permute-done.31.refs_3_ = f32[1232,256]{1,0:T(8,128)} collective-permute-done((f32[1232,256]{1,0:T(8,128)}, f32[1232,256]{1,0:T(8,128)}, u32[]{:S(2)}, u32[]{:S(2)}) %collective-permute-start.31) | collective-permute-done | bytes 1261600 | tf_op jit(solution)/shard_map/ppermute | solution.py:664
  580.3 1.3 collective-permute-start.44
  581.6 14.7 %spread.1 = bf16[16,512,1024]{2,1,0:T(8,128)(2,1)} custom-call(s32[1]{0:T(128)} %bitcast.vp, s32[16,1,80]{2,1,0:T(1,128)} %bitcast.34, bf16[1024,1024]{1,0:T(8,128)(2,1)} %w_ref.3, f32[1232,256]{1,0:T(8,128)} %get-tuple-element.128.refs_0_, f32[1232,256]{1,0:T(8,128)} %collective-permute-done.29.refs_1_, f32[1232,256]{1,0:T(8,128)} %collective-permute-done.30.refs_2_, ...), custom_call_target="tpu_custom_call" | custom-call | flops 21474836 | bytes 16777216 | tf_op jit(solution)/shard_map/spread/pallas_call | solution.py:637
  598.9 10.5 %put_rows.3.refs_0_ = f32[12576,1024]{1,0:T(8,128)} custom-call(s32[6]{0:T(128)} %stack.73.pos, f32[12576,1024]{1,0:T(8,128)} %get-tuple-element.136.refs_0_, f32[960,1024]{1,0:T(8,128)} %copy-done, f32[640,1024]{1,0:T(8,128)} %collective-permute-done.40.refs_2_, f32[640,1024]{1,0:T(8,128)} %collective-permute-done.41.refs_3_, ...), custom_call_target="tpu_custom_call", output_to_operand_aliasing={{}: (1, {})} | custom-call | flops 34160 | bytes 27328512 | tf_op jit(solution)/shard_map/put_rows/pallas_call | solution.py:489
  609.4 4.9 join.1
  617.7 1.5 fusion.3
  619.3 3.4 put_rows.4.refs_0_
  623.2 1.2 copy-done.6
  624.4 3.4 put_rows.5
  (130 shorter events, 29.9 us)
Async XLA Ops:
  7.2 289.7 %reduce-scatter.2.cloned.1.call-start = ((), (), s32[]{:S(2)}) async-start(), calls=%async_computation.1 | async-start | bytes 6307840 | tf_op jit(solution)/shard_map/reduce_scatter | solution.py:705
  24.8 112.6 %collective-permute-start.15 = (f32[608,1024]{1,0:T(8,128)}, f32[608,1024]{1,0:T(8,128)}, u32[]{:S(2)}, u32[]{:S(2)}) collective-permute-start(f32[608,1024]{1,0:T(8,128)} %get-tuple-element.89.refs_0_), channel_id=1, source_target_pairs={{0,2},{1,3},{2,0},{3,1},{4,6},{5,7},{6,4},{7,5},{8,10},{9,11},{10,... | collective-permute-start | bytes 7471112 | tf_op jit(solution)/shard_map/ppermute | solution.py:661
  27.8 110.1 %collective-permute-start.16 = (f32[624,1024]{1,0:T(8,128)}, f32[624,1024]{1,0:T(8,128)}, u32[]{:S(2)}, u32[]{:S(2)}) collective-permute-start(f32[624,1024]{1,0:T(8,128)} %get-tuple-element.90.refs_1_), channel_id=1, source_target_pairs={{0,4},{1,5},{2,6},{3,7},{4,0},{5,1},{6,2},{7,3},{8,12},{9,13},{10,... | collective-permute-start | bytes 7667720 | tf_op jit(solution)/shard_map/ppermute | solution.py:661
  74.9 4.5 collective-permute-start
  76.5 5.5 collective-permute-start.1
  79.1 6.0 collective-permute-start.2
  79.5 66.8 %collective-permute-start.5 = (f32[624,1024]{1,0:T(8,128)S(1)}, f32[624,1024]{1,0:T(8,128)}, u32[]{:S(2)}, u32[]{:S(2)}) collective-permute-start(f32[624,1024]{1,0:T(8,128)S(1)} %copy-done.1), channel_id=1, source_target_pairs={{0,1},{1,0},{2,3},{3,2},{4,5},{5,4},{6,7},{7,6},{8,9},{9,8},{10,11... | collective-permute-start | bytes 7667720 | tf_op jit(solution)/shard_map/ppermute | solution.py:661
  82.0 112.8 %collective-permute-start.9 = (f32[624,1024]{1,0:T(8,128)S(1)}, f32[624,1024]{1,0:T(8,128)}, u32[]{:S(2)}, u32[]{:S(2)}) collective-permute-start(f32[624,1024]{1,0:T(8,128)S(1)} %copy-done.1), channel_id=1, source_target_pairs={{0,2},{1,3},{2,0},{3,1},{4,6},{5,7},{6,4},{7,5},{8,10},{9,11},{10,... | collective-permute-start | bytes 7667720 | tf_op jit(solution)/shard_map/ppermute | solution.py:661
  135.9 1.2 collective-permute-start.3
  137.2 7.5 %collective-permute-start.4 = (f32[608,1024]{1,0:T(8,128)}, f32[608,1024]{1,0:T(8,128)}, u32[]{:S(2)}, u32[]{:S(2)}) collective-permute-start(f32[608,1024]{1,0:T(8,128)} %get-tuple-element.89.refs_0_), channel_id=1, source_target_pairs={{0,1},{1,0},{2,3},{3,2},{4,5},{5,4},{6,7},{7,6},{8,9},{9,8},{10,11... | collective-permute-start | bytes 7471112 | tf_op jit(solution)/shard_map/ppermute | solution.py:661
  137.4 57.5 %collective-permute-start.10 = (f32[608,1024]{1,0:T(8,128)}, f32[608,1024]{1,0:T(8,128)}, u32[]{:S(2)}, u32[]{:S(2)}) collective-permute-start(f32[608,1024]{1,0:T(8,128)} %get-tuple-element.89.refs_0_), channel_id=1, source_target_pairs={{0,4},{1,5},{2,6},{3,7},{4,0},{5,1},{6,2},{7,3},{8,12},{9,13},{10,... | collective-permute-start | bytes 7471112 | tf_op jit(solution)/shard_map/ppermute | solution.py:661
  137.9 3.7 collective-permute-start.11
  141.5 61.6 %collective-permute-start.17 = (f32[608,1024]{1,0:T(8,128)}, f32[608,1024]{1,0:T(8,128)}, u32[]{:S(2)}, u32[]{:S(2)}) collective-permute-start(f32[608,1024]{1,0:T(8,128)} %collective-permute-done.15.refs_0_), channel_id=1, source_target_pairs={{0,1},{1,0},{2,3},{3,2},{4,5},{5,4},{6,7},{7,6},{8,9},{9,8},{10,11... | collective-permute-start | bytes 7471112 | tf_op jit(solution)/shard_map/ppermute | solution.py:661
  141.6 275.1 %all-reduce.7.cloned.1.call-start = ((), (), s32[]{:S(2)}) async-start(), calls=%async_computation.2 | async-start | bytes 2244608 | tf_op jit(solution)/shard_map/psum | solution.py:761
  144.7 49.6 %collective-permute-start.12 = (f32[2,1280]{1,0:T(2,128)S(1)}, f32[2,1280]{1,0:T(2,128)S(1)}, u32[]{:S(2)}, u32[]{:S(2)}) collective-permute-start(f32[2,1280]{1,0:T(2,128)S(1)} %get-tuple-element.165), channel_id=1, source_target_pairs={{0,4},{1,5},{2,6},{3,7},{4,0},{5,1},{6,2},{7,3},{8,12},{9,13},{10,... | collective-permute-start | bytes 30728 | tf_op jit(solution)/shard_map/ppermute | solution.py:661
  146.2 48.1 %collective-permute-start.13 = (f32[2,1280]{1,0:T(2,128)S(1)}, f32[2,1280]{1,0:T(2,128)S(1)}, u32[]{:S(2)}, u32[]{:S(2)}) collective-permute-start(f32[2,1280]{1,0:T(2,128)S(1)} %get-tuple-element.165), channel_id=1, source_target_pairs={{0,6},{1,7},{2,4},{3,5},{4,2},{5,3},{6,0},{7,1},{8,14},{9,15},{10,... | collective-permute-start | bytes 30728 | tf_op jit(solution)/shard_map/ppermute | solution.py:661
  194.3 13.7 %collective-permute-start.20 = (f32[624,1024]{1,0:T(8,128)}, f32[624,1024]{1,0:T(8,128)}, u32[]{:S(2)}, u32[]{:S(2)}) collective-permute-start(f32[624,1024]{1,0:T(8,128)} %collective-permute-done.16.refs_5_), channel_id=1, source_target_pairs={{0,1},{1,0},{2,3},{3,2},{4,5},{5,4},{6,7},{7,6},{8,9},{9,8},{10,11... | collective-permute-start | bytes 7667720 | tf_op jit(solution)/shard_map/ppermute | solution.py:661
  194.3 65.5 %collective-permute-start.22 = (f32[624,1024]{1,0:T(8,128)}, f32[624,1024]{1,0:T(8,128)}, u32[]{:S(2)}, u32[]{:S(2)}) collective-permute-start(f32[624,1024]{1,0:T(8,128)} %collective-permute-done.16.refs_5_), channel_id=1, source_target_pairs={{0,2},{1,3},{2,0},{3,1},{4,6},{5,7},{6,4},{7,5},{8,10},{9,11},{10,... | collective-permute-start | bytes 7667720 | tf_op jit(solution)/shard_map/ppermute | solution.py:661
  194.9 13.1 %collective-permute-start.18 = (f32[624,1024]{1,0:T(8,128)}, f32[624,1024]{1,0:T(8,128)S(1)}, u32[]{:S(2)}, u32[]{:S(2)}) collective-permute-start(f32[624,1024]{1,0:T(8,128)} %collective-permute-done.9.refs_1_), channel_id=1, source_target_pairs={{0,1},{1,0},{2,3},{3,2},{4,5},{5,4},{6,7},{7,6},{8,9},{9,8},{10,11... | collective-permute-start | bytes 7667720 | tf_op jit(solution)/shard_map/ppermute | solution.py:661
  195.1 7.9 %collective-permute-start.14 = (f32[3,2,1280]{2,1,0:T(2,128)S(1)}, f32[3,2,1280]{2,1,0:T(2,128)S(1)}, u32[]{:S(2)}, u32[]{:S(2)}) collective-permute-start(f32[3,2,1280]{2,1,0:T(2,128)S(1)} %pad_maximum_fusion.2), channel_id=1, source_target_pairs={{0,1},{1,0},{2,3},{3,2},{4,5},{5,4},{6,7},{7,6},{8,9},{9,8},{10,11... | collective-permute-start | bytes 92168 | tf_op jit(solution)/shard_map/ppermute | solution.py:661
  203.0 4.9 collective-permute-start.19
  203.2 56.7 %collective-permute-start.21 = (f32[608,1024]{1,0:T(8,128)}, f32[608,1024]{1,0:T(8,128)}, u32[]{:S(2)}, u32[]{:S(2)}) collective-permute-start(f32[608,1024]{1,0:T(8,128)} %collective-permute-done.15.refs_0_), channel_id=1, source_target_pairs={{0,4},{1,5},{2,6},{3,7},{4,0},{5,1},{6,2},{7,3},{8,12},{9,13},{10,... | collective-permute-start | bytes 7471112 | tf_op jit(solution)/shard_map/ppermute | solution.py:661
  259.8 9.6 %collective-permute-start.24 = (f32[624,1024]{1,0:T(8,128)}, f32[624,1024]{1,0:T(8,128)S(1)}, u32[]{:S(2)}, u32[]{:S(2)}) collective-permute-start(f32[624,1024]{1,0:T(8,128)} %collective-permute-done.22.refs_1_), channel_id=1, source_target_pairs={{0,1},{1,0},{2,3},{3,2},{4,5},{5,4},{6,7},{7,6},{8,9},{9,8},{10,11... | collective-permute-start | bytes 7667720 | tf_op jit(solution)/shard_map/ppermute | solution.py:661
  259.8 9.5 %collective-permute-start.23 = (f32[608,1024]{1,0:T(8,128)}, f32[608,1024]{1,0:T(8,128)S(1)}, u32[]{:S(2)}, u32[]{:S(2)}) collective-permute-start(f32[608,1024]{1,0:T(8,128)} %collective-permute-done.21.refs_0_), channel_id=1, source_target_pairs={{0,1},{1,0},{2,3},{3,2},{4,5},{5,4},{6,7},{7,6},{8,9},{9,8},{10,11... | collective-permute-start | bytes 7471112 | tf_op jit(solution)/shard_map/ppermute | solution.py:661
  260.4 4.4 collective-permute-start.6
  260.4 5.8 collective-permute-start.7
  261.4 5.8 collective-permute-start.8
  294.1 9.9 %collective-permute-start.25 = (f32[1088,1024]{1,0:T(8,128)}, f32[1088,1024]{1,0:T(8,128)}, u32[]{:S(2)}, u32[]{:S(2)}) collective-permute-start(f32[1088,1024]{1,0:T(8,128)} %get-tuple-element.110), channel_id=1, source_target_pairs={{0,1},{1,0},{2,3},{3,2},{4,5},{5,4},{6,7},{7,6},{8,9},{9,8},{10,11... | collective-permute-start | bytes 13369352 | tf_op jit(solution)/shard_map/ppermute | solution.py:661
  294.2 61.0 %collective-permute-start.32 = (f32[1088,1024]{1,0:T(8,128)}, f32[1088,1024]{1,0:T(8,128)}, u32[]{:S(2)}, u32[]{:S(2)}) collective-permute-start(f32[1088,1024]{1,0:T(8,128)} %get-tuple-element.110), channel_id=1, source_target_pairs={{0,2},{1,5},{2,0},{3,7},{4,6},{5,1},{6,4},{7,3},{8,10},{9,13},{10,... | collective-permute-start | bytes 13369352 | tf_op jit(solution)/shard_map/ppermute | solution.py:667
  355.3 63.2 %collective-permute-start.33 = (f32[1088,1024]{1,0:T(8,128)}, f32[1088,1024]{1,0:T(8,128)}, u32[]{:S(2)}, u32[]{:S(2)}) collective-permute-start(f32[1088,1024]{1,0:T(8,128)} %collective-permute-done.32.refs_2_), channel_id=1, source_target_pairs={{0,1},{1,0},{2,3},{3,2},{4,5},{5,4},{6,7},{7,6},{8,9},{9,8},{10,11... | collective-permute-start | bytes 13369352 | tf_op jit(solution)/shard_map/ppermute | solution.py:661
  355.4 102.7 %collective-permute-start.35 = (f32[960,1024]{1,0:T(8,128)}, f32[960,1024]{1,0:T(8,128)}, u32[]{:S(2)}, u32[]{:S(2)}) collective-permute-start(f32[960,1024]{1,0:T(8,128)} %get-tuple-element.118), channel_id=1, source_target_pairs={{0,2},{1,5},{2,0},{3,7},{4,6},{5,1},{6,4},{7,3},{8,10},{9,13},{10,... | collective-permute-start | bytes 11796488 | tf_op jit(solution)/shard_map/ppermute | solution.py:667
  356.8 179.2 %collective-permute-start.34 = (f32[960,1024]{1,0:T(8,128)}, f32[960,1024]{1,0:T(8,128)}, u32[]{:S(2)}, u32[]{:S(2)}) collective-permute-start(f32[960,1024]{1,0:T(8,128)} %get-tuple-element.118), channel_id=1, source_target_pairs={{0,1},{1,0},{2,3},{3,2},{4,5},{5,4},{6,7},{7,6},{8,9},{9,8},{10,11... | collective-permute-start | bytes 11796488 | tf_op jit(solution)/shard_map/ppermute | solution.py:661
  455.0 83.1 %collective-permute-start.41 = (f32[640,1024]{1,0:T(8,128)}, f32[640,1024]{1,0:T(8,128)}, u32[]{:S(2)}, u32[]{:S(2)}) collective-permute-start(f32[640,1024]{1,0:T(8,128)} %get-tuple-element.125), channel_id=1, source_target_pairs={{0,2},{1,5},{2,0},{3,7},{4,6},{5,1},{6,4},{7,3},{8,10},{9,13},{10,... | collective-permute-start | bytes 7864328 | tf_op jit(solution)/shard_map/ppermute | solution.py:667
  456.2 56.2 %collective-permute-start.30 = (f32[1232,256]{1,0:T(8,128)}, f32[1232,256]{1,0:T(8,128)}, u32[]{:S(2)}, u32[]{:S(2)}) collective-permute-start(f32[1232,256]{1,0:T(8,128)} %get-tuple-element.128.refs_0_), channel_id=1, source_target_pairs={{0,16},{8,24},{16,0},{24,8},{1,17},{9,25},{17,1},{25,9},{2,18},{10... | collective-permute-start | bytes 3784712 | tf_op jit(solution)/shard_map/ppermute | solution.py:664
  458.1 138.9 %collective-permute-start.39 = (f32[960,1024]{1,0:T(8,128)}, f32[960,1024]{1,0:T(8,128)S(1)}, u32[]{:S(2)}, u32[]{:S(2)}) collective-permute-start(f32[960,1024]{1,0:T(8,128)} %collective-permute-done.35.refs_3_), channel_id=1, source_target_pairs={{0,1},{1,0},{2,3},{3,2},{4,5},{5,4},{6,7},{7,6},{8,9},{9,8},{10,11... | collective-permute-start | bytes 11796488 | tf_op jit(solution)/shard_map/ppermute | solution.py:661
  458.1 56.9 %collective-permute-start.29 = (f32[1232,256]{1,0:T(8,128)}, f32[1232,256]{1,0:T(8,128)}, u32[]{:S(2)}, u32[]{:S(2)}) collective-permute-start(f32[1232,256]{1,0:T(8,128)} %get-tuple-element.128.refs_0_), channel_id=1, source_target_pairs={{0,8},{8,0},{16,24},{24,16},{1,9},{9,1},{17,25},{25,17},{2,10},{10... | collective-permute-start | bytes 3784712 | tf_op jit(solution)/shard_map/ppermute | solution.py:664
  512.4 23.6 %collective-permute-start.26 = (f32[520,256]{1,0:T(8,128)}, f32[520,256]{1,0:T(8,128)}, u32[]{:S(2)}, u32[]{:S(2)}) collective-permute-start(f32[520,256]{1,0:T(8,128)} %constant_dynamic-slice_fusion), channel_id=1, source_target_pairs={{0,8},{8,0},{16,24},{24,16},{1,9},{9,1},{17,25},{25,17},{2,10},{10... | collective-permute-start | bytes 1597448 | tf_op jit(solution)/shard_map/ppermute | solution.py:664
  514.9 53.5 %collective-permute-start.27 = (f32[520,256]{1,0:T(8,128)}, f32[520,256]{1,0:T(8,128)}, u32[]{:S(2)}, u32[]{:S(2)}) collective-permute-start(f32[520,256]{1,0:T(8,128)} %constant_dynamic-slice_fusion), channel_id=1, source_target_pairs={{0,16},{8,24},{16,0},{24,8},{1,17},{9,25},{17,1},{25,9},{2,18},{10... | collective-permute-start | bytes 1597448 | tf_op jit(solution)/shard_map/ppermute | solution.py:664
  536.0 60.6 %collective-permute-start.40 = (f32[640,1024]{1,0:T(8,128)}, f32[640,1024]{1,0:T(8,128)}, u32[]{:S(2)}, u32[]{:S(2)}) collective-permute-start(f32[640,1024]{1,0:T(8,128)} %get-tuple-element.125), channel_id=1, source_target_pairs={{0,1},{1,0},{2,3},{3,2},{4,5},{5,4},{6,7},{7,6},{8,9},{9,8},{10,11... | collective-permute-start | bytes 7864328 | tf_op jit(solution)/shard_map/ppermute | solution.py:661
  536.0 32.7 %collective-permute-start.28 = (f32[520,256]{1,0:T(8,128)}, f32[520,256]{1,0:T(8,128)}, u32[]{:S(2)}, u32[]{:S(2)}) collective-permute-start(f32[520,256]{1,0:T(8,128)} %constant_dynamic-slice_fusion), channel_id=1, source_target_pairs={{0,24},{8,16},{16,8},{24,0},{1,25},{9,17},{17,9},{25,1},{2,26},{10... | collective-permute-start | bytes 1597448 | tf_op jit(solution)/shard_map/ppermute | solution.py:664
  538.1 42.2 %collective-permute-start.31 = (f32[1232,256]{1,0:T(8,128)}, f32[1232,256]{1,0:T(8,128)}, u32[]{:S(2)}, u32[]{:S(2)}) collective-permute-start(f32[1232,256]{1,0:T(8,128)} %collective-permute-done.30.refs_2_), channel_id=1, source_target_pairs={{0,8},{8,0},{16,24},{24,16},{1,9},{9,1},{17,25},{25,17},{2,10},{10... | collective-permute-start | bytes 3784712 | tf_op jit(solution)/shard_map/ppermute | solution.py:664
  568.4 29.4 %collective-permute-start.42 = (f32[640,1024]{1,0:T(8,128)}, f32[640,1024]{1,0:T(8,128)}, u32[]{:S(2)}, u32[]{:S(2)}) collective-permute-start(f32[640,1024]{1,0:T(8,128)} %collective-permute-done.41.refs_3_), channel_id=1, source_target_pairs={{0,1},{1,0},{2,3},{3,2},{4,5},{5,4},{6,7},{7,6},{8,9},{9,8},{10,11... | collective-permute-start | bytes 7864328 | tf_op jit(solution)/shard_map/ppermute | solution.py:661
  568.7 27.6 %collective-permute-start.43 = (f32[456,1024]{1,0:T(8,128)}, f32[456,1024]{1,0:T(8,128)}, u32[]{:S(2)}, u32[]{:S(2)}) collective-permute-start(f32[456,1024]{1,0:T(8,128)} %get-tuple-element.127), channel_id=1, source_target_pairs={{0,1},{1,0},{2,3},{3,2},{4,5},{5,4},{6,7},{7,6},{8,9},{9,8},{10,11... | collective-permute-start | bytes 5603336 | tf_op jit(solution)/shard_map/ppermute | solution.py:661
  580.3 38.8 %collective-permute-start.44 = (f32[456,1024]{1,0:T(8,128)}, f32[456,1024]{1,0:T(8,128)}, u32[]{:S(2)}, u32[]{:S(2)}) collective-permute-start(f32[456,1024]{1,0:T(8,128)} %get-tuple-element.127), channel_id=1, source_target_pairs={{0,2},{1,5},{2,0},{3,7},{4,6},{5,1},{6,4},{7,3},{8,10},{9,13},{10,... | collective-permute-start | bytes 5603336 | tf_op jit(solution)/shard_map/ppermute | solution.py:667
  596.4 13.0 %collective-permute-start.36 = (f32[520,256]{1,0:T(8,128)}, f32[520,256]{1,0:T(8,128)}, u32[]{:S(2)}, u32[]{:S(2)}) collective-permute-start(f32[520,256]{1,0:T(8,128)} %collective-permute-done.26.refs_1_), channel_id=1, source_target_pairs={{0,1},{1,0},{2,3},{3,2},{4,5},{5,4},{6,7},{7,6},{8,9},{9,8},{10,11... | collective-permute-start | bytes 1597448 | tf_op jit(solution)/shard_map/ppermute | solution.py:661
  596.6 12.8 %collective-permute-start.37 = (f32[520,256]{1,0:T(8,128)}, f32[520,256]{1,0:T(8,128)}, u32[]{:S(2)}, u32[]{:S(2)}) collective-permute-start(f32[520,256]{1,0:T(8,128)} %collective-permute-done.27.refs_2_), channel_id=1, source_target_pairs={{0,1},{1,0},{2,3},{3,2},{4,5},{5,4},{6,7},{7,6},{8,9},{9,8},{10,11... | collective-permute-start | bytes 1597448 | tf_op jit(solution)/shard_map/ppermute | solution.py:661
  597.0 12.4 %collective-permute-start.38 = (f32[520,256]{1,0:T(8,128)}, f32[520,256]{1,0:T(8,128)}, u32[]{:S(2)}, u32[]{:S(2)}) collective-permute-start(f32[520,256]{1,0:T(8,128)} %collective-permute-done.28.refs_3_), channel_id=1, source_target_pairs={{0,1},{1,0},{2,3},{3,2},{4,5},{5,4},{6,7},{7,6},{8,9},{9,8},{10,11... | collective-permute-start | bytes 1597448 | tf_op jit(solution)/shard_map/ppermute | solution.py:661
  619.2 4.0 collective-permute-start.45
  (12 other events, 171.1 us)
Sparse Core Ops, SparseCore 0:
  141.7 88.0 reduce-scatter.1
  357.0 59.5 all-reduce.6

commit v9 on v7

--- a/solution.py
+++ b/solution.py
@@ -12,7 +12,7 @@
 NT = (((1,), (1,)), ((), ()))
 NN = (((1,), (0,)), ((), ()))
 VB = 1024
-VMEM_LIMIT = 60 << 20
+VMEM_LIMIT = 67_000_000
 COVER = 100
 PARTS = 4
 LEAST = float(jnp.finfo(jnp.float32).min)
@@ -536,6 +536,26 @@
     )(idx, own, *mine, *theirs)
 
 
+def means_kernel(width, *refs):
+    (a, b, c, d), (m1_ref, m2_ref) = refs[:4], refs[4:]
+    total = ((a[...] + b[...]) + (c[...] + d[...])) * (1.0 / width)
+    for j, m_ref in enumerate((m1_ref, m2_ref)):
+        m_ref[...] = jnp.broadcast_to(total[j:j + 1, :], (128, total.shape[1])).T
+
+
+def means_pass(width, sums):
+    n = sums[0].shape[1]
+    return pl.pallas_call(
+        functools.partial(means_kernel, width),
+        in_specs=[VMEM] * 4,
+        out_specs=[VMEM] * 2,
+        out_shape=[jax.ShapeDtypeStruct((n, 128), F32)] * 2,
+        compiler_params=pltpu.CompilerParams(vmem_limit_bytes=VMEM_LIMIT),
+        cost_estimate=pl.CostEstimate(flops=(n * 256) // COVER, bytes_accessed=n * 1200, transcendentals=0),
+        name="means",
+    )(*sums)
+
+
 def back_kernel(base, vp, *refs):
     refs = list(refs)
     srcs = [refs.pop(0) for _ in range(7)]
@@ -565,15 +585,19 @@
             pack_ref[e + j:e + j + 1, cs] = jnp.sum(x, axis=0, keepdims=True)
     loss_ref, db_ref = extra
     pack_ref[:e, :] = lax.dot_general(z[...], dab_ref[...].astype(BF16), (((0,), (0,)), ((), ())), preferred_element_type=F32)
-    pack_ref[e + 3:e + 4, :] = loss_ref[...]
+    pack_ref[e + 3:e + 4, :] = jnp.broadcast_to(loss_ref[...], (1, cols))
     pack_ref[e + 4:e + 16, :] = jnp.zeros_like(pack_ref[e + 4:e + 16, :])
-    pack_ref[e + 16:, :] = db_ref[...]
+    n_db = db_ref.shape[1]
+    pack_ref[e + 16 + n_db // cols:, :] = jnp.zeros_like(pack_ref[e + 16 + n_db // cols:, :])
+    for j, c in enumerate(range(0, n_db, cols)):
+        w = min(cols, n_db - c)
+        pack_ref[e + 16 + j:e + 17 + j, :w] = db_ref[:, c:c + w]
 
 
 def back_pass(base, vp, pre, normed, rstd, z, m1, m2, du, gain, *extra):
     n, cols = du.shape
     e = z.shape[1]
-    n_pack = e + 16 + extra[1].shape[0]
+    n_pack = e + 16 + -(-extra[1].shape[1] // cols // 8) * 8
     block = lambda *s: pl.BlockSpec(s, lambda i, p: (0,) * len(s))
     gs = pltpu.PrefetchScalarGridSpec(
         num_scalar_prefetch=1,
@@ -715,7 +739,7 @@
         start = lambda h, c: h * half + c * quarter
         pos = jnp.stack([dp, start(mine, core), row_start + start(mine, core), start(mine, 1 - core), start(1 - mine, core), start(1 - mine, 1 - core)])
         bias_col = lax.dynamic_slice(b_vocab, (start(mine, core),), (quarter,))[:, None]
-        shares = (1088, 1088, 968)
+        shares = (1088, 1216, 840)
         ends = [0]
         for w in shares[:-1]:
             ends.append(ends[-1] + max(16, quarter * w // sum(shares) // 16 * 16))
@@ -747,19 +771,15 @@
         side, u_all = rows("side", 0, info=info, tokens=tokens, u_all=u_all)
         d_lo, d_hi = after((d_lo, d_hi), side)
         tokens[X | Y], tokens[X | Y | CORE] = (d_lo, d_hi), (swap(d_lo, CORE), swap(d_hi, CORE))
-        sums = order_sum(after(sums, side)) / width
-        m1, m2 = column(sums[0]), column(sums[1])
+        m1, m2 = means_pass(width, after(sums, side))
         chunk0, u_all, big = rows("far", 0, m1, m2, info=info, tokens=tokens, u_all=u_all, parts=((own, 0), (side, 0)))
         twin0, far0 = send(0, chunk0)
 
         du_share = after(du_share, chunk0)
-        loss_row = jnp.pad(loss_part[None, None], ((0, 0), (0, cols - 1)))
-        db_rows = -(-shard_rows // cols // 8) * 8
-        db_mat = jnp.pad(db_part[0], (0, db_rows * cols - shard_rows)).reshape(db_rows, cols)
-        dab, pack = back_pass(0, vp[None], pre, normed, rstd, z, m1, m2, du_share, ln_gain[None], loss_row, db_mat)
+        dab, pack = back_pass(0, vp[None], pre, normed, rstd, z, m1, m2, du_share, ln_gain[None], loss_part[None, None], db_part)
         back_done = dab
         pack = lax.psum(pack, "dp")
-        dab = [dab] + [swap_vp(dab, b) for b in range(1, n_shards)]
+        dab_1, dab_2 = swap_vp(dab, 1), swap_vp(dab, 2)
 
         chunk1, big = rows("whole", 1, back_done, info=info, u_all=u_all, big=big, puts=[twin0])
         twin1, far1 = send(1, chunk1)
@@ -768,15 +788,17 @@
         part = lax.dynamic_slice(pack, (core * n_half, 0), (n_half, cols))
         parts = [swap_vp(part, b) for b in range(1, n_shards)]
         far0, far_twin0 = forward(0, far0, chunk1)
+        dab_2 = after(dab_2, chunk1)
+        dab_3 = swap_vp(dab_2, 1)
 
         chunk2, big = rows("whole", 2, part, info=info, u_all=u_all, big=big, puts=[far0, far_twin0])
         twin2, far2 = send(2, chunk2)
-        big = put_rows(pos, big, [twin1, ((FAR, spans[1][0]), far1)])
-        far1, far_twin1 = forward(1, far1, big)
-        d_hidden = spread_pass(n_masks, hidden.shape, vp[None], pos_pad[:, None], w_trans, after(dab, big))
-        parts = after(parts, d_hidden)
+        d_hidden = spread_pass(n_masks, hidden.shape, vp[None], pos_pad[:, None], w_trans, after([dab, dab_1, dab_2, dab_3], chunk2))
+        far1, far_twin1 = forward(1, far1, d_hidden)
+        big = put_rows(after(pos, d_hidden), big, [twin1, far1])
+        parts = after(parts, big)
         others = [swap(p, CORE) for p in parts]
-        big = put_rows(after(pos, d_hidden), big, [far_twin1, twin2])
+        big = put_rows(pos, big, [far_twin1, twin2])
         pack, parts, others = after((pack, parts, others), big)
         d_w, vec = join_pass(jnp.stack([vp, core]), pack, parts, others)
         db = pack[width + 16:].reshape(-1)[:shard_rows]

time: 688 us -> 650 us (0.945)
  the two profiles are of different devices: /device:TPU:9 before, /device:TPU:21 now
where the time goes in v9:
time: 650 us; the launch traced here: 642 us
  Pallas kernels  344 us (53%)
  waiting for transfers between devices  218 us (34%)
  starting transfers between devices  42.1 us (6%)
  between operations  16.3 us (3%)
  local copies, waits for them, and re-layouts  15.9 us (2%)
    pallas_call x5, Pallas kernels, rows_pass(): pl.pallas_call(functools.partial(rows_kernel, kind, scale, s0, m, cut, n_...  183 us
    ppermute x12, waiting for transfers between devices, swap_vp(): return lax.ppermute(a, 'vp', [(d, d ^ bit) for d in range(n_shards)])  109 us
    ppermute x28, waiting for transfers between devices, swap(): return lax.ppermute(a, 'dp', [(d, d ^ bit) for d in range(n_groups)])  55.2 us
    psum x1, waiting for transfers between devices, local_step(): pack = lax.psum(pack, 'dp')  54.4 us
    pallas_call x1, Pallas kernels, du_pass(): pl.pallas_call(functools.partial(du_kernel, v, scale, base), grid=(n,), i...  48.1 us
    pallas_call x1, Pallas kernels, stats(): pl.pallas_call(functools.partial(stats_kernel, v), grid=(n,), in_specs=[w...  43.8 us
    ppermute x28, starting transfers between devices, swap(): return lax.ppermute(a, 'dp', [(d, d ^ bit) for d in range(n_groups)])  24.1 us
    pallas_call x4, Pallas kernels, put_rows(): pl.pallas_call(functools.partial(put_kernel, spots), in_specs=[SMEM] + [A...  23.4 us
  transfers between devices with their start and end apart: 45, of which 15 were waited for; matrix products, arithmetic and copies ran while one was open for 3% of the time, Pallas kernels for 50%

profile of v9, /device:TPU:21, one launch (start us, length us, event | category | flops | bytes accessed | tf_op | source)
XLA Modules:
  0.0 642.0 jit_solution(4439132879771875535)
XLA Ops:
  9.6 15.7 %head.1 = (bf16[1232,1024]{1,0:T(8,128)(2,1)}, f32[1232,1024]{1,0:T(8,128)}, f32[1232,1024]{1,0:T(8,128)}, f32[1232,128]{1,0:T(8,128)}, bf16[1232,1024]{1,0:T(8,...) custom-call(bf16[16,512,1024]{2,1,0:T(8,128)(2,1)} %hid.1, s32[16,80,128]{2,1,0:T(8,128)} %broadcast_in_dim.50.pos_ref, ...), custom_call_target="tpu_custom_call" | custom-call | flops 51673824 | bytes 42008576 | tf_op jit(solution)/shard_map/head/pallas_call | solution.py:255
  25.3 1.3 collective-permute-start.15
  26.9 1.5 broadcast_in_dim.54.b_ref
  29.5 43.8 %stats.1 = (f32[1232,12576]{1,0:T(8,128)}, f32[8,1232]{1,0:T(8,128)}) custom-call(bf16[1232,1024]{1,0:T(8,128)(2,1)} %get-tuple-element.81.u_ref, bf16[12576,1024]{1,0:T(8,128)(2,1)} %emb_hbm.9, f32[1,12576]{1,0:T(1,128)} %broadcast_in_dim.54.b_ref, s32[1232,128]{1,0:T(8,128)} %broadcast_in_dim.56.lab_ref), custom_call_target="tpu_custom_call" | custom-call | flops 317309568 | bytes 87730176 | tf_op jit(solution)/shard_map/stats/pallas_call | solution.py:96
  73.2 1.3 collective-permute-start
  74.6 1.3 collective-permute-start.2
  76.7 2.0 collective-permute-start.5
  81.7 48.1 %du_pass.1 = (f32[4,1232,256]{2,1,0:T(8,128)}, f32[1,12576]{1,0:T(1,128)}, f32[8,1232]{1,0:T(8,128)}) custom-call(f32[1232,12576]{1,0:T(8,128)} %get-tuple-element.82.logits_ref, bf16[12576,1024]{1,0:T(8,128)(2,1)} %emb_hbm.9, f32[1232,128]{1,0:T(8,128)} %broadcast_in_dim.57.lse_ref, s32[1232,128]{1,0:T(8,128)} %broadcast_in_dim.56.lab_ref, ...), custom_call_target="tpu_custom_call" | custom-call | flops 317309568 | bytes 87730176 | tf_op jit(solution)/shard_map/du_pass/pallas_call | solution.py:182
  130.4 2.7 collective-permute-start.3
  134.5 1.2 collective-permute-start.10
  135.8 1.2 collective-permute-start.11
  137.0 1.9 collective-permute-done.11
  141.0 1.6 broadcast_in_dim.61.bias_ref
  144.1 2.2 collective-permute-start.13
  146.3 19.9 %shard_map.152 = (f32[1088,1024]{1,0:T(8,128)}, bf16[8,1280,1024]{2,1,0:T(8,128)(2,1)}) custom-call(s32[6]{0:T(128)} %stack.73.pos, bf16[12576,1024]{1,0:T(8,128)(2,1)} %emb_hbm.9, f32[3144,1]{1,0:T(8,128)} %broadcast_in_dim.61.bias_ref, f32[2,2,1280]{2,1,0:T(2,128)} %pad_maximum_fusion.3.info_ref, f32[608,1024]{1,0:T(8,128)} %get-tuple-element.88.refs_0_, ...), custom_call_target="tpu_custom_call" | custom-call | flops 114085072 | bytes 11927552 | tf_op jit(solution)/shard_map/pallas_call | solution.py:456
  166.3 24.5 %collective-permute-done.12 = f32[2,1280]{1,0:T(2,128)} collective-permute-done((f32[2,1280]{1,0:T(2,128)}, f32[2,1280]{1,0:T(2,128)}, u32[]{:S(2)}, u32[]{:S(2)}) %collective-permute-start.12) | collective-permute-done | bytes 10272 | tf_op jit(solution)/shard_map/ppermute | solution.py:685
  194.3 5.9 collective-permute-done.14
  200.6 1.2 collective-permute-start.21
  203.3 2.0 collective-permute-done.19.refs_6_
  205.3 33.3 %shard_map.153 = (f32[1088,1024]{1,0:T(8,128)}, bf16[8,1280,1024]{2,1,0:T(8,128)(2,1)}) custom-call(s32[6]{0:T(128)} %stack.73.pos, bf16[12576,1024]{1,0:T(8,128)(2,1)} %emb_hbm.9, f32[3144,1]{1,0:T(8,128)} %broadcast_in_dim.61.bias_ref, f32[8,2,1280]{2,1,0:T(2,128)} %pad_maximum_fusion.info_ref, ...), custom_call_target="tpu_custom_call", output_to_operand_aliasing={{1}: (12, {})} | custom-call | flops 228170144 | bytes 17170432 | tf_op jit(solution)/shard_map/pallas_call | solution.py:456
  238.6 17.8 %collective-permute-done.21.refs_0_ = f32[608,1024]{1,0:T(8,128)} collective-permute-done((f32[608,1024]{1,0:T(8,128)}, f32[608,1024]{1,0:T(8,128)}, u32[]{:S(2)}, u32[]{:S(2)}) %collective-permute-start.21) | collective-permute-done | bytes 2490400 | tf_op jit(solution)/shard_map/ppermute | solution.py:685
  258.5 2.0 collective-permute-start.7
  260.7 1.7 collective-permute-done.7.refs_2_
  264.0 2.1 means.1
  266.2 21.6 %shard_map.154 = (f32[1088,1024]{1,0:T(8,128)}, bf16[8,1280,1024]{2,1,0:T(8,128)(2,1)}, f32[12576,1024]{1,0:T(8,128)}) custom-call(s32[6]{0:T(128)} %stack.73.pos, bf16[12576,1024]{1,0:T(8,128)(2,1)} %emb_hbm.9, f32[3144,1]{1,0:T(8,128)} %broadcast_in_dim.61.bias_ref, f32[8,2,1280]{2,1,0:T(2,128)} %pad_maximum_fusion.info_ref, ...), custom_call_target="tpu_custom_call", output_to_operand_aliasing={{1}: (8, {})} | custom-call | flops 114085072 | bytes 11927552 | tf_op jit(solution)/shard_map/pallas_call | solution.py:456
  287.8 1.5 collective-permute-start.25
  289.3 1.2 collective-permute-start.32
  290.5 7.8 %back.1 = (f32[1232,256]{1,0:T(8,128)}, f32[1096,256]{1,0:T(8,128)}) custom-call(s32[1]{0:T(128)} %bitcast.vp, f32[1232,1024]{1,0:T(8,128)} %get-tuple-element.77.refs_0_, f32[1232,1024]{1,0:T(8,128)} %get-tuple-element.78.norm_hbm.refs_1_, f32[1232,128]{1,0:T(8,128)} %get-tuple-element.79.refs_2_, bf16[1232,1024]{1,0:T(8,128)(2,1)} %get-tuple-element.80.refs_3_, ...), custom_call_target="tpu_custom_call" | custom-call | flops 6459228 | bytes 9461760 | tf_op jit(solution)/shard_map/back/pallas_call | solution.py:610
  298.4 63.5 %shard_map.155 = (f32[1216,1024]{1,0:T(8,128)}, f32[12576,1024]{1,0:T(8,128)}) custom-call(s32[6]{0:T(128)} %stack.73.pos, bf16[12576,1024]{1,0:T(8,128)(2,1)} %emb_hbm.9, f32[3144,1]{1,0:T(8,128)} %broadcast_in_dim.61.bias_ref, f32[8,2,1280]{2,1,0:T(2,128)} %pad_maximum_fusion.info_ref, ...), custom_call_target="tpu_custom_call", output_to_operand_aliasing={{1}: (5, {})} | custom-call | flops 510027360 | bytes 28442624 | tf_op jit(solution)/shard_map/pallas_call | solution.py:456
  362.8 2.5 collective-permute-start.30
  366.4 53.4 %collective-permute-done.30.refs_2_ = f32[1232,256]{1,0:T(8,128)} collective-permute-done((f32[1232,256]{1,0:T(8,128)}, f32[1232,256]{1,0:T(8,128)}, u32[]{:S(2)}, u32[]{:S(2)}) %collective-permute-start.30) | collective-permute-done | bytes 1261600 | tf_op jit(solution)/shard_map/ppermute | solution.py:688
  419.8 2.3 collective-permute-start.31
  423.0 54.4 %all-reduce.5.cloned.1.call-done.refs_0_ = f32[1096,256]{1,0:T(8,128)} async-done(((f32[1096,256]{1,0:T(8,128)}), f32[1096,256]{1,0:T(8,128)}) %all-reduce.5.cloned.1.call-update) | async-done | bytes 1122320 | tf_op jit(solution)/shard_map/psum | solution.py:781
  477.3 1.9 constant_dynamic-slice_fusion
  479.2 44.9 %shard_map.156 = (f32[840,1024]{1,0:T(8,128)}, f32[12576,1024]{1,0:T(8,128)}) custom-call(s32[6]{0:T(128)} %stack.73.pos, bf16[12576,1024]{1,0:T(8,128)(2,1)} %emb_hbm.9, f32[3144,1]{1,0:T(8,128)} %broadcast_in_dim.61.bias_ref, f32[8,2,1280]{2,1,0:T(2,128)} %pad_maximum_fusion.info_ref, ...), custom_call_target="tpu_custom_call", output_to_operand_aliasing={{1}: (5, {})} | custom-call | flops 352321536 | bytes 26132480 | tf_op jit(solution)/shard_map/pallas_call | solution.py:456
  524.2 14.7 %spread.1 = bf16[16,512,1024]{2,1,0:T(8,128)(2,1)} custom-call(s32[1]{0:T(128)} %bitcast.vp, s32[16,1,80]{2,1,0:T(1,128)} %bitcast.34, bf16[1024,1024]{1,0:T(8,128)(2,1)} %w_ref.3, f32[1232,256]{1,0:T(8,128)} %get-tuple-element.126.refs_0_, f32[1232,256]{1,0:T(8,128)} %collective-permute-done.29.refs_1_, f32[1232,256]{1,0:T(8,128)} %collective-permute-done.30.refs_2_, ...), custom_call_target="tpu_custom_call" | custom-call | flops 21474836 | bytes 16777216 | tf_op jit(solution)/shard_map/spread/pallas_call | solution.py:661
  538.9 1.8 collective-permute-start.39
  543.0 12.7 %collective-permute-done.26.refs_1_ = f32[520,256]{1,0:T(8,128)} collective-permute-done((f32[520,256]{1,0:T(8,128)}, f32[520,256]{1,0:T(8,128)}, u32[]{:S(2)}, u32[]{:S(2)}) %collective-permute-start.26) | collective-permute-done | bytes 532512 | tf_op jit(solution)/shard_map/ppermute | solution.py:688
  556.2 1.8 collective-permute-start.28
  558.0 8.1 %put_rows.4.refs_0_ = f32[12576,1024]{1,0:T(8,128)} custom-call(s32[6]{0:T(128)} %stack.73.pos, f32[12576,1024]{1,0:T(8,128)} %get-tuple-element.131.refs_0_, f32[1216,1024]{1,0:T(8,128)} %collective-permute-done.34.refs_1_, f32[1216,1024]{1,0:T(8,128)} %collective-permute-done.35.refs_2_), custom_call_target="tpu_custom_call", output_to_operand_aliasing={{}: (1, {})} | custom-call | flops 24903 | bytes 19922944 | tf_op jit(solution)/shard_map/put_rows/pallas_call | solution.py:489
  566.1 24.4 %collective-permute-done.27.refs_2_ = f32[520,256]{1,0:T(8,128)} collective-permute-done((f32[520,256]{1,0:T(8,128)}, f32[520,256]{1,0:T(8,128)}, u32[]{:S(2)}, u32[]{:S(2)}) %collective-permute-start.27) | collective-permute-done | bytes 532512 | tf_op jit(solution)/shard_map/ppermute | solution.py:688
  590.5 14.6 %collective-permute-done.28.refs_3_ = f32[520,256]{1,0:T(8,128)} collective-permute-done((f32[520,256]{1,0:T(8,128)}, f32[520,256]{1,0:T(8,128)}, u32[]{:S(2)}, u32[]{:S(2)}) %collective-permute-start.28) | collective-permute-done | bytes 532512 | tf_op jit(solution)/shard_map/ppermute | solution.py:688
  606.7 6.5 %put_rows.5.refs_0_ = f32[12576,1024]{1,0:T(8,128)} custom-call(s32[6]{0:T(128)} %stack.73.pos, f32[12576,1024]{1,0:T(8,128)} %put_rows.4.refs_0_, f32[1216,1024]{1,0:T(8,128)} %collective-permute-done.39.refs_1_, f32[840,1024]{1,0:T(8,128)} %collective-permute-done.40.refs_2_), custom_call_target="tpu_custom_call", output_to_operand_aliasing={{}: (1, {})} | custom-call | flops 21053 | bytes 16842752 | tf_op jit(solution)/shard_map/put_rows/pallas_call | solution.py:489
  613.3 4.9 join.1
  621.5 1.5 fusion.3
  623.0 4.4 put_rows.6.refs_0_
  627.4 2.0 collective-permute-done.42.refs_1_
  629.4 4.4 put_rows.7
  (103 shorter events, 32.4 us)
Async XLA Ops:
  7.2 283.4 %reduce-scatter.2.cloned.1.call-start = ((), (), s32[]{:S(2)}) async-start(), calls=%async_computation.1 | async-start | bytes 6307840 | tf_op jit(solution)/shard_map/reduce_scatter | solution.py:729
  9.6 17.2 %copy-start.4 = (s32[16,77]{1,0:T(8,128)S(1)}, s32[16,77]{1,0:T(8,128)}, u32[]{:S(2)}) copy-start(s32[16,77]{1,0:T(8,128)} %param.11) | copy-start | bytes 14788
  25.3 109.2 %collective-permute-start.15 = (f32[608,1024]{1,0:T(8,128)}, f32[608,1024]{1,0:T(8,128)}, u32[]{:S(2)}, u32[]{:S(2)}) collective-permute-start(f32[608,1024]{1,0:T(8,128)} %get-tuple-element.88.refs_0_), channel_id=1, source_target_pairs={{0,2},{1,3},{2,0},{3,1},{4,6},{5,7},{6,4},{7,5},{8,10},{9,11},{10,... | collective-permute-start | bytes 7471112 | tf_op jit(solution)/shard_map/ppermute | solution.py:685
  26.6 109.1 %collective-permute-start.16 = (f32[624,1024]{1,0:T(8,128)}, f32[624,1024]{1,0:T(8,128)}, u32[]{:S(2)}, u32[]{:S(2)}) collective-permute-start(f32[624,1024]{1,0:T(8,128)} %get-tuple-element.89.refs_1_), channel_id=1, source_target_pairs={{0,4},{1,5},{2,6},{3,7},{4,0},{5,1},{6,2},{7,3},{8,12},{9,13},{10,... | collective-permute-start | bytes 7667720 | tf_op jit(solution)/shard_map/ppermute | solution.py:685
  73.2 3.5 collective-permute-start
  74.5 4.1 collective-permute-start.1
  74.6 4.4 collective-permute-start.2
  76.7 67.4 %collective-permute-start.5 = (f32[624,1024]{1,0:T(8,128)}, f32[624,1024]{1,0:T(8,128)}, u32[]{:S(2)}, u32[]{:S(2)}) collective-permute-start(f32[624,1024]{1,0:T(8,128)} %get-tuple-element.89.refs_1_), channel_id=1, source_target_pairs={{0,1},{1,0},{2,3},{3,2},{4,5},{5,4},{6,7},{7,6},{8,9},{9,8},{10,11... | collective-permute-start | bytes 7667720 | tf_op jit(solution)/shard_map/ppermute | solution.py:685
  78.7 114.3 %collective-permute-start.9 = (f32[624,1024]{1,0:T(8,128)}, f32[624,1024]{1,0:T(8,128)}, u32[]{:S(2)}, u32[]{:S(2)}) collective-permute-start(f32[624,1024]{1,0:T(8,128)} %get-tuple-element.89.refs_1_), channel_id=1, source_target_pairs={{0,2},{1,3},{2,0},{3,1},{4,6},{5,7},{6,4},{7,5},{8,10},{9,11},{10,... | collective-permute-start | bytes 7667720 | tf_op jit(solution)/shard_map/ppermute | solution.py:685
  130.4 3.8 collective-permute-start.3
  134.2 9.7 %collective-permute-start.4 = (f32[608,1024]{1,0:T(8,128)}, f32[608,1024]{1,0:T(8,128)}, u32[]{:S(2)}, u32[]{:S(2)}) collective-permute-start(f32[608,1024]{1,0:T(8,128)} %get-tuple-element.88.refs_0_), channel_id=1, source_target_pairs={{0,1},{1,0},{2,3},{3,2},{4,5},{5,4},{6,7},{7,6},{8,9},{9,8},{10,11... | collective-permute-start | bytes 7471112 | tf_op jit(solution)/shard_map/ppermute | solution.py:685
  134.5 58.4 %collective-permute-start.10 = (f32[608,1024]{1,0:T(8,128)}, f32[608,1024]{1,0:T(8,128)}, u32[]{:S(2)}, u32[]{:S(2)}) collective-permute-start(f32[608,1024]{1,0:T(8,128)} %get-tuple-element.88.refs_0_), channel_id=1, source_target_pairs={{0,4},{1,5},{2,6},{3,7},{4,0},{5,1},{6,2},{7,3},{8,12},{9,13},{10,... | collective-permute-start | bytes 7471112 | tf_op jit(solution)/shard_map/ppermute | solution.py:685
  135.8 3.1 collective-permute-start.11
  138.9 61.7 %collective-permute-start.17 = (f32[608,1024]{1,0:T(8,128)}, f32[608,1024]{1,0:T(8,128)}, u32[]{:S(2)}, u32[]{:S(2)}) collective-permute-start(f32[608,1024]{1,0:T(8,128)} %collective-permute-done.15.refs_0_), channel_id=1, source_target_pairs={{0,1},{1,0},{2,3},{3,2},{4,5},{5,4},{6,7},{7,6},{8,9},{9,8},{10,11... | collective-permute-start | bytes 7471112 | tf_op jit(solution)/shard_map/ppermute | solution.py:685
  140.1 337.2 %all-reduce.5.cloned.1.call-start = ((), (), s32[]{:S(2)}) async-start(), calls=%async_computation.2 | async-start | bytes 2244608 | tf_op jit(solution)/shard_map/psum | solution.py:781
  143.9 46.9 %collective-permute-start.12 = (f32[2,1280]{1,0:T(2,128)}, f32[2,1280]{1,0:T(2,128)}, u32[]{:S(2)}, u32[]{:S(2)}) collective-permute-start(f32[2,1280]{1,0:T(2,128)} %get-tuple-element.161), channel_id=1, source_target_pairs={{0,4},{1,5},{2,6},{3,7},{4,0},{5,1},{6,2},{7,3},{8,12},{9,13},{10,... | collective-permute-start | bytes 30728 | tf_op jit(solution)/shard_map/ppermute | solution.py:685
  144.1 47.6 %collective-permute-start.13 = (f32[2,1280]{1,0:T(2,128)}, f32[2,1280]{1,0:T(2,128)}, u32[]{:S(2)}, u32[]{:S(2)}) collective-permute-start(f32[2,1280]{1,0:T(2,128)} %get-tuple-element.161), channel_id=1, source_target_pairs={{0,6},{1,7},{2,4},{3,5},{4,2},{5,3},{6,0},{7,1},{8,14},{9,15},{10,... | collective-permute-start | bytes 30728 | tf_op jit(solution)/shard_map/ppermute | solution.py:685
  190.7 14.5 %collective-permute-start.20 = (f32[624,1024]{1,0:T(8,128)}, f32[624,1024]{1,0:T(8,128)}, u32[]{:S(2)}, u32[]{:S(2)}) collective-permute-start(f32[624,1024]{1,0:T(8,128)} %collective-permute-done.16.refs_5_), channel_id=1, source_target_pairs={{0,1},{1,0},{2,3},{3,2},{4,5},{5,4},{6,7},{7,6},{8,9},{9,8},{10,11... | collective-permute-start | bytes 7667720 | tf_op jit(solution)/shard_map/ppermute | solution.py:685
  191.8 64.6 %collective-permute-start.22 = (f32[624,1024]{1,0:T(8,128)}, f32[624,1024]{1,0:T(8,128)}, u32[]{:S(2)}, u32[]{:S(2)}) collective-permute-start(f32[624,1024]{1,0:T(8,128)} %collective-permute-done.16.refs_5_), channel_id=1, source_target_pairs={{0,2},{1,3},{2,0},{3,1},{4,6},{5,7},{6,4},{7,5},{8,10},{9,11},{10,... | collective-permute-start | bytes 7667720 | tf_op jit(solution)/shard_map/ppermute | solution.py:685
  193.0 12.3 %collective-permute-start.18 = (f32[624,1024]{1,0:T(8,128)}, f32[624,1024]{1,0:T(8,128)}, u32[]{:S(2)}, u32[]{:S(2)}) collective-permute-start(f32[624,1024]{1,0:T(8,128)} %collective-permute-done.9.refs_1_), channel_id=1, source_target_pairs={{0,1},{1,0},{2,3},{3,2},{4,5},{5,4},{6,7},{7,6},{8,9},{9,8},{10,11... | collective-permute-start | bytes 7667720 | tf_op jit(solution)/shard_map/ppermute | solution.py:685
  194.0 6.2 collective-permute-start.14
  200.2 5.1 collective-permute-start.19
  200.6 55.8 %collective-permute-start.21 = (f32[608,1024]{1,0:T(8,128)}, f32[608,1024]{1,0:T(8,128)}, u32[]{:S(2)}, u32[]{:S(2)}) collective-permute-start(f32[608,1024]{1,0:T(8,128)} %collective-permute-done.15.refs_0_), channel_id=1, source_target_pairs={{0,4},{1,5},{2,6},{3,7},{4,0},{5,1},{6,2},{7,3},{8,12},{9,13},{10,... | collective-permute-start | bytes 7471112 | tf_op jit(solution)/shard_map/ppermute | solution.py:685
  205.3 52.1 %copy-start.1 = (f32[8,1232]{1,0:T(8,128)S(1)}, f32[8,1232]{1,0:T(8,128)}, u32[]{:S(2)}) copy-start(f32[8,1232]{1,0:T(8,128)} %get-tuple-element.101.refs_0_) | copy-start | bytes 118276
  256.4 9.8 %collective-permute-start.24 = (f32[624,1024]{1,0:T(8,128)}, f32[624,1024]{1,0:T(8,128)}, u32[]{:S(2)}, u32[]{:S(2)}) collective-permute-start(f32[624,1024]{1,0:T(8,128)} %collective-permute-done.22.refs_1_), channel_id=1, source_target_pairs={{0,1},{1,0},{2,3},{3,2},{4,5},{5,4},{6,7},{7,6},{8,9},{9,8},{10,11... | collective-permute-start | bytes 7667720 | tf_op jit(solution)/shard_map/ppermute | solution.py:685
  257.4 8.8 %collective-permute-start.23 = (f32[608,1024]{1,0:T(8,128)}, f32[608,1024]{1,0:T(8,128)}, u32[]{:S(2)}, u32[]{:S(2)}) collective-permute-start(f32[608,1024]{1,0:T(8,128)} %collective-permute-done.21.refs_0_), channel_id=1, source_target_pairs={{0,1},{1,0},{2,3},{3,2},{4,5},{5,4},{6,7},{7,6},{8,9},{9,8},{10,11... | collective-permute-start | bytes 7471112 | tf_op jit(solution)/shard_map/ppermute | solution.py:685
  257.4 3.3 collective-permute-start.6
  258.5 3.9 collective-permute-start.7
  260.4 3.6 collective-permute-start.8
  260.7 1.7 copy-start.2
  287.8 10.5 %collective-permute-start.25 = (f32[1088,1024]{1,0:T(8,128)}, f32[1088,1024]{1,0:T(8,128)}, u32[]{:S(2)}, u32[]{:S(2)}) collective-permute-start(f32[1088,1024]{1,0:T(8,128)} %get-tuple-element.111), channel_id=1, source_target_pairs={{0,1},{1,0},{2,3},{3,2},{4,5},{5,4},{6,7},{7,6},{8,9},{9,8},{10,11... | collective-permute-start | bytes 13369352 | tf_op jit(solution)/shard_map/ppermute | solution.py:685
  289.3 72.9 %collective-permute-start.32 = (f32[1088,1024]{1,0:T(8,128)}, f32[1088,1024]{1,0:T(8,128)}, u32[]{:S(2)}, u32[]{:S(2)}) collective-permute-start(f32[1088,1024]{1,0:T(8,128)} %get-tuple-element.111), channel_id=1, source_target_pairs={{0,2},{1,5},{2,0},{3,7},{4,6},{5,1},{6,4},{7,3},{8,10},{9,13},{10,... | collective-permute-start | bytes 13369352 | tf_op jit(solution)/shard_map/ppermute | solution.py:691
  361.9 177.1 %collective-permute-start.35 = (f32[1216,1024]{1,0:T(8,128)}, f32[1216,1024]{1,0:T(8,128)}, u32[]{:S(2)}, u32[]{:S(2)}) collective-permute-start(f32[1216,1024]{1,0:T(8,128)} %get-tuple-element.119), channel_id=1, source_target_pairs={{0,2},{1,5},{2,0},{3,7},{4,6},{5,1},{6,4},{7,3},{8,10},{9,13},{10,... | collective-permute-start | bytes 14942216 | tf_op jit(solution)/shard_map/ppermute | solution.py:691
  362.2 117.0 %collective-permute-start.33 = (f32[1088,1024]{1,0:T(8,128)}, f32[1088,1024]{1,0:T(8,128)}, u32[]{:S(2)}, u32[]{:S(2)}) collective-permute-start(f32[1088,1024]{1,0:T(8,128)} %collective-permute-done.32.refs_2_), channel_id=1, source_target_pairs={{0,1},{1,0},{2,3},{3,2},{4,5},{5,4},{6,7},{7,6},{8,9},{9,8},{10,11... | collective-permute-start | bytes 13369352 | tf_op jit(solution)/shard_map/ppermute | solution.py:685
  362.8 57.0 %collective-permute-start.30 = (f32[1232,256]{1,0:T(8,128)}, f32[1232,256]{1,0:T(8,128)}, u32[]{:S(2)}, u32[]{:S(2)}) collective-permute-start(f32[1232,256]{1,0:T(8,128)} %get-tuple-element.126.refs_0_), channel_id=1, source_target_pairs={{0,16},{8,24},{16,0},{24,8},{1,17},{9,25},{17,1},{25,9},{2,18},{10... | collective-permute-start | bytes 3784712 | tf_op jit(solution)/shard_map/ppermute | solution.py:688
  365.3 158.8 %collective-permute-start.29 = (f32[1232,256]{1,0:T(8,128)}, f32[1232,256]{1,0:T(8,128)}, u32[]{:S(2)}, u32[]{:S(2)}) collective-permute-start(f32[1232,256]{1,0:T(8,128)} %get-tuple-element.126.refs_0_), channel_id=1, source_target_pairs={{0,8},{8,0},{16,24},{24,16},{1,9},{9,1},{17,25},{25,17},{2,10},{10... | collective-permute-start | bytes 3784712 | tf_op jit(solution)/shard_map/ppermute | solution.py:688
  419.8 104.3 %collective-permute-start.31 = (f32[1232,256]{1,0:T(8,128)}, f32[1232,256]{1,0:T(8,128)}, u32[]{:S(2)}, u32[]{:S(2)}) collective-permute-start(f32[1232,256]{1,0:T(8,128)} %collective-permute-done.30.refs_2_), channel_id=1, source_target_pairs={{0,8},{8,0},{16,24},{24,16},{1,9},{9,1},{17,25},{25,17},{2,10},{10... | collective-permute-start | bytes 3784712 | tf_op jit(solution)/shard_map/ppermute | solution.py:688
  422.2 134.0 %collective-permute-start.34 = (f32[1216,1024]{1,0:T(8,128)}, f32[1216,1024]{1,0:T(8,128)}, u32[]{:S(2)}, u32[]{:S(2)}) collective-permute-start(f32[1216,1024]{1,0:T(8,128)} %get-tuple-element.119), channel_id=1, source_target_pairs={{0,1},{1,0},{2,3},{3,2},{4,5},{5,4},{6,7},{7,6},{8,9},{9,8},{10,11... | collective-permute-start | bytes 14942216 | tf_op jit(solution)/shard_map/ppermute | solution.py:685
  538.9 67.8 %collective-permute-start.39 = (f32[1216,1024]{1,0:T(8,128)}, f32[1216,1024]{1,0:T(8,128)}, u32[]{:S(2)}, u32[]{:S(2)}) collective-permute-start(f32[1216,1024]{1,0:T(8,128)} %collective-permute-done.35.refs_2_), channel_id=1, source_target_pairs={{0,1},{1,0},{2,3},{3,2},{4,5},{5,4},{6,7},{7,6},{8,9},{9,8},{10,11... | collective-permute-start | bytes 14942216 | tf_op jit(solution)/shard_map/ppermute | solution.py:685
  540.7 64.9 %collective-permute-start.40 = (f32[840,1024]{1,0:T(8,128)}, f32[840,1024]{1,0:T(8,128)}, u32[]{:S(2)}, u32[]{:S(2)}) collective-permute-start(f32[840,1024]{1,0:T(8,128)} %get-tuple-element.125), channel_id=1, source_target_pairs={{0,1},{1,0},{2,3},{3,2},{4,5},{5,4},{6,7},{7,6},{8,9},{9,8},{10,11... | collective-permute-start | bytes 10321928 | tf_op jit(solution)/shard_map/ppermute | solution.py:685
  540.8 82.2 %collective-permute-start.41 = (f32[840,1024]{1,0:T(8,128)}, f32[840,1024]{1,0:T(8,128)}, u32[]{:S(2)}, u32[]{:S(2)}) collective-permute-start(f32[840,1024]{1,0:T(8,128)} %get-tuple-element.125), channel_id=1, source_target_pairs={{0,2},{1,5},{2,0},{3,7},{4,6},{5,1},{6,4},{7,3},{8,10},{9,13},{10,... | collective-permute-start | bytes 10321928 | tf_op jit(solution)/shard_map/ppermute | solution.py:691
  541.8 13.9 %collective-permute-start.26 = (f32[520,256]{1,0:T(8,128)}, f32[520,256]{1,0:T(8,128)}, u32[]{:S(2)}, u32[]{:S(2)}) collective-permute-start(f32[520,256]{1,0:T(8,128)} %constant_dynamic-slice_fusion), channel_id=1, source_target_pairs={{0,8},{8,0},{16,24},{24,16},{1,9},{9,1},{17,25},{25,17},{2,10},{10... | collective-permute-start | bytes 1597448 | tf_op jit(solution)/shard_map/ppermute | solution.py:688
  555.6 34.9 %collective-permute-start.27 = (f32[520,256]{1,0:T(8,128)}, f32[520,256]{1,0:T(8,128)}, u32[]{:S(2)}, u32[]{:S(2)}) collective-permute-start(f32[520,256]{1,0:T(8,128)} %constant_dynamic-slice_fusion), channel_id=1, source_target_pairs={{0,16},{8,24},{16,0},{24,8},{1,17},{9,25},{17,1},{25,9},{2,18},{10... | collective-permute-start | bytes 1597448 | tf_op jit(solution)/shard_map/ppermute | solution.py:688
  556.2 48.9 %collective-permute-start.28 = (f32[520,256]{1,0:T(8,128)}, f32[520,256]{1,0:T(8,128)}, u32[]{:S(2)}, u32[]{:S(2)}) collective-permute-start(f32[520,256]{1,0:T(8,128)} %constant_dynamic-slice_fusion), channel_id=1, source_target_pairs={{0,24},{8,16},{16,8},{24,0},{1,25},{9,17},{17,9},{25,1},{2,26},{10... | collective-permute-start | bytes 1597448 | tf_op jit(solution)/shard_map/ppermute | solution.py:688
  605.1 8.1 %collective-permute-start.36 = (f32[520,256]{1,0:T(8,128)}, f32[520,256]{1,0:T(8,128)}, u32[]{:S(2)}, u32[]{:S(2)}) collective-permute-start(f32[520,256]{1,0:T(8,128)} %collective-permute-done.26.refs_1_), channel_id=1, source_target_pairs={{0,1},{1,0},{2,3},{3,2},{4,5},{5,4},{6,7},{7,6},{8,9},{9,8},{10,11... | collective-permute-start | bytes 1597448 | tf_op jit(solution)/shard_map/ppermute | solution.py:685
  605.6 7.6 %collective-permute-start.37 = (f32[520,256]{1,0:T(8,128)}, f32[520,256]{1,0:T(8,128)}, u32[]{:S(2)}, u32[]{:S(2)}) collective-permute-start(f32[520,256]{1,0:T(8,128)} %collective-permute-done.27.refs_2_), channel_id=1, source_target_pairs={{0,1},{1,0},{2,3},{3,2},{4,5},{5,4},{6,7},{7,6},{8,9},{9,8},{10,11... | collective-permute-start | bytes 1597448 | tf_op jit(solution)/shard_map/ppermute | solution.py:685
  605.6 7.6 %collective-permute-start.38 = (f32[520,256]{1,0:T(8,128)}, f32[520,256]{1,0:T(8,128)}, u32[]{:S(2)}, u32[]{:S(2)}) collective-permute-start(f32[520,256]{1,0:T(8,128)} %collective-permute-done.28.refs_3_), channel_id=1, source_target_pairs={{0,1},{1,0},{2,3},{3,2},{4,5},{5,4},{6,7},{7,6},{8,9},{9,8},{10,11... | collective-permute-start | bytes 1597448 | tf_op jit(solution)/shard_map/ppermute | solution.py:685
  623.0 6.4 %collective-permute-start.42 = (f32[840,1024]{1,0:T(8,128)}, f32[840,1024]{1,0:T(8,128)}, u32[]{:S(2)}, u32[]{:S(2)}) collective-permute-start(f32[840,1024]{1,0:T(8,128)} %collective-permute-done.41.refs_1_), channel_id=1, source_target_pairs={{0,1},{1,0},{2,3},{3,2},{4,5},{5,4},{6,7},{7,6},{8,9},{9,8},{10,11... | collective-permute-start | bytes 10321928 | tf_op jit(solution)/shard_map/ppermute | solution.py:685
  (2 other events, 1.2 us)
Sparse Core Ops, SparseCore 0:
  140.2 90.5 reduce-scatter.1
  423.1 54.1 all-reduce.4

commit v10 on v9

--- a/solution.py
+++ b/solution.py
@@ -739,7 +739,7 @@
         start = lambda h, c: h * half + c * quarter
         pos = jnp.stack([dp, start(mine, core), row_start + start(mine, core), start(mine, 1 - core), start(1 - mine, core), start(1 - mine, 1 - core)])
         bias_col = lax.dynamic_slice(b_vocab, (start(mine, core),), (quarter,))[:, None]
-        shares = (1088, 1216, 840)
+        shares = (1088, 1280, 776)
         ends = [0]
         for w in shares[:-1]:
             ends.append(ends[-1] + max(16, quarter * w // sum(shares) // 16 * 16))
@@ -791,11 +791,11 @@
         dab_2 = after(dab_2, chunk1)
         dab_3 = swap_vp(dab_2, 1)
 
-        chunk2, big = rows("whole", 2, part, info=info, u_all=u_all, big=big, puts=[far0, far_twin0])
+        chunk2, big = rows("whole", 2, part, info=info, u_all=u_all, big=big, puts=[far0])
         twin2, far2 = send(2, chunk2)
         d_hidden = spread_pass(n_masks, hidden.shape, vp[None], pos_pad[:, None], w_trans, after([dab, dab_1, dab_2, dab_3], chunk2))
         far1, far_twin1 = forward(1, far1, d_hidden)
-        big = put_rows(after(pos, d_hidden), big, [twin1, far1])
+        big = put_rows(after(pos, d_hidden), big, [far_twin0, twin1, far1])
         parts = after(parts, big)
         others = [swap(p, CORE) for p in parts]
         big = put_rows(pos, big, [far_twin1, twin2])

time: 650 us -> 654 us (level)
  the two profiles are of different devices: /device:TPU:21 before, /device:TPU:17 now
where the time goes in v10:
time: 654 us; the launch traced here: 646 us
  Pallas kernels  347 us (53%)
  waiting for transfers between devices  219 us (33%)
  starting transfers between devices  42.2 us (6%)
  between operations  16.3 us (2%)
  local copies, waits for them, and re-layouts  16 us (2%)
    pallas_call x5, Pallas kernels, rows_pass(): pl.pallas_call(functools.partial(rows_kernel, kind, scale, s0, m, cut, n_...  183 us
    ppermute x12, waiting for transfers between devices, swap_vp(): return lax.ppermute(a, 'vp', [(d, d ^ bit) for d in range(n_shards)])  105 us
    ppermute x3, waiting for transfers between devices, hop(): lax.ppermute(a, 'dp', [(d, d ^ (Y if d & CORE else X)) for d in range(n_g...  57.8 us
    ppermute x28, waiting for transfers between devices, swap(): return lax.ppermute(a, 'dp', [(d, d ^ bit) for d in range(n_groups)])  56.5 us
    pallas_call x1, Pallas kernels, du_pass(): pl.pallas_call(functools.partial(du_kernel, v, scale, base), grid=(n,), i...  48.1 us
    pallas_call x1, Pallas kernels, stats(): pl.pallas_call(functools.partial(stats_kernel, v), grid=(n,), in_specs=[w...  43.8 us
    pallas_call x4, Pallas kernels, put_rows(): pl.pallas_call(functools.partial(put_kernel, spots), in_specs=[SMEM] + [A...  26.9 us
    ppermute x28, starting transfers between devices, swap(): return lax.ppermute(a, 'dp', [(d, d ^ bit) for d in range(n_groups)])  22.4 us
  transfers between devices with their start and end apart: 45, of which 15 were waited for; matrix products, arithmetic and copies ran while one was open for 3% of the time, Pallas kernels for 40%

profile of v10, /device:TPU:17, one launch (start us, length us, event | category | flops | bytes accessed | tf_op | source)
XLA Modules:
  0.0 646.3 jit_solution(1961840194349093686)
XLA Ops:
  9.6 15.7 %head.1 = (bf16[1232,1024]{1,0:T(8,128)(2,1)}, f32[1232,1024]{1,0:T(8,128)}, f32[1232,1024]{1,0:T(8,128)}, f32[1232,128]{1,0:T(8,128)}, bf16[1232,1024]{1,0:T(8,...) custom-call(bf16[16,512,1024]{2,1,0:T(8,128)(2,1)} %hid.1, s32[16,80,128]{2,1,0:T(8,128)} %broadcast_in_dim.50.pos_ref, ...), custom_call_target="tpu_custom_call" | custom-call | flops 51673824 | bytes 42008576 | tf_op jit(solution)/shard_map/head/pallas_call | solution.py:255
  25.3 1.3 collective-permute-start.15
  26.6 1.2 collective-permute-start.16
  28.0 1.5 broadcast_in_dim.54.b_ref
  30.5 43.8 %stats.1 = (f32[1232,12576]{1,0:T(8,128)}, f32[8,1232]{1,0:T(8,128)}) custom-call(bf16[1232,1024]{1,0:T(8,128)(2,1)} %get-tuple-element.81.u_ref, bf16[12576,1024]{1,0:T(8,128)(2,1)} %emb_hbm.9, f32[1,12576]{1,0:T(1,128)} %broadcast_in_dim.54.b_ref, s32[1232,128]{1,0:T(8,128)} %broadcast_in_dim.56.lab_ref), custom_call_target="tpu_custom_call" | custom-call | flops 317309568 | bytes 87730176 | tf_op jit(solution)/shard_map/stats/pallas_call | solution.py:96
  74.2 1.3 collective-permute-start
  75.6 1.3 collective-permute-start.2
  77.7 2.0 collective-permute-start.5
  82.7 48.1 %du_pass.1 = (f32[4,1232,256]{2,1,0:T(8,128)}, f32[1,12576]{1,0:T(1,128)}, f32[8,1232]{1,0:T(8,128)}) custom-call(f32[1232,12576]{1,0:T(8,128)} %get-tuple-element.82.logits_ref, bf16[12576,1024]{1,0:T(8,128)(2,1)} %emb_hbm.9, f32[1232,128]{1,0:T(8,128)} %broadcast_in_dim.57.lse_ref, s32[1232,128]{1,0:T(8,128)} %broadcast_in_dim.56.lab_ref, ...), custom_call_target="tpu_custom_call" | custom-call | flops 317309568 | bytes 87730176 | tf_op jit(solution)/shard_map/du_pass/pallas_call | solution.py:182
  131.4 2.7 collective-permute-start.3
  137.0 1.5 collective-permute-done.11
  138.5 1.6 collective-permute-start.17
  141.0 1.7 broadcast_in_dim.61.bias_ref
  144.0 1.2 collective-permute-start.12
  146.3 19.9 %shard_map.152 = (f32[1088,1024]{1,0:T(8,128)}, bf16[8,1280,1024]{2,1,0:T(8,128)(2,1)}) custom-call(s32[6]{0:T(128)} %stack.73.pos, bf16[12576,1024]{1,0:T(8,128)(2,1)} %emb_hbm.9, f32[3144,1]{1,0:T(8,128)} %broadcast_in_dim.61.bias_ref, f32[2,2,1280]{2,1,0:T(2,128)} %pad_maximum_fusion.3.info_ref, f32[608,1024]{1,0:T(8,128)} %get-tuple-element.88.refs_0_, ...), custom_call_target="tpu_custom_call" | custom-call | flops 114085072 | bytes 11927552 | tf_op jit(solution)/shard_map/pallas_call | solution.py:456
  166.3 25.5 %collective-permute-done.12 = f32[2,1280]{1,0:T(2,128)} collective-permute-done((f32[2,1280]{1,0:T(2,128)}, f32[2,1280]{1,0:T(2,128)}, u32[]{:S(2)}, u32[]{:S(2)}) %collective-permute-start.12) | collective-permute-done | bytes 10272 | tf_op jit(solution)/shard_map/ppermute | solution.py:685
  192.8 1.2 collective-permute-start.22
  195.3 5.9 collective-permute-done.14
  203.3 3.0 collective-permute-done.19.refs_6_
  206.3 33.3 %shard_map.153 = (f32[1088,1024]{1,0:T(8,128)}, bf16[8,1280,1024]{2,1,0:T(8,128)(2,1)}) custom-call(s32[6]{0:T(128)} %stack.73.pos, bf16[12576,1024]{1,0:T(8,128)(2,1)} %emb_hbm.9, f32[3144,1]{1,0:T(8,128)} %broadcast_in_dim.61.bias_ref, f32[8,2,1280]{2,1,0:T(2,128)} %pad_maximum_fusion.info_ref, ...), custom_call_target="tpu_custom_call", output_to_operand_aliasing={{1}: (12, {})} | custom-call | flops 228170144 | bytes 17170432 | tf_op jit(solution)/shard_map/pallas_call | solution.py:456
  239.6 17.8 %collective-permute-done.21.refs_0_ = f32[608,1024]{1,0:T(8,128)} collective-permute-done((f32[608,1024]{1,0:T(8,128)}, f32[608,1024]{1,0:T(8,128)}, u32[]{:S(2)}, u32[]{:S(2)}) %collective-permute-start.21) | collective-permute-done | bytes 2490400 | tf_op jit(solution)/shard_map/ppermute | solution.py:685
  259.5 2.0 collective-permute-start.7
  261.7 1.7 collective-permute-done.7.refs_2_
  265.0 2.1 means.1
  267.2 21.7 %shard_map.154 = (f32[1088,1024]{1,0:T(8,128)}, bf16[8,1280,1024]{2,1,0:T(8,128)(2,1)}, f32[12576,1024]{1,0:T(8,128)}) custom-call(s32[6]{0:T(128)} %stack.73.pos, bf16[12576,1024]{1,0:T(8,128)(2,1)} %emb_hbm.9, f32[3144,1]{1,0:T(8,128)} %broadcast_in_dim.61.bias_ref, f32[8,2,1280]{2,1,0:T(2,128)} %pad_maximum_fusion.info_ref, ...), custom_call_target="tpu_custom_call", output_to_operand_aliasing={{1}: (8, {})} | custom-call | flops 114085072 | bytes 11927552 | tf_op jit(solution)/shard_map/pallas_call | solution.py:456
  288.8 1.4 collective-permute-start.25
  290.2 7.8 %back.1 = (f32[1232,256]{1,0:T(8,128)}, f32[1096,256]{1,0:T(8,128)}) custom-call(s32[1]{0:T(128)} %bitcast.vp, f32[1232,1024]{1,0:T(8,128)} %get-tuple-element.77.refs_0_, f32[1232,1024]{1,0:T(8,128)} %get-tuple-element.78.norm_hbm.refs_1_, f32[1232,128]{1,0:T(8,128)} %get-tuple-element.79.refs_2_, bf16[1232,1024]{1,0:T(8,128)(2,1)} %get-tuple-element.80.refs_3_, ...), custom_call_target="tpu_custom_call" | custom-call | flops 6459228 | bytes 9461760 | tf_op jit(solution)/shard_map/back/pallas_call | solution.py:610
  298.0 66.3 %shard_map.155 = (f32[1280,1024]{1,0:T(8,128)}, f32[12576,1024]{1,0:T(8,128)}) custom-call(s32[6]{0:T(128)} %stack.73.pos, bf16[12576,1024]{1,0:T(8,128)(2,1)} %emb_hbm.9, f32[3144,1]{1,0:T(8,128)} %broadcast_in_dim.61.bias_ref, f32[8,2,1280]{2,1,0:T(2,128)} %pad_maximum_fusion.info_ref, ...), custom_call_target="tpu_custom_call", output_to_operand_aliasing={{1}: (5, {})} | custom-call | flops 536870912 | bytes 28835840 | tf_op jit(solution)/shard_map/pallas_call | solution.py:456
  364.6 1.3 collective-permute-start.32
  365.9 2.5 collective-permute-start.30
  369.4 53.1 %collective-permute-done.30.refs_2_ = f32[1232,256]{1,0:T(8,128)} collective-permute-done((f32[1232,256]{1,0:T(8,128)}, f32[1232,256]{1,0:T(8,128)}, u32[]{:S(2)}, u32[]{:S(2)}) %collective-permute-start.30) | collective-permute-done | bytes 1261600 | tf_op jit(solution)/shard_map/ppermute | solution.py:688
  422.5 2.6 collective-permute-start.31
  426.0 57.8 %collective-permute-done.32.refs_2_ = f32[1088,1024]{1,0:T(8,128)} collective-permute-done((f32[1088,1024]{1,0:T(8,128)}, f32[1088,1024]{1,0:T(8,128)}, u32[]{:S(2)}, u32[]{:S(2)}) %collective-permute-start.32) | collective-permute-done | bytes 4456480 | tf_op jit(solution)/shard_map/ppermute | solution.py:691
  484.8 1.9 constant_dynamic-slice_fusion
  486.6 41.9 %shard_map.156 = (f32[776,1024]{1,0:T(8,128)}, f32[12576,1024]{1,0:T(8,128)}) custom-call(s32[6]{0:T(128)} %stack.73.pos, bf16[12576,1024]{1,0:T(8,128)(2,1)} %emb_hbm.9, f32[3144,1]{1,0:T(8,128)} %broadcast_in_dim.61.bias_ref, f32[8,2,1280]{2,1,0:T(2,128)} %pad_maximum_fusion.info_ref, ...), custom_call_target="tpu_custom_call", output_to_operand_aliasing={{1}: (5, {})} | custom-call | flops 325477984 | bytes 25739264 | tf_op jit(solution)/shard_map/pallas_call | solution.py:456
  528.6 14.7 %spread.1 = bf16[16,512,1024]{2,1,0:T(8,128)(2,1)} custom-call(s32[1]{0:T(128)} %bitcast.vp, s32[16,1,80]{2,1,0:T(1,128)} %bitcast.34, bf16[1024,1024]{1,0:T(8,128)(2,1)} %w_ref.3, f32[1232,256]{1,0:T(8,128)} %get-tuple-element.126.refs_0_, f32[1232,256]{1,0:T(8,128)} %collective-permute-done.29.refs_1_, f32[1232,256]{1,0:T(8,128)} %collective-permute-done.30.refs_2_, ...), custom_call_target="tpu_custom_call" | custom-call | flops 21474836 | bytes 16777216 | tf_op jit(solution)/shard_map/spread/pallas_call | solution.py:661
  543.9 3.5 collective-permute-start.26
  547.4 12.7 %collective-permute-done.26.refs_1_ = f32[520,256]{1,0:T(8,128)} collective-permute-done((f32[520,256]{1,0:T(8,128)}, f32[520,256]{1,0:T(8,128)}, u32[]{:S(2)}, u32[]{:S(2)}) %collective-permute-start.26) | collective-permute-done | bytes 532512 | tf_op jit(solution)/shard_map/ppermute | solution.py:688
  560.6 2.2 collective-permute-start.28
  562.8 11.8 %put_rows.4.refs_0_ = f32[12576,1024]{1,0:T(8,128)} custom-call(s32[6]{0:T(128)} %stack.73.pos, f32[12576,1024]{1,0:T(8,128)} %get-tuple-element.131.refs_0_, f32[1088,1024]{1,0:T(8,128)} %collective-permute-done.33.refs_1_, f32[1280,1024]{1,0:T(8,128)} %collective-permute-done.34.refs_2_, ...), custom_call_target="tpu_custom_call", output_to_operand_aliasing={{}: (1, {})} | custom-call | flops 37355 | bytes 29884416 | tf_op jit(solution)/shard_map/put_rows/pallas_call | solution.py:489
  574.6 20.2 %collective-permute-done.27.refs_2_ = f32[520,256]{1,0:T(8,128)} collective-permute-done((f32[520,256]{1,0:T(8,128)}, f32[520,256]{1,0:T(8,128)}, u32[]{:S(2)}, u32[]{:S(2)}) %collective-permute-start.27) | collective-permute-done | bytes 532512 | tf_op jit(solution)/shard_map/ppermute | solution.py:688
  594.7 15.1 %collective-permute-done.28.refs_3_ = f32[520,256]{1,0:T(8,128)} collective-permute-done((f32[520,256]{1,0:T(8,128)}, f32[520,256]{1,0:T(8,128)}, u32[]{:S(2)}, u32[]{:S(2)}) %collective-permute-start.28) | collective-permute-done | bytes 532512 | tf_op jit(solution)/shard_map/ppermute | solution.py:688
  611.5 6.6 %put_rows.5.refs_0_ = f32[12576,1024]{1,0:T(8,128)} custom-call(s32[6]{0:T(128)} %stack.73.pos, f32[12576,1024]{1,0:T(8,128)} %put_rows.4.refs_0_, f32[1280,1024]{1,0:T(8,128)} %collective-permute-done.39.refs_1_, f32[776,1024]{1,0:T(8,128)} %collective-permute-done.40.refs_2_), custom_call_target="tpu_custom_call", output_to_operand_aliasing={{}: (1, {})} | custom-call | flops 21053 | bytes 16842752 | tf_op jit(solution)/shard_map/put_rows/pallas_call | solution.py:489
  618.1 5.0 join.1
  626.4 1.5 fusion.3
  627.9 4.2 put_rows.6.refs_0_
  632.1 1.8 collective-permute-done.42.refs_1_
  633.9 4.3 put_rows.7
  (103 shorter events, 30.8 us)
Async XLA Ops:
  7.2 283.0 %reduce-scatter.2.cloned.1.call-start = ((), (), s32[]{:S(2)}) async-start(), calls=%async_computation.1 | async-start | bytes 6307840 | tf_op jit(solution)/shard_map/reduce_scatter | solution.py:729
  9.6 18.2 %copy-start.4 = (s32[16,77]{1,0:T(8,128)S(1)}, s32[16,77]{1,0:T(8,128)}, u32[]{:S(2)}) copy-start(s32[16,77]{1,0:T(8,128)} %param.11) | copy-start | bytes 14788
  25.3 110.2 %collective-permute-start.15 = (f32[608,1024]{1,0:T(8,128)}, f32[608,1024]{1,0:T(8,128)}, u32[]{:S(2)}, u32[]{:S(2)}) collective-permute-start(f32[608,1024]{1,0:T(8,128)} %get-tuple-element.88.refs_0_), channel_id=1, source_target_pairs={{0,2},{1,3},{2,0},{3,1},{4,6},{5,7},{6,4},{7,5},{8,10},{9,11},{10,... | collective-permute-start | bytes 7471112 | tf_op jit(solution)/shard_map/ppermute | solution.py:685
  26.6 109.2 %collective-permute-start.16 = (f32[624,1024]{1,0:T(8,128)}, f32[624,1024]{1,0:T(8,128)}, u32[]{:S(2)}, u32[]{:S(2)}) collective-permute-start(f32[624,1024]{1,0:T(8,128)} %get-tuple-element.89.refs_1_), channel_id=1, source_target_pairs={{0,4},{1,5},{2,6},{3,7},{4,0},{5,1},{6,2},{7,3},{8,12},{9,13},{10,... | collective-permute-start | bytes 7667720 | tf_op jit(solution)/shard_map/ppermute | solution.py:685
  74.2 3.5 collective-permute-start
  75.5 4.2 collective-permute-start.1
  75.6 4.3 collective-permute-start.2
  77.7 67.5 %collective-permute-start.5 = (f32[624,1024]{1,0:T(8,128)}, f32[624,1024]{1,0:T(8,128)}, u32[]{:S(2)}, u32[]{:S(2)}) collective-permute-start(f32[624,1024]{1,0:T(8,128)} %get-tuple-element.89.refs_1_), channel_id=1, source_target_pairs={{0,1},{1,0},{2,3},{3,2},{4,5},{5,4},{6,7},{7,6},{8,9},{9,8},{10,11... | collective-permute-start | bytes 7667720 | tf_op jit(solution)/shard_map/ppermute | solution.py:685
  79.7 114.3 %collective-permute-start.9 = (f32[624,1024]{1,0:T(8,128)}, f32[624,1024]{1,0:T(8,128)}, u32[]{:S(2)}, u32[]{:S(2)}) collective-permute-start(f32[624,1024]{1,0:T(8,128)} %get-tuple-element.89.refs_1_), channel_id=1, source_target_pairs={{0,2},{1,3},{2,0},{3,1},{4,6},{5,7},{6,4},{7,5},{8,10},{9,11},{10,... | collective-permute-start | bytes 7667720 | tf_op jit(solution)/shard_map/ppermute | solution.py:685
  131.4 3.8 collective-permute-start.3
  135.2 8.8 %collective-permute-start.4 = (f32[608,1024]{1,0:T(8,128)}, f32[608,1024]{1,0:T(8,128)}, u32[]{:S(2)}, u32[]{:S(2)}) collective-permute-start(f32[608,1024]{1,0:T(8,128)} %get-tuple-element.88.refs_0_), channel_id=1, source_target_pairs={{0,1},{1,0},{2,3},{3,2},{4,5},{5,4},{6,7},{7,6},{8,9},{9,8},{10,11... | collective-permute-start | bytes 7471112 | tf_op jit(solution)/shard_map/ppermute | solution.py:685
  135.5 58.5 %collective-permute-start.10 = (f32[608,1024]{1,0:T(8,128)}, f32[608,1024]{1,0:T(8,128)}, u32[]{:S(2)}, u32[]{:S(2)}) collective-permute-start(f32[608,1024]{1,0:T(8,128)} %get-tuple-element.88.refs_0_), channel_id=1, source_target_pairs={{0,4},{1,5},{2,6},{3,7},{4,0},{5,1},{6,2},{7,3},{8,12},{9,13},{10,... | collective-permute-start | bytes 7471112 | tf_op jit(solution)/shard_map/ppermute | solution.py:685
  135.8 2.7 collective-permute-start.11
  138.5 63.1 %collective-permute-start.17 = (f32[608,1024]{1,0:T(8,128)}, f32[608,1024]{1,0:T(8,128)}, u32[]{:S(2)}, u32[]{:S(2)}) collective-permute-start(f32[608,1024]{1,0:T(8,128)} %collective-permute-done.15.refs_0_), channel_id=1, source_target_pairs={{0,1},{1,0},{2,3},{3,2},{4,5},{5,4},{6,7},{7,6},{8,9},{9,8},{10,11... | collective-permute-start | bytes 7471112 | tf_op jit(solution)/shard_map/ppermute | solution.py:685
  140.1 344.6 %all-reduce.5.cloned.1.call-start = ((), (), s32[]{:S(2)}) async-start(), calls=%async_computation.2 | async-start | bytes 2244608 | tf_op jit(solution)/shard_map/psum | solution.py:781
  144.0 47.8 %collective-permute-start.12 = (f32[2,1280]{1,0:T(2,128)}, f32[2,1280]{1,0:T(2,128)}, u32[]{:S(2)}, u32[]{:S(2)}) collective-permute-start(f32[2,1280]{1,0:T(2,128)} %get-tuple-element.161), channel_id=1, source_target_pairs={{0,4},{1,5},{2,6},{3,7},{4,0},{5,1},{6,2},{7,3},{8,12},{9,13},{10,... | collective-permute-start | bytes 30728 | tf_op jit(solution)/shard_map/ppermute | solution.py:685
  145.2 47.6 %collective-permute-start.13 = (f32[2,1280]{1,0:T(2,128)}, f32[2,1280]{1,0:T(2,128)}, u32[]{:S(2)}, u32[]{:S(2)}) collective-permute-start(f32[2,1280]{1,0:T(2,128)} %get-tuple-element.161), channel_id=1, source_target_pairs={{0,6},{1,7},{2,4},{3,5},{4,2},{5,3},{6,0},{7,1},{8,14},{9,15},{10,... | collective-permute-start | bytes 30728 | tf_op jit(solution)/shard_map/ppermute | solution.py:685
  191.7 14.5 %collective-permute-start.20 = (f32[624,1024]{1,0:T(8,128)}, f32[624,1024]{1,0:T(8,128)}, u32[]{:S(2)}, u32[]{:S(2)}) collective-permute-start(f32[624,1024]{1,0:T(8,128)} %collective-permute-done.16.refs_5_), channel_id=1, source_target_pairs={{0,1},{1,0},{2,3},{3,2},{4,5},{5,4},{6,7},{7,6},{8,9},{9,8},{10,11... | collective-permute-start | bytes 7667720 | tf_op jit(solution)/shard_map/ppermute | solution.py:685
  192.8 64.6 %collective-permute-start.22 = (f32[624,1024]{1,0:T(8,128)}, f32[624,1024]{1,0:T(8,128)}, u32[]{:S(2)}, u32[]{:S(2)}) collective-permute-start(f32[624,1024]{1,0:T(8,128)} %collective-permute-done.16.refs_5_), channel_id=1, source_target_pairs={{0,2},{1,3},{2,0},{3,1},{4,6},{5,7},{6,4},{7,5},{8,10},{9,11},{10,... | collective-permute-start | bytes 7667720 | tf_op jit(solution)/shard_map/ppermute | solution.py:685
  194.0 12.3 %collective-permute-start.18 = (f32[624,1024]{1,0:T(8,128)}, f32[624,1024]{1,0:T(8,128)}, u32[]{:S(2)}, u32[]{:S(2)}) collective-permute-start(f32[624,1024]{1,0:T(8,128)} %collective-permute-done.9.refs_1_), channel_id=1, source_target_pairs={{0,1},{1,0},{2,3},{3,2},{4,5},{5,4},{6,7},{7,6},{8,9},{9,8},{10,11... | collective-permute-start | bytes 7667720 | tf_op jit(solution)/shard_map/ppermute | solution.py:685
  195.0 6.2 collective-permute-start.14
  201.2 5.1 collective-permute-start.19
  201.6 55.8 %collective-permute-start.21 = (f32[608,1024]{1,0:T(8,128)}, f32[608,1024]{1,0:T(8,128)}, u32[]{:S(2)}, u32[]{:S(2)}) collective-permute-start(f32[608,1024]{1,0:T(8,128)} %collective-permute-done.15.refs_0_), channel_id=1, source_target_pairs={{0,4},{1,5},{2,6},{3,7},{4,0},{5,1},{6,2},{7,3},{8,12},{9,13},{10,... | collective-permute-start | bytes 7471112 | tf_op jit(solution)/shard_map/ppermute | solution.py:685
  206.3 52.1 %copy-start.1 = (f32[8,1232]{1,0:T(8,128)S(1)}, f32[8,1232]{1,0:T(8,128)}, u32[]{:S(2)}) copy-start(f32[8,1232]{1,0:T(8,128)} %get-tuple-element.101.refs_0_) | copy-start | bytes 118276
  257.4 9.8 %collective-permute-start.24 = (f32[624,1024]{1,0:T(8,128)}, f32[624,1024]{1,0:T(8,128)}, u32[]{:S(2)}, u32[]{:S(2)}) collective-permute-start(f32[624,1024]{1,0:T(8,128)} %collective-permute-done.22.refs_1_), channel_id=1, source_target_pairs={{0,1},{1,0},{2,3},{3,2},{4,5},{5,4},{6,7},{7,6},{8,9},{9,8},{10,11... | collective-permute-start | bytes 7667720 | tf_op jit(solution)/shard_map/ppermute | solution.py:685
  258.4 8.8 %collective-permute-start.23 = (f32[608,1024]{1,0:T(8,128)}, f32[608,1024]{1,0:T(8,128)}, u32[]{:S(2)}, u32[]{:S(2)}) collective-permute-start(f32[608,1024]{1,0:T(8,128)} %collective-permute-done.21.refs_0_), channel_id=1, source_target_pairs={{0,1},{1,0},{2,3},{3,2},{4,5},{5,4},{6,7},{7,6},{8,9},{9,8},{10,11... | collective-permute-start | bytes 7471112 | tf_op jit(solution)/shard_map/ppermute | solution.py:685
  258.4 3.3 collective-permute-start.6
  259.5 3.9 collective-permute-start.7
  261.5 3.6 collective-permute-start.8
  261.7 1.7 copy-start.2
  288.8 9.2 %collective-permute-start.25 = (f32[1088,1024]{1,0:T(8,128)}, f32[1088,1024]{1,0:T(8,128)}, u32[]{:S(2)}, u32[]{:S(2)}) collective-permute-start(f32[1088,1024]{1,0:T(8,128)} %get-tuple-element.111), channel_id=1, source_target_pairs={{0,1},{1,0},{2,3},{3,2},{4,5},{5,4},{6,7},{7,6},{8,9},{9,8},{10,11... | collective-permute-start | bytes 13369352 | tf_op jit(solution)/shard_map/ppermute | solution.py:685
  364.4 179.0 %collective-permute-start.35 = (f32[1280,1024]{1,0:T(8,128)}, f32[1280,1024]{1,0:T(8,128)}, u32[]{:S(2)}, u32[]{:S(2)}) collective-permute-start(f32[1280,1024]{1,0:T(8,128)} %get-tuple-element.119), channel_id=1, source_target_pairs={{0,2},{1,5},{2,0},{3,7},{4,6},{5,1},{6,4},{7,3},{8,10},{9,13},{10,... | collective-permute-start | bytes 15728648 | tf_op jit(solution)/shard_map/ppermute | solution.py:691
  364.6 119.2 %collective-permute-start.32 = (f32[1088,1024]{1,0:T(8,128)}, f32[1088,1024]{1,0:T(8,128)}, u32[]{:S(2)}, u32[]{:S(2)}) collective-permute-start(f32[1088,1024]{1,0:T(8,128)} %get-tuple-element.111), channel_id=1, source_target_pairs={{0,2},{1,5},{2,0},{3,7},{4,6},{5,1},{6,4},{7,3},{8,10},{9,13},{10,... | collective-permute-start | bytes 13369352 | tf_op jit(solution)/shard_map/ppermute | solution.py:691
  365.9 56.6 %collective-permute-start.30 = (f32[1232,256]{1,0:T(8,128)}, f32[1232,256]{1,0:T(8,128)}, u32[]{:S(2)}, u32[]{:S(2)}) collective-permute-start(f32[1232,256]{1,0:T(8,128)} %get-tuple-element.126.refs_0_), channel_id=1, source_target_pairs={{0,16},{8,24},{16,0},{24,8},{1,17},{9,25},{17,1},{25,9},{2,18},{10... | collective-permute-start | bytes 3784712 | tf_op jit(solution)/shard_map/ppermute | solution.py:688
  368.4 160.2 %collective-permute-start.29 = (f32[1232,256]{1,0:T(8,128)}, f32[1232,256]{1,0:T(8,128)}, u32[]{:S(2)}, u32[]{:S(2)}) collective-permute-start(f32[1232,256]{1,0:T(8,128)} %get-tuple-element.126.refs_0_), channel_id=1, source_target_pairs={{0,8},{8,0},{16,24},{24,16},{1,9},{9,1},{17,25},{25,17},{2,10},{10... | collective-permute-start | bytes 3784712 | tf_op jit(solution)/shard_map/ppermute | solution.py:688
  422.5 106.0 %collective-permute-start.31 = (f32[1232,256]{1,0:T(8,128)}, f32[1232,256]{1,0:T(8,128)}, u32[]{:S(2)}, u32[]{:S(2)}) collective-permute-start(f32[1232,256]{1,0:T(8,128)} %collective-permute-done.30.refs_2_), channel_id=1, source_target_pairs={{0,8},{8,0},{16,24},{24,16},{1,9},{9,1},{17,25},{25,17},{2,10},{10... | collective-permute-start | bytes 3784712 | tf_op jit(solution)/shard_map/ppermute | solution.py:688
  425.2 135.4 %collective-permute-start.34 = (f32[1280,1024]{1,0:T(8,128)}, f32[1280,1024]{1,0:T(8,128)}, u32[]{:S(2)}, u32[]{:S(2)}) collective-permute-start(f32[1280,1024]{1,0:T(8,128)} %get-tuple-element.119), channel_id=1, source_target_pairs={{0,1},{1,0},{2,3},{3,2},{4,5},{5,4},{6,7},{7,6},{8,9},{9,8},{10,11... | collective-permute-start | bytes 15728648 | tf_op jit(solution)/shard_map/ppermute | solution.py:685
  483.9 76.5 %collective-permute-start.33 = (f32[1088,1024]{1,0:T(8,128)}, f32[1088,1024]{1,0:T(8,128)}, u32[]{:S(2)}, u32[]{:S(2)}) collective-permute-start(f32[1088,1024]{1,0:T(8,128)} %collective-permute-done.32.refs_2_), channel_id=1, source_target_pairs={{0,1},{1,0},{2,3},{3,2},{4,5},{5,4},{6,7},{7,6},{8,9},{9,8},{10,11... | collective-permute-start | bytes 13369352 | tf_op jit(solution)/shard_map/ppermute | solution.py:685
  543.3 68.1 %collective-permute-start.39 = (f32[1280,1024]{1,0:T(8,128)}, f32[1280,1024]{1,0:T(8,128)}, u32[]{:S(2)}, u32[]{:S(2)}) collective-permute-start(f32[1280,1024]{1,0:T(8,128)} %collective-permute-done.35.refs_3_), channel_id=1, source_target_pairs={{0,1},{1,0},{2,3},{3,2},{4,5},{5,4},{6,7},{7,6},{8,9},{9,8},{10,11... | collective-permute-start | bytes 15728648 | tf_op jit(solution)/shard_map/ppermute | solution.py:685
  543.4 67.0 %collective-permute-start.40 = (f32[776,1024]{1,0:T(8,128)}, f32[776,1024]{1,0:T(8,128)}, u32[]{:S(2)}, u32[]{:S(2)}) collective-permute-start(f32[776,1024]{1,0:T(8,128)} %get-tuple-element.125), channel_id=1, source_target_pairs={{0,1},{1,0},{2,3},{3,2},{4,5},{5,4},{6,7},{7,6},{8,9},{9,8},{10,11... | collective-permute-start | bytes 9535496 | tf_op jit(solution)/shard_map/ppermute | solution.py:685
  543.9 16.2 %collective-permute-start.26 = (f32[520,256]{1,0:T(8,128)}, f32[520,256]{1,0:T(8,128)}, u32[]{:S(2)}, u32[]{:S(2)}) collective-permute-start(f32[520,256]{1,0:T(8,128)} %constant_dynamic-slice_fusion), channel_id=1, source_target_pairs={{0,8},{8,0},{16,24},{24,16},{1,9},{9,1},{17,25},{25,17},{2,10},{10... | collective-permute-start | bytes 1597448 | tf_op jit(solution)/shard_map/ppermute | solution.py:688
  560.1 67.7 %collective-permute-start.41 = (f32[776,1024]{1,0:T(8,128)}, f32[776,1024]{1,0:T(8,128)}, u32[]{:S(2)}, u32[]{:S(2)}) collective-permute-start(f32[776,1024]{1,0:T(8,128)} %get-tuple-element.125), channel_id=1, source_target_pairs={{0,2},{1,5},{2,0},{3,7},{4,6},{5,1},{6,4},{7,3},{8,10},{9,13},{10,... | collective-permute-start | bytes 9535496 | tf_op jit(solution)/shard_map/ppermute | solution.py:691
  560.4 34.3 %collective-permute-start.27 = (f32[520,256]{1,0:T(8,128)}, f32[520,256]{1,0:T(8,128)}, u32[]{:S(2)}, u32[]{:S(2)}) collective-permute-start(f32[520,256]{1,0:T(8,128)} %constant_dynamic-slice_fusion), channel_id=1, source_target_pairs={{0,16},{8,24},{16,0},{24,8},{1,17},{9,25},{17,1},{25,9},{2,18},{10... | collective-permute-start | bytes 1597448 | tf_op jit(solution)/shard_map/ppermute | solution.py:688
  560.6 49.3 %collective-permute-start.28 = (f32[520,256]{1,0:T(8,128)}, f32[520,256]{1,0:T(8,128)}, u32[]{:S(2)}, u32[]{:S(2)}) collective-permute-start(f32[520,256]{1,0:T(8,128)} %constant_dynamic-slice_fusion), channel_id=1, source_target_pairs={{0,24},{8,16},{16,8},{24,0},{1,25},{9,17},{17,9},{25,1},{2,26},{10... | collective-permute-start | bytes 1597448 | tf_op jit(solution)/shard_map/ppermute | solution.py:688
  609.9 8.2 %collective-permute-start.36 = (f32[520,256]{1,0:T(8,128)}, f32[520,256]{1,0:T(8,128)}, u32[]{:S(2)}, u32[]{:S(2)}) collective-permute-start(f32[520,256]{1,0:T(8,128)} %collective-permute-done.26.refs_1_), channel_id=1, source_target_pairs={{0,1},{1,0},{2,3},{3,2},{4,5},{5,4},{6,7},{7,6},{8,9},{9,8},{10,11... | collective-permute-start | bytes 1597448 | tf_op jit(solution)/shard_map/ppermute | solution.py:685
  610.4 7.7 %collective-permute-start.37 = (f32[520,256]{1,0:T(8,128)}, f32[520,256]{1,0:T(8,128)}, u32[]{:S(2)}, u32[]{:S(2)}) collective-permute-start(f32[520,256]{1,0:T(8,128)} %collective-permute-done.27.refs_2_), channel_id=1, source_target_pairs={{0,1},{1,0},{2,3},{3,2},{4,5},{5,4},{6,7},{7,6},{8,9},{9,8},{10,11... | collective-permute-start | bytes 1597448 | tf_op jit(solution)/shard_map/ppermute | solution.py:685
  610.4 7.7 %collective-permute-start.38 = (f32[520,256]{1,0:T(8,128)}, f32[520,256]{1,0:T(8,128)}, u32[]{:S(2)}, u32[]{:S(2)}) collective-permute-start(f32[520,256]{1,0:T(8,128)} %collective-permute-done.28.refs_3_), channel_id=1, source_target_pairs={{0,1},{1,0},{2,3},{3,2},{4,5},{5,4},{6,7},{7,6},{8,9},{9,8},{10,11... | collective-permute-start | bytes 1597448 | tf_op jit(solution)/shard_map/ppermute | solution.py:685
  627.9 6.0 collective-permute-start.42
  (2 other events, 1.2 us)
Sparse Core Ops, SparseCore 0:
  140.3 90.6 reduce-scatter.1
  426.1 56.7 all-reduce.4
